TPU v7x, 32 devices: a whole 2x2x4 slice. The times are simulated.
32 devices in a mesh: events: 2 (over y), blk: 4 (over z), sub: 2 (over x), pair: 2 (over core).
Axes of the slice: x: 2, y: 2, z: 4, core: 2. Of those that a mesh axis runs over, the one named last changes fastest.
Arguments:
- synthetic: bfloat16 [2560, 4096], P(('events', 'sub', 'pair'), 'blk'), parts along dimension 0, may hold values from -6 to 6
- observed: bfloat16 [2560, 4096], P(('events', 'sub', 'pair'), 'blk'), parts along dimension 0, may hold values from -6 to 6
- station_weights: int32 [2560], P('events'), parts along dimension 0, may hold values from 1 to 4
- pair_mask: int32 [32, 16], P('events'), parts along dimension 0, may hold values from 0 to 1, as said below
Outputs:
- adjoint_traces: bfloat16 [2560, 4096], P(('events', 'sub', 'pair'), 'blk'), parts along dimension 0
There are 2 independent parts, one for each index of `events`. A program takes and returns all parts, laid end to end along the dimension named above; each array names one. Nothing has to cross between parts.
Inputs may be any that keep to these rules, and one draw needn't show every extreme that they name: pair_mask[p, q] is 1 where station pieces p and q are coupled; piece p holds stations p * 80 to (p + 1) * 80 - 1.
All inputs are finite; a program needn't handle non-finite values.
Results may differ from a plain program's by a relative error of at most 0.025.
Values may be sent and summed in bfloat16 or wider, within the bound.
No kernel may reach another device: no remote copies, remote signals or barrier semaphores. Data moves between devices by JAX's collectives and lax.ppermute only.
A program may use at most 64 MiB of HBM per device.

v0:
```python
import math

import jax
import jax.numpy as jnp
from jax import lax
from jax.sharding import PartitionSpec as P

NT = 4096
NF = 512
F_LO = 64


epsilon = 1e-06


def from_behind(value, axis, steps):
    count = lax.axis_size(axis)
    pairs = [(source, (source + steps) % count) for source in range(count)]
    return lax.ppermute(value, axis, pairs)


def make_basis(first_sample, sample_count):
    sample_index = first_sample + jnp.arange(sample_count, dtype=jnp.int32)
    bin_index = F_LO + jnp.arange(NF, dtype=jnp.int32)
    phases = sample_index[:, None] * bin_index[None, :] % NT
    angles = phases.astype(jnp.float32) * (2.0 * math.pi / NT)
    return jnp.concatenate([jnp.cos(angles), -jnp.sin(angles)], axis=1).astype(jnp.bfloat16)


def spectral_rate(spectrum):
    angular = 2.0 * math.pi / NT * (F_LO + jnp.arange(NF, dtype=jnp.int32)).astype(jnp.float32)
    widened = spectrum.astype(jnp.float32)
    return jnp.concatenate([-angular * widened[:, NF:], angular * widened[:, :NF]], axis=1).astype(
        jnp.bfloat16
    )


def shards(synthetic, observed, station_weights, pair_mask):
    cycle_size = lax.axis_size("blk")
    groups = lax.axis_size("sub") * lax.axis_size("pair")
    block_index = lax.axis_index("blk")
    member = lax.axis_index("sub") * lax.axis_size("pair") + lax.axis_index("pair")
    time_span = synthetic.shape[1]
    piece_rows = synthetic.shape[0] // cycle_size
    stations = station_weights.shape[0]
    scale_factor = 1.0 / math.sqrt(NT)
    inverse_scale = 1.0 / math.sqrt(NF)
    contract_last = (((1,), (1,)), ((), ()))
    basis_rows = make_basis(block_index * time_span, time_span)
    summed = lax.psum_scatter(
        jnp.concatenate(
            [
                jnp.dot(synthetic, basis_rows, preferred_element_type=jnp.float32),
                jnp.dot(observed, basis_rows, preferred_element_type=jnp.float32),
            ],
            axis=1,
        ).astype(jnp.bfloat16),
        "blk",
        scatter_dimension=0,
        tiled=True,
    ).astype(jnp.float32)
    model_spec = (summed[:, : 2 * NF] * scale_factor).astype(jnp.bfloat16)
    data_spec = (summed[:, 2 * NF :] * scale_factor).astype(jnp.bfloat16)
    own_rates = jnp.concatenate([spectral_rate(model_spec), spectral_rate(data_spec)], axis=1)
    block_model, block_data = (
        lax.all_gather(model_spec, ("sub", "pair"), axis=0, tiled=True),
        lax.all_gather(data_spec, ("sub", "pair"), axis=0, tiled=True),
    )
    block_power = jnp.sum(jnp.square(spectral_rate(block_model).astype(jnp.float32)), axis=1)
    gains = station_weights.astype(jnp.float32).reshape(groups * cycle_size, piece_rows)
    block_gain = lax.dynamic_slice_in_dim(
        gains.reshape(groups, cycle_size, piece_rows), block_index, 1, 1
    ).reshape(groups * piece_rows)
    link_piece = jnp.maximum(pair_mask, pair_mask.T)
    block_link = lax.dynamic_slice_in_dim(
        link_piece.reshape(groups, cycle_size, groups * cycle_size), block_index, 1, 1
    ).reshape(groups, groups * cycle_size)
    factor = 4.0 / math.sqrt(stations)

    def pair_tile(running, carried, source):
        column_model = carried[:, : 2 * NF]
        column_data = carried[:, 2 * NF :]
        column_piece = member * cycle_size + source
        column_gain = lax.dynamic_slice_in_dim(gains, column_piece, 1, 0)[0]
        column_power = jnp.sum(jnp.square(column_model.astype(jnp.float32)), axis=1)
        active_flags = lax.dynamic_slice_in_dim(block_link, column_piece, 1, 1)[:, 0]
        link_rows = jnp.broadcast_to(
            active_flags.astype(jnp.float32)[:, None], (groups, piece_rows)
        ).reshape(groups * piece_rows)
        cross_model = lax.dot_general(
            block_model, column_model, contract_last, preferred_element_type=jnp.float32
        )
        cross_data = lax.dot_general(
            block_data, column_data, contract_last, preferred_element_type=jnp.float32
        )
        normalizer = 0.5 * (block_power[:, None] + column_power[None, :]) + epsilon
        coupling = (
            factor
            * block_gain[:, None]
            * column_gain[None, :]
            * link_rows[:, None]
            * (cross_model - cross_data)
            / normalizer
        ).astype(jnp.bfloat16)
        return running + jnp.dot(coupling, column_model, preferred_element_type=jnp.float32)

    running = jnp.zeros((groups * piece_rows, 2 * NF), jnp.float32)
    running = pair_tile(running, own_rates, block_index)

    def cycle_turn(turn_index, loop_state):
        current, ahead_rates, behind_rates = loop_state
        ahead_rates = from_behind(ahead_rates, "blk", 1)
        behind_rates = from_behind(behind_rates, "blk", -1)
        current = pair_tile(current, ahead_rates, (block_index - turn_index) % cycle_size)
        current = pair_tile(current, behind_rates, (block_index + turn_index) % cycle_size)
        return (current, ahead_rates, behind_rates)

    running, ahead_rates, behind_rates = lax.fori_loop(
        1, cycle_size // 2, cycle_turn, (running, own_rates, own_rates)
    )
    ahead_rates = from_behind(ahead_rates, "blk", 1)
    running = pair_tile(running, ahead_rates, (block_index - cycle_size // 2) % cycle_size)
    adjoint_spec = lax.psum_scatter(
        running.astype(jnp.bfloat16), ("sub", "pair"), scatter_dimension=0, tiled=True
    )
    return (
        lax.dot_general(
            lax.all_gather(adjoint_spec, "blk", axis=0, tiled=True),
            basis_rows,
            contract_last,
            preferred_element_type=jnp.float32,
        )
        * inverse_scale
    ).astype(jnp.bfloat16)


def solution(mesh):
    placed = (
        P(("events", "sub", "pair"), "blk"),
        P(("events", "sub", "pair"), "blk"),
        P("events"),
        P("events", None),
    )
    return jax.shard_map(
        shards,
        mesh=mesh,
        in_specs=placed,
        out_specs=P(("events", "sub", "pair"), "blk"),
        check_vma=False,
    )
```

profile of v0, /device:TPU:0, one launch (start us, length us, event | category | flops | bytes accessed | tf_op | source)
XLA Modules:
  0.0 146.9 jit_solution(12198449554490275419)
XLA Ops:
  6.5 0.0 copy-start
  6.5 0.0 reduce-scatter.3.cloned.1.call-start
  6.5 9.1 %cosine_convert_fusion = (bf16[1024,512]{1,0:T(8,128)(2,1)S(1)}, bf16[1024,512]{1,0:T(8,128)(2,1)S(1)}) fusion(s32[512]{0:T(512)S(1)} %iota_add_fusion.1, s32[1024]{0:T(1024)S(1)} %iota_add_fusion), kind=kLoop, calls=%fused_computation.10 | loop fusion | flops 8912896 | bytes 2103296 | tf_op jit(solution)/shard_map/convert.10
  15.7 0.0 copy-start.1
  15.7 0.0 copy-start.8
  15.7 0.9 fusion.6
  16.6 0.1 copy-done.1
  16.7 0.4 copy-done.3
  17.1 0.2 copy-done.8
  17.3 0.8 fusion.5
  18.1 1.2 pad_maximum_fusion.1
  19.3 0.0 reduce-scatter.3.cloned.1.call-update
  19.4 0.0 reduce-scatter.5.cloned.1.call-start
  19.5 0.6 copy-done.6
  20.0 0.1 reshape.76
  20.1 0.1 reshape_reshape.3
  20.2 0.1 copy.5
  20.3 0.1 constant_dynamic-slice_fusion
  20.4 0.1 copy.10
  20.5 0.1 broadcast_in_dim.19
  20.5 0.1 mul.278
  20.7 0.1 mul.271
  20.7 0.1 copy.11
  20.8 0.1 broadcast_in_dim.20
  20.9 0.1 mul.305
  21.0 0.1 copy.12
  21.1 0.1 broadcast_in_dim.21
  21.2 0.1 mul.313
  21.3 0.1 copy.13
  21.4 0.1 broadcast_in_dim.22
  21.4 0.1 mul.321
  21.5 0.6 fusion.101
  22.1 31.5 %reduce-scatter.3.cloned.1.call-done = bf16[80,2048]{1,0:T(8,128)(2,1)} async-done(((bf16[320,2048]{1,0:T(8,128)(2,1)}), bf16[80,2048]{1,0:T(8,128)(2,1)}) %reduce-scatter.3.cloned.1.call-update) | async-done | bytes 327696 | tf_op jit(solution)/shard_map/reduce_scatter | solution.py:50
  53.6 1.0 convert_element_type.134
  54.7 0.1 fusion.116
  54.8 7.9 %all_gather.9 = bf16[320,1024]{1,0:T(8,128)(2,1)S(1)} all-gather(bf16[80,1024]{1,0:T(8,128)(2,1)S(1)} %get-tuple-element.36), channel_id=1, replica_groups=mesh['events'=2,'blk'=4,'sub'=2,'pair'=2] {'sub','pair'}, dimensions={0}, use_global_device_ids=true | all-gather | bytes 819200 | tf_op jit(solution)/shard_map/all_gather | solution.py:66
  62.6 0.1 convert_element_type.140
  62.8 0.1 fusion.33
  62.9 1.0 fusion.94
  63.8 0.7 pad_maximum_fusion.5
  64.6 0.0 collective-permute-start
  64.6 3.8 %collective-permute-start.1 = (bf16[80,2048]{1,0:T(8,128)(2,1)}, bf16[80,2048]{1,0:T(8,128)(2,1)}, u32[]{:S(2)}, u32[]{:S(2)}) collective-permute-start(bf16[80,2048]{1,0:T(8,128)(2,1)} %pad_maximum_fusion.5), channel_id=1, source_target_pairs={{0,12},{4,0},{8,4},{12,8},{1,13},{5,1},{9,5},{13,9},{2,14},{6,2},{... | collective-permute-start | bytes 983048 | tf_op jit(solution)/shard_map/while/body/eval_jaxpr/ppermute | solution.py:19
  68.4 0.2 fusion.21
  68.6 7.4 %all_gather.10 = bf16[320,1024]{1,0:T(8,128)(2,1)S(1)} all-gather(bf16[80,1024]{1,0:T(8,128)(2,1)S(1)} %get-tuple-element.30), channel_id=1, replica_groups=mesh['events'=2,'blk'=4,'sub'=2,'pair'=2] {'sub','pair'}, dimensions={0}, use_global_device_ids=true | all-gather | bytes 819200 | tf_op jit(solution)/shard_map/all_gather | solution.py:67
  76.0 0.7 multiply_reduce_fusion.4
  76.7 0.2 multiply_reduce_fusion
  76.9 1.8 %fusion.19 = f32[320,1024]{1,0:T(8,128)S(1)} fusion(f32[320,80]{1,0:T(8,128)} %fusion.94, bf16[320,1024]{1,0:T(8,128)(2,1)S(1)} %all_gather.10, bf16[80,512]{1,0:T(8,128)(2,1)S(1)} %get-tuple-element.66, bf16[80,512]{1,0:T(8,128)(2,1)} %copy-done.4, f32[80]{0:T(128)} %multiply_reduce_fusion.4, f32[320]{0:T(512)S(1)} %multiply_reduce_fusion, ...), kind=kOutput, calls=%fused_computation.39 | convolution fusion | flops 105743360 | bytes 2400640 | tf_op jit(solution)/shard_map/dot_general | solution.py:105
  78.8 0.0 collective-permute-done
  78.8 0.1 collective-permute-start.2
  78.9 1.1 multiply_reduce_fusion.3
  79.9 1.2 fusion.28
  81.2 0.7 collective-permute-done.1
  81.9 1.9 %fusion.26 = f32[320,80]{1,0:T(8,128)} fusion(bf16[320,1024]{1,0:T(8,128)(2,1)S(1)} %all_gather.10, bf16[80,2048]{1,0:T(8,128)(2,1)} %collective-permute-done.1), kind=kOutput, calls=%fused_computation.55 | convolution fusion | flops 52428800 | bytes 921600 | tf_op jit(solution)/shard_map/while/body/eval_jaxpr/dot_general | solution.py:93
  83.8 2.9 %convolution_add_fusion.2 = f32[320,1024]{1,0:T(8,128)} fusion(f32[320,1024]{1,0:T(8,128)S(1)} %fusion.19, f32[320,80]{1,0:T(8,128)S(1)} %fusion.28, bf16[320,1024]{1,0:T(8,128)(2,1)S(1)} %all_gather.9, bf16[80,2048]{1,0:T(8,128)(2,1)} %collective-permute-done, f32[80]{0:T(128)S(1)} %multiply_reduce_fusion.3, f32[320]{0:T(512)S(1)} %mul.305, ...), kind=kOutput, calls=%fused_computation.14 | convolution fusion | flops 105415680 | bytes 3711360 | tf_op jit(solution)/shard_map/while/body/eval_jaxpr/dot_general | solution.py:105
  86.7 1.0 multiply_reduce_fusion.2
  87.8 2.4 %convolution_add_fusion.1 = f32[320,1024]{1,0:T(8,128)S(1)} fusion(f32[320,1024]{1,0:T(8,128)} %convolution_add_fusion.2, f32[320,80]{1,0:T(8,128)} %fusion.26, bf16[320,1024]{1,0:T(8,128)(2,1)S(1)} %all_gather.9, bf16[80,2048]{1,0:T(8,128)(2,1)} %collective-permute-done.1, f32[80]{0:T(128)S(1)} %multiply_reduce_fusion.2, f32[320]{0:T(512)S(1)} %mul.313, ...), kind=kOutput, calls=%fused_computation.13 | convolution fusion | flops 105415680 | bytes 3711360 | tf_op jit(solution)/shard_map/while/body/eval_jaxpr/dot_general | solution.py:105
  90.2 0.7 collective-permute-done.2
  90.9 1.2 fusion.24
  92.2 1.0 multiply_reduce_fusion.1
  93.2 2.7 %fusion.3 = bf16[320,1024]{1,0:T(8,128)(2,1)} fusion(f32[320,1024]{1,0:T(8,128)S(1)} %convolution_add_fusion.1, f32[320,80]{1,0:T(8,128)S(1)} %fusion.24, bf16[320,1024]{1,0:T(8,128)(2,1)S(1)} %all_gather.9, bf16[80,2048]{1,0:T(8,128)(2,1)} %collective-permute-done.2, f32[80]{0:T(128)S(1)} %multiply_reduce_fusion.1, f32[320]{0:T(512)S(1)} %mul.321, ...), kind=kOutput, calls=%fused_computation.15 | convolution fusion | flops 105743360 | bytes 3056000 | tf_op jit(solution)/shard_map/dot_general | solution.py:105
  95.9 0.0 reduce-scatter.5.cloned.1.call-update
  95.9 23.2 %reduce-scatter.5.cloned.1.call-done = bf16[80,1024]{1,0:T(8,128)(2,1)} async-done(((bf16[320,1024]{1,0:T(8,128)(2,1)}), bf16[80,1024]{1,0:T(8,128)(2,1)}) %reduce-scatter.5.cloned.1.call-update) | async-done | bytes 163856 | tf_op jit(solution)/shard_map/reduce_scatter | solution.py:123
  119.1 18.0 %all_gather.11 = bf16[320,1024]{1,0:T(8,128)(2,1)S(1)} all-gather(bf16[80,1024]{1,0:T(8,128)(2,1)} %reduce-scatter.5.cloned.1.call-done), channel_id=1, replica_groups=mesh['events'=2,'blk'=4,'sub'=2,'pair'=2] {'blk'}, dimensions={0}, use_global_device_ids=true | all-gather | bytes 819200 | tf_op jit(solution)/shard_map/all_gather | solution.py:128
  137.1 3.0 %fusion.4 = bf16[320,1024]{1,0:T(8,128)(2,1)} fusion(bf16[320,1024]{1,0:T(8,128)(2,1)S(1)} %all_gather.11, bf16[1024,512]{1,0:T(8,128)(2,1)} %copy-done.3, bf16[1024,512]{1,0:T(8,128)(2,1)S(1)} %copy-done.2), kind=kOutput, calls=%fused_computation.16 | convolution fusion | flops 675938304 | bytes 3407872 | tf_op jit(solution)/shard_map/dot_general | solution.py:127
  (21 shorter events, 0.1 us)
Async XLA Ops:
  6.5 9.2 %copy-start = (bf16[320,1024]{1,0:T(8,128)(2,1)S(1)}, bf16[320,1024]{1,0:T(8,128)(2,1)}, u32[]{:S(2)}) copy-start(bf16[320,1024]{1,0:T(8,128)(2,1)} %param.5) | copy-start | bytes 1966084
  6.5 47.1 %reduce-scatter.3.cloned.1.call-start = ((), (), s32[]{:S(2)}) async-start(), calls=%async_computation.2 | async-start | bytes 1638400 | tf_op jit(solution)/shard_map/reduce_scatter | solution.py:50
  15.7 1.0 copy-start.1
  15.7 1.4 copy-start.3
  15.7 1.6 %copy-start.8 = (bf16[320,1024]{1,0:T(8,128)(2,1)S(1)}, bf16[320,1024]{1,0:T(8,128)(2,1)}, u32[]{:S(2)}) copy-start(bf16[320,1024]{1,0:T(8,128)(2,1)} %param.4) | copy-start | bytes 1966084
  19.3 0.7 copy-start.6
  19.3 0.9 copy-start.5
  19.4 99.8 %reduce-scatter.5.cloned.1.call-start = ((), (), s32[]{:S(2)}) async-start(), calls=%async_computation.3 | async-start | bytes 819200 | tf_op jit(solution)/shard_map/reduce_scatter | solution.py:123
  62.9 1.7 %copy-start.4 = (bf16[80,512]{1,0:T(8,128)(2,1)}, bf16[80,512]{1,0:T(8,128)(2,1)S(1)}, u32[]{:S(2)}) copy-start(bf16[80,512]{1,0:T(8,128)(2,1)S(1)} %get-tuple-element.67) | copy-start | bytes 245764
  64.6 14.2 %collective-permute-start = (bf16[80,2048]{1,0:T(8,128)(2,1)}, bf16[80,2048]{1,0:T(8,128)(2,1)}, u32[]{:S(2)}, u32[]{:S(2)}) collective-permute-start(bf16[80,2048]{1,0:T(8,128)(2,1)} %pad_maximum_fusion.5), channel_id=1, source_target_pairs={{0,4},{4,8},{8,12},{12,0},{1,5},{5,9},{9,13},{13,1},{2,6},{6,10},{... | collective-permute-start | bytes 983048 | tf_op jit(solution)/shard_map/while/body/eval_jaxpr/ppermute | solution.py:19
  64.6 17.3 %collective-permute-start.1 = (bf16[80,2048]{1,0:T(8,128)(2,1)}, bf16[80,2048]{1,0:T(8,128)(2,1)}, u32[]{:S(2)}, u32[]{:S(2)}) collective-permute-start(bf16[80,2048]{1,0:T(8,128)(2,1)} %pad_maximum_fusion.5), channel_id=1, source_target_pairs={{0,12},{4,0},{8,4},{12,8},{1,13},{5,1},{9,5},{13,9},{2,14},{6,2},{... | collective-permute-start | bytes 983048 | tf_op jit(solution)/shard_map/while/body/eval_jaxpr/ppermute | solution.py:19
  78.8 5.0 %copy-start.7 = (f32[80]{0:T(128)S(1)}, f32[80]{0:T(128)}, u32[]{:S(2)}) copy-start(f32[80]{0:T(128)} %get-tuple-element.58) | copy-start | bytes 964
  78.8 12.1 %collective-permute-start.2 = (bf16[80,2048]{1,0:T(8,128)(2,1)}, bf16[80,2048]{1,0:T(8,128)(2,1)}, u32[]{:S(2)}, u32[]{:S(2)}) collective-permute-start(bf16[80,2048]{1,0:T(8,128)(2,1)} %collective-permute-done), channel_id=1, source_target_pairs={{0,4},{4,8},{8,12},{12,0},{1,5},{5,9},{9,13},{13,1},{2,6},{6,10},{... | collective-permute-start | bytes 983048 | tf_op jit(solution)/shard_map/ppermute | solution.py:19
  95.9 41.2 %copy-start.2 = (bf16[1024,512]{1,0:T(8,128)(2,1)S(1)}, bf16[1024,512]{1,0:T(8,128)(2,1)}, u32[]{:S(2)}) copy-start(bf16[1024,512]{1,0:T(8,128)(2,1)} %copy-done.1) | copy-start | bytes 3145732
Sparse Core Ops, SparseCore 0:
  19.5 34.1 reduce-scatter.2
  96.1 23.0 reduce-scatter.4
where the time goes:
time: 147 us
  waiting for transfers between devices  56.2 us (38%)
  blocking collectives  33.3 us (23%)
  matrix products  19.9 us (14%)
  other arithmetic  16.7 us (11%)
  between operations  13.7 us (9%)
  starting transfers between devices  3.93 us (3%)
  local copies, waits for them, and re-layouts  3.28 us (2%)
    reduce_scatter x1, waiting for transfers between devices, shards(): lax.psum_scatter(jnp.concatenate([jnp.dot(synthetic, basis_rows, preferre...  31.5 us
    reduce_scatter x1, waiting for transfers between devices, shards(): lax.psum_scatter(running.astype(jnp.bfloat16), ('sub', 'pair'), scatter_d...  23.2 us
    all_gather x1, blocking collectives, shards(): lax.all_gather(adjoint_spec, 'blk', axis=0, tiled=True)  18 us
    dot_general x4, matrix products, pair_tile(): jnp.dot(coupling, column_model, preferred_element_type=jnp.float32)  9.86 us
    another operation x3, other arithmetic  9.36 us
    all_gather x1, blocking collectives, shards(): lax.all_gather(model_spec, ('sub', 'pair'), axis=0, tiled=True)  7.88 us
    all_gather x1, blocking collectives, shards(): lax.all_gather(data_spec, ('sub', 'pair'), axis=0, tiled=True)  7.43 us
    dot_general x3, matrix products, pair_tile(): lax.dot_general(block_data, column_data, contract_last, preferred_element...  4.38 us
  transfers between devices with their start and end apart: 5, of which 4 were waited for; matrix products, arithmetic and copies ran while one was open for 11% of the time, Pallas kernels for 0%

commit v1 on v0

v1 whole, which is shorter than its diff:
```python
import functools
import math

import jax
import jax.numpy as jnp
from jax import lax
from jax.experimental import pallas as pl
from jax.experimental.pallas import tpu as pltpu
from jax.sharding import PartitionSpec as P

NT = 4096
NF = 512
F_LO = 64

epsilon = 1e-06
CONTRACT_LAST = (((1,), (1,)), ((), ()))


def shift(value, axis, steps):
    count = lax.axis_size(axis)
    pairs = [(source, (source + steps) % count) for source in range(count)]
    return lax.ppermute(value, axis, pairs)


def sweep(count):
    order = []
    for near in range(1, count // 2 + 1):
        order.append(near)
        if (count - near) % count != near:
            order.append(count - near)
    return order


def cos_sin(samples):
    bins = F_LO + jnp.arange(NF, dtype=jnp.int32)
    phases = samples[:, None] * bins[None, :] % NT
    angles = phases.astype(jnp.float32) * (2.0 * math.pi / NT)
    return jnp.cos(angles), jnp.sin(angles)


def basis_kernel(per_step, low_rows, hc_ref, hs_ref, lc_ref, ls_ref, out_ref):
    step = pl.program_id(0)
    for h in range(per_step):
        hc = hc_ref[pl.ds(step * per_step + h, 1), :]
        hs = hs_ref[pl.ds(step * per_step + h, 1), :]
        lc = lc_ref[...]
        ls = ls_ref[...]
        rows = slice(h * low_rows, (h + 1) * low_rows)
        out_ref[rows, :NF] = (hc * lc - hs * ls).astype(jnp.bfloat16)
        out_ref[rows, NF:] = (-(hs * lc + hc * ls)).astype(jnp.bfloat16)


def make_basis(firsts, span):
    low_rows = math.gcd(span, 64)
    low_c, low_s = cos_sin(jnp.arange(low_rows, dtype=jnp.int32))
    highs = (firsts[:, None] + jnp.arange(0, span, low_rows, dtype=jnp.int32)[None, :]).reshape(-1)
    high_c, high_s = cos_sin(highs)
    per_step = math.gcd(highs.shape[0], 4)
    whole = lambda a: pl.BlockSpec(a.shape, lambda i: (0, 0))
    rows = highs.shape[0] * low_rows
    return pl.pallas_call(
        functools.partial(basis_kernel, per_step, low_rows),
        grid=(highs.shape[0] // per_step,),
        in_specs=[whole(high_c), whole(high_s), whole(low_c), whole(low_s)],
        out_specs=pl.BlockSpec((per_step * low_rows, 2 * NF), lambda i: (i, 0)),
        out_shape=jax.ShapeDtypeStruct((rows, 2 * NF), jnp.bfloat16),
        cost_estimate=pl.CostEstimate(
            flops=8 * rows * NF, bytes_accessed=4 * rows * NF, transcendentals=0
        ),
        name="basis",
    )(high_c, high_s, low_c, low_s)


def angular_row():
    bins = F_LO + lax.broadcasted_iota(jnp.int32, (1, NF), 1)
    return 2.0 * math.pi / NT * bins.astype(jnp.float32)


def rate_of(re, im):
    angular = angular_row()
    return jnp.concatenate([-angular * im, angular * re], axis=1).astype(jnp.bfloat16)


def tile_kernel(first, rows_ref, power_ref, coef_ref, gain_ref, col_ref, *rest):
    out_ref = rest[-1]
    col = col_ref[...].astype(jnp.float32)
    model_rate = rate_of(col[:, :NF], col[:, NF : 2 * NF])
    data_rate = rate_of(-col[:, 2 * NF : 3 * NF], -col[:, 3 * NF :])
    both = jnp.concatenate([model_rate, data_rate], axis=1)
    cross = lax.dot_general(
        rows_ref[...], both, CONTRACT_LAST, preferred_element_type=jnp.float32
    )
    col_power = lax.dot_general(
        jnp.ones((8, 2 * NF), jnp.float32),
        jnp.square(model_rate.astype(jnp.float32)),
        CONTRACT_LAST,
        precision=lax.Precision.HIGHEST,
        preferred_element_type=jnp.float32,
    )[0:1, :]
    normalizer = 0.5 * (power_ref[...] + col_power) + epsilon
    coupling = (coef_ref[...] * gain_ref[...] * cross / normalizer).astype(jnp.bfloat16)
    update = jnp.dot(coupling, model_rate, preferred_element_type=jnp.float32)
    if first:
        out_ref[...] = update
    else:
        out_ref[...] = rest[0][...] + update


def pair_tile(running, rows, row_power, coef, gain, col):
    args = [rows, row_power, coef, gain, col]
    aliases = {}
    if running is not None:
        aliases = {len(args): 0}
        args.append(running)
    height, width = rows.shape[0], col.shape[0]
    return pl.pallas_call(
        functools.partial(tile_kernel, running is None),
        in_specs=[pl.BlockSpec(memory_space=pltpu.VMEM)] * len(args),
        out_specs=pl.BlockSpec(memory_space=pltpu.VMEM),
        out_shape=jax.ShapeDtypeStruct((height, 2 * NF), jnp.float32),
        input_output_aliases=aliases,
        cost_estimate=pl.CostEstimate(
            flops=12 * height * width * NF,
            bytes_accessed=16 * height * NF,
            transcendentals=0,
        ),
        name="pair_tile",
    )(*args)


def shards(synthetic, observed, station_weights, pair_mask):
    levels = lax.axis_size("blk")
    subs = lax.axis_size("sub")
    pairs = lax.axis_size("pair")
    level = lax.axis_index("blk")
    sub = lax.axis_index("sub")
    pair = lax.axis_index("pair")
    span = synthetic.shape[1]
    piece = synthetic.shape[0] // levels
    stations = station_weights.shape[0]

    def owned_by(steps):
        owner = (level + steps) % levels
        return jnp.concatenate(
            [
                lax.dynamic_slice_in_dim(synthetic, owner * piece, piece, 0),
                lax.dynamic_slice_in_dim(observed, owner * piece, piece, 0),
            ],
            axis=0,
        )

    order = sweep(levels)
    blocks = {0: owned_by(0)}
    for steps in order:
        blocks[steps] = shift(owned_by(steps), "blk", steps)
    arrivals = [0] + order
    firsts = jnp.stack([(level - steps) % levels * span for steps in arrivals]).astype(jnp.int32)
    basis = make_basis(firsts, span)
    total = None
    for place, steps in enumerate(arrivals):
        part = jnp.dot(
            blocks[steps],
            basis[place * span : (place + 1) * span],
            preferred_element_type=jnp.float32,
        )
        total = part if total is None else total + part
    spec = (total * (1.0 / math.sqrt(NT))).astype(jnp.bfloat16)
    own = jnp.concatenate([spec[:piece], spec[piece:]], axis=1)

    columns = {0: own}
    for steps in order:
        columns[steps] = shift(own, "blk", steps)
    blocks_of_rows = []
    members = []
    for s in range(subs):
        here = own if s == 0 else shift(own, "sub", s)
        for q in range(pairs):
            blocks_of_rows.append(here if q == 0 else shift(here, "pair", q))
            members.append((sub - s) % subs * pairs + (pair - q) % pairs)
    rows = jnp.concatenate(blocks_of_rows, axis=0)
    members = jnp.stack(members)
    member = sub * pairs + pair

    gains = station_weights.astype(jnp.float32).reshape(-1, piece)
    link = jnp.maximum(pair_mask, pair_mask.T).astype(jnp.float32)
    row_pieces = members * levels + level
    row_gain = gains[row_pieces].reshape(-1, 1)
    row_link = link[row_pieces]
    factor = 4.0 / math.sqrt(stations)
    widened = rows[:, : 2 * NF].astype(jnp.float32)
    row_rate = rate_of(widened[:, :NF], widened[:, NF:])
    row_power = jnp.sum(jnp.square(row_rate.astype(jnp.float32)), axis=1, keepdims=True)

    running = None
    for steps in arrivals:
        column_piece = member * levels + (level - steps) % levels
        active = lax.dynamic_slice_in_dim(row_link, column_piece, 1, 1)
        coef = factor * row_gain * jnp.repeat(active, piece, axis=0)
        gain = lax.dynamic_slice_in_dim(gains, column_piece, 1, 0)
        running = pair_tile(running, rows, row_power, coef, gain, columns[steps])

    partial = running.reshape(subs, pairs, piece, 2 * NF)
    held = partial[:, 0]
    for q in range(1, pairs):
        sent = partial[:, q].astype(jnp.bfloat16)
        held = held + shift(sent, "pair", -q).astype(jnp.float32)
    adjoint = held[0]
    for s in range(1, subs):
        adjoint = adjoint + shift(held[s].astype(jnp.bfloat16), "sub", -s).astype(jnp.float32)
    adjoint = adjoint.astype(jnp.bfloat16)

    gathered = jnp.zeros((levels * piece, 2 * NF), jnp.bfloat16)
    for steps in arrivals:
        arrived = adjoint if steps == 0 else shift(adjoint, "blk", steps)
        gathered = lax.dynamic_update_slice_in_dim(
            gathered, arrived, (level - steps) % levels * piece, 0
        )
    return (
        lax.dot_general(
            gathered, basis[:span], CONTRACT_LAST, preferred_element_type=jnp.float32
        )
        * (1.0 / math.sqrt(NF))
    ).astype(jnp.bfloat16)


def solution(mesh):
    placed = (
        P(("events", "sub", "pair"), "blk"),
        P(("events", "sub", "pair"), "blk"),
        P("events"),
        P("events", None),
    )
    return jax.shard_map(
        shards,
        mesh=mesh,
        in_specs=placed,
        out_specs=P(("events", "sub", "pair"), "blk"),
        check_vma=False,
    )
```

time: 147 us -> 121 us (0.82)
  blocking collectives: 33.3 us -> 0 us
  Pallas kernels: 0 us -> 25.1 us
  starting transfers between devices: 3.93 us -> 18.9 us
  between operations: 13.7 us -> 0.28 us
  other arithmetic: 16.7 us -> 4.2 us
  local copies, waits for them, and re-layouts: 3.28 us -> 11.5 us
  matrix products: 19.9 us -> 11.8 us
  waiting for transfers between devices: 56.2 us -> 48.3 us
    reduce_scatter x2 -> x0, waiting for transfers between devices: 54.7 us -> none  [the longest x1 31.5 us: shards(): lax.psum_scatter(jnp.concatenate([jnp.dot(synthetic, basis_rows, preferre...]
    ppermute x3 -> x14, waiting for transfers between devices: 1.43 us -> 48.3 us  [shift(): return lax.ppermute(value, axis, pairs)]
    all_gather x3 -> x0, blocking collectives: 33.3 us -> none  [the longest x1 18 us: shards(): lax.all_gather(adjoint_spec, 'blk', axis=0, tiled=True)]
    pallas_call x0 -> x5, Pallas kernels: none -> 25.1 us  [the longest x4 16.1 us: pair_tile(): pl.pallas_call(functools.partial(tile_kernel, running is None), in_specs=...]
    ppermute x3 -> x14, starting transfers between devices: 3.88 us -> 18.9 us  [shift(): return lax.ppermute(value, axis, pairs)]
    another operation x3 -> x2, other arithmetic: 9.36 us -> 0.24 us
    dot_general x11 -> x5, matrix products: 19.9 us -> 11.8 us  [the longest x4 8.52 us: shards(): jnp.dot(blocks[steps], basis[place * span:(place + 1) * span], preferred_...]
    reduce_sum x5 -> x1, other arithmetic: 4.09 us -> 0.23 us  [shards(): jnp.sum(jnp.square(row_rate.astype(jnp.float32)), axis=1, keepdims=True)]
  transfers between devices with their start and end apart: 5 -> 14, of which waited for: 4 -> 9; matrix products, arithmetic and copies ran while one was open for 11% -> 13% of each run, Pallas kernels for 0% -> 17%
where the time goes in v1:
time: 121 us; the launch traced here: 120 us
  waiting for transfers between devices  48.3 us (40%)
  Pallas kernels  25.1 us (21%)
  starting transfers between devices  18.9 us (16%)
  matrix products  11.8 us (10%)
  local copies, waits for them, and re-layouts  11.5 us (10%)
  other arithmetic  4.2 us (3%)
    ppermute x14, waiting for transfers between devices, shift(): return lax.ppermute(value, axis, pairs)  48.3 us
    ppermute x14, starting transfers between devices, shift(): return lax.ppermute(value, axis, pairs)  18.9 us
    pallas_call x4, Pallas kernels, pair_tile(): pl.pallas_call(functools.partial(tile_kernel, running is None), in_specs=...  16.1 us
    pallas_call x1, Pallas kernels, make_basis(): pl.pallas_call(functools.partial(basis_kernel, per_step, low_rows), grid=...  8.94 us
    dot_general x4, matrix products, shards(): jnp.dot(blocks[steps], basis[place * span:(place + 1) * span], preferred_...  8.52 us
    dot_general x1, matrix products, shards(): lax.dot_general(gathered, basis[:span], CONTRACT_LAST, preferred_element_...  3.31 us
    mul x4, local copies, waits for them, and re-layouts, shards(): coef = factor * row_gain * jnp.repeat(active, piece, axis=0)  3.25 us
    unnamed x15, local copies, waits for them, and re-layouts  2.83 us
  transfers between devices with their start and end apart: 14, of which 9 were waited for; matrix products, arithmetic and copies ran while one was open for 13% of the time, Pallas kernels for 17%

profile of v1, /device:TPU:0, one launch (start us, length us, event | category | flops | bytes accessed | tf_op | source)
XLA Modules:
  0.0 120.1 jit_solution(8553822353541152208)
XLA Ops:
  0.0 1.5 %constant_dynamic-slice_fusion.12 = (bf16[80,1024]{1,0:T(8,128)(2,1)S(1)}, bf16[80,1024]{1,0:T(8,128)(2,1)S(1)}, bf16[80,1024]{1,0:T(8,128)(2,1)S(1)}, bf16[80,1...) fusion(bf16[320,1024]{1,0:T(8,128)(2,1)} %param.5, ...), kind=kLoop, calls=%fused_computation.81 | loop fusion | bytes 2621456 | tf_op jit(solution)/shard_map/dynamic_slice | solution.py:147
  1.6 5.1 %collective-permute-start.1 = (bf16[160,1024]{1,0:T(8,128)(2,1)S(1)}, bf16[160,1024]{1,0:T(8,128)(2,1)S(1)}, u32[]{:S(2)}, u32[]{:S(2)}) collective-permute-start(bf16[160,1024]{1,0:T(8,128)(2,1)S(1)} %pad_maximum_fusion.2), channel_id=1, source_target_pairs={{0,12},{4,0},{8,4},{12,8},{1,13},{5,1},{9,5},{13,9},{2,14},{6,2},{... | collective-permute-start | bytes 983048 | tf_op jit(solution)/shard_map/ppermute | solution.py:22
  6.7 0.1 collective-permute-start.2
  6.8 1.0 collective-permute-start
  7.9 0.1 pad_add_fusion
  8.0 0.1 broadcast_add_fusion
  8.0 0.1 add.234
  8.1 1.7 %fusion.50 = (f32[64,512]{1,0:T(8,128)}, f32[64,512]{1,0:T(8,128)}, f32[64,512]{1,0:T(8,128)}, f32[64,512]{1,0:T(8,128)}) fusion(s32[512]{0:T(512)S(1)} %iota_add_fusion, s32[64]{0:T(128)S(1)} %add.234), kind=kLoop, calls=%fused_computation.59 | loop fusion | flops 917504 | bytes 526592 | tf_op jit(solution)/shard_map/sin | solution.py:38
  9.9 8.9 %basis.1 = bf16[4096,1024]{1,0:T(8,128)(2,1)} custom-call(f32[64,512]{1,0:T(8,128)} %get-tuple-element.35.hc_ref, f32[64,512]{1,0:T(8,128)} %get-tuple-element.36.hs_ref, f32[64,512]{1,0:T(8,128)} %get-tuple-element.34.lc_ref, f32[64,512]{1,0:T(8,128)} %get-tuple-element.33.ls_ref), custom_call_target="tpu_custom_call" | custom-call | flops 16777216 | bytes 8388608 | tf_op jit(solution)/shard_map/basis/pallas_call | solution.py:61
  18.8 2.1 %fusion.8 = f32[160,1024]{1,0:T(8,128)S(1)} fusion(bf16[4096,1024]{1,0:T(8,128)(2,1)} %basis.1, bf16[80,1024]{1,0:T(8,128)(2,1)S(1)} %get-tuple-element.18, bf16[80,1024]{1,0:T(8,128)(2,1)S(1)} %get-tuple-element.39), kind=kOutput, calls=%fused_computation.10 | convolution fusion | flops 336199680 | bytes 3080192 | tf_op jit(solution)/shard_map/dot_general | solution.py:161
  20.9 0.1 fusion.64
  21.0 0.1 copy.10
  21.1 0.1 reshape.219
  21.2 0.0 collective-permute-done.1
  21.2 2.1 %fusion.2 = f32[160,1024]{1,0:T(8,128)S(1)} fusion(bf16[160,1024]{1,0:T(8,128)(2,1)S(1)} %collective-permute-done.1, bf16[4096,1024]{1,0:T(8,128)(2,1)} %basis.1), kind=kOutput, calls=%fused_computation.4 | convolution fusion | flops 335544320 | bytes 3080192 | tf_op jit(solution)/shard_map/dot_general | solution.py:161
  23.3 11.3 %collective-permute-done.2 = bf16[160,1024]{1,0:T(8,128)(2,1)S(1)} collective-permute-done((bf16[160,1024]{1,0:T(8,128)(2,1)S(1)}, bf16[160,1024]{1,0:T(8,128)(2,1)S(1)}, u32[]{:S(2)}, u32[]{:S(2)}) %collective-permute-start.2) | collective-permute-done | bytes 327712 | tf_op jit(solution)/shard_map/ppermute | solution.py:22
  34.6 2.1 %fusion = f32[160,1024]{1,0:T(8,128)S(1)} fusion(bf16[160,1024]{1,0:T(8,128)(2,1)S(1)} %collective-permute-done.2, bf16[4096,1024]{1,0:T(8,128)(2,1)} %basis.1), kind=kOutput, calls=%fused_computation.2 | convolution fusion | flops 335544320 | bytes 3080192 | tf_op jit(solution)/shard_map/dot_general | solution.py:161
  36.7 0.0 collective-permute-done
  36.7 2.2 %fusion.28 = bf16[160,1024]{1,0:T(8,128)(2,1)S(1)} fusion(f32[160,1024]{1,0:T(8,128)S(1)} %fusion, f32[160,1024]{1,0:T(8,128)S(1)} %fusion.2, f32[160,1024]{1,0:T(8,128)S(1)} %fusion.8, bf16[160,1024]{1,0:T(8,128)(2,1)S(1)} %collective-permute-done, bf16[4096,1024]{1,0:T(8,128)(2,1)} %basis.1), kind=kOutput, calls=%fused_computation.20 | convolution fusion | flops 336363520 | bytes 4718592 | tf_op jit(solution)/shard_map/dot_general | solution.py:161
  39.0 0.0 copy-start.1
  39.0 1.6 %collective-permute-start.4 = (bf16[80,2048]{1,0:T(8,128)(2,1)S(1)}, bf16[80,2048]{1,0:T(8,128)(2,1)S(1)}, u32[]{:S(2)}, u32[]{:S(2)}) collective-permute-start(bf16[80,2048]{1,0:T(8,128)(2,1)S(1)} %pad_maximum_fusion.4.col_ref), channel_id=1, source_target_pairs={{0,2},{2,0},{1,3},{3,1},{4,6},{6,4},{5,7},{7,5},{8,10},{10,8},{9,1... | collective-permute-start | bytes 983048 | tf_op jit(solution)/shard_map/ppermute | solution.py:22
  40.6 0.6 gather_fusion.1
  41.2 0.6 gather_fusion
  41.7 0.2 fusion.62
  42.0 0.1 collective-permute-start.3
  42.0 5.7 %collective-permute-done.4 = bf16[80,2048]{1,0:T(8,128)(2,1)S(1)} collective-permute-done((bf16[80,2048]{1,0:T(8,128)(2,1)S(1)}, bf16[80,2048]{1,0:T(8,128)(2,1)S(1)}, u32[]{:S(2)}, u32[]{:S(2)}) %collective-permute-start.4) | collective-permute-done | bytes 327712 | tf_op jit(solution)/shard_map/ppermute | solution.py:22
  47.7 0.1 broadcast_multiply_fusion
  47.8 0.8 mul.285.coef_ref
  48.6 0.8 mul.284.coef_ref
  49.4 0.8 mul.283.coef_ref
  50.2 0.8 mul.282.coef_ref
  51.0 0.6 constant_dynamic-slice_fusion
  51.6 0.0 collective-permute-start.8
  51.6 3.8 %collective-permute-start.7 = (bf16[80,2048]{1,0:T(8,128)(2,1)S(1)}, bf16[80,2048]{1,0:T(8,128)(2,1)S(1)}, u32[]{:S(2)}, u32[]{:S(2)}) collective-permute-start(bf16[80,2048]{1,0:T(8,128)(2,1)S(1)} %pad_maximum_fusion.4.col_ref), channel_id=1, source_target_pairs={{0,12},{4,0},{8,4},{12,8},{1,13},{5,1},{9,5},{13,9},{2,14},{6,2},{... | collective-permute-start | bytes 983048 | tf_op jit(solution)/shard_map/ppermute | solution.py:22
  55.5 0.0 collective-permute-start.6
  55.5 0.1 pad_maximum_fusion.rows_ref
  55.6 0.1 slice_convert_fusion.1
  55.7 0.2 fusion.33
  55.9 0.2 multiply_reduce_fusion
  56.1 0.6 copy-done
  56.7 0.8 broadcast_in_dim.6.power_ref
  57.5 3.7 %pair_tile.4.rest_0_ = f32[320,1024]{1,0:T(8,128)} custom-call(bf16[320,2048]{1,0:T(8,128)(2,1)} %copy-done, f32[320,1]{1,0:T(8,128)} %broadcast_in_dim.6.power_ref, f32[320,1]{1,0:T(8,128)} %mul.285.coef_ref, f32[1,80]{1,0:T(1,128)} %get-tuple-element.23.gain_ref, bf16[80,2048]{1,0:T(8,128)(2,1)} %copy-done.1), custom_call_target="tpu_custom_call" | custom-call | flops 157286400 | bytes 2621440 | tf_op jit(solution)/shard_map/pair_tile/pallas_call | solution.py:116
  61.2 2.9 %collective-permute-done.8.col_ref = bf16[80,2048]{1,0:T(8,128)(2,1)S(1)} collective-permute-done((bf16[80,2048]{1,0:T(8,128)(2,1)S(1)}, bf16[80,2048]{1,0:T(8,128)(2,1)S(1)}, u32[]{:S(2)}, u32[]{:S(2)}) %collective-permute-start.8) | collective-permute-done | bytes 327712 | tf_op jit(solution)/shard_map/ppermute | solution.py:22
  64.1 0.7 copy-done.4
  64.8 4.1 %pair_tile.5.rest_0_ = f32[320,1024]{1,0:T(8,128)} custom-call(bf16[320,2048]{1,0:T(8,128)(2,1)} %copy-done, f32[320,1]{1,0:T(8,128)} %broadcast_in_dim.6.power_ref, f32[320,1]{1,0:T(8,128)} %mul.284.coef_ref, f32[1,80]{1,0:T(1,128)} %get-tuple-element.24.gain_ref, bf16[80,2048]{1,0:T(8,128)(2,1)} %copy-done.4, ...), custom_call_target="tpu_custom_call", output_to_operand_aliasing={{}: (5, {})} | custom-call | flops 157286400 | bytes 2621440 | tf_op jit(solution)/shard_map/pair_tile/pallas_call | solution.py:116
  68.9 0.7 copy-done.3
  69.7 4.1 %pair_tile.6.rest_0_ = f32[320,1024]{1,0:T(8,128)} custom-call(bf16[320,2048]{1,0:T(8,128)(2,1)} %copy-done, f32[320,1]{1,0:T(8,128)} %broadcast_in_dim.6.power_ref, f32[320,1]{1,0:T(8,128)} %mul.283.coef_ref, f32[1,80]{1,0:T(1,128)} %get-tuple-element.25.gain_ref, bf16[80,2048]{1,0:T(8,128)(2,1)} %copy-done.3, ...), custom_call_target="tpu_custom_call", output_to_operand_aliasing={{}: (5, {})} | custom-call | flops 157286400 | bytes 2621440 | tf_op jit(solution)/shard_map/pair_tile/pallas_call | solution.py:116
  73.8 9.9 %collective-permute-done.6.col_ref = bf16[80,2048]{1,0:T(8,128)(2,1)S(1)} collective-permute-done((bf16[80,2048]{1,0:T(8,128)(2,1)S(1)}, bf16[80,2048]{1,0:T(8,128)(2,1)S(1)}, u32[]{:S(2)}, u32[]{:S(2)}) %collective-permute-start.6) | collective-permute-done | bytes 327712 | tf_op jit(solution)/shard_map/ppermute | solution.py:22
  83.7 0.7 copy-done.2
  84.4 4.1 %pair_tile.7 = f32[320,1024]{1,0:T(8,128)} custom-call(bf16[320,2048]{1,0:T(8,128)(2,1)} %copy-done, f32[320,1]{1,0:T(8,128)} %broadcast_in_dim.6.power_ref, f32[320,1]{1,0:T(8,128)} %mul.282.coef_ref, f32[1,80]{1,0:T(1,128)} %get-tuple-element.26.gain_ref, bf16[80,2048]{1,0:T(8,128)(2,1)} %copy-done.2, ...), custom_call_target="tpu_custom_call", output_to_operand_aliasing={{}: (5, {})} | custom-call | flops 157286400 | bytes 2621440 | tf_op jit(solution)/shard_map/pair_tile/pallas_call | solution.py:116
  88.6 1.1 fusion.34
  89.7 0.1 collective-permute-start.9
  89.8 1.6 %collective-permute-done.9 = bf16[2,80,1024]{2,1,0:T(8,128)(2,1)S(1)} collective-permute-done((bf16[2,80,1024]{2,1,0:T(8,128)(2,1)S(1)}, bf16[2,80,1024]{2,1,0:T(8,128)(2,1)S(1)}, u32[]{:S(2)}, u32[]{:S(2)}) %collective-permute-start.9) | collective-permute-done | bytes 327712 | tf_op jit(solution)/shard_map/ppermute | solution.py:22
  91.4 1.2 fusion.31
  92.6 1.6 %collective-permute-start.10 = (bf16[80,1024]{1,0:T(8,128)(2,1)S(1)}, bf16[80,1024]{1,0:T(8,128)(2,1)S(1)}, u32[]{:S(2)}, u32[]{:S(2)}) collective-permute-start(bf16[80,1024]{1,0:T(8,128)(2,1)S(1)} %fusion.40), channel_id=1, source_target_pairs={{0,2},{2,0},{1,3},{3,1},{4,6},{6,4},{5,7},{7,5},{8,10},{10,8},{9,1... | collective-permute-start | bytes 491528 | tf_op jit(solution)/shard_map/ppermute | solution.py:22
  94.2 4.7 %collective-permute-done.10 = bf16[80,1024]{1,0:T(8,128)(2,1)S(1)} collective-permute-done((bf16[80,1024]{1,0:T(8,128)(2,1)S(1)}, bf16[80,1024]{1,0:T(8,128)(2,1)S(1)}, u32[]{:S(2)}, u32[]{:S(2)}) %collective-permute-start.10) | collective-permute-done | bytes 163872 | tf_op jit(solution)/shard_map/ppermute | solution.py:22
  98.9 0.1 broadcast_in_dim.4
  99.0 0.1 collective-permute-start.11
  99.1 3.8 %collective-permute-start.12 = (bf16[80,1024]{1,0:T(8,128)(2,1)S(1)}, bf16[80,1024]{1,0:T(8,128)(2,1)S(1)}, u32[]{:S(2)}, u32[]{:S(2)}) collective-permute-start(bf16[80,1024]{1,0:T(8,128)(2,1)S(1)} %get-tuple-element.10), channel_id=1, source_target_pairs={{0,12},{4,0},{8,4},{12,8},{1,13},{5,1},{9,5},{13,9},{2,14},{6,2},{... | collective-permute-start | bytes 491528 | tf_op jit(solution)/shard_map/ppermute | solution.py:22
  102.9 1.7 %collective-permute-start.13 = (bf16[80,1024]{1,0:T(8,128)(2,1)S(1)}, bf16[80,1024]{1,0:T(8,128)(2,1)S(1)}, u32[]{:S(2)}, u32[]{:S(2)}) collective-permute-start(bf16[80,1024]{1,0:T(8,128)(2,1)S(1)} %get-tuple-element.10), channel_id=1, source_target_pairs={{0,8},{4,12},{8,0},{12,4},{1,9},{5,13},{9,1},{13,5},{2,10},{6,14},... | collective-permute-start | bytes 491528 | tf_op jit(solution)/shard_map/ppermute | solution.py:22
  104.6 3.4 %collective-permute-done.11 = bf16[80,1024]{1,0:T(8,128)(2,1)S(1)} collective-permute-done((bf16[80,1024]{1,0:T(8,128)(2,1)S(1)}, bf16[80,1024]{1,0:T(8,128)(2,1)S(1)}, u32[]{:S(2)}, u32[]{:S(2)}) %collective-permute-start.11) | collective-permute-done | bytes 163872 | tf_op jit(solution)/shard_map/ppermute | solution.py:22
  108.0 1.8 %collective-permute-done.12 = bf16[80,1024]{1,0:T(8,128)(2,1)S(1)} collective-permute-done((bf16[80,1024]{1,0:T(8,128)(2,1)S(1)}, bf16[80,1024]{1,0:T(8,128)(2,1)S(1)}, u32[]{:S(2)}, u32[]{:S(2)}) %collective-permute-start.12) | collective-permute-done | bytes 163872 | tf_op jit(solution)/shard_map/ppermute | solution.py:22
  109.8 7.0 %collective-permute-done.13 = bf16[80,1024]{1,0:T(8,128)(2,1)S(1)} collective-permute-done((bf16[80,1024]{1,0:T(8,128)(2,1)S(1)}, bf16[80,1024]{1,0:T(8,128)(2,1)S(1)}, u32[]{:S(2)}, u32[]{:S(2)}) %collective-permute-start.13) | collective-permute-done | bytes 163872 | tf_op jit(solution)/shard_map/ppermute | solution.py:22
  116.8 3.3 %fusion.13 = bf16[320,1024]{1,0:T(8,128)(2,1)} fusion(bf16[320,1024]{1,0:T(8,128)(2,1)S(1)} %constant_dynamic-update-slice_fusion, bf16[4096,1024]{1,0:T(8,128)(2,1)} %basis.1), kind=kOutput, calls=%fused_computation.13 | convolution fusion | flops 671744000 | bytes 3407872 | tf_op jit(solution)/shard_map/dot_general | solution.py:219
  (29 shorter events, 0.3 us)
Async XLA Ops:
  1.6 19.6 %collective-permute-start.1 = (bf16[160,1024]{1,0:T(8,128)(2,1)S(1)}, bf16[160,1024]{1,0:T(8,128)(2,1)S(1)}, u32[]{:S(2)}, u32[]{:S(2)}) collective-permute-start(bf16[160,1024]{1,0:T(8,128)(2,1)S(1)} %pad_maximum_fusion.2), channel_id=1, source_target_pairs={{0,12},{4,0},{8,4},{12,8},{1,13},{5,1},{9,5},{13,9},{2,14},{6,2},{... | collective-permute-start | bytes 983048 | tf_op jit(solution)/shard_map/ppermute | solution.py:22
  6.7 27.9 %collective-permute-start.2 = (bf16[160,1024]{1,0:T(8,128)(2,1)S(1)}, bf16[160,1024]{1,0:T(8,128)(2,1)S(1)}, u32[]{:S(2)}, u32[]{:S(2)}) collective-permute-start(bf16[160,1024]{1,0:T(8,128)(2,1)S(1)} %pad_maximum_fusion.3), channel_id=1, source_target_pairs={{0,8},{4,12},{8,0},{12,4},{1,9},{5,13},{9,1},{13,5},{2,10},{6,14},... | collective-permute-start | bytes 983048 | tf_op jit(solution)/shard_map/ppermute | solution.py:22
  6.8 29.9 %collective-permute-start = (bf16[160,1024]{1,0:T(8,128)(2,1)S(1)}, bf16[160,1024]{1,0:T(8,128)(2,1)S(1)}, u32[]{:S(2)}, u32[]{:S(2)}) collective-permute-start(bf16[160,1024]{1,0:T(8,128)(2,1)S(1)} %pad_maximum_fusion.1), channel_id=1, source_target_pairs={{0,4},{4,8},{8,12},{12,0},{1,5},{5,9},{9,13},{13,1},{2,6},{6,10},{... | collective-permute-start | bytes 983048 | tf_op jit(solution)/shard_map/ppermute | solution.py:22
  18.8 2.2 %copy-start.5 = (s32[16,16]{1,0:T(8,128)S(1)}, s32[16,16]{1,0:T(8,128)}, u32[]{:S(2)}) copy-start(s32[16,16]{1,0:T(8,128)} %param.7) | copy-start | bytes 3076
  18.8 2.3 %copy-start.6 = (s32[1280]{0:T(1024)S(1)}, s32[1280]{0:T(1024)}, u32[]{:S(2)}) copy-start(s32[1280]{0:T(1024)} %param.6) | copy-start | bytes 15364
  39.0 16.7 %copy-start.1 = (bf16[80,2048]{1,0:T(8,128)(2,1)}, bf16[80,2048]{1,0:T(8,128)(2,1)S(1)}, u32[]{:S(2)}) copy-start(bf16[80,2048]{1,0:T(8,128)(2,1)S(1)} %pad_maximum_fusion.4.col_ref) | copy-start | bytes 983044
  39.0 8.7 %collective-permute-start.4 = (bf16[80,2048]{1,0:T(8,128)(2,1)S(1)}, bf16[80,2048]{1,0:T(8,128)(2,1)S(1)}, u32[]{:S(2)}, u32[]{:S(2)}) collective-permute-start(bf16[80,2048]{1,0:T(8,128)(2,1)S(1)} %pad_maximum_fusion.4.col_ref), channel_id=1, source_target_pairs={{0,2},{2,0},{1,3},{3,1},{4,6},{6,4},{5,7},{7,5},{8,10},{10,8},{9,1... | collective-permute-start | bytes 983048 | tf_op jit(solution)/shard_map/ppermute | solution.py:22
  42.0 13.5 %collective-permute-start.3 = (bf16[80,2048]{1,0:T(8,128)(2,1)S(1)}, bf16[80,2048]{1,0:T(8,128)(2,1)S(1)}, u32[]{:S(2)}, u32[]{:S(2)}) collective-permute-start(bf16[80,2048]{1,0:T(8,128)(2,1)S(1)} %pad_maximum_fusion.4.col_ref), channel_id=1, source_target_pairs={{0,1},{1,0},{2,3},{3,2},{4,5},{5,4},{6,7},{7,6},{8,9},{9,8},{10,11... | collective-permute-start | bytes 983048 | tf_op jit(solution)/shard_map/ppermute | solution.py:22
  47.7 7.8 %collective-permute-start.5 = (bf16[80,2048]{1,0:T(8,128)(2,1)S(1)}, bf16[80,2048]{1,0:T(8,128)(2,1)S(1)}, u32[]{:S(2)}, u32[]{:S(2)}) collective-permute-start(bf16[80,2048]{1,0:T(8,128)(2,1)S(1)} %collective-permute-done.4), channel_id=1, source_target_pairs={{0,1},{1,0},{2,3},{3,2},{4,5},{5,4},{6,7},{7,6},{8,9},{9,8},{10,11... | collective-permute-start | bytes 983048 | tf_op jit(solution)/shard_map/ppermute | solution.py:22
  51.6 12.4 %collective-permute-start.8 = (bf16[80,2048]{1,0:T(8,128)(2,1)S(1)}, bf16[80,2048]{1,0:T(8,128)(2,1)S(1)}, u32[]{:S(2)}, u32[]{:S(2)}) collective-permute-start(bf16[80,2048]{1,0:T(8,128)(2,1)S(1)} %pad_maximum_fusion.4.col_ref), channel_id=1, source_target_pairs={{0,4},{4,8},{8,12},{12,0},{1,5},{5,9},{9,13},{13,1},{2,6},{6,10},{... | collective-permute-start | bytes 983048 | tf_op jit(solution)/shard_map/ppermute | solution.py:22
  51.6 17.3 %collective-permute-start.7 = (bf16[80,2048]{1,0:T(8,128)(2,1)S(1)}, bf16[80,2048]{1,0:T(8,128)(2,1)S(1)}, u32[]{:S(2)}, u32[]{:S(2)}) collective-permute-start(bf16[80,2048]{1,0:T(8,128)(2,1)S(1)} %pad_maximum_fusion.4.col_ref), channel_id=1, source_target_pairs={{0,12},{4,0},{8,4},{12,8},{1,13},{5,1},{9,5},{13,9},{2,14},{6,2},{... | collective-permute-start | bytes 983048 | tf_op jit(solution)/shard_map/ppermute | solution.py:22
  55.5 28.2 %collective-permute-start.6 = (bf16[80,2048]{1,0:T(8,128)(2,1)S(1)}, bf16[80,2048]{1,0:T(8,128)(2,1)S(1)}, u32[]{:S(2)}, u32[]{:S(2)}) collective-permute-start(bf16[80,2048]{1,0:T(8,128)(2,1)S(1)} %pad_maximum_fusion.4.col_ref), channel_id=1, source_target_pairs={{0,8},{4,12},{8,0},{12,4},{1,9},{5,13},{9,1},{13,5},{2,10},{6,14},... | collective-permute-start | bytes 983048 | tf_op jit(solution)/shard_map/ppermute | solution.py:22
  55.6 1.1 copy-start
  64.1 0.7 copy-start.4
  68.9 0.7 copy-start.3
  83.7 0.7 copy-start.2
  89.7 1.7 %collective-permute-start.9 = (bf16[2,80,1024]{2,1,0:T(8,128)(2,1)S(1)}, bf16[2,80,1024]{2,1,0:T(8,128)(2,1)S(1)}, u32[]{:S(2)}, u32[]{:S(2)}) collective-permute-start(bf16[2,80,1024]{2,1,0:T(8,128)(2,1)S(1)} %fusion.34), channel_id=1, source_target_pairs={{0,1},{1,0},{2,3},{3,2},{4,5},{5,4},{6,7},{7,6},{8,9},{9,8},{10,11... | collective-permute-start | bytes 983048 | tf_op jit(solution)/shard_map/ppermute | solution.py:22
  92.6 6.3 %collective-permute-start.10 = (bf16[80,1024]{1,0:T(8,128)(2,1)S(1)}, bf16[80,1024]{1,0:T(8,128)(2,1)S(1)}, u32[]{:S(2)}, u32[]{:S(2)}) collective-permute-start(bf16[80,1024]{1,0:T(8,128)(2,1)S(1)} %fusion.40), channel_id=1, source_target_pairs={{0,2},{2,0},{1,3},{3,1},{4,6},{6,4},{5,7},{7,5},{8,10},{10,8},{9,1... | collective-permute-start | bytes 491528 | tf_op jit(solution)/shard_map/ppermute | solution.py:22
  99.0 8.9 %collective-permute-start.11 = (bf16[80,1024]{1,0:T(8,128)(2,1)S(1)}, bf16[80,1024]{1,0:T(8,128)(2,1)S(1)}, u32[]{:S(2)}, u32[]{:S(2)}) collective-permute-start(bf16[80,1024]{1,0:T(8,128)(2,1)S(1)} %get-tuple-element.10), channel_id=1, source_target_pairs={{0,4},{4,8},{8,12},{12,0},{1,5},{5,9},{9,13},{13,1},{2,6},{6,10},{... | collective-permute-start | bytes 491528 | tf_op jit(solution)/shard_map/ppermute | solution.py:22
  99.1 10.7 %collective-permute-start.12 = (bf16[80,1024]{1,0:T(8,128)(2,1)S(1)}, bf16[80,1024]{1,0:T(8,128)(2,1)S(1)}, u32[]{:S(2)}, u32[]{:S(2)}) collective-permute-start(bf16[80,1024]{1,0:T(8,128)(2,1)S(1)} %get-tuple-element.10), channel_id=1, source_target_pairs={{0,12},{4,0},{8,4},{12,8},{1,13},{5,1},{9,5},{13,9},{2,14},{6,2},{... | collective-permute-start | bytes 491528 | tf_op jit(solution)/shard_map/ppermute | solution.py:22
  102.9 13.9 %collective-permute-start.13 = (bf16[80,1024]{1,0:T(8,128)(2,1)S(1)}, bf16[80,1024]{1,0:T(8,128)(2,1)S(1)}, u32[]{:S(2)}, u32[]{:S(2)}) collective-permute-start(bf16[80,1024]{1,0:T(8,128)(2,1)S(1)} %get-tuple-element.10), channel_id=1, source_target_pairs={{0,8},{4,12},{8,0},{12,4},{1,9},{5,13},{9,1},{13,5},{2,10},{6,14},... | collective-permute-start | bytes 491528 | tf_op jit(solution)/shard_map/ppermute | solution.py:22

commit v2 on v1

--- a/solution.py
+++ b/solution.py
@@ -7,6 +7,7 @@
 from jax.experimental import pallas as pl
 from jax.experimental.pallas import tpu as pltpu
 from jax.sharding import PartitionSpec as P
+
 
 NT = 4096
 NF = 512
@@ -128,7 +129,7 @@
     )(*args)
 
 
-def shards(synthetic, observed, station_weights, pair_mask):
+def body(synthetic, observed, station_weights, pair_mask):
     levels = lax.axis_size("blk")
     subs = lax.axis_size("sub")
     pairs = lax.axis_size("pair")
@@ -156,6 +157,28 @@
     arrivals = [0] + order
     firsts = jnp.stack([(level - steps) % levels * span for steps in arrivals]).astype(jnp.int32)
     basis = make_basis(firsts, span)
+    member = sub * pairs + pair
+    members = jnp.stack(
+        [
+            (sub - s) % subs * pairs + (pair - q) % pairs
+            for s in range(subs)
+            for q in range(pairs)
+        ]
+    )
+    gains = station_weights.astype(jnp.float32).reshape(-1, piece)
+    link = jnp.maximum(pair_mask, pair_mask.T).astype(jnp.float32)
+    row_pieces = members * levels + level
+    row_gain = gains[row_pieces].reshape(-1, 1)
+    row_link = link[row_pieces]
+    factor = 4.0 / math.sqrt(stations)
+    coefs, col_gains = [], []
+    for steps in arrivals:
+        column_piece = member * levels + (level - steps) % levels
+        active = lax.dynamic_slice_in_dim(row_link, column_piece, 1, 1)
+        coefs.append(factor * row_gain * jnp.repeat(active, piece, axis=0))
+        col_gains.append(lax.dynamic_slice_in_dim(gains, column_piece, 1, 0))
+    last = order[-1]
+    blocks[last], coefs, col_gains = lax.optimization_barrier((blocks[last], coefs, col_gains))
     total = None
     for place, steps in enumerate(arrivals):
         part = jnp.dot(
@@ -171,33 +194,20 @@
     for steps in order:
         columns[steps] = shift(own, "blk", steps)
     blocks_of_rows = []
-    members = []
     for s in range(subs):
         here = own if s == 0 else shift(own, "sub", s)
         for q in range(pairs):
             blocks_of_rows.append(here if q == 0 else shift(here, "pair", q))
-            members.append((sub - s) % subs * pairs + (pair - q) % pairs)
     rows = jnp.concatenate(blocks_of_rows, axis=0)
-    members = jnp.stack(members)
-    member = sub * pairs + pair
-
-    gains = station_weights.astype(jnp.float32).reshape(-1, piece)
-    link = jnp.maximum(pair_mask, pair_mask.T).astype(jnp.float32)
-    row_pieces = members * levels + level
-    row_gain = gains[row_pieces].reshape(-1, 1)
-    row_link = link[row_pieces]
-    factor = 4.0 / math.sqrt(stations)
     widened = rows[:, : 2 * NF].astype(jnp.float32)
     row_rate = rate_of(widened[:, :NF], widened[:, NF:])
     row_power = jnp.sum(jnp.square(row_rate.astype(jnp.float32)), axis=1, keepdims=True)
 
     running = None
-    for steps in arrivals:
-        column_piece = member * levels + (level - steps) % levels
-        active = lax.dynamic_slice_in_dim(row_link, column_piece, 1, 1)
-        coef = factor * row_gain * jnp.repeat(active, piece, axis=0)
-        gain = lax.dynamic_slice_in_dim(gains, column_piece, 1, 0)
-        running = pair_tile(running, rows, row_power, coef, gain, columns[steps])
+    for place, steps in enumerate(arrivals):
+        running = pair_tile(
+            running, rows, row_power, coefs[place], col_gains[place], columns[steps]
+        )
 
     partial = running.reshape(subs, pairs, piece, 2 * NF)
     held = partial[:, 0]
@@ -231,7 +241,7 @@
         P("events", None),
     )
     return jax.shard_map(
-        shards,
+        body,
         mesh=mesh,
         in_specs=placed,
         out_specs=P(("events", "sub", "pair"), "blk"),

time: 121 us -> 115 us (0.950)
  waiting for transfers between devices: 48.3 us -> 44.3 us
  starting transfers between devices: 18.9 us -> 17.1 us
    ppermute x14, waiting for transfers between devices: 48.3 us -> 44.3 us  [shift(): return lax.ppermute(value, axis, pairs)]
    optimization_barrier x0 -> x4, local copies, waits for them, and re-layouts: none -> 3.22 us  [body(): lax.optimization_barrier((blocks[last], coefs, col_gains))]
    mul x4, local copies, waits for them, and re-layouts: 3.25 us -> 0.33 us  [body(): coefs.append(factor * row_gain * jnp.repeat(active, piece, axis=0))]
    ppermute x14, starting transfers between devices: 18.9 us -> 17.1 us  [shift(): return lax.ppermute(value, axis, pairs)]
  transfers between devices with their start and end apart: 14 -> 14, of which waited for: 9 -> 9; matrix products, arithmetic and copies ran while one was open for 13% -> 14% of each run, Pallas kernels for 17% -> 18%
where the time goes in v2:
time: 115 us
  waiting for transfers between devices  44.3 us (39%)
  Pallas kernels  25.1 us (22%)
  starting transfers between devices  17.1 us (15%)
  local copies, waits for them, and re-layouts  11.9 us (10%)
  matrix products  11.8 us (10%)
  other arithmetic  4.23 us (4%)
    ppermute x14, waiting for transfers between devices, shift(): return lax.ppermute(value, axis, pairs)  44.3 us
    ppermute x14, starting transfers between devices, shift(): return lax.ppermute(value, axis, pairs)  17.1 us
    pallas_call x4, Pallas kernels, pair_tile(): pl.pallas_call(functools.partial(tile_kernel, running is None), in_specs=...  16.1 us
    pallas_call x1, Pallas kernels, make_basis(): pl.pallas_call(functools.partial(basis_kernel, per_step, low_rows), grid=...  8.94 us
    dot_general x4, matrix products, body(): jnp.dot(blocks[steps], basis[place * span:(place + 1) * span], preferred_...  8.49 us
    dot_general x1, matrix products, body(): lax.dot_general(gathered, basis[:span], CONTRACT_LAST, preferred_element_...  3.31 us
    optimization_barrier x4, local copies, waits for them, and re-layouts, body(): lax.optimization_barrier((blocks[last], coefs, col_gains))  3.22 us
    unnamed x15, local copies, waits for them, and re-layouts  2.83 us
  transfers between devices with their start and end apart: 14, of which 9 were waited for; matrix products, arithmetic and copies ran while one was open for 14% of the time, Pallas kernels for 18%

profile of v2, /device:TPU:0, one launch (start us, length us, event | category | flops | bytes accessed | tf_op | source)
XLA Modules:
  0.0 114.6 jit_solution(2231351814481828835)
XLA Ops:
  0.0 1.6 %constant_dynamic-slice_fusion.12 = (bf16[80,1024]{1,0:T(8,128)(2,1)S(1)}, bf16[80,1024]{1,0:T(8,128)(2,1)S(1)}, bf16[80,1024]{1,0:T(8,128)(2,1)S(1)}, bf16[80,1...) fusion(bf16[320,1024]{1,0:T(8,128)(2,1)} %param.5, ...), kind=kLoop, calls=%fused_computation.81 | loop fusion | bytes 2621456 | tf_op jit(solution)/shard_map/dynamic_slice | solution.py:148
  1.6 5.1 %collective-permute-start.1 = (bf16[160,1024]{1,0:T(8,128)(2,1)S(1)}, bf16[160,1024]{1,0:T(8,128)(2,1)S(1)}, u32[]{:S(2)}, u32[]{:S(2)}) collective-permute-start(bf16[160,1024]{1,0:T(8,128)(2,1)S(1)} %pad_maximum_fusion.2), channel_id=1, source_target_pairs={{0,12},{4,0},{8,4},{12,8},{1,13},{5,1},{9,5},{13,9},{2,14},{6,2},{... | collective-permute-start | bytes 983048 | tf_op jit(solution)/shard_map/ppermute | solution.py:23
  6.8 0.1 collective-permute-start.2
  6.9 1.0 collective-permute-start
  7.9 0.1 pad_add_fusion
  8.0 0.1 broadcast_add_fusion
  8.1 0.1 add.234
  8.2 0.1 fusion.64
  8.3 0.1 copy.10
  8.3 0.1 reshape.219
  8.4 0.6 gather_fusion.1
  9.0 0.6 gather_fusion
  9.5 1.8 %fusion.50 = (f32[64,512]{1,0:T(8,128)}, f32[64,512]{1,0:T(8,128)}, f32[64,512]{1,0:T(8,128)}, f32[64,512]{1,0:T(8,128)}) fusion(s32[512]{0:T(512)S(1)} %iota_add_fusion, s32[64]{0:T(128)S(1)} %add.234), kind=kLoop, calls=%fused_computation.59 | loop fusion | flops 917504 | bytes 526592 | tf_op jit(solution)/shard_map/sin | solution.py:39
  11.3 8.9 %basis.1 = bf16[4096,1024]{1,0:T(8,128)(2,1)} custom-call(f32[64,512]{1,0:T(8,128)} %get-tuple-element.49.hc_ref, f32[64,512]{1,0:T(8,128)} %get-tuple-element.50.hs_ref, f32[64,512]{1,0:T(8,128)} %get-tuple-element.48.lc_ref, f32[64,512]{1,0:T(8,128)} %get-tuple-element.47.ls_ref), custom_call_target="tpu_custom_call" | custom-call | flops 16777216 | bytes 8388608 | tf_op jit(solution)/shard_map/basis/pallas_call | solution.py:62
  20.2 2.1 %fusion.8 = f32[160,1024]{1,0:T(8,128)S(1)} fusion(bf16[4096,1024]{1,0:T(8,128)(2,1)} %basis.1, bf16[80,1024]{1,0:T(8,128)(2,1)S(1)} %get-tuple-element.36, bf16[80,1024]{1,0:T(8,128)(2,1)S(1)} %get-tuple-element.57), kind=kOutput, calls=%fused_computation.10 | convolution fusion | flops 336199680 | bytes 3080192 | tf_op jit(solution)/shard_map/dot_general | solution.py:184
  22.3 0.2 fusion.62
  22.6 0.1 broadcast_multiply_fusion
  22.6 0.6 constant_dynamic-slice_fusion
  23.3 0.1 mul.289
  23.3 0.1 mul.294
  23.4 0.1 mul.299
  23.5 0.1 mul.304
  23.6 11.1 %collective-permute-done.2 = bf16[160,1024]{1,0:T(8,128)(2,1)S(1)} collective-permute-done((bf16[160,1024]{1,0:T(8,128)(2,1)S(1)}, bf16[160,1024]{1,0:T(8,128)(2,1)S(1)}, u32[]{:S(2)}, u32[]{:S(2)}) %collective-permute-start.2) | collective-permute-done | bytes 327712 | tf_op jit(solution)/shard_map/ppermute | solution.py:23
  34.7 2.1 %fusion = f32[160,1024]{1,0:T(8,128)S(1)} fusion(bf16[160,1024]{1,0:T(8,128)(2,1)S(1)} %collective-permute-done.2, bf16[4096,1024]{1,0:T(8,128)(2,1)} %basis.1), kind=kOutput, calls=%fused_computation.2 | convolution fusion | flops 335544320 | bytes 3080192 | tf_op jit(solution)/shard_map/dot_general | solution.py:184
  36.8 0.0 collective-permute-done.1
  36.8 2.1 %fusion.2 = f32[160,1024]{1,0:T(8,128)S(1)} fusion(bf16[160,1024]{1,0:T(8,128)(2,1)S(1)} %collective-permute-done.1, bf16[4096,1024]{1,0:T(8,128)(2,1)} %basis.1), kind=kOutput, calls=%fused_computation.4 | convolution fusion | flops 335544320 | bytes 3080192 | tf_op jit(solution)/shard_map/dot_general | solution.py:184
  38.9 2.2 %fusion.28 = bf16[160,1024]{1,0:T(8,128)(2,1)S(1)} fusion(f32[160,1024]{1,0:T(8,128)S(1)} %fusion, f32[160,1024]{1,0:T(8,128)S(1)} %fusion.2, f32[160,1024]{1,0:T(8,128)S(1)} %fusion.8, bf16[160,1024]{1,0:T(8,128)(2,1)S(1)} %collective-permute-done, bf16[4096,1024]{1,0:T(8,128)(2,1)} %basis.1), kind=kOutput, calls=%fused_computation.20 | convolution fusion | flops 336363520 | bytes 4718592 | tf_op jit(solution)/shard_map/dot_general | solution.py:184
  41.2 0.0 copy-start.1
  41.2 1.6 %collective-permute-start.4 = (bf16[80,2048]{1,0:T(8,128)(2,1)S(1)}, bf16[80,2048]{1,0:T(8,128)(2,1)S(1)}, u32[]{:S(2)}, u32[]{:S(2)}) collective-permute-start(bf16[80,2048]{1,0:T(8,128)(2,1)S(1)} %pad_maximum_fusion.4.col_ref), channel_id=1, source_target_pairs={{0,2},{2,0},{1,3},{3,1},{4,6},{6,4},{5,7},{7,5},{8,10},{10,8},{9,1... | collective-permute-start | bytes 983048 | tf_op jit(solution)/shard_map/ppermute | solution.py:23
  42.7 7.1 %collective-permute-done.4 = bf16[80,2048]{1,0:T(8,128)(2,1)S(1)} collective-permute-done((bf16[80,2048]{1,0:T(8,128)(2,1)S(1)}, bf16[80,2048]{1,0:T(8,128)(2,1)S(1)}, u32[]{:S(2)}, u32[]{:S(2)}) %collective-permute-start.4) | collective-permute-done | bytes 327712 | tf_op jit(solution)/shard_map/ppermute | solution.py:23
  49.8 0.0 collective-permute-start.5
  49.8 3.8 %collective-permute-start.7 = (bf16[80,2048]{1,0:T(8,128)(2,1)S(1)}, bf16[80,2048]{1,0:T(8,128)(2,1)S(1)}, u32[]{:S(2)}, u32[]{:S(2)}) collective-permute-start(bf16[80,2048]{1,0:T(8,128)(2,1)S(1)} %pad_maximum_fusion.4.col_ref), channel_id=1, source_target_pairs={{0,12},{4,0},{8,4},{12,8},{1,13},{5,1},{9,5},{13,9},{2,14},{6,2},{... | collective-permute-start | bytes 983048 | tf_op jit(solution)/shard_map/ppermute | solution.py:23
  53.7 0.8 copy.12.coef_ref
  54.5 0.8 copy.14.coef_ref
  55.3 0.8 copy.16.coef_ref
  56.1 0.8 copy.18.coef_ref
  56.9 0.1 pad_maximum_fusion.rows_ref
  57.0 0.1 slice_convert_fusion.1
  57.1 0.2 fusion.33
  57.3 0.2 multiply_reduce_fusion
  57.5 0.6 copy-done
  58.1 0.8 broadcast_in_dim.6.power_ref
  58.9 3.7 %pair_tile.4.rest_0_ = f32[320,1024]{1,0:T(8,128)} custom-call(bf16[320,2048]{1,0:T(8,128)(2,1)} %copy-done, f32[320,1]{1,0:T(8,128)} %broadcast_in_dim.6.power_ref, f32[320,1]{1,0:T(8,128)} %copy.12.coef_ref, f32[1,80]{1,0:T(1,128)} %get-tuple-element.22.gain_ref, bf16[80,2048]{1,0:T(8,128)(2,1)} %copy-done.1), custom_call_target="tpu_custom_call" | custom-call | flops 157286400 | bytes 2621440 | tf_op jit(solution)/shard_map/pair_tile/pallas_call | solution.py:117
  62.6 0.7 copy-done.4
  63.3 4.1 %pair_tile.5.rest_0_ = f32[320,1024]{1,0:T(8,128)} custom-call(bf16[320,2048]{1,0:T(8,128)(2,1)} %copy-done, f32[320,1]{1,0:T(8,128)} %broadcast_in_dim.6.power_ref, f32[320,1]{1,0:T(8,128)} %copy.14.coef_ref, f32[1,80]{1,0:T(1,128)} %get-tuple-element.20.gain_ref, bf16[80,2048]{1,0:T(8,128)(2,1)} %copy-done.4, ...), custom_call_target="tpu_custom_call", output_to_operand_aliasing={{}: (5, {})} | custom-call | flops 157286400 | bytes 2621440 | tf_op jit(solution)/shard_map/pair_tile/pallas_call | solution.py:117
  67.5 2.2 %collective-permute-done.7.col_ref = bf16[80,2048]{1,0:T(8,128)(2,1)S(1)} collective-permute-done((bf16[80,2048]{1,0:T(8,128)(2,1)S(1)}, bf16[80,2048]{1,0:T(8,128)(2,1)S(1)}, u32[]{:S(2)}, u32[]{:S(2)}) %collective-permute-start.7) | collective-permute-done | bytes 327712 | tf_op jit(solution)/shard_map/ppermute | solution.py:23
  69.6 0.7 copy-done.3
  70.3 4.1 %pair_tile.6.rest_0_ = f32[320,1024]{1,0:T(8,128)} custom-call(bf16[320,2048]{1,0:T(8,128)(2,1)} %copy-done, f32[320,1]{1,0:T(8,128)} %broadcast_in_dim.6.power_ref, f32[320,1]{1,0:T(8,128)} %copy.16.coef_ref, f32[1,80]{1,0:T(1,128)} %get-tuple-element.18.gain_ref, bf16[80,2048]{1,0:T(8,128)(2,1)} %copy-done.3, ...), custom_call_target="tpu_custom_call", output_to_operand_aliasing={{}: (5, {})} | custom-call | flops 157286400 | bytes 2621440 | tf_op jit(solution)/shard_map/pair_tile/pallas_call | solution.py:117
  74.5 5.9 %collective-permute-done.6.col_ref = bf16[80,2048]{1,0:T(8,128)(2,1)S(1)} collective-permute-done((bf16[80,2048]{1,0:T(8,128)(2,1)S(1)}, bf16[80,2048]{1,0:T(8,128)(2,1)S(1)}, u32[]{:S(2)}, u32[]{:S(2)}) %collective-permute-start.6) | collective-permute-done | bytes 327712 | tf_op jit(solution)/shard_map/ppermute | solution.py:23
  80.3 0.7 copy-done.2
  81.1 4.1 %pair_tile.7 = f32[320,1024]{1,0:T(8,128)} custom-call(bf16[320,2048]{1,0:T(8,128)(2,1)} %copy-done, f32[320,1]{1,0:T(8,128)} %broadcast_in_dim.6.power_ref, f32[320,1]{1,0:T(8,128)} %copy.18.coef_ref, f32[1,80]{1,0:T(1,128)} %get-tuple-element.16.gain_ref, bf16[80,2048]{1,0:T(8,128)(2,1)} %copy-done.2, ...), custom_call_target="tpu_custom_call", output_to_operand_aliasing={{}: (5, {})} | custom-call | flops 157286400 | bytes 2621440 | tf_op jit(solution)/shard_map/pair_tile/pallas_call | solution.py:117
  85.2 1.1 fusion.34
  86.3 0.1 collective-permute-start.9
  86.4 1.6 %collective-permute-done.9 = bf16[2,80,1024]{2,1,0:T(8,128)(2,1)S(1)} collective-permute-done((bf16[2,80,1024]{2,1,0:T(8,128)(2,1)S(1)}, bf16[2,80,1024]{2,1,0:T(8,128)(2,1)S(1)}, u32[]{:S(2)}, u32[]{:S(2)}) %collective-permute-start.9) | collective-permute-done | bytes 327712 | tf_op jit(solution)/shard_map/ppermute | solution.py:23
  88.0 1.2 %fusion.31 = f32[2,80,1024]{2,1,0:T(8,128)S(1)} fusion(f32[2,2,80,1024]{3,2,1,0:T(8,128)} %bitcast.37, bf16[2,80,1024]{2,1,0:T(8,128)(2,1)S(1)} %collective-permute-done.9), kind=kLoop, calls=%fused_computation.23 | loop fusion | flops 327680 | bytes 1638400 | tf_op jit(solution)/shard_map/add | solution.py:216
  89.2 1.6 %collective-permute-start.10 = (bf16[80,1024]{1,0:T(8,128)(2,1)S(1)}, bf16[80,1024]{1,0:T(8,128)(2,1)S(1)}, u32[]{:S(2)}, u32[]{:S(2)}) collective-permute-start(bf16[80,1024]{1,0:T(8,128)(2,1)S(1)} %fusion.40), channel_id=1, source_target_pairs={{0,2},{2,0},{1,3},{3,1},{4,6},{6,4},{5,7},{7,5},{8,10},{10,8},{9,1... | collective-permute-start | bytes 491528 | tf_op jit(solution)/shard_map/ppermute | solution.py:23
  90.8 4.8 %collective-permute-done.10 = bf16[80,1024]{1,0:T(8,128)(2,1)S(1)} collective-permute-done((bf16[80,1024]{1,0:T(8,128)(2,1)S(1)}, bf16[80,1024]{1,0:T(8,128)(2,1)S(1)}, u32[]{:S(2)}, u32[]{:S(2)}) %collective-permute-start.10) | collective-permute-done | bytes 163872 | tf_op jit(solution)/shard_map/ppermute | solution.py:23
  95.6 0.1 broadcast_in_dim.4
  95.7 0.1 collective-permute-start.11
  95.7 3.8 %collective-permute-start.12 = (bf16[80,1024]{1,0:T(8,128)(2,1)S(1)}, bf16[80,1024]{1,0:T(8,128)(2,1)S(1)}, u32[]{:S(2)}, u32[]{:S(2)}) collective-permute-start(bf16[80,1024]{1,0:T(8,128)(2,1)S(1)} %get-tuple-element.28), channel_id=1, source_target_pairs={{0,12},{4,0},{8,4},{12,8},{1,13},{5,1},{9,5},{13,9},{2,14},{6,2},{... | collective-permute-start | bytes 491528 | tf_op jit(solution)/shard_map/ppermute | solution.py:23
  99.6 5.0 %collective-permute-done.11 = bf16[80,1024]{1,0:T(8,128)(2,1)S(1)} collective-permute-done((bf16[80,1024]{1,0:T(8,128)(2,1)S(1)}, bf16[80,1024]{1,0:T(8,128)(2,1)S(1)}, u32[]{:S(2)}, u32[]{:S(2)}) %collective-permute-start.11) | collective-permute-done | bytes 163872 | tf_op jit(solution)/shard_map/ppermute | solution.py:23
  104.6 1.1 collective-permute-done.12
  105.8 5.6 %collective-permute-done.13 = bf16[80,1024]{1,0:T(8,128)(2,1)S(1)} collective-permute-done((bf16[80,1024]{1,0:T(8,128)(2,1)S(1)}, bf16[80,1024]{1,0:T(8,128)(2,1)S(1)}, u32[]{:S(2)}, u32[]{:S(2)}) %collective-permute-start.13) | collective-permute-done | bytes 163872 | tf_op jit(solution)/shard_map/ppermute | solution.py:23
  111.3 3.3 %fusion.13 = bf16[320,1024]{1,0:T(8,128)(2,1)} fusion(bf16[320,1024]{1,0:T(8,128)(2,1)S(1)} %constant_dynamic-update-slice_fusion, bf16[4096,1024]{1,0:T(8,128)(2,1)} %basis.1), kind=kOutput, calls=%fused_computation.13 | convolution fusion | flops 671744000 | bytes 3407872 | tf_op jit(solution)/shard_map/dot_general | solution.py:229
  (33 shorter events, 0.3 us)
Async XLA Ops:
  0.0 8.2 %copy-start.5 = (s32[16,16]{1,0:T(8,128)S(1)}, s32[16,16]{1,0:T(8,128)}, u32[]{:S(2)}) copy-start(s32[16,16]{1,0:T(8,128)} %param.7) | copy-start | bytes 3076
  0.0 8.3 %copy-start.6 = (s32[1280]{0:T(1024)S(1)}, s32[1280]{0:T(1024)}, u32[]{:S(2)}) copy-start(s32[1280]{0:T(1024)} %param.6) | copy-start | bytes 15364
  1.6 35.2 %collective-permute-start.1 = (bf16[160,1024]{1,0:T(8,128)(2,1)S(1)}, bf16[160,1024]{1,0:T(8,128)(2,1)S(1)}, u32[]{:S(2)}, u32[]{:S(2)}) collective-permute-start(bf16[160,1024]{1,0:T(8,128)(2,1)S(1)} %pad_maximum_fusion.2), channel_id=1, source_target_pairs={{0,12},{4,0},{8,4},{12,8},{1,13},{5,1},{9,5},{13,9},{2,14},{6,2},{... | collective-permute-start | bytes 983048 | tf_op jit(solution)/shard_map/ppermute | solution.py:23
  6.8 27.9 %collective-permute-start.2 = (bf16[160,1024]{1,0:T(8,128)(2,1)S(1)}, bf16[160,1024]{1,0:T(8,128)(2,1)S(1)}, u32[]{:S(2)}, u32[]{:S(2)}) collective-permute-start(bf16[160,1024]{1,0:T(8,128)(2,1)S(1)} %pad_maximum_fusion.3), channel_id=1, source_target_pairs={{0,8},{4,12},{8,0},{12,4},{1,9},{5,13},{9,1},{13,5},{2,10},{6,14},... | collective-permute-start | bytes 983048 | tf_op jit(solution)/shard_map/ppermute | solution.py:23
  6.9 32.0 %collective-permute-start = (bf16[160,1024]{1,0:T(8,128)(2,1)S(1)}, bf16[160,1024]{1,0:T(8,128)(2,1)S(1)}, u32[]{:S(2)}, u32[]{:S(2)}) collective-permute-start(bf16[160,1024]{1,0:T(8,128)(2,1)S(1)} %pad_maximum_fusion.1), channel_id=1, source_target_pairs={{0,4},{4,8},{8,12},{12,0},{1,5},{5,9},{9,13},{13,1},{2,6},{6,10},{... | collective-permute-start | bytes 983048 | tf_op jit(solution)/shard_map/ppermute | solution.py:23
  41.2 16.0 %copy-start.1 = (bf16[80,2048]{1,0:T(8,128)(2,1)}, bf16[80,2048]{1,0:T(8,128)(2,1)S(1)}, u32[]{:S(2)}) copy-start(bf16[80,2048]{1,0:T(8,128)(2,1)S(1)} %pad_maximum_fusion.4.col_ref) | copy-start | bytes 983044
  41.2 8.7 %collective-permute-start.4 = (bf16[80,2048]{1,0:T(8,128)(2,1)S(1)}, bf16[80,2048]{1,0:T(8,128)(2,1)S(1)}, u32[]{:S(2)}, u32[]{:S(2)}) collective-permute-start(bf16[80,2048]{1,0:T(8,128)(2,1)S(1)} %pad_maximum_fusion.4.col_ref), channel_id=1, source_target_pairs={{0,2},{2,0},{1,3},{3,1},{4,6},{6,4},{5,7},{7,5},{8,10},{10,8},{9,1... | collective-permute-start | bytes 983048 | tf_op jit(solution)/shard_map/ppermute | solution.py:23
  42.7 14.2 %collective-permute-start.3 = (bf16[80,2048]{1,0:T(8,128)(2,1)S(1)}, bf16[80,2048]{1,0:T(8,128)(2,1)S(1)}, u32[]{:S(2)}, u32[]{:S(2)}) collective-permute-start(bf16[80,2048]{1,0:T(8,128)(2,1)S(1)} %pad_maximum_fusion.4.col_ref), channel_id=1, source_target_pairs={{0,1},{1,0},{2,3},{3,2},{4,5},{5,4},{6,7},{7,6},{8,9},{9,8},{10,11... | collective-permute-start | bytes 983048 | tf_op jit(solution)/shard_map/ppermute | solution.py:23
  49.8 7.1 %collective-permute-start.5 = (bf16[80,2048]{1,0:T(8,128)(2,1)S(1)}, bf16[80,2048]{1,0:T(8,128)(2,1)S(1)}, u32[]{:S(2)}, u32[]{:S(2)}) collective-permute-start(bf16[80,2048]{1,0:T(8,128)(2,1)S(1)} %collective-permute-done.4), channel_id=1, source_target_pairs={{0,1},{1,0},{2,3},{3,2},{4,5},{5,4},{6,7},{7,6},{8,9},{9,8},{10,11... | collective-permute-start | bytes 983048 | tf_op jit(solution)/shard_map/ppermute | solution.py:23
  49.8 12.7 %collective-permute-start.8 = (bf16[80,2048]{1,0:T(8,128)(2,1)S(1)}, bf16[80,2048]{1,0:T(8,128)(2,1)S(1)}, u32[]{:S(2)}, u32[]{:S(2)}) collective-permute-start(bf16[80,2048]{1,0:T(8,128)(2,1)S(1)} %pad_maximum_fusion.4.col_ref), channel_id=1, source_target_pairs={{0,4},{4,8},{8,12},{12,0},{1,5},{5,9},{9,13},{13,1},{2,6},{6,10},{... | collective-permute-start | bytes 983048 | tf_op jit(solution)/shard_map/ppermute | solution.py:23
  49.8 19.8 %collective-permute-start.7 = (bf16[80,2048]{1,0:T(8,128)(2,1)S(1)}, bf16[80,2048]{1,0:T(8,128)(2,1)S(1)}, u32[]{:S(2)}, u32[]{:S(2)}) collective-permute-start(bf16[80,2048]{1,0:T(8,128)(2,1)S(1)} %pad_maximum_fusion.4.col_ref), channel_id=1, source_target_pairs={{0,12},{4,0},{8,4},{12,8},{1,13},{5,1},{9,5},{13,9},{2,14},{6,2},{... | collective-permute-start | bytes 983048 | tf_op jit(solution)/shard_map/ppermute | solution.py:23
  53.7 26.7 %collective-permute-start.6 = (bf16[80,2048]{1,0:T(8,128)(2,1)S(1)}, bf16[80,2048]{1,0:T(8,128)(2,1)S(1)}, u32[]{:S(2)}, u32[]{:S(2)}) collective-permute-start(bf16[80,2048]{1,0:T(8,128)(2,1)S(1)} %pad_maximum_fusion.4.col_ref), channel_id=1, source_target_pairs={{0,8},{4,12},{8,0},{12,4},{1,9},{5,13},{9,1},{13,5},{2,10},{6,14},... | collective-permute-start | bytes 983048 | tf_op jit(solution)/shard_map/ppermute | solution.py:23
  57.0 1.1 copy-start
  62.6 0.7 copy-start.4
  69.6 0.7 copy-start.3
  80.3 0.7 copy-start.2
  86.3 1.7 %collective-permute-start.9 = (bf16[2,80,1024]{2,1,0:T(8,128)(2,1)S(1)}, bf16[2,80,1024]{2,1,0:T(8,128)(2,1)S(1)}, u32[]{:S(2)}, u32[]{:S(2)}) collective-permute-start(bf16[2,80,1024]{2,1,0:T(8,128)(2,1)S(1)} %fusion.34), channel_id=1, source_target_pairs={{0,1},{1,0},{2,3},{3,2},{4,5},{5,4},{6,7},{7,6},{8,9},{9,8},{10,11... | collective-permute-start | bytes 983048 | tf_op jit(solution)/shard_map/ppermute | solution.py:23
  89.2 6.3 %collective-permute-start.10 = (bf16[80,1024]{1,0:T(8,128)(2,1)S(1)}, bf16[80,1024]{1,0:T(8,128)(2,1)S(1)}, u32[]{:S(2)}, u32[]{:S(2)}) collective-permute-start(bf16[80,1024]{1,0:T(8,128)(2,1)S(1)} %fusion.40), channel_id=1, source_target_pairs={{0,2},{2,0},{1,3},{3,1},{4,6},{6,4},{5,7},{7,5},{8,10},{10,8},{9,1... | collective-permute-start | bytes 491528 | tf_op jit(solution)/shard_map/ppermute | solution.py:23
  95.7 8.9 %collective-permute-start.11 = (bf16[80,1024]{1,0:T(8,128)(2,1)S(1)}, bf16[80,1024]{1,0:T(8,128)(2,1)S(1)}, u32[]{:S(2)}, u32[]{:S(2)}) collective-permute-start(bf16[80,1024]{1,0:T(8,128)(2,1)S(1)} %get-tuple-element.28), channel_id=1, source_target_pairs={{0,4},{4,8},{8,12},{12,0},{1,5},{5,9},{9,13},{13,1},{2,6},{6,10},{... | collective-permute-start | bytes 491528 | tf_op jit(solution)/shard_map/ppermute | solution.py:23
  95.7 10.0 %collective-permute-start.12 = (bf16[80,1024]{1,0:T(8,128)(2,1)S(1)}, bf16[80,1024]{1,0:T(8,128)(2,1)S(1)}, u32[]{:S(2)}, u32[]{:S(2)}) collective-permute-start(bf16[80,1024]{1,0:T(8,128)(2,1)S(1)} %get-tuple-element.28), channel_id=1, source_target_pairs={{0,12},{4,0},{8,4},{12,8},{1,13},{5,1},{9,5},{13,9},{2,14},{6,2},{... | collective-permute-start | bytes 491528 | tf_op jit(solution)/shard_map/ppermute | solution.py:23
  99.6 11.8 %collective-permute-start.13 = (bf16[80,1024]{1,0:T(8,128)(2,1)S(1)}, bf16[80,1024]{1,0:T(8,128)(2,1)S(1)}, u32[]{:S(2)}, u32[]{:S(2)}) collective-permute-start(bf16[80,1024]{1,0:T(8,128)(2,1)S(1)} %get-tuple-element.28), channel_id=1, source_target_pairs={{0,8},{4,12},{8,0},{12,4},{1,9},{5,13},{9,1},{13,5},{2,10},{6,14},... | collective-permute-start | bytes 491528 | tf_op jit(solution)/shard_map/ppermute | solution.py:23

commit v3 on v2

--- a/solution.py
+++ b/solution.py
@@ -129,7 +129,7 @@
     )(*args)
 
 
-def body(synthetic, observed, station_weights, pair_mask):
+def ring_body(synthetic, observed, station_weights, pair_mask):
     levels = lax.axis_size("blk")
     subs = lax.axis_size("sub")
     pairs = lax.axis_size("pair")
@@ -233,6 +233,154 @@
     ).astype(jnp.bfloat16)
 
 
+def power_of(spec):
+    wide = spec.astype(jnp.float32)
+    rate = rate_of(wide[:, :NF], wide[:, NF:])
+    return rate, jnp.sum(jnp.square(rate.astype(jnp.float32)), axis=1, keepdims=True)
+
+
+def couple_kernel(row_count, col_count, *refs):
+    row_refs = refs[:row_count]
+    col_refs = refs[row_count : row_count + col_count]
+    weight_ref, out_ref = refs[-2:]
+    half = row_refs[0].shape[0] // 2
+    row_model = jnp.concatenate([ref[:half] for ref in row_refs], axis=0)
+    row_data = jnp.concatenate([ref[half:] for ref in row_refs], axis=0)
+    row_power = jnp.concatenate([power_of(ref[:half])[1] for ref in row_refs], axis=0)
+    models, datas, powers = [], [], []
+    for ref in col_refs:
+        rate, power = power_of(ref[:half])
+        models.append(rate)
+        powers.append(power)
+        wide = ref[half:].astype(jnp.float32)
+        datas.append(rate_of(wide[:, :NF], wide[:, NF:]))
+    col_model = jnp.concatenate(models, axis=0)
+    col_data = jnp.concatenate(datas, axis=0)
+    powers = jnp.concatenate(powers, axis=0)
+    width = powers.shape[0]
+    diagonal = lax.broadcasted_iota(jnp.int32, (width, width), 0) == lax.broadcasted_iota(
+        jnp.int32, (width, width), 1
+    )
+    col_power = jnp.sum(jnp.where(diagonal, powers, 0.0), axis=0, keepdims=True)
+    cross = lax.dot_general(
+        row_model, col_model, CONTRACT_LAST, preferred_element_type=jnp.float32
+    ) - lax.dot_general(row_data, col_data, CONTRACT_LAST, preferred_element_type=jnp.float32)
+    normalizer = 0.5 * (row_power + col_power) + epsilon
+    coupling = (weight_ref[...] * cross / normalizer).astype(jnp.bfloat16)
+    out_ref[...] = jnp.dot(coupling, col_model, preferred_element_type=jnp.float32)
+
+
+def couple(rows, cols, weights):
+    args = [*rows, *cols, weights]
+    height, width = weights.shape
+    return pl.pallas_call(
+        functools.partial(couple_kernel, len(rows), len(cols)),
+        in_specs=[pl.BlockSpec(memory_space=pltpu.VMEM)] * len(args),
+        out_specs=pl.BlockSpec(memory_space=pltpu.VMEM),
+        out_shape=jax.ShapeDtypeStruct((height, 2 * NF), jnp.float32),
+        cost_estimate=pl.CostEstimate(
+            flops=12 * height * width * NF,
+            bytes_accessed=8 * (height + width) * NF,
+            transcendentals=0,
+        ),
+        name="couple",
+    )(*args)
+
+
+def inner_body(synthetic, observed, station_weights, pair_mask):
+    levels = lax.axis_size("blk")
+    subs = lax.axis_size("sub")
+    pairs = lax.axis_size("pair")
+    level = lax.axis_index("blk")
+    sub = lax.axis_index("sub")
+    pair = lax.axis_index("pair")
+    span = synthetic.shape[1]
+    half = synthetic.shape[0] // 2
+    per_half = levels // 2
+    stations = station_weights.shape[0]
+    piece = half // per_half
+    side = level // 2
+    inward, across, swapped = [(0, 1), (3, 2)], [(0, 2), (3, 1)], [(1, 2), (2, 1)]
+    outward, beyond = [(1, 0), (2, 3)], [(1, 3), (2, 0)]
+
+    def stations_of(which):
+        return jnp.concatenate(
+            [
+                lax.dynamic_slice_in_dim(synthetic, which * half, half, 0),
+                lax.dynamic_slice_in_dim(observed, which * half, half, 0),
+            ],
+            axis=0,
+        )
+
+    kept, sent = stations_of(side), stations_of(1 - side)
+    near = lax.ppermute(kept, "blk", inward)
+    middle = lax.ppermute(sent, "blk", swapped)
+    far = lax.ppermute(sent, "blk", across)
+
+    member = sub * pairs + pair
+    hops = [(s, q) for s in range(subs) for q in range(pairs)]
+    members = jnp.stack([(sub - s) % subs * pairs + (pair - q) % pairs for s, q in hops])
+    within = jnp.arange(per_half, dtype=jnp.int32)
+    row_pieces = member * levels + jnp.concatenate(
+        [side * per_half + within, (1 - side) * per_half + within]
+    )
+    col_pieces = (members[:, None] * levels + side * per_half + within[None, :]).reshape(-1)
+    gains = station_weights.astype(jnp.float32).reshape(-1, piece)
+    link = jnp.maximum(pair_mask, pair_mask.T).astype(jnp.float32)
+    active = link[row_pieces][:, col_pieces]
+    weights = (
+        4.0
+        / math.sqrt(stations)
+        * gains[row_pieces].reshape(-1, 1)
+        * gains[col_pieces].reshape(1, -1)
+        * jnp.repeat(jnp.repeat(active, piece, axis=0), piece, axis=1)
+    )
+
+    sources = [level, level ^ 1, levels - 1 - level, (level + 2) % levels]
+    basis = make_basis(jnp.stack(sources).astype(jnp.int32) * span, span)
+    total = None
+    far, weights = lax.optimization_barrier((far, weights))
+    for place, block in enumerate([kept, near, middle, far]):
+        part = jnp.dot(
+            block,
+            basis[place * span : (place + 1) * span],
+            preferred_element_type=jnp.float32,
+        )
+        total = part if total is None else total + part
+    own = (total * (1.0 / math.sqrt(NT))).astype(jnp.bfloat16)
+
+    other = lax.ppermute(own, "blk", swapped)
+    cols = []
+    for s, q in hops:
+        if q == 0:
+            here = own if s == 0 else shift(own, "sub", s)
+        cols.append(here if q == 0 else shift(here, "pair", q))
+    running = couple([own, other], cols, weights)
+
+    received = lax.ppermute(running[half:].astype(jnp.bfloat16), "blk", swapped)
+    adjoint = (running[:half] + received.astype(jnp.float32)).astype(jnp.bfloat16)
+    first = lax.ppermute(adjoint, "blk", outward)
+    second = lax.ppermute(adjoint, "blk", swapped)
+    third = lax.ppermute(adjoint, "blk", beyond)
+    is_inner = (level == 1) | (level == 2)
+    mine = jnp.where(is_inner, adjoint, first)
+    theirs = jnp.where(is_inner, second, third)
+    gathered = jnp.concatenate(
+        [jnp.where(side == 0, mine, theirs), jnp.where(side == 0, theirs, mine)], axis=0
+    )
+    return (
+        lax.dot_general(
+            gathered, basis[:span], CONTRACT_LAST, preferred_element_type=jnp.float32
+        )
+        * (1.0 / math.sqrt(NF))
+    ).astype(jnp.bfloat16)
+
+
+def shards(*args):
+    body = inner_body if lax.axis_size("blk") == 4 else ring_body
+    return body(*args)
+
+
 def solution(mesh):
     placed = (
         P(("events", "sub", "pair"), "blk"),
@@ -241,7 +389,7 @@
         P("events", None),
     )
     return jax.shard_map(
-        body,
+        shards,
         mesh=mesh,
         in_specs=placed,
         out_specs=P(("events", "sub", "pair"), "blk"),

time: 115 us -> 105 us (0.913)
  Pallas kernels: 25.1 us -> 14.3 us
  local copies, waits for them, and re-layouts: 11.9 us -> 6.73 us
  waiting for transfers between devices: 44.3 us -> 46.8 us
  other arithmetic: 4.23 us -> 6.32 us
  matrix products: 11.8 us -> 13.8 us
    ppermute x0 -> x8, waiting for transfers between devices: none -> 30.8 us  [the longest x1 25.6 us: inner_body(): third = lax.ppermute(adjoint, 'blk', beyond)]
    ppermute x14 -> x3, waiting for transfers between devices: 44.3 us -> 16 us  [shift(): return lax.ppermute(value, axis, pairs)]
    ppermute x14 -> x3, starting transfers between devices: 17.1 us -> 1.56 us  [shift(): return lax.ppermute(value, axis, pairs)]
    ppermute x0 -> x8, starting transfers between devices: none -> 15.2 us  [the longest x1 6.9 us: inner_body(): far = lax.ppermute(sent, 'blk', across)]
    pallas_call x4 -> x1, Pallas kernels: 16.1 us -> 5.39 us  [couple(): pl.pallas_call(functools.partial(couple_kernel, len(rows), len(cols)), in...]
    optimization_barrier x4 -> x0, local copies, waits for them, and re-layouts: 3.22 us -> none  [body(): lax.optimization_barrier((blocks[last], coefs, col_gains))]
    dot_general x5, matrix products: 11.8 us -> 13.8 us  [the longest x4 10.5 us: inner_body(): jnp.dot(block, basis[place * span:(place + 1) * span], preferred_element_...]
    unnamed x15, local copies, waits for them, and re-layouts: 2.83 us -> 0.99 us
  transfers between devices with their start and end apart: 14 -> 11, of which waited for: 9 -> 4; matrix products, arithmetic and copies ran while one was open for 14% -> 15% of each run, Pallas kernels for 18% -> 8%
where the time goes in v3:
time: 105 us
  waiting for transfers between devices  46.8 us (45%)
  starting transfers between devices  16.8 us (16%)
  Pallas kernels  14.3 us (14%)
  matrix products  13.8 us (13%)
  local copies, waits for them, and re-layouts  6.73 us (6%)
  other arithmetic  6.32 us (6%)
    ppermute x1, waiting for transfers between devices, inner_body(): third = lax.ppermute(adjoint, 'blk', beyond)  25.6 us
    ppermute x3, waiting for transfers between devices, shift(): return lax.ppermute(value, axis, pairs)  16 us
    dot_general x4, matrix products, inner_body(): jnp.dot(block, basis[place * span:(place + 1) * span], preferred_element_...  10.5 us
    pallas_call x1, Pallas kernels, make_basis(): pl.pallas_call(functools.partial(basis_kernel, per_step, low_rows), grid=...  8.89 us
    ppermute x1, starting transfers between devices, inner_body(): far = lax.ppermute(sent, 'blk', across)  6.9 us
    pallas_call x1, Pallas kernels, couple(): pl.pallas_call(functools.partial(couple_kernel, len(rows), len(cols)), in...  5.39 us
    ppermute x1, waiting for transfers between devices, inner_body(): first = lax.ppermute(adjoint, 'blk', outward)  5.11 us
    dot_general x1, matrix products, inner_body(): lax.dot_general(gathered, basis[:span], CONTRACT_LAST, preferred_element_...  3.32 us
  transfers between devices with their start and end apart: 11, of which 4 were waited for; matrix products, arithmetic and copies ran while one was open for 15% of the time, Pallas kernels for 8%

profile of v3, /device:TPU:0, one launch (start us, length us, event | category | flops | bytes accessed | tf_op | source)
XLA Modules:
  0.0 104.9 jit_solution(13810519293336272988)
XLA Ops:
  0.0 1.4 %constant_dynamic-slice_fusion.2 = (bf16[160,1024]{1,0:T(8,128)(2,1)S(1)}, bf16[160,1024]{1,0:T(8,128)(2,1)S(1)}, bf16[160,1024]{1,0:T(8,128)(2,1)S(1)}, bf16[160,1024]{1,0:T(8,128)(2,1)S(1)}) fusion(bf16[320,1024]{1,0:T(8,128)(2,1)} %param.5, s32[]{:T(128)S(6)} %select_n.102, s32[]{:T(128)S(6)} %select_n.106, bf16[320,1024]{1,0:T(8,128)(2,1)} %param.4), kind=kLoop, calls=%fused_computation.67 | loop fusion | bytes 2621448 | tf_op jit(solution)/shard_map/dynamic_slice | solution.py:310
  1.4 0.0 copy-start.6
  1.4 0.0 copy-start.5
  1.4 0.9 pad_maximum_fusion.1
  2.3 6.9 %collective-permute-start.2 = (bf16[320,1024]{1,0:T(8,128)(2,1)}, bf16[320,1024]{1,0:T(8,128)(2,1)}, u32[]{:S(2)}, u32[]{:S(2)}) collective-permute-start(bf16[320,1024]{1,0:T(8,128)(2,1)} %pad_maximum_fusion.1), channel_id=1, source_target_pairs={{0,8},{12,4},{1,9},{13,5},{2,10},{14,6},{3,11},{15,7},{16,24},{28,... | collective-permute-start | bytes 1966088 | tf_op jit(solution)/shard_map/ppermute | solution.py:318
  9.2 1.5 %collective-permute-start.1 = (bf16[320,1024]{1,0:T(8,128)(2,1)}, bf16[320,1024]{1,0:T(8,128)(2,1)}, u32[]{:S(2)}, u32[]{:S(2)}) collective-permute-start(bf16[320,1024]{1,0:T(8,128)(2,1)} %pad_maximum_fusion.1), channel_id=1, source_target_pairs={{4,8},{8,4},{5,9},{9,5},{6,10},{10,6},{7,11},{11,7},{20,24},{24,20... | collective-permute-start | bytes 1966088 | tf_op jit(solution)/shard_map/ppermute | solution.py:317
  10.7 0.9 pad_maximum_fusion
  11.6 2.2 %collective-permute-start = (bf16[320,1024]{1,0:T(8,128)(2,1)}, bf16[320,1024]{1,0:T(8,128)(2,1)}, u32[]{:S(2)}, u32[]{:S(2)}) collective-permute-start(bf16[320,1024]{1,0:T(8,128)(2,1)} %pad_maximum_fusion), channel_id=1, source_target_pairs={{0,4},{12,8},{1,5},{13,9},{2,6},{14,10},{3,7},{15,11},{16,20},{28,... | collective-permute-start | bytes 1966088 | tf_op jit(solution)/shard_map/ppermute | solution.py:316
  13.7 0.1 add_multiply_fusion
  13.8 0.1 broadcast_add_fusion
  13.9 0.1 add.205
  14.0 0.1 iota_add_fusion
  14.1 0.1 add.233
  14.2 0.1 fusion.49
  14.2 0.0 copy-done.6
  14.3 0.1 reshape.174
  14.3 0.6 gather_fusion
  14.9 0.0 copy-done.5
  14.9 0.1 copy.8
  15.0 1.9 %fusion.46 = (f32[64,512]{1,0:T(8,128)}, f32[64,512]{1,0:T(8,128)}, f32[64,512]{1,0:T(8,128)}, f32[64,512]{1,0:T(8,128)}) fusion(s32[512]{0:T(512)S(1)} %iota_add_fusion.1, s32[64]{0:T(128)S(1)} %add.205), kind=kLoop, calls=%fused_computation.53 | loop fusion | flops 917504 | bytes 526592 | tf_op jit(solution)/shard_map/sin | solution.py:39
  16.9 8.9 %basis.1 = bf16[4096,1024]{1,0:T(8,128)(2,1)} custom-call(f32[64,512]{1,0:T(8,128)} %get-tuple-element.16.hc_ref, f32[64,512]{1,0:T(8,128)} %get-tuple-element.15.hs_ref, f32[64,512]{1,0:T(8,128)} %get-tuple-element.18.lc_ref, f32[64,512]{1,0:T(8,128)} %get-tuple-element.17.ls_ref), custom_call_target="tpu_custom_call" | custom-call | flops 16777216 | bytes 8388608 | tf_op jit(solution)/shard_map/basis/pallas_call | solution.py:62
  25.8 2.4 %fusion.8 = f32[320,1024]{1,0:T(8,128)S(1)} fusion(bf16[4096,1024]{1,0:T(8,128)(2,1)} %basis.1, bf16[160,1024]{1,0:T(8,128)(2,1)S(1)} %get-tuple-element.13, bf16[160,1024]{1,0:T(8,128)(2,1)S(1)} %get-tuple-element.22), kind=kOutput, calls=%fused_computation.12 | convolution fusion | flops 672399360 | bytes 4063232 | tf_op jit(solution)/shard_map/dot_general | solution.py:344
  28.3 0.6 gather_fusion.1
  28.8 0.1 mul.157
  28.9 0.1 mul.152
  29.0 0.6 gather_fusion.2
  29.5 0.1 copy.9
  29.6 0.6 gather_fusion.3
  30.2 0.1 broadcast_in_dim.4
  30.2 0.1 reshape.175
  30.3 0.1 broadcast_in_dim.5
  30.4 0.3 copy.10
  30.7 1.1 %multiply_multiply_fusion.refs_6_ = f32[320,640]{1,0:T(8,128)} fusion(f32[320,640]{1,0:T(8,128)S(1)} %copy.10, f32[640]{0:T(1024)S(1)} %mul.157, f32[320]{0:T(512)S(1)} %mul.152), kind=kLoop, calls=%fused_computation.21 | loop fusion | flops 409600 | bytes 1642240 | tf_op jit(solution)/shard_map/mul | solution.py:332
  31.8 0.0 collective-permute-done.2
  31.8 2.6 %fusion = f32[320,1024]{1,0:T(8,128)S(1)} fusion(bf16[320,1024]{1,0:T(8,128)(2,1)} %collective-permute-done.2, bf16[4096,1024]{1,0:T(8,128)(2,1)} %basis.1), kind=kOutput, calls=%fused_computation.4 | convolution fusion | flops 671088640 | bytes 4063232 | tf_op jit(solution)/shard_map/dot_general | solution.py:344
  34.4 0.0 collective-permute-done.1
  34.4 2.6 %fusion.2 = f32[320,1024]{1,0:T(8,128)S(1)} fusion(bf16[320,1024]{1,0:T(8,128)(2,1)} %collective-permute-done.1, bf16[4096,1024]{1,0:T(8,128)(2,1)} %basis.1), kind=kOutput, calls=%fused_computation.6 | convolution fusion | flops 671088640 | bytes 4063232 | tf_op jit(solution)/shard_map/dot_general | solution.py:344
  37.1 0.0 collective-permute-done
  37.1 2.8 %fusion.25.refs_0_.refs_2_ = bf16[320,1024]{1,0:T(8,128)(2,1)S(1)} fusion(f32[320,1024]{1,0:T(8,128)S(1)} %fusion, f32[320,1024]{1,0:T(8,128)S(1)} %fusion.2, f32[320,1024]{1,0:T(8,128)S(1)} %fusion.8, bf16[320,1024]{1,0:T(8,128)(2,1)} %collective-permute-done, bf16[4096,1024]{1,0:T(8,128)(2,1)} %basis.1), kind=kOutput, calls=%fused_computation.19 | convolution fusion | flops 672727040 | bytes 7340032 | tf_op jit(solution)/shard_map/dot_general | solution.py:344
  39.9 0.0 copy-start
  39.9 1.6 %collective-permute-start.5 = (bf16[320,1024]{1,0:T(8,128)(2,1)S(1)}, bf16[320,1024]{1,0:T(8,128)(2,1)S(1)}, u32[]{:S(2)}, u32[]{:S(2)}) collective-permute-start(bf16[320,1024]{1,0:T(8,128)(2,1)S(1)} %fusion.25.refs_0_.refs_2_), channel_id=1, source_target_pairs={{0,2},{2,0},{1,3},{3,1},{4,6},{6,4},{5,7},{7,5},{8,10},{10,8},{9,1... | collective-permute-start | bytes 1966088 | tf_op jit(solution)/shard_map/ppermute | solution.py:23
  41.4 0.0 collective-permute-start.4
  41.4 0.7 collective-permute-start.3
  42.1 13.9 %collective-permute-done.5.refs_4_ = bf16[320,1024]{1,0:T(8,128)(2,1)S(1)} collective-permute-done((bf16[320,1024]{1,0:T(8,128)(2,1)S(1)}, bf16[320,1024]{1,0:T(8,128)(2,1)S(1)}, u32[]{:S(2)}, u32[]{:S(2)}) %collective-permute-start.5) | collective-permute-done | bytes 655392 | tf_op jit(solution)/shard_map/ppermute | solution.py:23
  56.1 0.0 collective-permute-start.6
  56.1 0.0 collective-permute-done.4.refs_3_
  56.1 0.0 copy-start.2
  56.1 0.0 collective-permute-done.3.refs_1_
  56.1 0.0 copy-start.3
  56.1 2.1 %collective-permute-done.6.refs_5_ = bf16[320,1024]{1,0:T(8,128)(2,1)S(1)} collective-permute-done((bf16[320,1024]{1,0:T(8,128)(2,1)S(1)}, bf16[320,1024]{1,0:T(8,128)(2,1)S(1)}, u32[]{:S(2)}, u32[]{:S(2)}) %collective-permute-start.6) | collective-permute-done | bytes 655392 | tf_op jit(solution)/shard_map/ppermute | solution.py:23
  58.2 0.9 copy-done.4
  59.1 5.4 %couple.1 = f32[320,1024]{1,0:T(8,128)} custom-call(bf16[320,1024]{1,0:T(8,128)(2,1)} %copy-done, bf16[320,1024]{1,0:T(8,128)(2,1)} %copy-done.3, bf16[320,1024]{1,0:T(8,128)(2,1)} %copy-done, bf16[320,1024]{1,0:T(8,128)(2,1)} %copy-done.2, bf16[320,1024]{1,0:T(8,128)(2,1)} %copy-done.1, bf16[320,1024]{1,0:T(8,128)(2,1)} %copy-done.4, ...), custom_call_target="tpu_custom_call" | custom-call | flops 1258291200 | bytes 3932160 | tf_op jit(solution)/shard_map/couple/pallas_call | solution.py:276
  64.5 1.1 %slice.68 = bf16[160,1024]{1,0:T(8,128)(2,1)S(1)} slice(f32[320,1024]{1,0:T(8,128)} %couple.1), slice={[160:320], [0:1024]} | slice | bytes 655360 | tf_op jit(solution)/shard_map/slice | solution.py:360
  65.6 0.7 collective-permute-start.7
  66.3 0.0 collective-permute-done.7
  66.3 1.2 %fusion.31 = bf16[160,1024]{1,0:T(8,128)(2,1)S(1)} fusion(f32[320,1024]{1,0:T(8,128)} %couple.1, bf16[160,1024]{1,0:T(8,128)(2,1)S(1)} %collective-permute-done.7), kind=kLoop, calls=%fused_computation.24 | loop fusion | flops 491520 | bytes 1310720 | tf_op jit(solution)/shard_map/convert_element_type | solution.py:361
  67.5 1.3 %collective-permute-start.10 = (bf16[160,1024]{1,0:T(8,128)(2,1)S(1)}, bf16[160,1024]{1,0:T(8,128)(2,1)S(1)}, u32[]{:S(2)}, u32[]{:S(2)}) collective-permute-start(bf16[160,1024]{1,0:T(8,128)(2,1)S(1)} %fusion.31), channel_id=1, source_target_pairs={{4,12},{8,0},{5,13},{9,1},{6,14},{10,2},{7,15},{11,3},{20,28},{24,... | collective-permute-start | bytes 983048 | tf_op jit(solution)/shard_map/ppermute | solution.py:364
  68.8 0.7 collective-permute-start.9
  69.5 1.3 %collective-permute-start.8 = (bf16[160,1024]{1,0:T(8,128)(2,1)S(1)}, bf16[160,1024]{1,0:T(8,128)(2,1)S(1)}, u32[]{:S(2)}, u32[]{:S(2)}) collective-permute-start(bf16[160,1024]{1,0:T(8,128)(2,1)S(1)} %fusion.31), channel_id=1, source_target_pairs={{4,0},{8,12},{5,1},{9,13},{6,2},{10,14},{7,3},{11,15},{20,16},{24,... | collective-permute-start | bytes 983048 | tf_op jit(solution)/shard_map/ppermute | solution.py:362
  70.8 25.6 %collective-permute-done.10 = bf16[160,1024]{1,0:T(8,128)(2,1)S(1)} collective-permute-done((bf16[160,1024]{1,0:T(8,128)(2,1)S(1)}, bf16[160,1024]{1,0:T(8,128)(2,1)S(1)}, u32[]{:S(2)}, u32[]{:S(2)}) %collective-permute-start.10) | collective-permute-done | bytes 327712 | tf_op jit(solution)/shard_map/ppermute | solution.py:364
  96.4 0.0 collective-permute-done.9
  96.4 5.1 %collective-permute-done.8 = bf16[160,1024]{1,0:T(8,128)(2,1)S(1)} collective-permute-done((bf16[160,1024]{1,0:T(8,128)(2,1)S(1)}, bf16[160,1024]{1,0:T(8,128)(2,1)S(1)}, u32[]{:S(2)}, u32[]{:S(2)}) %collective-permute-start.8) | collective-permute-done | bytes 327712 | tf_op jit(solution)/shard_map/ppermute | solution.py:362
  101.5 0.1 broadcast_select_fusion.3
  101.6 3.3 %fusion.28 = bf16[320,1024]{1,0:T(8,128)(2,1)} fusion(bf16[4096,1024]{1,0:T(8,128)(2,1)} %basis.1, bf16[160,1024]{1,0:T(8,128)(2,1)S(1)} %get-tuple-element.10, bf16[160,1024]{1,0:T(8,128)(2,1)S(1)} %get-tuple-element.9), kind=kOutput, calls=%fused_computation.20 | convolution fusion | flops 673054720 | bytes 3407872 | tf_op jit(solution)/shard_map/dot_general | solution.py:372
  (15 shorter events, 0.1 us)
Async XLA Ops:
  1.4 12.9 %copy-start.6 = (s32[1280]{0:T(1024)S(1)}, s32[1280]{0:T(1024)}, u32[]{:S(2)}) copy-start(s32[1280]{0:T(1024)} %param.6) | copy-start | bytes 15364
  1.4 13.5 %copy-start.5 = (s32[16,16]{1,0:T(8,128)S(1)}, s32[16,16]{1,0:T(8,128)}, u32[]{:S(2)}) copy-start(s32[16,16]{1,0:T(8,128)} %param.7) | copy-start | bytes 3076
  2.3 29.5 %collective-permute-start.2 = (bf16[320,1024]{1,0:T(8,128)(2,1)}, bf16[320,1024]{1,0:T(8,128)(2,1)}, u32[]{:S(2)}, u32[]{:S(2)}) collective-permute-start(bf16[320,1024]{1,0:T(8,128)(2,1)} %pad_maximum_fusion.1), channel_id=1, source_target_pairs={{0,8},{12,4},{1,9},{13,5},{2,10},{14,6},{3,11},{15,7},{16,24},{28,... | collective-permute-start | bytes 1966088 | tf_op jit(solution)/shard_map/ppermute | solution.py:318
  9.2 25.3 %collective-permute-start.1 = (bf16[320,1024]{1,0:T(8,128)(2,1)}, bf16[320,1024]{1,0:T(8,128)(2,1)}, u32[]{:S(2)}, u32[]{:S(2)}) collective-permute-start(bf16[320,1024]{1,0:T(8,128)(2,1)} %pad_maximum_fusion.1), channel_id=1, source_target_pairs={{4,8},{8,4},{5,9},{9,5},{6,10},{10,6},{7,11},{11,7},{20,24},{24,20... | collective-permute-start | bytes 1966088 | tf_op jit(solution)/shard_map/ppermute | solution.py:317
  11.6 25.5 %collective-permute-start = (bf16[320,1024]{1,0:T(8,128)(2,1)}, bf16[320,1024]{1,0:T(8,128)(2,1)}, u32[]{:S(2)}, u32[]{:S(2)}) collective-permute-start(bf16[320,1024]{1,0:T(8,128)(2,1)} %pad_maximum_fusion), channel_id=1, source_target_pairs={{0,4},{12,8},{1,5},{13,9},{2,6},{14,10},{3,7},{15,11},{16,20},{28,... | collective-permute-start | bytes 1966088 | tf_op jit(solution)/shard_map/ppermute | solution.py:316
  39.9 18.3 %copy-start = (bf16[320,1024]{1,0:T(8,128)(2,1)}, bf16[320,1024]{1,0:T(8,128)(2,1)S(1)}, u32[]{:S(2)}) copy-start(bf16[320,1024]{1,0:T(8,128)(2,1)S(1)} %fusion.25.refs_0_.refs_2_) | copy-start | bytes 1966084
  39.9 16.2 %collective-permute-start.5 = (bf16[320,1024]{1,0:T(8,128)(2,1)S(1)}, bf16[320,1024]{1,0:T(8,128)(2,1)S(1)}, u32[]{:S(2)}, u32[]{:S(2)}) collective-permute-start(bf16[320,1024]{1,0:T(8,128)(2,1)S(1)} %fusion.25.refs_0_.refs_2_), channel_id=1, source_target_pairs={{0,2},{2,0},{1,3},{3,1},{4,6},{6,4},{5,7},{7,5},{8,10},{10,8},{9,1... | collective-permute-start | bytes 1966088 | tf_op jit(solution)/shard_map/ppermute | solution.py:23
  41.4 14.7 %collective-permute-start.4 = (bf16[320,1024]{1,0:T(8,128)(2,1)S(1)}, bf16[320,1024]{1,0:T(8,128)(2,1)S(1)}, u32[]{:S(2)}, u32[]{:S(2)}) collective-permute-start(bf16[320,1024]{1,0:T(8,128)(2,1)S(1)} %fusion.25.refs_0_.refs_2_), channel_id=1, source_target_pairs={{0,1},{1,0},{2,3},{3,2},{4,5},{5,4},{6,7},{7,6},{8,9},{9,8},{10,11... | collective-permute-start | bytes 1966088 | tf_op jit(solution)/shard_map/ppermute | solution.py:23
  41.4 14.7 %collective-permute-start.3 = (bf16[320,1024]{1,0:T(8,128)(2,1)S(1)}, bf16[320,1024]{1,0:T(8,128)(2,1)S(1)}, u32[]{:S(2)}, u32[]{:S(2)}) collective-permute-start(bf16[320,1024]{1,0:T(8,128)(2,1)S(1)} %fusion.25.refs_0_.refs_2_), channel_id=1, source_target_pairs={{4,8},{8,4},{5,9},{9,5},{6,10},{10,6},{7,11},{11,7},{20,24},{24,20... | collective-permute-start | bytes 1966088 | tf_op jit(solution)/shard_map/ppermute | solution.py:352
  56.1 2.1 %copy-start.1 = (bf16[320,1024]{1,0:T(8,128)(2,1)}, bf16[320,1024]{1,0:T(8,128)(2,1)S(1)}, u32[]{:S(2)}) copy-start(bf16[320,1024]{1,0:T(8,128)(2,1)S(1)} %collective-permute-done.5.refs_4_) | copy-start | bytes 1966084
  56.1 2.1 %collective-permute-start.6 = (bf16[320,1024]{1,0:T(8,128)(2,1)S(1)}, bf16[320,1024]{1,0:T(8,128)(2,1)S(1)}, u32[]{:S(2)}, u32[]{:S(2)}) collective-permute-start(bf16[320,1024]{1,0:T(8,128)(2,1)S(1)} %collective-permute-done.5.refs_4_), channel_id=1, source_target_pairs={{0,1},{1,0},{2,3},{3,2},{4,5},{5,4},{6,7},{7,6},{8,9},{9,8},{10,11... | collective-permute-start | bytes 1966088 | tf_op jit(solution)/shard_map/ppermute | solution.py:23
  56.1 2.1 %copy-start.2 = (bf16[320,1024]{1,0:T(8,128)(2,1)}, bf16[320,1024]{1,0:T(8,128)(2,1)S(1)}, u32[]{:S(2)}) copy-start(bf16[320,1024]{1,0:T(8,128)(2,1)S(1)} %collective-permute-done.4.refs_3_) | copy-start | bytes 1966084
  56.1 2.1 %copy-start.3 = (bf16[320,1024]{1,0:T(8,128)(2,1)}, bf16[320,1024]{1,0:T(8,128)(2,1)S(1)}, u32[]{:S(2)}) copy-start(bf16[320,1024]{1,0:T(8,128)(2,1)S(1)} %collective-permute-done.3.refs_1_) | copy-start | bytes 1966084
  58.2 0.9 copy-start.4
  65.6 0.7 collective-permute-start.7
  67.5 28.9 %collective-permute-start.10 = (bf16[160,1024]{1,0:T(8,128)(2,1)S(1)}, bf16[160,1024]{1,0:T(8,128)(2,1)S(1)}, u32[]{:S(2)}, u32[]{:S(2)}) collective-permute-start(bf16[160,1024]{1,0:T(8,128)(2,1)S(1)} %fusion.31), channel_id=1, source_target_pairs={{4,12},{8,0},{5,13},{9,1},{6,14},{10,2},{7,15},{11,3},{20,28},{24,... | collective-permute-start | bytes 983048 | tf_op jit(solution)/shard_map/ppermute | solution.py:364
  68.8 27.6 %collective-permute-start.9 = (bf16[160,1024]{1,0:T(8,128)(2,1)S(1)}, bf16[160,1024]{1,0:T(8,128)(2,1)S(1)}, u32[]{:S(2)}, u32[]{:S(2)}) collective-permute-start(bf16[160,1024]{1,0:T(8,128)(2,1)S(1)} %fusion.31), channel_id=1, source_target_pairs={{4,8},{8,4},{5,9},{9,5},{6,10},{10,6},{7,11},{11,7},{20,24},{24,20... | collective-permute-start | bytes 983048 | tf_op jit(solution)/shard_map/ppermute | solution.py:363
  69.5 32.1 %collective-permute-start.8 = (bf16[160,1024]{1,0:T(8,128)(2,1)S(1)}, bf16[160,1024]{1,0:T(8,128)(2,1)S(1)}, u32[]{:S(2)}, u32[]{:S(2)}) collective-permute-start(bf16[160,1024]{1,0:T(8,128)(2,1)S(1)} %fusion.31), channel_id=1, source_target_pairs={{4,0},{8,12},{5,1},{9,13},{6,2},{10,14},{7,3},{11,15},{20,16},{24,... | collective-permute-start | bytes 983048 | tf_op jit(solution)/shard_map/ppermute | solution.py:362

commit v4 on v3

--- a/solution.py
+++ b/solution.py
@@ -267,17 +267,19 @@
     ) - lax.dot_general(row_data, col_data, CONTRACT_LAST, preferred_element_type=jnp.float32)
     normalizer = 0.5 * (row_power + col_power) + epsilon
     coupling = (weight_ref[...] * cross / normalizer).astype(jnp.bfloat16)
-    out_ref[...] = jnp.dot(coupling, col_model, preferred_element_type=jnp.float32)
-
-
-def couple(rows, cols, weights):
+    out_ref[...] = jnp.dot(
+        coupling, col_model, preferred_element_type=jnp.float32
+    ).astype(out_ref.dtype)
+
+
+def couple(rows, cols, weights, kind):
     args = [*rows, *cols, weights]
     height, width = weights.shape
     return pl.pallas_call(
         functools.partial(couple_kernel, len(rows), len(cols)),
         in_specs=[pl.BlockSpec(memory_space=pltpu.VMEM)] * len(args),
         out_specs=pl.BlockSpec(memory_space=pltpu.VMEM),
-        out_shape=jax.ShapeDtypeStruct((height, 2 * NF), jnp.float32),
+        out_shape=jax.ShapeDtypeStruct((height, 2 * NF), kind),
         cost_estimate=pl.CostEstimate(
             flops=12 * height * width * NF,
             bytes_accessed=8 * (height + width) * NF,
@@ -285,6 +287,43 @@
         ),
         name="couple",
     )(*args)
+
+
+def to_time_kernel(flag_ref, here_ref, there_ref, basis_ref, *rest):
+    out_ref = rest[-1]
+    adjoint = jnp.where(flag_ref[1] == 1, here_ref[...], there_ref[...])
+    traces = lax.dot_general(
+        adjoint, basis_ref[...], CONTRACT_LAST, preferred_element_type=jnp.float32
+    )
+    out_ref[...] = (traces * (1.0 / math.sqrt(NF))).astype(jnp.bfloat16)
+
+
+def to_time(place, is_inner, here, there, basis, span, rows, before):
+    half = here.shape[0]
+    wide = math.gcd(span, 256)
+    whole = pl.BlockSpec(here.shape, lambda j, flags: (0, 0))
+    specs = [whole, whole, pl.BlockSpec((wide, 2 * NF), lambda j, flags: (j, 0))]
+    args = [here, there, basis]
+    aliases = {}
+    if before is not None:
+        specs.append(pl.BlockSpec(memory_space=pl.ANY))
+        args.append(before)
+        aliases = {4: 0}
+    return pl.pallas_call(
+        to_time_kernel,
+        grid_spec=pltpu.PrefetchScalarGridSpec(
+            num_scalar_prefetch=1,
+            grid=(span // wide,),
+            in_specs=specs,
+            out_specs=pl.BlockSpec((half, wide), lambda j, flags: (flags[0], j)),
+        ),
+        out_shape=jax.ShapeDtypeStruct((rows, span), jnp.bfloat16),
+        input_output_aliases=aliases,
+        cost_estimate=pl.CostEstimate(
+            flops=4 * half * span * NF, bytes_accessed=4 * span * NF, transcendentals=0
+        ),
+        name="to_time",
+    )(jnp.stack([place, is_inner.astype(jnp.int32)]).astype(jnp.int32), *args)
 
 
 def inner_body(synthetic, observed, station_weights, pair_mask):
@@ -300,8 +339,7 @@
     stations = station_weights.shape[0]
     piece = half // per_half
     side = level // 2
-    inward, across, swapped = [(0, 1), (3, 2)], [(0, 2), (3, 1)], [(1, 2), (2, 1)]
-    outward, beyond = [(1, 0), (2, 3)], [(1, 3), (2, 0)]
+    inward, swapped, outward = [(0, 1), (3, 2)], [(1, 2), (2, 1)], [(1, 0), (2, 3)]
 
     def stations_of(which):
         return jnp.concatenate(
@@ -312,10 +350,9 @@
             axis=0,
         )
 
-    kept, sent = stations_of(side), stations_of(1 - side)
-    near = lax.ppermute(kept, "blk", inward)
-    middle = lax.ppermute(sent, "blk", swapped)
-    far = lax.ppermute(sent, "blk", across)
+    passed, kept = stations_of(1 - side), stations_of(side)
+    near_passed = lax.ppermute(passed, "blk", inward)
+    near_kept = lax.ppermute(kept, "blk", inward)
 
     member = sub * pairs + pair
     hops = [(s, q) for s in range(subs) for q in range(pairs)]
@@ -335,45 +372,45 @@
         * gains[col_pieces].reshape(1, -1)
         * jnp.repeat(jnp.repeat(active, piece, axis=0), piece, axis=1)
     )
-
-    sources = [level, level ^ 1, levels - 1 - level, (level + 2) % levels]
-    basis = make_basis(jnp.stack(sources).astype(jnp.int32) * span, span)
-    total = None
-    far, weights = lax.optimization_barrier((far, weights))
-    for place, block in enumerate([kept, near, middle, far]):
-        part = jnp.dot(
-            block,
-            basis[place * span : (place + 1) * span],
-            preferred_element_type=jnp.float32,
-        )
-        total = part if total is None else total + part
-    own = (total * (1.0 / math.sqrt(NT))).astype(jnp.bfloat16)
-
-    other = lax.ppermute(own, "blk", swapped)
+    own_weights, other_weights = weights[:half], weights[half:]
+
+    basis = make_basis(jnp.stack([level, level ^ 1]).astype(jnp.int32) * span, span)
+    scale = 1.0 / math.sqrt(NT)
+
+    def transform(here, near):
+        return (
+            jnp.dot(here, basis[:span], preferred_element_type=jnp.float32)
+            + jnp.dot(near, basis[span:], preferred_element_type=jnp.float32)
+        ) * scale
+
+    to_pass = transform(passed, near_passed).astype(jnp.bfloat16)
+    kept_rest = lax.ppermute(to_pass, "blk", swapped)
+    near_kept, own_weights, other_weights = lax.optimization_barrier(
+        (near_kept, own_weights, other_weights)
+    )
+    kept_sum = transform(kept, near_kept)
+    passed_rest = lax.ppermute(kept_sum.astype(jnp.bfloat16), "blk", swapped)
+    own = (kept_sum + kept_rest.astype(jnp.float32)).astype(jnp.bfloat16)
     cols = []
     for s, q in hops:
         if q == 0:
             here = own if s == 0 else shift(own, "sub", s)
         cols.append(here if q == 0 else shift(here, "pair", q))
-    running = couple([own, other], cols, weights)
-
-    received = lax.ppermute(running[half:].astype(jnp.bfloat16), "blk", swapped)
-    adjoint = (running[:half] + received.astype(jnp.float32)).astype(jnp.bfloat16)
-    first = lax.ppermute(adjoint, "blk", outward)
-    second = lax.ppermute(adjoint, "blk", swapped)
-    third = lax.ppermute(adjoint, "blk", beyond)
+    other = (to_pass.astype(jnp.float32) + passed_rest.astype(jnp.float32)).astype(jnp.bfloat16)
+
+    other_part = couple([other], cols, other_weights, jnp.bfloat16)
+    own_rest = lax.ppermute(other_part, "blk", swapped)
+    own_part = couple([own], cols, own_weights, jnp.bfloat16)
+    other_rest = lax.ppermute(own_part, "blk", swapped)
+    widen = lambda a: a.astype(jnp.float32)
+    own_adjoint = (widen(own_part) + widen(own_rest)).astype(jnp.bfloat16)
+    near_own = lax.ppermute(own_adjoint, "blk", outward)
+    other_adjoint = (widen(other_part) + widen(other_rest)).astype(jnp.bfloat16)
+    near_other = lax.ppermute(other_adjoint, "blk", outward)
     is_inner = (level == 1) | (level == 2)
-    mine = jnp.where(is_inner, adjoint, first)
-    theirs = jnp.where(is_inner, second, third)
-    gathered = jnp.concatenate(
-        [jnp.where(side == 0, mine, theirs), jnp.where(side == 0, theirs, mine)], axis=0
-    )
-    return (
-        lax.dot_general(
-            gathered, basis[:span], CONTRACT_LAST, preferred_element_type=jnp.float32
-        )
-        * (1.0 / math.sqrt(NF))
-    ).astype(jnp.bfloat16)
+    rows = synthetic.shape[0]
+    traces = to_time(side, is_inner, own_adjoint, near_own, basis, span, rows, None)
+    return to_time(1 - side, is_inner, other_adjoint, near_other, basis, span, rows, traces)
 
 
 def shards(*args):

time: 105 us -> 116 us (1.10)
  Pallas kernels: 14.3 us -> 23 us
  waiting for transfers between devices: 46.8 us -> 54.3 us
  matrix products: 13.8 us -> 7.41 us
  starting transfers between devices: 16.8 us -> 15 us
  local copies, waits for them, and re-layouts: 6.73 us -> 7.98 us
  other arithmetic: 6.32 us -> 7.52 us
    pallas_call x0 -> x2, Pallas kernels: none -> 9.81 us  [to_time(): pl.pallas_call(to_time_kernel, grid_spec=pltpu.PrefetchScalarGridSpec(num...]
    ppermute x8, waiting for transfers between devices: 30.8 us -> 40 us  [the longest x1 29.2 us: inner_body(): near_own = lax.ppermute(own_adjoint, 'blk', outward)]
    dot_general x5 -> x4, matrix products: 13.8 us -> 7.41 us  [the longest x2 3.98 us: transform(): jnp.dot(near, basis[span:], preferred_element_type=jnp.float32)]
    pallas_call x1, Pallas kernels: 8.89 us -> 5 us  [make_basis(): pl.pallas_call(functools.partial(basis_kernel, per_step, low_rows), grid=...]
    pallas_call x1 -> x2, Pallas kernels: 5.39 us -> 8.21 us  [couple(): pl.pallas_call(functools.partial(couple_kernel, len(rows), len(cols)), in...]
    ppermute x8, starting transfers between devices: 15.2 us -> 13.4 us  [the longest x1 5.83 us: inner_body(): near_kept = lax.ppermute(kept, 'blk', inward)]
    ppermute x3, waiting for transfers between devices: 16 us -> 14.3 us  [shift(): return lax.ppermute(value, axis, pairs)]
    unnamed x15 -> x25, local copies, waits for them, and re-layouts: 0.99 us -> 2.42 us
  transfers between devices with their start and end apart: 11 -> 11, of which waited for: 4 -> 4; matrix products, arithmetic and copies ran while one was open for 15% -> 14% of each run, Pallas kernels for 8% -> 12%
where the time goes in v4:
time: 116 us
  waiting for transfers between devices  54.3 us (47%)
  Pallas kernels  23 us (20%)
  starting transfers between devices  15 us (13%)
  local copies, waits for them, and re-layouts  7.98 us (7%)
  other arithmetic  7.52 us (6%)
  matrix products  7.41 us (6%)
    ppermute x1, waiting for transfers between devices, inner_body(): near_own = lax.ppermute(own_adjoint, 'blk', outward)  29.2 us
    ppermute x3, waiting for transfers between devices, shift(): return lax.ppermute(value, axis, pairs)  14.3 us
    ppermute x1, waiting for transfers between devices, inner_body(): near_passed = lax.ppermute(passed, 'blk', inward)  10.8 us
    pallas_call x2, Pallas kernels, to_time(): pl.pallas_call(to_time_kernel, grid_spec=pltpu.PrefetchScalarGridSpec(num...  9.81 us
    pallas_call x2, Pallas kernels, couple(): pl.pallas_call(functools.partial(couple_kernel, len(rows), len(cols)), in...  8.21 us
    ppermute x1, starting transfers between devices, inner_body(): near_kept = lax.ppermute(kept, 'blk', inward)  5.83 us
    pallas_call x1, Pallas kernels, make_basis(): pl.pallas_call(functools.partial(basis_kernel, per_step, low_rows), grid=...  5 us
    dot_general x2, matrix products, transform(): jnp.dot(near, basis[span:], preferred_element_type=jnp.float32)  3.98 us
  transfers between devices with their start and end apart: 11, of which 4 were waited for; matrix products, arithmetic and copies ran while one was open for 14% of the time, Pallas kernels for 12%

profile of v4, /device:TPU:0, one launch (start us, length us, event | category | flops | bytes accessed | tf_op | source)
XLA Modules:
  0.0 115.6 jit_solution(13861680802706889536)
XLA Ops:
  0.0 1.4 %constant_dynamic-slice_fusion.2 = (bf16[160,1024]{1,0:T(8,128)(2,1)S(1)}, bf16[160,1024]{1,0:T(8,128)(2,1)S(1)}, bf16[160,1024]{1,0:T(8,128)(2,1)S(1)}, bf16[160,1024]{1,0:T(8,128)(2,1)S(1)}) fusion(bf16[320,1024]{1,0:T(8,128)(2,1)} %param.5, s32[]{:T(128)S(6)} %select_n.76, s32[]{:T(128)S(6)} %select_n.79, bf16[320,1024]{1,0:T(8,128)(2,1)} %param.4), kind=kLoop, calls=%fused_computation.56 | loop fusion | bytes 2621448 | tf_op jit(solution)/shard_map/dynamic_slice | solution.py:348
  1.4 0.0 copy-start.11
  1.4 0.0 copy-start.10
  1.4 0.9 pad_maximum_fusion.1
  2.3 5.8 %collective-permute-start.1 = (bf16[320,1024]{1,0:T(8,128)(2,1)}, bf16[320,1024]{1,0:T(8,128)(2,1)}, u32[]{:S(2)}, u32[]{:S(2)}) collective-permute-start(bf16[320,1024]{1,0:T(8,128)(2,1)} %pad_maximum_fusion.1), channel_id=1, source_target_pairs={{0,4},{12,8},{1,5},{13,9},{2,6},{14,10},{3,7},{15,11},{16,20},{28,... | collective-permute-start | bytes 1966088 | tf_op jit(solution)/shard_map/ppermute | solution.py:355
  8.1 0.9 pad_maximum_fusion
  9.0 2.1 %collective-permute-start = (bf16[320,1024]{1,0:T(8,128)(2,1)}, bf16[320,1024]{1,0:T(8,128)(2,1)}, u32[]{:S(2)}, u32[]{:S(2)}) collective-permute-start(bf16[320,1024]{1,0:T(8,128)(2,1)} %pad_maximum_fusion), channel_id=1, source_target_pairs={{0,4},{12,8},{1,5},{13,9},{2,6},{14,10},{3,7},{15,11},{16,20},{28,... | collective-permute-start | bytes 1966088 | tf_op jit(solution)/shard_map/ppermute | solution.py:354
  11.1 0.1 add_multiply_fusion
  11.2 0.1 broadcast_add_fusion
  11.3 0.1 add.205
  11.4 0.1 fusion.39
  11.5 0.1 iota_add_fusion
  11.5 0.1 add.232
  11.6 0.1 fusion.37
  11.7 0.1 reshape.158
  11.8 0.6 gather_fusion
  12.4 0.6 gather_fusion.1
  12.9 0.1 mul.161
  13.0 0.1 mul.156
  13.1 0.1 copy.9
  13.2 1.0 fusion.34
  14.2 0.6 gather_fusion.2
  14.7 0.1 copy.10
  14.8 0.6 gather_fusion.3
  15.4 0.1 broadcast_in_dim.4
  15.5 0.1 reshape.159
  15.5 0.1 broadcast_in_dim.5
  15.6 0.3 copy.11
  15.9 1.2 %fusion.32 = (f32[64,512]{1,0:T(8,128)}, f32[64,512]{1,0:T(8,128)}) fusion(s32[512]{0:T(512)S(1)} %iota_add_fusion.1), kind=kLoop, calls=%fused_computation.41 | loop fusion | flops 458752 | bytes 264192 | tf_op jit(solution)/shard_map/sin | solution.py:39
  17.2 5.0 %basis.1.basis_ref = bf16[2048,1024]{1,0:T(8,128)(2,1)} custom-call(f32[32,512]{1,0:T(8,128)} %get-tuple-element.20.hc_ref, f32[32,512]{1,0:T(8,128)} %get-tuple-element.19.hs_ref, f32[64,512]{1,0:T(8,128)} %get-tuple-element.22.lc_ref, f32[64,512]{1,0:T(8,128)} %get-tuple-element.21.ls_ref), custom_call_target="tpu_custom_call" | custom-call | flops 8388608 | bytes 4194304 | tf_op jit(solution)/shard_map/basis/pallas_call | solution.py:62
  22.2 2.6 %fusion.6 = f32[320,1024]{1,0:T(8,128)S(1)} fusion(bf16[2048,1024]{1,0:T(8,128)(2,1)} %basis.1.basis_ref, bf16[160,1024]{1,0:T(8,128)(2,1)S(1)} %get-tuple-element.17, bf16[160,1024]{1,0:T(8,128)(2,1)S(1)} %get-tuple-element.26), kind=kOutput, calls=%fused_computation.10 | convolution fusion | flops 672399360 | bytes 4063232 | tf_op jit(solution)/shard_map/dot_general | solution.py:382
  24.8 10.8 %collective-permute-done = bf16[320,1024]{1,0:T(8,128)(2,1)} collective-permute-done((bf16[320,1024]{1,0:T(8,128)(2,1)}, bf16[320,1024]{1,0:T(8,128)(2,1)}, u32[]{:S(2)}, u32[]{:S(2)}) %collective-permute-start) | collective-permute-done | bytes 655392 | tf_op jit(solution)/shard_map/ppermute | solution.py:354
  35.6 2.0 %fusion.20 = bf16[320,1024]{1,0:T(8,128)(2,1)S(1)} fusion(f32[320,1024]{1,0:T(8,128)S(1)} %fusion.6, bf16[320,1024]{1,0:T(8,128)(2,1)} %collective-permute-done, bf16[2048,1024]{1,0:T(8,128)(2,1)S(1)} %copy-done), kind=kOutput, calls=%fused_computation.16 | convolution fusion | flops 672071680 | bytes 4718592 | tf_op jit(solution)/shard_map/dot_general | solution.py:383
  37.5 0.7 collective-permute-start.3
  38.2 0.1 multiply_multiply_fusion
  38.4 0.9 fusion.41
  39.3 0.9 fusion.4
  40.2 0.0 collective-permute-done.3
  40.2 2.0 %fusion.40 = (bf16[320,1024]{1,0:T(8,128)(2,1)S(1)}, bf16[320,1024]{1,0:T(8,128)(2,1)S(1)}) fusion(bf16[320,1024]{1,0:T(8,128)(2,1)S(1)} %collective-permute-done.3, f32[320,1024]{1,0:T(8,128)S(1)} %fusion.4, bf16[320,1024]{1,0:T(8,128)(2,1)} %collective-permute-done.1, bf16[2048,1024]{1,0:T(8,128)(2,1)S(1)} %copy-done), kind=kOutput, calls=%fused_computation.70 | convolution fusion | flops 673054720 | bytes 6029312 | tf_op jit(solution)/shard_map/dot_general | solution.py:383
  42.2 0.0 copy-start.1
  42.2 1.6 %collective-permute-start.5 = (bf16[320,1024]{1,0:T(8,128)(2,1)S(1)}, bf16[320,1024]{1,0:T(8,128)(2,1)S(1)}, u32[]{:S(2)}, u32[]{:S(2)}) collective-permute-start(bf16[320,1024]{1,0:T(8,128)(2,1)S(1)} %get-tuple-element.12.refs_1_.refs_0_), channel_id=1, source_target_pairs={{0,2},{2,0},{1,3},{3,1},{4,6},{6,4},{5,7},{7,5},{8,10},{10,8},{9,1... | collective-permute-start | bytes 1966088 | tf_op jit(solution)/shard_map/ppermute | solution.py:23
  43.8 0.7 collective-permute-start.2
  44.5 0.1 collective-permute-start.4
  44.6 13.4 %collective-permute-done.5.refs_3_ = bf16[320,1024]{1,0:T(8,128)(2,1)S(1)} collective-permute-done((bf16[320,1024]{1,0:T(8,128)(2,1)S(1)}, bf16[320,1024]{1,0:T(8,128)(2,1)S(1)}, u32[]{:S(2)}, u32[]{:S(2)}) %collective-permute-start.5) | collective-permute-done | bytes 655392 | tf_op jit(solution)/shard_map/ppermute | solution.py:23
  57.9 0.0 collective-permute-start.6
  57.9 0.0 collective-permute-done.2
  57.9 1.1 add_convert_fusion.1.refs_0_
  59.0 1.0 collective-permute-done.6.refs_4_
  60.0 0.8 copy-done.4
  60.9 4.1 %couple.2 = bf16[160,1024]{1,0:T(8,128)(2,1)} custom-call(bf16[320,1024]{1,0:T(8,128)(2,1)} %add_convert_fusion.1.refs_0_, bf16[320,1024]{1,0:T(8,128)(2,1)} %copy-done.1, bf16[320,1024]{1,0:T(8,128)(2,1)} %copy-done.3, bf16[320,1024]{1,0:T(8,128)(2,1)} %copy-done.2, bf16[320,1024]{1,0:T(8,128)(2,1)} %copy-done.4, f32[160,640]{1,0:T(8,128)} %get-tuple-element.9.refs_5_), custom_call_target="tpu_custom_call" | custom-call | flops 629145600 | bytes 3276800 | tf_op jit(solution)/shard_map/couple/pallas_call | solution.py:278
  65.0 0.8 collective-permute-start.9
  65.8 4.1 %couple.3 = bf16[160,1024]{1,0:T(8,128)(2,1)} custom-call(bf16[320,1024]{1,0:T(8,128)(2,1)} %copy-done.1, bf16[320,1024]{1,0:T(8,128)(2,1)} %copy-done.1, bf16[320,1024]{1,0:T(8,128)(2,1)} %copy-done.3, bf16[320,1024]{1,0:T(8,128)(2,1)} %copy-done.2, bf16[320,1024]{1,0:T(8,128)(2,1)} %copy-done.4, f32[160,640]{1,0:T(8,128)} %get-tuple-element.10.refs_5_), custom_call_target="tpu_custom_call" | custom-call | flops 629145600 | bytes 3276800 | tf_op jit(solution)/shard_map/couple/pallas_call | solution.py:278
  69.9 0.7 collective-permute-start.7
  70.6 1.1 add_convert_fusion.2.here_ref
  71.7 1.3 %collective-permute-start.10 = (bf16[160,1024]{1,0:T(8,128)(2,1)S(1)}, bf16[160,1024]{1,0:T(8,128)(2,1)S(1)}, u32[]{:S(2)}, u32[]{:S(2)}) collective-permute-start(bf16[160,1024]{1,0:T(8,128)(2,1)S(1)} %add_convert_fusion.2.here_ref), channel_id=1, source_target_pairs={{4,0},{8,12},{5,1},{9,13},{6,2},{10,14},{7,3},{11,15},{20,16},{24,... | collective-permute-start | bytes 983048 | tf_op jit(solution)/shard_map/ppermute | solution.py:407
  73.0 0.0 collective-permute-done.7
  73.0 0.1 add_convert_fusion.3.here_ref
  73.1 1.3 %collective-permute-start.8 = (bf16[160,1024]{1,0:T(8,128)(2,1)S(1)}, bf16[160,1024]{1,0:T(8,128)(2,1)S(1)}, u32[]{:S(2)}, u32[]{:S(2)}) collective-permute-start(bf16[160,1024]{1,0:T(8,128)(2,1)S(1)} %add_convert_fusion.3.here_ref), channel_id=1, source_target_pairs={{4,0},{8,12},{5,1},{9,13},{6,2},{10,14},{7,3},{11,15},{20,16},{24,... | collective-permute-start | bytes 983048 | tf_op jit(solution)/shard_map/ppermute | solution.py:409
  74.4 0.7 pad_add_fusion
  75.1 29.2 %collective-permute-done.10.there_ref = bf16[160,1024]{1,0:T(8,128)(2,1)S(1)} collective-permute-done((bf16[160,1024]{1,0:T(8,128)(2,1)S(1)}, bf16[160,1024]{1,0:T(8,128)(2,1)S(1)}, u32[]{:S(2)}, u32[]{:S(2)}) %collective-permute-start.10) | collective-permute-done | bytes 327712 | tf_op jit(solution)/shard_map/ppermute | solution.py:407
  104.3 0.7 copy-done.8
  105.0 4.9 %to_time.2.rest_0_ = bf16[320,1024]{1,0:T(8,128)(2,1)} custom-call(s32[2]{0:T(128)} %get-tuple-element.24.flag_ref, bf16[160,1024]{1,0:T(8,128)(2,1)} %copy-done.5, bf16[160,1024]{1,0:T(8,128)(2,1)} %copy-done.8, bf16[2048,1024]{1,0:T(8,128)(2,1)} %basis.1.basis_ref), custom_call_target="tpu_custom_call" | custom-call | flops 335544320 | bytes 2097152 | tf_op jit(solution)/shard_map/to_time/pallas_call | solution.py:312
  110.0 0.7 copy-done.9
  110.7 4.9 %to_time.3 = bf16[320,1024]{1,0:T(8,128)(2,1)} custom-call(s32[2]{0:T(128)} %get-tuple-element.23.flag_ref, bf16[160,1024]{1,0:T(8,128)(2,1)} %copy-done.6, bf16[160,1024]{1,0:T(8,128)(2,1)} %copy-done.9, bf16[2048,1024]{1,0:T(8,128)(2,1)} %basis.1.basis_ref, bf16[320,1024]{1,0:T(8,128)(2,1)} %to_time.2.rest_0_), custom_call_target="tpu_custom_call", output_to_operand_aliasing={{}: (4, {})} | custom-call | flops 335544320 | bytes 2097152 | tf_op jit(solution)/shard_map/to_time/pallas_call | solution.py:312
  (31 shorter events, 0.1 us)
Async XLA Ops:
  1.4 10.4 %copy-start.11 = (s32[1280]{0:T(1024)S(1)}, s32[1280]{0:T(1024)}, u32[]{:S(2)}) copy-start(s32[1280]{0:T(1024)} %param.6) | copy-start | bytes 15364
  1.4 11.7 %copy-start.10 = (s32[16,16]{1,0:T(8,128)S(1)}, s32[16,16]{1,0:T(8,128)}, u32[]{:S(2)}) copy-start(s32[16,16]{1,0:T(8,128)} %param.7) | copy-start | bytes 3076
  2.3 37.9 %collective-permute-start.1 = (bf16[320,1024]{1,0:T(8,128)(2,1)}, bf16[320,1024]{1,0:T(8,128)(2,1)}, u32[]{:S(2)}, u32[]{:S(2)}) collective-permute-start(bf16[320,1024]{1,0:T(8,128)(2,1)} %pad_maximum_fusion.1), channel_id=1, source_target_pairs={{0,4},{12,8},{1,5},{13,9},{2,6},{14,10},{3,7},{15,11},{16,20},{28,... | collective-permute-start | bytes 1966088 | tf_op jit(solution)/shard_map/ppermute | solution.py:355
  9.0 26.6 %collective-permute-start = (bf16[320,1024]{1,0:T(8,128)(2,1)}, bf16[320,1024]{1,0:T(8,128)(2,1)}, u32[]{:S(2)}, u32[]{:S(2)}) collective-permute-start(bf16[320,1024]{1,0:T(8,128)(2,1)} %pad_maximum_fusion), channel_id=1, source_target_pairs={{0,4},{12,8},{1,5},{13,9},{2,6},{14,10},{3,7},{15,11},{16,20},{28,... | collective-permute-start | bytes 1966088 | tf_op jit(solution)/shard_map/ppermute | solution.py:354
  22.2 13.4 %copy-start = (bf16[2048,1024]{1,0:T(8,128)(2,1)S(1)}, bf16[2048,1024]{1,0:T(8,128)(2,1)}, u32[]{:S(2)}) copy-start(bf16[2048,1024]{1,0:T(8,128)(2,1)} %basis.1.basis_ref) | copy-start | bytes 12582916
  37.5 2.7 %collective-permute-start.3 = (bf16[320,1024]{1,0:T(8,128)(2,1)S(1)}, bf16[320,1024]{1,0:T(8,128)(2,1)S(1)}, u32[]{:S(2)}, u32[]{:S(2)}) collective-permute-start(bf16[320,1024]{1,0:T(8,128)(2,1)S(1)} %fusion.20), channel_id=1, source_target_pairs={{4,8},{8,4},{5,9},{9,5},{6,10},{10,6},{7,11},{11,7},{20,24},{24,20... | collective-permute-start | bytes 1966088 | tf_op jit(solution)/shard_map/ppermute | solution.py:387
  42.2 17.8 %copy-start.1 = (bf16[320,1024]{1,0:T(8,128)(2,1)}, bf16[320,1024]{1,0:T(8,128)(2,1)S(1)}, u32[]{:S(2)}) copy-start(bf16[320,1024]{1,0:T(8,128)(2,1)S(1)} %get-tuple-element.12.refs_1_.refs_0_) | copy-start | bytes 1966084
  42.2 15.7 %collective-permute-start.5 = (bf16[320,1024]{1,0:T(8,128)(2,1)S(1)}, bf16[320,1024]{1,0:T(8,128)(2,1)S(1)}, u32[]{:S(2)}, u32[]{:S(2)}) collective-permute-start(bf16[320,1024]{1,0:T(8,128)(2,1)S(1)} %get-tuple-element.12.refs_1_.refs_0_), channel_id=1, source_target_pairs={{0,2},{2,0},{1,3},{3,1},{4,6},{6,4},{5,7},{7,5},{8,10},{10,8},{9,1... | collective-permute-start | bytes 1966088 | tf_op jit(solution)/shard_map/ppermute | solution.py:23
  43.8 14.1 %collective-permute-start.2 = (bf16[320,1024]{1,0:T(8,128)(2,1)S(1)}, bf16[320,1024]{1,0:T(8,128)(2,1)S(1)}, u32[]{:S(2)}, u32[]{:S(2)}) collective-permute-start(bf16[320,1024]{1,0:T(8,128)(2,1)S(1)} %get-tuple-element.11), channel_id=1, source_target_pairs={{4,8},{8,4},{5,9},{9,5},{6,10},{10,6},{7,11},{11,7},{20,24},{24,20... | collective-permute-start | bytes 1966088 | tf_op jit(solution)/shard_map/ppermute | solution.py:392
  44.5 14.5 %collective-permute-start.4 = (bf16[320,1024]{1,0:T(8,128)(2,1)S(1)}, bf16[320,1024]{1,0:T(8,128)(2,1)S(1)}, u32[]{:S(2)}, u32[]{:S(2)}) collective-permute-start(bf16[320,1024]{1,0:T(8,128)(2,1)S(1)} %get-tuple-element.12.refs_1_.refs_0_), channel_id=1, source_target_pairs={{0,1},{1,0},{2,3},{3,2},{4,5},{5,4},{6,7},{7,6},{8,9},{9,8},{10,11... | collective-permute-start | bytes 1966088 | tf_op jit(solution)/shard_map/ppermute | solution.py:23
  57.9 2.1 %copy-start.2 = (bf16[320,1024]{1,0:T(8,128)(2,1)}, bf16[320,1024]{1,0:T(8,128)(2,1)S(1)}, u32[]{:S(2)}) copy-start(bf16[320,1024]{1,0:T(8,128)(2,1)S(1)} %collective-permute-done.5.refs_3_) | copy-start | bytes 1966084
  57.9 2.1 %collective-permute-start.6 = (bf16[320,1024]{1,0:T(8,128)(2,1)S(1)}, bf16[320,1024]{1,0:T(8,128)(2,1)S(1)}, u32[]{:S(2)}, u32[]{:S(2)}) collective-permute-start(bf16[320,1024]{1,0:T(8,128)(2,1)S(1)} %collective-permute-done.5.refs_3_), channel_id=1, source_target_pairs={{0,1},{1,0},{2,3},{3,2},{4,5},{5,4},{6,7},{7,6},{8,9},{9,8},{10,11... | collective-permute-start | bytes 1966088 | tf_op jit(solution)/shard_map/ppermute | solution.py:23
  59.0 1.0 copy-start.3
  60.0 0.8 copy-start.4
  65.0 8.0 %copy-start.7 = (bf16[160,1024]{1,0:T(8,128)(2,1)S(1)}, bf16[160,1024]{1,0:T(8,128)(2,1)}, u32[]{:S(2)}) copy-start(bf16[160,1024]{1,0:T(8,128)(2,1)} %couple.2) | copy-start | bytes 983044
  65.0 5.6 %collective-permute-start.9 = (bf16[160,1024]{1,0:T(8,128)(2,1)}, bf16[160,1024]{1,0:T(8,128)(2,1)S(1)}, u32[]{:S(2)}, u32[]{:S(2)}) collective-permute-start(bf16[160,1024]{1,0:T(8,128)(2,1)} %couple.2), channel_id=1, source_target_pairs={{4,8},{8,4},{5,9},{9,5},{6,10},{10,6},{7,11},{11,7},{20,24},{24,20... | collective-permute-start | bytes 983048 | tf_op jit(solution)/shard_map/ppermute | solution.py:402
  69.9 3.1 %collective-permute-start.7 = (bf16[160,1024]{1,0:T(8,128)(2,1)}, bf16[160,1024]{1,0:T(8,128)(2,1)S(1)}, u32[]{:S(2)}, u32[]{:S(2)}) collective-permute-start(bf16[160,1024]{1,0:T(8,128)(2,1)} %couple.3), channel_id=1, source_target_pairs={{4,8},{8,4},{5,9},{9,5},{6,10},{10,6},{7,11},{11,7},{20,24},{24,20... | collective-permute-start | bytes 983048 | tf_op jit(solution)/shard_map/ppermute | solution.py:404
  71.7 32.6 %copy-start.5 = (bf16[160,1024]{1,0:T(8,128)(2,1)}, bf16[160,1024]{1,0:T(8,128)(2,1)S(1)}, u32[]{:S(2)}) copy-start(bf16[160,1024]{1,0:T(8,128)(2,1)S(1)} %add_convert_fusion.2.here_ref) | copy-start | bytes 983044
  71.7 32.6 %collective-permute-start.10 = (bf16[160,1024]{1,0:T(8,128)(2,1)S(1)}, bf16[160,1024]{1,0:T(8,128)(2,1)S(1)}, u32[]{:S(2)}, u32[]{:S(2)}) collective-permute-start(bf16[160,1024]{1,0:T(8,128)(2,1)S(1)} %add_convert_fusion.2.here_ref), channel_id=1, source_target_pairs={{4,0},{8,12},{5,1},{9,13},{6,2},{10,14},{7,3},{11,15},{20,16},{24,... | collective-permute-start | bytes 983048 | tf_op jit(solution)/shard_map/ppermute | solution.py:407
  73.1 36.8 %copy-start.6 = (bf16[160,1024]{1,0:T(8,128)(2,1)}, bf16[160,1024]{1,0:T(8,128)(2,1)S(1)}, u32[]{:S(2)}) copy-start(bf16[160,1024]{1,0:T(8,128)(2,1)S(1)} %add_convert_fusion.3.here_ref) | copy-start | bytes 983044
  73.1 36.8 %collective-permute-start.8 = (bf16[160,1024]{1,0:T(8,128)(2,1)S(1)}, bf16[160,1024]{1,0:T(8,128)(2,1)S(1)}, u32[]{:S(2)}, u32[]{:S(2)}) collective-permute-start(bf16[160,1024]{1,0:T(8,128)(2,1)S(1)} %add_convert_fusion.3.here_ref), channel_id=1, source_target_pairs={{4,0},{8,12},{5,1},{9,13},{6,2},{10,14},{7,3},{11,15},{20,16},{24,... | collective-permute-start | bytes 983048 | tf_op jit(solution)/shard_map/ppermute | solution.py:409
  104.3 0.7 copy-start.8
  110.0 0.7 copy-start.9

commit v5 on v4

--- a/solution.py
+++ b/solution.py
@@ -68,6 +68,7 @@
         cost_estimate=pl.CostEstimate(
             flops=8 * rows * NF, bytes_accessed=4 * rows * NF, transcendentals=0
         ),
+        compiler_params=pltpu.CompilerParams(vmem_limit_bytes=16 << 20),
         name="basis",
     )(high_c, high_s, low_c, low_s)
 
@@ -239,20 +240,29 @@
     return rate, jnp.sum(jnp.square(rate.astype(jnp.float32)), axis=1, keepdims=True)
 
 
-def couple_kernel(row_count, col_count, *refs):
+def planes(ref, piece):
+    starts = range(0, ref.shape[0], 2 * piece)
+    return tuple(
+        jnp.concatenate([ref[at + off : at + off + piece] for at in starts], axis=0)
+        for off in (0, piece)
+    )
+
+
+def couple_kernel(piece, row_count, col_count, *refs):
     row_refs = refs[:row_count]
     col_refs = refs[row_count : row_count + col_count]
     weight_ref, out_ref = refs[-2:]
-    half = row_refs[0].shape[0] // 2
-    row_model = jnp.concatenate([ref[:half] for ref in row_refs], axis=0)
-    row_data = jnp.concatenate([ref[half:] for ref in row_refs], axis=0)
-    row_power = jnp.concatenate([power_of(ref[:half])[1] for ref in row_refs], axis=0)
+    row_planes = [planes(ref, piece) for ref in row_refs]
+    row_model = jnp.concatenate([model for model, _ in row_planes], axis=0)
+    row_data = jnp.concatenate([data for _, data in row_planes], axis=0)
+    row_power = power_of(row_model)[1]
     models, datas, powers = [], [], []
     for ref in col_refs:
-        rate, power = power_of(ref[:half])
+        model, data = planes(ref, piece)
+        rate, power = power_of(model)
         models.append(rate)
         powers.append(power)
-        wide = ref[half:].astype(jnp.float32)
+        wide = data.astype(jnp.float32)
         datas.append(rate_of(wide[:, :NF], wide[:, NF:]))
     col_model = jnp.concatenate(models, axis=0)
     col_data = jnp.concatenate(datas, axis=0)
@@ -272,19 +282,20 @@
     ).astype(out_ref.dtype)
 
 
-def couple(rows, cols, weights, kind):
+def couple(rows, cols, weights, piece):
     args = [*rows, *cols, weights]
     height, width = weights.shape
     return pl.pallas_call(
-        functools.partial(couple_kernel, len(rows), len(cols)),
+        functools.partial(couple_kernel, piece, len(rows), len(cols)),
         in_specs=[pl.BlockSpec(memory_space=pltpu.VMEM)] * len(args),
         out_specs=pl.BlockSpec(memory_space=pltpu.VMEM),
-        out_shape=jax.ShapeDtypeStruct((height, 2 * NF), kind),
+        out_shape=jax.ShapeDtypeStruct((height, 2 * NF), jnp.bfloat16),
         cost_estimate=pl.CostEstimate(
             flops=12 * height * width * NF,
             bytes_accessed=8 * (height + width) * NF,
             transcendentals=0,
         ),
+        compiler_params=pltpu.CompilerParams(vmem_limit_bytes=16 << 20),
         name="couple",
     )(*args)
 
@@ -322,6 +333,7 @@
         cost_estimate=pl.CostEstimate(
             flops=4 * half * span * NF, bytes_accessed=4 * span * NF, transcendentals=0
         ),
+        compiler_params=pltpu.CompilerParams(vmem_limit_bytes=12 << 20),
         name="to_time",
     )(jnp.stack([place, is_inner.astype(jnp.int32)]).astype(jnp.int32), *args)
 
@@ -341,19 +353,38 @@
     side = level // 2
     inward, swapped, outward = [(0, 1), (3, 2)], [(1, 2), (2, 1)], [(1, 0), (2, 3)]
 
-    def stations_of(which):
-        return jnp.concatenate(
-            [
-                lax.dynamic_slice_in_dim(synthetic, which * half, half, 0),
-                lax.dynamic_slice_in_dim(observed, which * half, half, 0),
-            ],
-            axis=0,
-        )
-
-    passed, kept = stations_of(1 - side), stations_of(side)
-    near_passed = lax.ppermute(passed, "blk", inward)
+    def pieces_of(which):
+        halves = [
+            lax.dynamic_slice_in_dim(source, which * half, half, 0)
+            for source in (synthetic, observed)
+        ]
+        return [
+            jnp.concatenate([rows[at : at + piece] for rows in halves], axis=0)
+            for at in range(0, half, piece)
+        ]
+
+    passed, kept = pieces_of(1 - side), jnp.concatenate(pieces_of(side), axis=0)
+    near_passed = []
+    for block in passed:
+        near_passed.append(lax.ppermute(block, "blk", inward))
     near_kept = lax.ppermute(kept, "blk", inward)
 
+    basis = make_basis(jnp.stack([level, level ^ 1]).astype(jnp.int32) * span, span)
+    scale = 1.0 / math.sqrt(NT)
+
+    def transform(here, near):
+        return (
+            jnp.dot(here, basis[:span], preferred_element_type=jnp.float32)
+            + jnp.dot(near, basis[span:], preferred_element_type=jnp.float32)
+        ) * scale
+
+    to_pass, kept_rest = [], []
+    for here, near in zip(passed, near_passed):
+        to_pass.append(transform(here, near).astype(jnp.bfloat16))
+        kept_rest.append(lax.ppermute(to_pass[-1], "blk", swapped))
+    station_weights, pair_mask, kept_rest[0] = lax.optimization_barrier(
+        (station_weights, pair_mask, kept_rest[0])
+    )
     member = sub * pairs + pair
     hops = [(s, q) for s in range(subs) for q in range(pairs)]
     members = jnp.stack([(sub - s) % subs * pairs + (pair - q) % pairs for s, q in hops])
@@ -374,33 +405,24 @@
     )
     own_weights, other_weights = weights[:half], weights[half:]
 
-    basis = make_basis(jnp.stack([level, level ^ 1]).astype(jnp.int32) * span, span)
-    scale = 1.0 / math.sqrt(NT)
-
-    def transform(here, near):
-        return (
-            jnp.dot(here, basis[:span], preferred_element_type=jnp.float32)
-            + jnp.dot(near, basis[span:], preferred_element_type=jnp.float32)
-        ) * scale
-
-    to_pass = transform(passed, near_passed).astype(jnp.bfloat16)
-    kept_rest = lax.ppermute(to_pass, "blk", swapped)
     near_kept, own_weights, other_weights = lax.optimization_barrier(
         (near_kept, own_weights, other_weights)
     )
     kept_sum = transform(kept, near_kept)
     passed_rest = lax.ppermute(kept_sum.astype(jnp.bfloat16), "blk", swapped)
+    kept_rest = jnp.concatenate(kept_rest, axis=0)
     own = (kept_sum + kept_rest.astype(jnp.float32)).astype(jnp.bfloat16)
     cols = []
     for s, q in hops:
         if q == 0:
             here = own if s == 0 else shift(own, "sub", s)
         cols.append(here if q == 0 else shift(here, "pair", q))
+    to_pass = jnp.concatenate(to_pass, axis=0)
     other = (to_pass.astype(jnp.float32) + passed_rest.astype(jnp.float32)).astype(jnp.bfloat16)
 
-    other_part = couple([other], cols, other_weights, jnp.bfloat16)
+    other_part = couple([other], cols, other_weights, piece)
     own_rest = lax.ppermute(other_part, "blk", swapped)
-    own_part = couple([own], cols, own_weights, jnp.bfloat16)
+    own_part = couple([own], cols, own_weights, piece)
     other_rest = lax.ppermute(own_part, "blk", swapped)
     widen = lambda a: a.astype(jnp.float32)
     own_adjoint = (widen(own_part) + widen(own_rest)).astype(jnp.bfloat16)

time: 116 us -> 90 us (0.78)
  Pallas kernels: 23 us -> 9.68 us
  waiting for transfers between devices: 54.3 us -> 42.6 us
  other arithmetic: 7.52 us -> 2.03 us
  matrix products: 7.41 us -> 10.6 us
    ppermute x2 -> x4, waiting for transfers between devices: 10.8 us -> 0.28 us  [the longest x2 0.28 us: inner_body(): near_passed.append(lax.ppermute(block, 'blk', inward))]
    ppermute x1, waiting for transfers between devices: 29.2 us -> 18.8 us  [inner_body(): near_own = lax.ppermute(own_adjoint, 'blk', outward)]
    ppermute x1, waiting for transfers between devices: 0.01 us -> 7.51 us  [inner_body(): near_kept = lax.ppermute(kept, 'blk', inward)]
    pallas_call x2, Pallas kernels: 8.21 us -> 2.78 us  [couple(): pl.pallas_call(functools.partial(couple_kernel, piece, len(rows), len(col...]
    ppermute x2 -> x4, starting transfers between devices: 2.84 us -> 7.65 us  [the longest x2 6.29 us: inner_body(): near_passed.append(lax.ppermute(block, 'blk', inward))]
    pallas_call x2, Pallas kernels: 9.81 us -> 5.64 us  [to_time(): pl.pallas_call(to_time_kernel, grid_spec=pltpu.PrefetchScalarGridSpec(num...]
    pallas_call x1, Pallas kernels: 5 us -> 1.25 us  [make_basis(): pl.pallas_call(functools.partial(basis_kernel, per_step, low_rows), grid=...]
    ppermute x1, starting transfers between devices: 5.83 us -> 2.15 us  [inner_body(): near_kept = lax.ppermute(kept, 'blk', inward)]
  transfers between devices with their start and end apart: 11 -> 13, of which waited for: 4 -> 6; matrix products, arithmetic and copies ran while one was open for 14% -> 15% of each run, Pallas kernels for 12% -> 6%
where the time goes in v5:
time: 90 us; the launch traced here: 89.6 us
  waiting for transfers between devices  42.6 us (47%)
  starting transfers between devices  16.1 us (18%)
  matrix products  10.6 us (12%)
  Pallas kernels  9.68 us (11%)
  local copies, waits for them, and re-layouts  8.32 us (9%)
  other arithmetic  2.03 us (2%)
    ppermute x1, waiting for transfers between devices, inner_body(): near_own = lax.ppermute(own_adjoint, 'blk', outward)  18.8 us
    ppermute x3, waiting for transfers between devices, shift(): return lax.ppermute(value, axis, pairs)  15.2 us
    ppermute x1, waiting for transfers between devices, inner_body(): near_kept = lax.ppermute(kept, 'blk', inward)  7.51 us
    dot_general x3, matrix products, transform(): jnp.dot(here, basis[:span], preferred_element_type=jnp.float32)  6.76 us
    ppermute x2, starting transfers between devices, inner_body(): near_passed.append(lax.ppermute(block, 'blk', inward))  6.29 us
    pallas_call x2, Pallas kernels, to_time(): pl.pallas_call(to_time_kernel, grid_spec=pltpu.PrefetchScalarGridSpec(num...  5.64 us
    dot_general x3, matrix products, transform(): jnp.dot(near, basis[span:], preferred_element_type=jnp.float32)  3.81 us
    unnamed x20, local copies, waits for them, and re-layouts  3.4 us
  transfers between devices with their start and end apart: 13, of which 6 were waited for; matrix products, arithmetic and copies ran while one was open for 15% of the time, Pallas kernels for 6%

profile of v5, /device:TPU:0, one launch (start us, length us, event | category | flops | bytes accessed | tf_op | source)
XLA Modules:
  0.0 89.6 jit_solution(9388122953838578693)
XLA Ops:
  0.0 1.5 %constant_dynamic-slice_fusion.6 = (bf16[80,1024]{1,0:T(8,128)(2,1)S(1)}, bf16[80,1024]{1,0:T(8,128)(2,1)S(1)}, bf16[80,1024]{1,0:T(8,128)(2,1)S(1)}, bf16[80,10...) fusion(bf16[320,1024]{1,0:T(8,128)(2,1)} %param.5, ...), kind=kLoop, calls=%fused_computation.67 | loop fusion | bytes 2621456 | tf_op jit(solution)/shard_map/slice | solution.py:362
  1.6 5.0 %collective-permute-start = (bf16[160,1024]{1,0:T(8,128)(2,1)S(1)}, bf16[160,1024]{1,0:T(8,128)(2,1)S(1)}, u32[]{:S(2)}, u32[]{:S(2)}) collective-permute-start(bf16[160,1024]{1,0:T(8,128)(2,1)S(1)} %pad_maximum_fusion.1), channel_id=1, source_target_pairs={{0,4},{12,8},{1,5},{13,9},{2,6},{14,10},{3,7},{15,11},{16,20},{28,... | collective-permute-start | bytes 983048 | tf_op jit(solution)/shard_map/ppermute | solution.py:369
  6.6 1.3 %collective-permute-start.1 = (bf16[160,1024]{1,0:T(8,128)(2,1)S(1)}, bf16[160,1024]{1,0:T(8,128)(2,1)S(1)}, u32[]{:S(2)}, u32[]{:S(2)}) collective-permute-start(bf16[160,1024]{1,0:T(8,128)(2,1)S(1)} %pad_maximum_fusion.2), channel_id=1, source_target_pairs={{0,4},{12,8},{1,5},{13,9},{2,6},{14,10},{3,7},{15,11},{16,20},{28,... | collective-permute-start | bytes 983048 | tf_op jit(solution)/shard_map/ppermute | solution.py:369
  8.0 2.1 %collective-permute-start.2 = (bf16[320,1024]{1,0:T(8,128)(2,1)S(1)}, bf16[320,1024]{1,0:T(8,128)(2,1)}, u32[]{:S(2)}, u32[]{:S(2)}) collective-permute-start(bf16[320,1024]{1,0:T(8,128)(2,1)S(1)} %pad_maximum_fusion), channel_id=1, source_target_pairs={{0,4},{12,8},{1,5},{13,9},{2,6},{14,10},{3,7},{15,11},{16,20},{28,... | collective-permute-start | bytes 1966088 | tf_op jit(solution)/shard_map/ppermute | solution.py:370
  10.1 0.1 add_multiply_fusion
  10.2 0.1 broadcast_add_fusion
  10.3 0.1 add.208
  10.3 0.5 fusion.45
  10.9 0.3 fusion.47
  11.2 1.3 %basis.1.basis_ref = bf16[2048,1024]{1,0:T(8,128)(2,1)S(1)} custom-call(f32[32,512]{1,0:T(8,128)S(1)} %get-tuple-element.30.hc_ref, f32[32,512]{1,0:T(8,128)S(1)} %get-tuple-element.29.hs_ref, f32[64,512]{1,0:T(8,128)S(1)} %get-tuple-element.32.lc_ref, f32[64,512]{1,0:T(8,128)S(1)} %get-tuple-element.31.ls_ref), custom_call_target="tpu_custom_call" | custom-call | flops 8388608 | bytes 4194304 | tf_op jit(solution)/shard_map/basis/pallas_call | solution.py:62
  12.5 1.7 %fusion.8 = f32[160,1024]{1,0:T(8,128)} fusion(bf16[2048,1024]{1,0:T(8,128)(2,1)S(1)} %basis.1.basis_ref, bf16[80,1024]{1,0:T(8,128)(2,1)S(1)} %get-tuple-element.25, bf16[80,1024]{1,0:T(8,128)(2,1)S(1)} %get-tuple-element.38), kind=kOutput, calls=%fused_computation.12 | convolution fusion | flops 336199680 | bytes 3080192 | tf_op jit(solution)/shard_map/dot_general | solution.py:377
  14.2 0.5 copy-done
  14.7 1.4 %fusion.10 = f32[160,1024]{1,0:T(8,128)} fusion(bf16[2048,1024]{1,0:T(8,128)(2,1)S(1)} %basis.1.basis_ref, bf16[80,1024]{1,0:T(8,128)(2,1)S(1)} %get-tuple-element.27, bf16[80,1024]{1,0:T(8,128)(2,1)S(1)} %get-tuple-element.36), kind=kOutput, calls=%fused_computation.14 | convolution fusion | flops 336199680 | bytes 3080192 | tf_op jit(solution)/shard_map/dot_general | solution.py:377
  16.0 0.1 fusion.52
  16.1 0.1 iota_add_fusion
  16.2 0.1 add.236
  16.3 0.1 fusion.50
  16.4 3.7 %fusion.6 = f32[320,1024]{1,0:T(8,128)} fusion(bf16[2048,1024]{1,0:T(8,128)(2,1)} %copy-done, bf16[80,1024]{1,0:T(8,128)(2,1)S(1)} %get-tuple-element.28, bf16[80,1024]{1,0:T(8,128)(2,1)S(1)} %get-tuple-element.35, bf16[80,1024]{1,0:T(8,128)(2,1)S(1)} %get-tuple-element.26, bf16[80,1024]{1,0:T(8,128)(2,1)S(1)} %get-tuple-element.37), kind=kOutput, calls=%fused_computation.10 | convolution fusion | flops 673710080 | bytes 4063232 | tf_op jit(solution)/shard_map/dot_general | solution.py:377
  20.1 0.5 fusion.33
  20.6 0.7 collective-permute-start.3
  21.3 0.0 copy-start.4
  21.4 0.0 copy-start.3
  21.4 0.3 collective-permute-done.1
  21.6 0.6 fusion.30
  22.2 0.7 collective-permute-start.5
  22.9 0.0 copy-start.5
  22.9 0.7 copy-done.5
  23.6 0.1 reshape.158
  23.7 0.6 gather_fusion
  24.3 0.6 gather_fusion.1
  24.8 0.1 mul.168
  24.9 0.1 mul.163
  25.0 0.1 copy.9
  25.1 0.6 gather_fusion.2
  25.6 0.1 copy.10
  25.7 0.6 gather_fusion.3
  26.3 0.1 broadcast_in_dim.4
  26.4 0.1 reshape.159
  26.4 0.1 broadcast_in_dim.5
  26.5 0.3 copy.11
  26.8 0.1 multiply_multiply_fusion
  27.0 0.1 fusion.54
  27.0 7.5 %collective-permute-done.2 = bf16[320,1024]{1,0:T(8,128)(2,1)} collective-permute-done((bf16[320,1024]{1,0:T(8,128)(2,1)S(1)}, bf16[320,1024]{1,0:T(8,128)(2,1)}, u32[]{:S(2)}, u32[]{:S(2)}) %collective-permute-start.2) | collective-permute-done | bytes 655392 | tf_op jit(solution)/shard_map/ppermute | solution.py:370
  34.6 2.7 %fusion.53 = (bf16[320,1024]{1,0:T(8,128)(2,1)S(1)}, bf16[320,1024]{1,0:T(8,128)(2,1)S(1)}) fusion(bf16[160,1024]{1,0:T(8,128)(2,1)S(1)} %collective-permute-done.5, bf16[160,1024]{1,0:T(8,128)(2,1)S(1)} %copy-done.6, f32[320,1024]{1,0:T(8,128)S(1)} %copy-done.9, bf16[320,1024]{1,0:T(8,128)(2,1)} %collective-permute-done.2, bf16[2048,1024]{1,0:T(8,128)(2,1)} %copy-done), kind=kOutput, calls=%fused_computation.82 | convolution fusion | flops 674037760 | bytes 6029312 | tf_op jit(solution)/shard_map/dot_general | solution.py:378
  37.3 1.6 %collective-permute-start.7 = (bf16[320,1024]{1,0:T(8,128)(2,1)S(1)}, bf16[320,1024]{1,0:T(8,128)(2,1)S(1)}, u32[]{:S(2)}, u32[]{:S(2)}) collective-permute-start(bf16[320,1024]{1,0:T(8,128)(2,1)S(1)} %get-tuple-element.18.refs_1_.refs_0_), channel_id=1, source_target_pairs={{0,2},{2,0},{1,3},{3,1},{4,6},{6,4},{5,7},{7,5},{8,10},{10,8},{9,1... | collective-permute-start | bytes 1966088 | tf_op jit(solution)/shard_map/ppermute | solution.py:23
  38.8 0.7 collective-permute-start.4
  39.5 0.1 collective-permute-start.6
  39.6 13.3 %collective-permute-done.7.refs_3_ = bf16[320,1024]{1,0:T(8,128)(2,1)S(1)} collective-permute-done((bf16[320,1024]{1,0:T(8,128)(2,1)S(1)}, bf16[320,1024]{1,0:T(8,128)(2,1)S(1)}, u32[]{:S(2)}, u32[]{:S(2)}) %collective-permute-start.7) | collective-permute-done | bytes 655392 | tf_op jit(solution)/shard_map/ppermute | solution.py:23
  53.0 0.2 add_convert_fusion.1.refs_0_
  53.2 1.8 %collective-permute-done.8.refs_4_ = bf16[320,1024]{1,0:T(8,128)(2,1)S(1)} collective-permute-done((bf16[320,1024]{1,0:T(8,128)(2,1)S(1)}, bf16[320,1024]{1,0:T(8,128)(2,1)S(1)}, u32[]{:S(2)}, u32[]{:S(2)}) %collective-permute-start.8) | collective-permute-done | bytes 655392 | tf_op jit(solution)/shard_map/ppermute | solution.py:23
  55.1 1.4 %couple.2 = bf16[160,1024]{1,0:T(8,128)(2,1)S(1)} custom-call(bf16[320,1024]{1,0:T(8,128)(2,1)S(1)} %add_convert_fusion.1.refs_0_, bf16[320,1024]{1,0:T(8,128)(2,1)S(1)} %get-tuple-element.18.refs_1_.refs_0_, bf16[320,1024]{1,0:T(8,128)(2,1)S(1)} %collective-permute-done.6.refs_2_, bf16[320,1024]{1,0:T(8,128)(2,1)S(1)} %collective-permute-done.7.refs_3_, ...), custom_call_target="tpu_custom_call" | custom-call | flops 629145600 | bytes 3276800 | tf_op jit(solution)/shard_map/couple/pallas_call | solution.py:288
  56.5 0.7 collective-permute-start.11
  57.2 1.4 %couple.3 = bf16[160,1024]{1,0:T(8,128)(2,1)S(1)} custom-call(bf16[320,1024]{1,0:T(8,128)(2,1)S(1)} %get-tuple-element.18.refs_1_.refs_0_, bf16[320,1024]{1,0:T(8,128)(2,1)S(1)} %get-tuple-element.18.refs_1_.refs_0_, bf16[320,1024]{1,0:T(8,128)(2,1)S(1)} %collective-permute-done.6.refs_2_, bf16[320,1024]{1,0:T(8,128)(2,1)S(1)} %collective-permute-done.7.refs_3_, ...), custom_call_target="tpu_custom_call" | custom-call | flops 629145600 | bytes 3276800 | tf_op jit(solution)/shard_map/couple/pallas_call | solution.py:288
  58.6 0.7 collective-permute-start.9
  59.3 0.1 add_convert_fusion.2.here_ref
  59.4 1.3 %collective-permute-start.12 = (bf16[160,1024]{1,0:T(8,128)(2,1)S(1)}, bf16[160,1024]{1,0:T(8,128)(2,1)S(1)}, u32[]{:S(2)}, u32[]{:S(2)}) collective-permute-start(bf16[160,1024]{1,0:T(8,128)(2,1)S(1)} %add_convert_fusion.2.here_ref), channel_id=1, source_target_pairs={{4,0},{8,12},{5,1},{9,13},{6,2},{10,14},{7,3},{11,15},{20,16},{24,... | collective-permute-start | bytes 983048 | tf_op jit(solution)/shard_map/ppermute | solution.py:429
  60.7 0.1 add_convert_fusion.3.here_ref
  60.8 1.3 %collective-permute-start.10 = (bf16[160,1024]{1,0:T(8,128)(2,1)S(1)}, bf16[160,1024]{1,0:T(8,128)(2,1)S(1)}, u32[]{:S(2)}, u32[]{:S(2)}) collective-permute-start(bf16[160,1024]{1,0:T(8,128)(2,1)S(1)} %add_convert_fusion.3.here_ref), channel_id=1, source_target_pairs={{4,0},{8,12},{5,1},{9,13},{6,2},{10,14},{7,3},{11,15},{20,16},{24,... | collective-permute-start | bytes 983048 | tf_op jit(solution)/shard_map/ppermute | solution.py:431
  62.1 0.1 pad_add_fusion
  62.2 18.8 %collective-permute-done.12.there_ref = bf16[160,1024]{1,0:T(8,128)(2,1)S(1)} collective-permute-done((bf16[160,1024]{1,0:T(8,128)(2,1)S(1)}, bf16[160,1024]{1,0:T(8,128)(2,1)S(1)}, u32[]{:S(2)}, u32[]{:S(2)}) %collective-permute-start.12) | collective-permute-done | bytes 327712 | tf_op jit(solution)/shard_map/ppermute | solution.py:429
  81.0 2.2 %copy-done.2 = bf16[2048,1024]{1,0:T(8,128)(2,1)S(1)} copy-done((bf16[2048,1024]{1,0:T(8,128)(2,1)S(1)}, bf16[2048,1024]{1,0:T(8,128)(2,1)}, u32[]{:S(2)}) %copy-start.2) | copy-done | bytes 4194328
  83.2 2.8 %to_time.2.rest_0_ = bf16[320,1024]{1,0:T(8,128)(2,1)} custom-call(s32[2]{0:T(128)S(1)} %get-tuple-element.34.flag_ref, bf16[160,1024]{1,0:T(8,128)(2,1)S(1)} %add_convert_fusion.2.here_ref, bf16[160,1024]{1,0:T(8,128)(2,1)S(1)} %collective-permute-done.12.there_ref, bf16[2048,1024]{1,0:T(8,128)(2,1)S(1)} %copy-done.2), custom_call_target="tpu_custom_call" | custom-call | flops 335544320 | bytes 2097152 | tf_op jit(solution)/shard_map/to_time/pallas_call | solution.py:323
  86.0 0.8 collective-permute-done.10.there_ref
  86.8 2.8 %to_time.3 = bf16[320,1024]{1,0:T(8,128)(2,1)} custom-call(s32[2]{0:T(128)S(1)} %get-tuple-element.33.flag_ref, bf16[160,1024]{1,0:T(8,128)(2,1)S(1)} %add_convert_fusion.3.here_ref, bf16[160,1024]{1,0:T(8,128)(2,1)S(1)} %collective-permute-done.10.there_ref, bf16[2048,1024]{1,0:T(8,128)(2,1)S(1)} %copy-done.2, ...), custom_call_target="tpu_custom_call", output_to_operand_aliasing={{}: (4, {})} | custom-call | flops 335544320 | bytes 2097152 | tf_op jit(solution)/shard_map/to_time/pallas_call | solution.py:323
  (34 shorter events, 0.2 us)
Async XLA Ops:
  1.6 18.5 %collective-permute-start = (bf16[160,1024]{1,0:T(8,128)(2,1)S(1)}, bf16[160,1024]{1,0:T(8,128)(2,1)S(1)}, u32[]{:S(2)}, u32[]{:S(2)}) collective-permute-start(bf16[160,1024]{1,0:T(8,128)(2,1)S(1)} %pad_maximum_fusion.1), channel_id=1, source_target_pairs={{0,4},{12,8},{1,5},{13,9},{2,6},{14,10},{3,7},{15,11},{16,20},{28,... | collective-permute-start | bytes 983048 | tf_op jit(solution)/shard_map/ppermute | solution.py:369
  6.6 15.1 %collective-permute-start.1 = (bf16[160,1024]{1,0:T(8,128)(2,1)S(1)}, bf16[160,1024]{1,0:T(8,128)(2,1)S(1)}, u32[]{:S(2)}, u32[]{:S(2)}) collective-permute-start(bf16[160,1024]{1,0:T(8,128)(2,1)S(1)} %pad_maximum_fusion.2), channel_id=1, source_target_pairs={{0,4},{12,8},{1,5},{13,9},{2,6},{14,10},{3,7},{15,11},{16,20},{28,... | collective-permute-start | bytes 983048 | tf_op jit(solution)/shard_map/ppermute | solution.py:369
  8.0 26.6 %collective-permute-start.2 = (bf16[320,1024]{1,0:T(8,128)(2,1)S(1)}, bf16[320,1024]{1,0:T(8,128)(2,1)}, u32[]{:S(2)}, u32[]{:S(2)}) collective-permute-start(bf16[320,1024]{1,0:T(8,128)(2,1)S(1)} %pad_maximum_fusion), channel_id=1, source_target_pairs={{0,4},{12,8},{1,5},{13,9},{2,6},{14,10},{3,7},{15,11},{16,20},{28,... | collective-permute-start | bytes 1966088 | tf_op jit(solution)/shard_map/ppermute | solution.py:370
  12.5 2.2 %copy-start = (bf16[2048,1024]{1,0:T(8,128)(2,1)}, bf16[2048,1024]{1,0:T(8,128)(2,1)S(1)}, u32[]{:S(2)}) copy-start(bf16[2048,1024]{1,0:T(8,128)(2,1)S(1)} %basis.1.basis_ref) | copy-start | bytes 12582916
  16.4 3.7 %copy-start.1 = (bf16[2048,1024]{1,0:T(8,128)(2,1)S(1)}, bf16[2048,1024]{1,0:T(8,128)(2,1)}, u32[]{:S(2)}) copy-start(bf16[2048,1024]{1,0:T(8,128)(2,1)} %copy-done) | copy-start | bytes 12582916
  16.4 3.7 %copy-start.8 = (f32[160,1024]{1,0:T(8,128)S(1)}, f32[160,1024]{1,0:T(8,128)}, u32[]{:S(2)}) copy-start(f32[160,1024]{1,0:T(8,128)} %fusion.10) | copy-start | bytes 1966084
  20.1 1.6 %copy-start.7 = (f32[160,1024]{1,0:T(8,128)S(1)}, f32[160,1024]{1,0:T(8,128)}, u32[]{:S(2)}) copy-start(f32[160,1024]{1,0:T(8,128)} %fusion.8) | copy-start | bytes 1966084
  20.6 2.3 %collective-permute-start.3 = (bf16[160,1024]{1,0:T(8,128)(2,1)S(1)}, bf16[160,1024]{1,0:T(8,128)(2,1)S(1)}, u32[]{:S(2)}, u32[]{:S(2)}) collective-permute-start(bf16[160,1024]{1,0:T(8,128)(2,1)S(1)} %fusion.33), channel_id=1, source_target_pairs={{4,8},{8,4},{5,9},{9,5},{6,10},{10,6},{7,11},{11,7},{20,24},{24,20... | collective-permute-start | bytes 983048 | tf_op jit(solution)/shard_map/ppermute | solution.py:384
  21.3 2.3 %copy-start.4 = (s32[1280]{0:T(1024)S(1)}, s32[1280]{0:T(1024)}, u32[]{:S(2)}) copy-start(s32[1280]{0:T(1024)} %param.6) | copy-start | bytes 15364
  21.4 3.6 %copy-start.3 = (s32[16,16]{1,0:T(8,128)S(1)}, s32[16,16]{1,0:T(8,128)}, u32[]{:S(2)}) copy-start(s32[16,16]{1,0:T(8,128)} %param.7) | copy-start | bytes 3076
  22.2 12.4 %collective-permute-start.5 = (bf16[160,1024]{1,0:T(8,128)(2,1)S(1)}, bf16[160,1024]{1,0:T(8,128)(2,1)S(1)}, u32[]{:S(2)}, u32[]{:S(2)}) collective-permute-start(bf16[160,1024]{1,0:T(8,128)(2,1)S(1)} %fusion.30), channel_id=1, source_target_pairs={{4,8},{8,4},{5,9},{9,5},{6,10},{10,6},{7,11},{11,7},{20,24},{24,20... | collective-permute-start | bytes 983048 | tf_op jit(solution)/shard_map/ppermute | solution.py:384
  22.9 0.7 copy-start.5
  26.8 7.7 %copy-start.6 = (bf16[160,1024]{1,0:T(8,128)(2,1)S(1)}, bf16[160,1024]{1,0:T(8,128)(2,1)}, u32[]{:S(2)}) copy-start(bf16[160,1024]{1,0:T(8,128)(2,1)} %copy-done.5) | copy-start | bytes 983044
  26.8 7.7 %copy-start.9 = (f32[320,1024]{1,0:T(8,128)S(1)}, f32[320,1024]{1,0:T(8,128)}, u32[]{:S(2)}) copy-start(f32[320,1024]{1,0:T(8,128)} %fusion.6) | copy-start | bytes 3932164
  37.3 15.7 %collective-permute-start.7 = (bf16[320,1024]{1,0:T(8,128)(2,1)S(1)}, bf16[320,1024]{1,0:T(8,128)(2,1)S(1)}, u32[]{:S(2)}, u32[]{:S(2)}) collective-permute-start(bf16[320,1024]{1,0:T(8,128)(2,1)S(1)} %get-tuple-element.18.refs_1_.refs_0_), channel_id=1, source_target_pairs={{0,2},{2,0},{1,3},{3,1},{4,6},{6,4},{5,7},{7,5},{8,10},{10,8},{9,1... | collective-permute-start | bytes 1966088 | tf_op jit(solution)/shard_map/ppermute | solution.py:23
  38.8 14.1 %collective-permute-start.4 = (bf16[320,1024]{1,0:T(8,128)(2,1)S(1)}, bf16[320,1024]{1,0:T(8,128)(2,1)S(1)}, u32[]{:S(2)}, u32[]{:S(2)}) collective-permute-start(bf16[320,1024]{1,0:T(8,128)(2,1)S(1)} %get-tuple-element.17), channel_id=1, source_target_pairs={{4,8},{8,4},{5,9},{9,5},{6,10},{10,6},{7,11},{11,7},{20,24},{24,20... | collective-permute-start | bytes 1966088 | tf_op jit(solution)/shard_map/ppermute | solution.py:412
  39.5 13.7 %collective-permute-start.6 = (bf16[320,1024]{1,0:T(8,128)(2,1)S(1)}, bf16[320,1024]{1,0:T(8,128)(2,1)S(1)}, u32[]{:S(2)}, u32[]{:S(2)}) collective-permute-start(bf16[320,1024]{1,0:T(8,128)(2,1)S(1)} %get-tuple-element.18.refs_1_.refs_0_), channel_id=1, source_target_pairs={{0,1},{1,0},{2,3},{3,2},{4,5},{5,4},{6,7},{7,6},{8,9},{9,8},{10,11... | collective-permute-start | bytes 1966088 | tf_op jit(solution)/shard_map/ppermute | solution.py:23
  53.0 2.1 %collective-permute-start.8 = (bf16[320,1024]{1,0:T(8,128)(2,1)S(1)}, bf16[320,1024]{1,0:T(8,128)(2,1)S(1)}, u32[]{:S(2)}, u32[]{:S(2)}) collective-permute-start(bf16[320,1024]{1,0:T(8,128)(2,1)S(1)} %collective-permute-done.7.refs_3_), channel_id=1, source_target_pairs={{0,1},{1,0},{2,3},{3,2},{4,5},{5,4},{6,7},{7,6},{8,9},{9,8},{10,11... | collective-permute-start | bytes 1966088 | tf_op jit(solution)/shard_map/ppermute | solution.py:23
  56.5 2.8 %collective-permute-start.11 = (bf16[160,1024]{1,0:T(8,128)(2,1)S(1)}, bf16[160,1024]{1,0:T(8,128)(2,1)S(1)}, u32[]{:S(2)}, u32[]{:S(2)}) collective-permute-start(bf16[160,1024]{1,0:T(8,128)(2,1)S(1)} %couple.2), channel_id=1, source_target_pairs={{4,8},{8,4},{5,9},{9,5},{6,10},{10,6},{7,11},{11,7},{20,24},{24,20... | collective-permute-start | bytes 983048 | tf_op jit(solution)/shard_map/ppermute | solution.py:424
  58.6 2.1 %collective-permute-start.9 = (bf16[160,1024]{1,0:T(8,128)(2,1)S(1)}, bf16[160,1024]{1,0:T(8,128)(2,1)S(1)}, u32[]{:S(2)}, u32[]{:S(2)}) collective-permute-start(bf16[160,1024]{1,0:T(8,128)(2,1)S(1)} %couple.3), channel_id=1, source_target_pairs={{4,8},{8,4},{5,9},{9,5},{6,10},{10,6},{7,11},{11,7},{20,24},{24,20... | collective-permute-start | bytes 983048 | tf_op jit(solution)/shard_map/ppermute | solution.py:426
  59.4 21.7 %collective-permute-start.12 = (bf16[160,1024]{1,0:T(8,128)(2,1)S(1)}, bf16[160,1024]{1,0:T(8,128)(2,1)S(1)}, u32[]{:S(2)}, u32[]{:S(2)}) collective-permute-start(bf16[160,1024]{1,0:T(8,128)(2,1)S(1)} %add_convert_fusion.2.here_ref), channel_id=1, source_target_pairs={{4,0},{8,12},{5,1},{9,13},{6,2},{10,14},{7,3},{11,15},{20,16},{24,... | collective-permute-start | bytes 983048 | tf_op jit(solution)/shard_map/ppermute | solution.py:429
  60.8 26.0 %collective-permute-start.10 = (bf16[160,1024]{1,0:T(8,128)(2,1)S(1)}, bf16[160,1024]{1,0:T(8,128)(2,1)S(1)}, u32[]{:S(2)}, u32[]{:S(2)}) collective-permute-start(bf16[160,1024]{1,0:T(8,128)(2,1)S(1)} %add_convert_fusion.3.here_ref), channel_id=1, source_target_pairs={{4,0},{8,12},{5,1},{9,13},{6,2},{10,14},{7,3},{11,15},{20,16},{24,... | collective-permute-start | bytes 983048 | tf_op jit(solution)/shard_map/ppermute | solution.py:431
  81.0 2.2 %copy-start.2 = (bf16[2048,1024]{1,0:T(8,128)(2,1)S(1)}, bf16[2048,1024]{1,0:T(8,128)(2,1)}, u32[]{:S(2)}) copy-start(bf16[2048,1024]{1,0:T(8,128)(2,1)} %copy-done) | copy-start | bytes 12582916

commit v6 on v5

--- a/solution.py
+++ b/solution.py
@@ -338,6 +338,92 @@
     )(jnp.stack([place, is_inner.astype(jnp.int32)]).astype(jnp.int32), *args)
 
 
+VMEM = pl.BlockSpec(memory_space=pltpu.VMEM)
+
+
+def two_bases_kernel(per_step, low_rows, *refs):
+    lc_ref, ls_ref = refs[4:6]
+    for high, out_ref in zip((refs[:2], refs[2:4]), refs[6:]):
+        basis_kernel(per_step, low_rows, *high, lc_ref, ls_ref, out_ref)
+
+
+def two_bases(first, second, span):
+    low_rows = math.gcd(span, 64)
+    tables = []
+    for start in (first, second):
+        tables += cos_sin(start + jnp.arange(0, span, low_rows, dtype=jnp.int32))
+    tables += cos_sin(jnp.arange(low_rows, dtype=jnp.int32))
+    per_step = math.gcd(span // low_rows, 4)
+    block = pl.BlockSpec((per_step * low_rows, 2 * NF), lambda i: (i, 0))
+    return pl.pallas_call(
+        functools.partial(two_bases_kernel, per_step, low_rows),
+        grid=(span // low_rows // per_step,),
+        in_specs=[pl.BlockSpec(table.shape, lambda i: (0, 0)) for table in tables],
+        out_specs=[block, block],
+        out_shape=[jax.ShapeDtypeStruct((span, 2 * NF), jnp.bfloat16)] * 2,
+        compiler_params=pltpu.CompilerParams(vmem_limit_bytes=12 << 20),
+        cost_estimate=pl.CostEstimate(
+            flops=16 * span * NF, bytes_accessed=8 * span * NF, transcendentals=0
+        ),
+        name="two_bases",
+    )(*tables)
+
+
+def own_parts_kernel(count, *refs):
+    basis_ref = refs[count]
+    for block_ref, out_ref in zip(refs[:count], refs[count + 1 :]):
+        out_ref[...] = jnp.dot(
+            block_ref[...], basis_ref[...], preferred_element_type=jnp.float32
+        )
+
+
+def own_parts(blocks, basis):
+    rows, span = blocks[0].shape
+    return pl.pallas_call(
+        functools.partial(own_parts_kernel, len(blocks)),
+        in_specs=[VMEM] * (len(blocks) + 1),
+        out_specs=[VMEM] * len(blocks),
+        out_shape=[jax.ShapeDtypeStruct((rows, 2 * NF), jnp.float32)] * len(blocks),
+        compiler_params=pltpu.CompilerParams(vmem_limit_bytes=12 << 20),
+        cost_estimate=pl.CostEstimate(
+            flops=4 * len(blocks) * rows * span * NF,
+            bytes_accessed=4 * span * NF,
+            transcendentals=0,
+        ),
+        name="own_parts",
+    )(*blocks, basis)
+
+
+def sum_kernel(part_ref, near_ref, basis_ref, *rest):
+    total = part_ref[...] + jnp.dot(
+        near_ref[...], basis_ref[...], preferred_element_type=jnp.float32
+    )
+    total = total * (1.0 / math.sqrt(NT))
+    if len(rest) == 3:
+        rest_ref, own_ref, sum_ref = rest
+        own_ref[...] = (total + rest_ref[...].astype(jnp.float32)).astype(jnp.bfloat16)
+    else:
+        sum_ref = rest[0]
+    sum_ref[...] = total.astype(jnp.bfloat16)
+
+
+def spectra(part, near, basis, others=None):
+    rows, span = near.shape
+    args = [part, near, basis] + ([] if others is None else [others])
+    outs = 1 if others is None else 2
+    return pl.pallas_call(
+        sum_kernel,
+        in_specs=[VMEM] * len(args),
+        out_specs=[VMEM] * outs,
+        out_shape=[jax.ShapeDtypeStruct((rows, 2 * NF), jnp.bfloat16)] * outs,
+        compiler_params=pltpu.CompilerParams(vmem_limit_bytes=12 << 20),
+        cost_estimate=pl.CostEstimate(
+            flops=4 * rows * span * NF, bytes_accessed=4 * span * NF, transcendentals=0
+        ),
+        name="spectra",
+    )(*args)
+
+
 def inner_body(synthetic, observed, station_weights, pair_mask):
     levels = lax.axis_size("blk")
     subs = lax.axis_size("sub")
@@ -354,39 +440,54 @@
     inward, swapped, outward = [(0, 1), (3, 2)], [(1, 2), (2, 1)], [(1, 0), (2, 3)]
 
     def pieces_of(which):
-        halves = [
-            lax.dynamic_slice_in_dim(source, which * half, half, 0)
-            for source in (synthetic, observed)
-        ]
         return [
-            jnp.concatenate([rows[at : at + piece] for rows in halves], axis=0)
+            jnp.concatenate(
+                [
+                    lax.dynamic_slice_in_dim(source, which * half + at, piece, 0)
+                    for source in (synthetic, observed)
+                ],
+                axis=0,
+            )
             for at in range(0, half, piece)
         ]
 
-    passed, kept = pieces_of(1 - side), jnp.concatenate(pieces_of(side), axis=0)
-    near_passed = []
-    for block in passed:
-        near_passed.append(lax.ppermute(block, "blk", inward))
-    near_kept = lax.ppermute(kept, "blk", inward)
-
-    basis = make_basis(jnp.stack([level, level ^ 1]).astype(jnp.int32) * span, span)
-    scale = 1.0 / math.sqrt(NT)
-
-    def transform(here, near):
-        return (
-            jnp.dot(here, basis[:span], preferred_element_type=jnp.float32)
-            + jnp.dot(near, basis[span:], preferred_element_type=jnp.float32)
-        ) * scale
-
+    passed, kept = pieces_of(1 - side), pieces_of(side)
+    near_passed, near_kept = [], []
+    for blocks, arrived in ((passed, near_passed), (kept, near_kept)):
+        for block in blocks:
+            arrived.append(lax.ppermute(block, "blk", inward))
+
+    here_basis, near_basis = two_bases(level * span, (level ^ 1) * span, span)
+    passed_parts = own_parts(passed, here_basis)
+    kept_parts = own_parts(kept, here_basis)
     to_pass, kept_rest = [], []
-    for here, near in zip(passed, near_passed):
-        to_pass.append(transform(here, near).astype(jnp.bfloat16))
-        kept_rest.append(lax.ppermute(to_pass[-1], "blk", swapped))
-    station_weights, pair_mask, kept_rest[0] = lax.optimization_barrier(
-        (station_weights, pair_mask, kept_rest[0])
+    for place in range(per_half):
+        (summed,) = spectra(passed_parts[place], near_passed[place], near_basis)
+        to_pass.append(summed)
+        kept_rest.append(lax.ppermute(summed, "blk", swapped))
+    hops = [(s, q) for s in range(subs) for q in range(pairs)]
+    own, passed_rest, cols = [], [], {}
+    for place in range(per_half):
+        whole, summed = spectra(
+            kept_parts[place], near_kept[place], near_basis, kept_rest[place]
+        )
+        own.append(whole)
+        for s, q in hops:
+            if q == 0:
+                cols[s, q, place] = whole if s == 0 else shift(whole, "sub", s)
+            else:
+                cols[s, q, place] = shift(cols[s, 0, place], "pair", q)
+        passed_rest.append(lax.ppermute(summed, "blk", swapped))
+    other = [
+        (mine.astype(jnp.float32) + theirs.astype(jnp.float32)).astype(jnp.bfloat16)
+        for mine, theirs in zip(to_pass, passed_rest)
+    ]
+
+    early = (subs - 1, 0, 0)
+    station_weights, pair_mask, cols[early] = lax.optimization_barrier(
+        (station_weights, pair_mask, cols[early])
     )
     member = sub * pairs + pair
-    hops = [(s, q) for s in range(subs) for q in range(pairs)]
     members = jnp.stack([(sub - s) % subs * pairs + (pair - q) % pairs for s, q in hops])
     within = jnp.arange(per_half, dtype=jnp.int32)
     row_pieces = member * levels + jnp.concatenate(
@@ -405,24 +506,10 @@
     )
     own_weights, other_weights = weights[:half], weights[half:]
 
-    near_kept, own_weights, other_weights = lax.optimization_barrier(
-        (near_kept, own_weights, other_weights)
-    )
-    kept_sum = transform(kept, near_kept)
-    passed_rest = lax.ppermute(kept_sum.astype(jnp.bfloat16), "blk", swapped)
-    kept_rest = jnp.concatenate(kept_rest, axis=0)
-    own = (kept_sum + kept_rest.astype(jnp.float32)).astype(jnp.bfloat16)
-    cols = []
-    for s, q in hops:
-        if q == 0:
-            here = own if s == 0 else shift(own, "sub", s)
-        cols.append(here if q == 0 else shift(here, "pair", q))
-    to_pass = jnp.concatenate(to_pass, axis=0)
-    other = (to_pass.astype(jnp.float32) + passed_rest.astype(jnp.float32)).astype(jnp.bfloat16)
-
-    other_part = couple([other], cols, other_weights, piece)
+    cols = [cols[s, q, place] for s, q in hops for place in range(per_half)]
+    other_part = couple(other, cols, other_weights, piece)
     own_rest = lax.ppermute(other_part, "blk", swapped)
-    own_part = couple([own], cols, own_weights, piece)
+    own_part = couple(own, cols, own_weights, piece)
     other_rest = lax.ppermute(own_part, "blk", swapped)
     widen = lambda a: a.astype(jnp.float32)
     own_adjoint = (widen(own_part) + widen(own_rest)).astype(jnp.bfloat16)
@@ -431,8 +518,8 @@
     near_other = lax.ppermute(other_adjoint, "blk", outward)
     is_inner = (level == 1) | (level == 2)
     rows = synthetic.shape[0]
-    traces = to_time(side, is_inner, own_adjoint, near_own, basis, span, rows, None)
-    return to_time(1 - side, is_inner, other_adjoint, near_other, basis, span, rows, traces)
+    traces = to_time(side, is_inner, own_adjoint, near_own, here_basis, span, rows, None)
+    return to_time(1 - side, is_inner, other_adjoint, near_other, here_basis, span, rows, traces)
 
 
 def shards(*args):

time: 90 us -> 103 us (1.14)
  Pallas kernels: 9.68 us -> 22.3 us
  matrix products: 10.6 us -> 0 us
  starting transfers between devices: 16.1 us -> 23.8 us
  waiting for transfers between devices: 42.6 us -> 36.9 us
  other arithmetic: 2.03 us -> 6.31 us
  local copies, waits for them, and re-layouts: 8.32 us -> 12.5 us
    dot_general x6 -> x0, matrix products: 10.6 us -> none  [the longest x3 6.76 us: transform(): jnp.dot(here, basis[:span], preferred_element_type=jnp.float32)]
    pallas_call x1 -> x7, Pallas kernels: 1.25 us -> 11.2 us  [the longest x4 8.29 us: spectra(): pl.pallas_call(sum_kernel, in_specs=[VMEM] * len(args), out_specs=[VMEM]...]
    ppermute x3 -> x6, waiting for transfers between devices: 15.2 us -> 8.09 us  [shift(): return lax.ppermute(value, axis, pairs)]
    ppermute x6 -> x8, starting transfers between devices: 10.5 us -> 16.8 us  [the longest x4 11.8 us: inner_body(): arrived.append(lax.ppermute(block, 'blk', inward))]
    ppermute x6 -> x8, waiting for transfers between devices: 7.79 us -> 3.34 us  [the longest x4 3.33 us: inner_body(): arrived.append(lax.ppermute(block, 'blk', inward))]
    ppermute x1, waiting for transfers between devices: 0.76 us -> 4.2 us  [inner_body(): near_other = lax.ppermute(other_adjoint, 'blk', outward)]
    pallas_call x2, Pallas kernels: 2.78 us -> 5.45 us  [couple(): pl.pallas_call(functools.partial(couple_kernel, piece, len(rows), len(col...]
    ppermute x1, waiting for transfers between devices: 18.8 us -> 21.2 us  [inner_body(): near_own = lax.ppermute(own_adjoint, 'blk', outward)]
  transfers between devices with their start and end apart: 13 -> 18, of which waited for: 6 -> 4; matrix products, arithmetic and copies ran while one was open for 15% -> 12% of each run, Pallas kernels for 6% -> 16%
where the time goes in v6:
time: 103 us; the launch traced here: 102 us
  waiting for transfers between devices  36.9 us (36%)
  starting transfers between devices  23.8 us (23%)
  Pallas kernels  22.3 us (22%)
  local copies, waits for them, and re-layouts  12.5 us (12%)
  other arithmetic  6.31 us (6%)
    ppermute x1, waiting for transfers between devices, inner_body(): near_own = lax.ppermute(own_adjoint, 'blk', outward)  21.2 us
    ppermute x4, starting transfers between devices, inner_body(): arrived.append(lax.ppermute(block, 'blk', inward))  11.8 us
    pallas_call x4, Pallas kernels, spectra(): pl.pallas_call(sum_kernel, in_specs=[VMEM] * len(args), out_specs=[VMEM]...  8.29 us
    ppermute x6, waiting for transfers between devices, shift(): return lax.ppermute(value, axis, pairs)  8.09 us
    pallas_call x2, Pallas kernels, to_time(): pl.pallas_call(to_time_kernel, grid_spec=pltpu.PrefetchScalarGridSpec(num...  5.65 us
    pallas_call x2, Pallas kernels, couple(): pl.pallas_call(functools.partial(couple_kernel, piece, len(rows), len(col...  5.45 us
    unnamed x18, local copies, waits for them, and re-layouts  4.58 us
    ppermute x1, waiting for transfers between devices, inner_body(): near_other = lax.ppermute(other_adjoint, 'blk', outward)  4.2 us
  transfers between devices with their start and end apart: 18, of which 4 were waited for; matrix products, arithmetic and copies ran while one was open for 12% of the time, Pallas kernels for 16%

profile of v6, /device:TPU:0, one launch (start us, length us, event | category | flops | bytes accessed | tf_op | source)
XLA Modules:
  0.0 102.1 jit_solution(5730740751344937734)
XLA Ops:
  0.0 1.5 %constant_dynamic-slice_fusion.4 = (bf16[80,1024]{1,0:T(8,128)(2,1)S(1)}, bf16[80,1024]{1,0:T(8,128)(2,1)S(1)}, bf16[80,1024]{1,0:T(8,128)(2,1)S(1)}, bf16[80,10...) fusion(bf16[320,1024]{1,0:T(8,128)(2,1)} %param.5, ...), kind=kLoop, calls=%fused_computation.56 | loop fusion | bytes 2621456 | tf_op jit(solution)/shard_map/dynamic_slice | solution.py:446
  1.6 5.7 %collective-permute-start.4 = (bf16[160,1024]{1,0:T(8,128)(2,1)S(1)}, bf16[160,1024]{1,0:T(8,128)(2,1)}, u32[]{:S(2)}, u32[]{:S(2)}) collective-permute-start(bf16[160,1024]{1,0:T(8,128)(2,1)S(1)} %pad_maximum_fusion.1.refs_1_), channel_id=1, source_target_pairs={{0,4},{12,8},{1,5},{13,9},{2,6},{14,10},{3,7},{15,11},{16,20},{28,... | collective-permute-start | bytes 983048 | tf_op jit(solution)/shard_map/ppermute | solution.py:458
  7.3 2.0 %collective-permute-start.5 = (bf16[160,1024]{1,0:T(8,128)(2,1)S(1)}, bf16[160,1024]{1,0:T(8,128)(2,1)}, u32[]{:S(2)}, u32[]{:S(2)}) collective-permute-start(bf16[160,1024]{1,0:T(8,128)(2,1)S(1)} %pad_maximum_fusion.3.refs_1_), channel_id=1, source_target_pairs={{0,4},{12,8},{1,5},{13,9},{2,6},{14,10},{3,7},{15,11},{16,20},{28,... | collective-permute-start | bytes 983048 | tf_op jit(solution)/shard_map/ppermute | solution.py:458
  9.3 2.0 %collective-permute-start = (bf16[160,1024]{1,0:T(8,128)(2,1)S(1)}, bf16[160,1024]{1,0:T(8,128)(2,1)}, u32[]{:S(2)}, u32[]{:S(2)}) collective-permute-start(bf16[160,1024]{1,0:T(8,128)(2,1)S(1)} %pad_maximum_fusion.refs_0_), channel_id=1, source_target_pairs={{0,4},{12,8},{1,5},{13,9},{2,6},{14,10},{3,7},{15,11},{16,20},{28,... | collective-permute-start | bytes 983048 | tf_op jit(solution)/shard_map/ppermute | solution.py:458
  11.4 2.0 %collective-permute-start.1 = (bf16[160,1024]{1,0:T(8,128)(2,1)S(1)}, bf16[160,1024]{1,0:T(8,128)(2,1)}, u32[]{:S(2)}, u32[]{:S(2)}) collective-permute-start(bf16[160,1024]{1,0:T(8,128)(2,1)S(1)} %pad_maximum_fusion.2.refs_0_), channel_id=1, source_target_pairs={{0,4},{12,8},{1,5},{13,9},{2,6},{14,10},{3,7},{15,11},{16,20},{28,... | collective-permute-start | bytes 983048 | tf_op jit(solution)/shard_map/ppermute | solution.py:458
  13.4 1.2 %fusion.6 = (f32[64,512]{1,0:T(8,128)S(1)}, f32[64,512]{1,0:T(8,128)}) fusion(s32[512]{0:T(512)S(1)} %iota_add_fusion.1), kind=kLoop, calls=%fused_computation.22 | loop fusion | flops 458752 | bytes 264192 | tf_op jit(solution)/shard_map/sin | solution.py:39
  14.6 1.0 fusion.14
  15.6 0.1 fusion.21
  15.7 0.9 copy-done.2
  16.6 0.8 copy-done.3
  17.4 0.8 copy-done.4
  18.1 0.8 copy-done.5
  18.9 0.8 copy-done.6
  19.6 1.2 %two_bases.1 = (bf16[1024,1024]{1,0:T(8,128)(2,1)S(1)}, bf16[1024,1024]{1,0:T(8,128)(2,1)S(1)}) custom-call(f32[16,512]{1,0:T(8,128)S(1)} %copy-done.5, f32[16,512]{1,0:T(8,128)S(1)} %copy-done.6, f32[16,512]{1,0:T(8,128)S(1)} %copy-done.4, f32[16,512]{1,0:T(8,128)S(1)} %copy-done.3, f32[64,512]{1,0:T(8,128)S(1)} %copy-done.2, ...), custom_call_target="tpu_custom_call" | custom-call | flops 8388608 | bytes 4194304 | tf_op jit(solution)/shard_map/two_bases/pallas_call | solution.py:358
  20.8 0.8 own_parts.2
  21.7 0.1 iota_add_fusion
  21.7 2.2 %spectra.6 = bf16[160,1024]{1,0:T(8,128)(2,1)} custom-call(f32[160,1024]{1,0:T(8,128)S(1)} %get-tuple-element.23.part_ref, bf16[160,1024]{1,0:T(8,128)(2,1)} %collective-permute-done.4.near_ref, bf16[1024,1024]{1,0:T(8,128)(2,1)S(1)} %get-tuple-element.20.basis_ref), custom_call_target="tpu_custom_call" | custom-call | flops 335544320 | bytes 2097152 | tf_op jit(solution)/shard_map/spectra/pallas_call | solution.py:414
  24.0 1.4 %collective-permute-start.6 = (bf16[160,1024]{1,0:T(8,128)(2,1)}, bf16[160,1024]{1,0:T(8,128)(2,1)}, u32[]{:S(2)}, u32[]{:S(2)}) collective-permute-start(bf16[160,1024]{1,0:T(8,128)(2,1)} %spectra.6), channel_id=1, source_target_pairs={{4,8},{8,4},{5,9},{9,5},{6,10},{10,6},{7,11},{11,7},{20,24},{24,20... | collective-permute-start | bytes 983048 | tf_op jit(solution)/shard_map/ppermute | solution.py:467
  25.3 3.3 %collective-permute-done.near_ref = bf16[160,1024]{1,0:T(8,128)(2,1)} collective-permute-done((bf16[160,1024]{1,0:T(8,128)(2,1)S(1)}, bf16[160,1024]{1,0:T(8,128)(2,1)}, u32[]{:S(2)}, u32[]{:S(2)}) %collective-permute-start) | collective-permute-done | bytes 327712 | tf_op jit(solution)/shard_map/ppermute | solution.py:458
  28.7 1.5 %spectra.4 = bf16[160,1024]{1,0:T(8,128)(2,1)S(1)} custom-call(f32[160,1024]{1,0:T(8,128)S(1)} %get-tuple-element.19.part_ref, bf16[160,1024]{1,0:T(8,128)(2,1)} %collective-permute-done.near_ref, bf16[1024,1024]{1,0:T(8,128)(2,1)S(1)} %get-tuple-element.20.basis_ref), custom_call_target="tpu_custom_call" | custom-call | flops 335544320 | bytes 2097152 | tf_op jit(solution)/shard_map/spectra/pallas_call | solution.py:414
  30.2 0.7 collective-permute-start.2
  30.9 0.1 add.259
  31.0 0.8 own_parts.3
  31.8 0.1 fusion.19
  31.9 0.6 copy-done.1
  32.5 2.3 %spectra.7 = (bf16[160,1024]{1,0:T(8,128)(2,1)S(1)}, bf16[160,1024]{1,0:T(8,128)(2,1)}) custom-call(f32[160,1024]{1,0:T(8,128)S(1)} %get-tuple-element.24.part_ref, bf16[160,1024]{1,0:T(8,128)(2,1)} %collective-permute-done.5.near_ref, bf16[1024,1024]{1,0:T(8,128)(2,1)S(1)} %copy-done.1, bf16[160,1024]{1,0:T(8,128)(2,1)} %collective-permute-done.6.rest_0_), custom_call_target="tpu_custom_call" | custom-call | flops 335544320 | bytes 2097152 | tf_op jit(solution)/shard_map/spectra/pallas_call | solution.py:414
  34.9 1.5 %collective-permute-start.7 = (bf16[160,1024]{1,0:T(8,128)(2,1)}, bf16[160,1024]{1,0:T(8,128)(2,1)}, u32[]{:S(2)}, u32[]{:S(2)}) collective-permute-start(bf16[160,1024]{1,0:T(8,128)(2,1)} %get-tuple-element.25), channel_id=1, source_target_pairs={{4,8},{8,4},{5,9},{9,5},{6,10},{10,6},{7,11},{11,7},{20,24},{24,20... | collective-permute-start | bytes 983048 | tf_op jit(solution)/shard_map/ppermute | solution.py:480
  36.4 2.3 %spectra.5 = (bf16[160,1024]{1,0:T(8,128)(2,1)S(1)}, bf16[160,1024]{1,0:T(8,128)(2,1)}) custom-call(f32[160,1024]{1,0:T(8,128)S(1)} %get-tuple-element.21.part_ref, bf16[160,1024]{1,0:T(8,128)(2,1)} %collective-permute-done.1.near_ref, bf16[1024,1024]{1,0:T(8,128)(2,1)S(1)} %copy-done.1, bf16[160,1024]{1,0:T(8,128)(2,1)S(1)} %collective-permute-done.2.rest_0_), custom_call_target="tpu_custom_call" | custom-call | flops 335544320 | bytes 2097152 | tf_op jit(solution)/shard_map/spectra/pallas_call | solution.py:414
  38.7 1.5 %collective-permute-start.10 = (bf16[160,1024]{1,0:T(8,128)(2,1)S(1)}, bf16[160,1024]{1,0:T(8,128)(2,1)}, u32[]{:S(2)}, u32[]{:S(2)}) collective-permute-start(bf16[160,1024]{1,0:T(8,128)(2,1)S(1)} %get-tuple-element.26.refs_2_.refs_0_), channel_id=1, source_target_pairs={{0,2},{2,0},{1,3},{3,1},{4,6},{6,4},{5,7},{7,5},{8,10},{10,8},{9,1... | collective-permute-start | bytes 983048 | tf_op jit(solution)/shard_map/ppermute | solution.py:23
  40.2 0.6 collective-permute-start.11
  40.8 0.5 collective-permute-start.8
  41.3 8.1 %collective-permute-done.10.refs_6_ = bf16[160,1024]{1,0:T(8,128)(2,1)} collective-permute-done((bf16[160,1024]{1,0:T(8,128)(2,1)S(1)}, bf16[160,1024]{1,0:T(8,128)(2,1)}, u32[]{:S(2)}, u32[]{:S(2)}) %collective-permute-start.10) | collective-permute-done | bytes 327712 | tf_op jit(solution)/shard_map/ppermute | solution.py:23
  49.4 1.4 %collective-permute-start.3 = (bf16[160,1024]{1,0:T(8,128)(2,1)}, bf16[160,1024]{1,0:T(8,128)(2,1)}, u32[]{:S(2)}, u32[]{:S(2)}) collective-permute-start(bf16[160,1024]{1,0:T(8,128)(2,1)} %get-tuple-element.22), channel_id=1, source_target_pairs={{4,8},{8,4},{5,9},{9,5},{6,10},{10,6},{7,11},{11,7},{20,24},{24,20... | collective-permute-start | bytes 983048 | tf_op jit(solution)/shard_map/ppermute | solution.py:480
  50.7 0.1 copy.9
  50.8 1.2 %add_convert_fusion.2.refs_1_ = bf16[160,1024]{1,0:T(8,128)(2,1)S(1)} fusion(bf16[160,1024]{1,0:T(8,128)(2,1)} %collective-permute-done.7, bf16[160,1024]{1,0:T(8,128)(2,1)} %spectra.6), kind=kLoop, calls=%fused_computation.7 | loop fusion | flops 655360 | bytes 983040 | tf_op jit(solution)/shard_map/convert_element_type | solution.py:482
  52.0 0.1 reshape.131
  52.1 0.6 gather_fusion
  52.7 0.6 gather_fusion.2
  53.3 0.1 copy.10
  53.3 0.6 gather_fusion.1
  53.9 0.6 gather_fusion.3
  54.5 0.1 broadcast_in_dim.4
  54.5 0.1 reshape.132
  54.6 1.0 %broadcast_in_dim.5 = f32[320,8,80]{0,2,1:T(8,128)} broadcast(f32[320,8]{0,1:T(8,128)S(1)} %reshape.132), dimensions={0,1} | broadcast | bytes 829440 | tf_op jit(solution)/shard_map/broadcast_in_dim | solution.py:505
  55.7 2.4 %copy.11 = f32[320,640]{1,0:T(8,128)} copy(f32[320,640]{0,1:T(8,128)} %bitcast.23) | data formatting | bytes 1638400 | tf_op jit(solution)/shard_map/reshape | solution.py:505
  58.1 0.1 mul.179
  58.2 0.1 mul.174
  58.2 0.5 collective-permute-start.13
  58.8 1.3 %multiply_multiply_fusion = f32[320,640]{1,0:T(8,128)S(1)} fusion(f32[320,640]{1,0:T(8,128)} %copy.11, f32[640]{0:T(1024)S(1)} %mul.179, f32[320]{0:T(512)S(1)} %mul.174), kind=kLoop, calls=%fused_computation.4 | loop fusion | flops 409600 | bytes 1642240 | tf_op jit(solution)/shard_map/mul | solution.py:501
  60.0 1.1 %add_convert_fusion.3.refs_0_ = bf16[160,1024]{1,0:T(8,128)(2,1)S(1)} fusion(bf16[160,1024]{1,0:T(8,128)(2,1)} %collective-permute-done.3, bf16[160,1024]{1,0:T(8,128)(2,1)S(1)} %spectra.4), kind=kLoop, calls=%fused_computation.8 | loop fusion | flops 655360 | bytes 983040 | tf_op jit(solution)/shard_map/convert_element_type | solution.py:482
  61.1 0.1 fusion.24
  61.2 2.7 %couple.2 = bf16[160,1024]{1,0:T(8,128)(2,1)S(1)} custom-call(bf16[160,1024]{1,0:T(8,128)(2,1)S(1)} %add_convert_fusion.3.refs_0_, bf16[160,1024]{1,0:T(8,128)(2,1)S(1)} %add_convert_fusion.2.refs_1_, bf16[160,1024]{1,0:T(8,128)(2,1)S(1)} %get-tuple-element.26.refs_2_.refs_0_, bf16[160,1024]{1,0:T(8,128)(2,1)S(1)} %get-tuple-element.27.refs_3_.refs_1_, ...), custom_call_target="tpu_custom_call" | custom-call | flops 629145600 | bytes 3276800 | tf_op jit(solution)/shard_map/couple/pallas_call | solution.py:288
  64.0 0.7 collective-permute-start.16
  64.7 2.7 %couple.3 = bf16[160,1024]{1,0:T(8,128)(2,1)S(1)} custom-call(bf16[160,1024]{1,0:T(8,128)(2,1)S(1)} %get-tuple-element.26.refs_2_.refs_0_, bf16[160,1024]{1,0:T(8,128)(2,1)S(1)} %get-tuple-element.27.refs_3_.refs_1_, bf16[160,1024]{1,0:T(8,128)(2,1)S(1)} %get-tuple-element.26.refs_2_.refs_0_, bf16[160,1024]{1,0:T(8,128)(2,1)S(1)} %get-tuple-element.27.refs_3_.refs_1_, ...), custom_call_target="tpu_custom_call" | custom-call | flops 629145600 | bytes 3276800 | tf_op jit(solution)/shard_map/couple/pallas_call | solution.py:288
  67.4 0.7 collective-permute-start.14
  68.1 0.1 add_convert_fusion.here_ref
  68.2 1.3 %collective-permute-start.17 = (bf16[160,1024]{1,0:T(8,128)(2,1)S(1)}, bf16[160,1024]{1,0:T(8,128)(2,1)S(1)}, u32[]{:S(2)}, u32[]{:S(2)}) collective-permute-start(bf16[160,1024]{1,0:T(8,128)(2,1)S(1)} %add_convert_fusion.here_ref), channel_id=1, source_target_pairs={{4,0},{8,12},{5,1},{9,13},{6,2},{10,14},{7,3},{11,15},{20,16},{24,... | collective-permute-start | bytes 983048 | tf_op jit(solution)/shard_map/ppermute | solution.py:516
  69.5 0.1 add_convert_fusion.1.here_ref
  69.6 1.3 %collective-permute-start.15 = (bf16[160,1024]{1,0:T(8,128)(2,1)S(1)}, bf16[160,1024]{1,0:T(8,128)(2,1)S(1)}, u32[]{:S(2)}, u32[]{:S(2)}) collective-permute-start(bf16[160,1024]{1,0:T(8,128)(2,1)S(1)} %add_convert_fusion.1.here_ref), channel_id=1, source_target_pairs={{4,0},{8,12},{5,1},{9,13},{6,2},{10,14},{7,3},{11,15},{20,16},{24,... | collective-permute-start | bytes 983048 | tf_op jit(solution)/shard_map/ppermute | solution.py:518
  70.9 0.1 pad_add_fusion
  71.0 21.2 %collective-permute-done.17.there_ref = bf16[160,1024]{1,0:T(8,128)(2,1)S(1)} collective-permute-done((bf16[160,1024]{1,0:T(8,128)(2,1)S(1)}, bf16[160,1024]{1,0:T(8,128)(2,1)S(1)}, u32[]{:S(2)}, u32[]{:S(2)}) %collective-permute-start.17) | collective-permute-done | bytes 327712 | tf_op jit(solution)/shard_map/ppermute | solution.py:516
  92.2 2.8 %to_time.2.rest_0_ = bf16[320,1024]{1,0:T(8,128)(2,1)} custom-call(s32[2]{0:T(128)S(1)} %get-tuple-element.50.flag_ref, bf16[160,1024]{1,0:T(8,128)(2,1)S(1)} %add_convert_fusion.here_ref, bf16[160,1024]{1,0:T(8,128)(2,1)S(1)} %collective-permute-done.17.there_ref, bf16[1024,1024]{1,0:T(8,128)(2,1)S(1)} %get-tuple-element.18.refs_2_.basis_ref), custom_call_target="tpu_custom_call" | custom-call | flops 335544320 | bytes 2097152 | tf_op jit(solution)/shard_map/to_time/pallas_call | solution.py:323
  95.0 4.2 %collective-permute-done.15.there_ref = bf16[160,1024]{1,0:T(8,128)(2,1)S(1)} collective-permute-done((bf16[160,1024]{1,0:T(8,128)(2,1)S(1)}, bf16[160,1024]{1,0:T(8,128)(2,1)S(1)}, u32[]{:S(2)}, u32[]{:S(2)}) %collective-permute-start.15) | collective-permute-done | bytes 327712 | tf_op jit(solution)/shard_map/ppermute | solution.py:518
  99.2 2.8 %to_time.3 = bf16[320,1024]{1,0:T(8,128)(2,1)} custom-call(s32[2]{0:T(128)S(1)} %get-tuple-element.49.flag_ref, bf16[160,1024]{1,0:T(8,128)(2,1)S(1)} %add_convert_fusion.1.here_ref, bf16[160,1024]{1,0:T(8,128)(2,1)S(1)} %collective-permute-done.15.there_ref, ...), custom_call_target="tpu_custom_call", output_to_operand_aliasing={{}: (4, {})} | custom-call | flops 335544320 | bytes 2097152 | tf_op jit(solution)/shard_map/to_time/pallas_call | solution.py:323
  (41 shorter events, 0.2 us)
Async XLA Ops:
  1.6 20.2 %collective-permute-start.4 = (bf16[160,1024]{1,0:T(8,128)(2,1)S(1)}, bf16[160,1024]{1,0:T(8,128)(2,1)}, u32[]{:S(2)}, u32[]{:S(2)}) collective-permute-start(bf16[160,1024]{1,0:T(8,128)(2,1)S(1)} %pad_maximum_fusion.1.refs_1_), channel_id=1, source_target_pairs={{0,4},{12,8},{1,5},{13,9},{2,6},{14,10},{3,7},{15,11},{16,20},{28,... | collective-permute-start | bytes 983048 | tf_op jit(solution)/shard_map/ppermute | solution.py:458
  7.3 24.6 %collective-permute-start.5 = (bf16[160,1024]{1,0:T(8,128)(2,1)S(1)}, bf16[160,1024]{1,0:T(8,128)(2,1)}, u32[]{:S(2)}, u32[]{:S(2)}) collective-permute-start(bf16[160,1024]{1,0:T(8,128)(2,1)S(1)} %pad_maximum_fusion.3.refs_1_), channel_id=1, source_target_pairs={{0,4},{12,8},{1,5},{13,9},{2,6},{14,10},{3,7},{15,11},{16,20},{28,... | collective-permute-start | bytes 983048 | tf_op jit(solution)/shard_map/ppermute | solution.py:458
  9.3 19.3 %collective-permute-start = (bf16[160,1024]{1,0:T(8,128)(2,1)S(1)}, bf16[160,1024]{1,0:T(8,128)(2,1)}, u32[]{:S(2)}, u32[]{:S(2)}) collective-permute-start(bf16[160,1024]{1,0:T(8,128)(2,1)S(1)} %pad_maximum_fusion.refs_0_), channel_id=1, source_target_pairs={{0,4},{12,8},{1,5},{13,9},{2,6},{14,10},{3,7},{15,11},{16,20},{28,... | collective-permute-start | bytes 983048 | tf_op jit(solution)/shard_map/ppermute | solution.py:458
  11.4 25.0 %collective-permute-start.1 = (bf16[160,1024]{1,0:T(8,128)(2,1)S(1)}, bf16[160,1024]{1,0:T(8,128)(2,1)}, u32[]{:S(2)}, u32[]{:S(2)}) collective-permute-start(bf16[160,1024]{1,0:T(8,128)(2,1)S(1)} %pad_maximum_fusion.2.refs_0_), channel_id=1, source_target_pairs={{0,4},{12,8},{1,5},{13,9},{2,6},{14,10},{3,7},{15,11},{16,20},{28,... | collective-permute-start | bytes 983048 | tf_op jit(solution)/shard_map/ppermute | solution.py:458
  15.7 0.9 copy-start.2
  16.6 0.8 copy-start.3
  17.3 0.8 copy-start.4
  18.1 0.8 copy-start.5
  18.9 0.8 copy-start.6
  20.8 7.9 %copy-start = (bf16[1024,1024]{1,0:T(8,128)(2,1)}, bf16[1024,1024]{1,0:T(8,128)(2,1)S(1)}, u32[]{:S(2)}) copy-start(bf16[1024,1024]{1,0:T(8,128)(2,1)S(1)} %get-tuple-element.20.basis_ref) | copy-start | bytes 6291460
  24.0 7.9 %collective-permute-start.6 = (bf16[160,1024]{1,0:T(8,128)(2,1)}, bf16[160,1024]{1,0:T(8,128)(2,1)}, u32[]{:S(2)}, u32[]{:S(2)}) collective-permute-start(bf16[160,1024]{1,0:T(8,128)(2,1)} %spectra.6), channel_id=1, source_target_pairs={{4,8},{8,4},{5,9},{9,5},{6,10},{10,6},{7,11},{11,7},{20,24},{24,20... | collective-permute-start | bytes 983048 | tf_op jit(solution)/shard_map/ppermute | solution.py:467
  30.2 6.3 %collective-permute-start.2 = (bf16[160,1024]{1,0:T(8,128)(2,1)S(1)}, bf16[160,1024]{1,0:T(8,128)(2,1)S(1)}, u32[]{:S(2)}, u32[]{:S(2)}) collective-permute-start(bf16[160,1024]{1,0:T(8,128)(2,1)S(1)} %spectra.4), channel_id=1, source_target_pairs={{4,8},{8,4},{5,9},{9,5},{6,10},{10,6},{7,11},{11,7},{20,24},{24,20... | collective-permute-start | bytes 983048 | tf_op jit(solution)/shard_map/ppermute | solution.py:467
  31.0 1.6 %copy-start.1 = (bf16[1024,1024]{1,0:T(8,128)(2,1)S(1)}, bf16[1024,1024]{1,0:T(8,128)(2,1)}, u32[]{:S(2)}) copy-start(bf16[1024,1024]{1,0:T(8,128)(2,1)} %copy-done) | copy-start | bytes 6291460
  34.9 15.9 %copy-start.7 = (s32[16,16]{1,0:T(8,128)S(1)}, s32[16,16]{1,0:T(8,128)}, u32[]{:S(2)}) copy-start(s32[16,16]{1,0:T(8,128)} %param.7) | copy-start | bytes 3076
  34.9 15.9 %collective-permute-start.7 = (bf16[160,1024]{1,0:T(8,128)(2,1)}, bf16[160,1024]{1,0:T(8,128)(2,1)}, u32[]{:S(2)}, u32[]{:S(2)}) collective-permute-start(bf16[160,1024]{1,0:T(8,128)(2,1)} %get-tuple-element.25), channel_id=1, source_target_pairs={{4,8},{8,4},{5,9},{9,5},{6,10},{10,6},{7,11},{11,7},{20,24},{24,20... | collective-permute-start | bytes 983048 | tf_op jit(solution)/shard_map/ppermute | solution.py:480
  36.4 15.6 %copy-start.8 = (s32[1280]{0:T(1024)S(1)}, s32[1280]{0:T(1024)}, u32[]{:S(2)}) copy-start(s32[1280]{0:T(1024)} %param.6) | copy-start | bytes 15364
  38.7 10.7 %collective-permute-start.10 = (bf16[160,1024]{1,0:T(8,128)(2,1)S(1)}, bf16[160,1024]{1,0:T(8,128)(2,1)}, u32[]{:S(2)}, u32[]{:S(2)}) collective-permute-start(bf16[160,1024]{1,0:T(8,128)(2,1)S(1)} %get-tuple-element.26.refs_2_.refs_0_), channel_id=1, source_target_pairs={{0,2},{2,0},{1,3},{3,1},{4,6},{6,4},{5,7},{7,5},{8,10},{10,8},{9,1... | collective-permute-start | bytes 983048 | tf_op jit(solution)/shard_map/ppermute | solution.py:23
  40.2 18.1 %collective-permute-start.11 = (bf16[160,1024]{1,0:T(8,128)(2,1)S(1)}, bf16[160,1024]{1,0:T(8,128)(2,1)}, u32[]{:S(2)}, u32[]{:S(2)}) collective-permute-start(bf16[160,1024]{1,0:T(8,128)(2,1)S(1)} %get-tuple-element.27.refs_3_.refs_1_), channel_id=1, source_target_pairs={{0,2},{2,0},{1,3},{3,1},{4,6},{6,4},{5,7},{7,5},{8,10},{10,8},{9,1... | collective-permute-start | bytes 983048 | tf_op jit(solution)/shard_map/ppermute | solution.py:23
  40.8 20.4 %collective-permute-start.9 = (bf16[160,1024]{1,0:T(8,128)(2,1)S(1)}, bf16[160,1024]{1,0:T(8,128)(2,1)}, u32[]{:S(2)}, u32[]{:S(2)}) collective-permute-start(bf16[160,1024]{1,0:T(8,128)(2,1)S(1)} %get-tuple-element.27.refs_3_.refs_1_), channel_id=1, source_target_pairs={{0,1},{1,0},{2,3},{3,2},{4,5},{5,4},{6,7},{7,6},{8,9},{9,8},{10,11... | collective-permute-start | bytes 983048 | tf_op jit(solution)/shard_map/ppermute | solution.py:23
  40.8 20.4 %collective-permute-start.8 = (bf16[160,1024]{1,0:T(8,128)(2,1)S(1)}, bf16[160,1024]{1,0:T(8,128)(2,1)}, u32[]{:S(2)}, u32[]{:S(2)}) collective-permute-start(bf16[160,1024]{1,0:T(8,128)(2,1)S(1)} %get-tuple-element.26.refs_2_.refs_0_), channel_id=1, source_target_pairs={{0,1},{1,0},{2,3},{3,2},{4,5},{5,4},{6,7},{7,6},{8,9},{9,8},{10,11... | collective-permute-start | bytes 983048 | tf_op jit(solution)/shard_map/ppermute | solution.py:23
  49.4 10.7 %collective-permute-start.3 = (bf16[160,1024]{1,0:T(8,128)(2,1)}, bf16[160,1024]{1,0:T(8,128)(2,1)}, u32[]{:S(2)}, u32[]{:S(2)}) collective-permute-start(bf16[160,1024]{1,0:T(8,128)(2,1)} %get-tuple-element.22), channel_id=1, source_target_pairs={{4,8},{8,4},{5,9},{9,5},{6,10},{10,6},{7,11},{11,7},{20,24},{24,20... | collective-permute-start | bytes 983048 | tf_op jit(solution)/shard_map/ppermute | solution.py:480
  50.8 10.4 %collective-permute-start.12 = (bf16[160,1024]{1,0:T(8,128)(2,1)}, bf16[160,1024]{1,0:T(8,128)(2,1)}, u32[]{:S(2)}, u32[]{:S(2)}) collective-permute-start(bf16[160,1024]{1,0:T(8,128)(2,1)} %collective-permute-done.10.refs_6_), channel_id=1, source_target_pairs={{0,1},{1,0},{2,3},{3,2},{4,5},{5,4},{6,7},{7,6},{8,9},{9,8},{10,11... | collective-permute-start | bytes 983048 | tf_op jit(solution)/shard_map/ppermute | solution.py:23
  58.2 3.0 %collective-permute-start.13 = (bf16[160,1024]{1,0:T(8,128)(2,1)}, bf16[160,1024]{1,0:T(8,128)(2,1)S(1)}, u32[]{:S(2)}, u32[]{:S(2)}) collective-permute-start(bf16[160,1024]{1,0:T(8,128)(2,1)} %collective-permute-done.11.refs_7_), channel_id=1, source_target_pairs={{0,1},{1,0},{2,3},{3,2},{4,5},{5,4},{6,7},{7,6},{8,9},{9,8},{10,11... | collective-permute-start | bytes 983048 | tf_op jit(solution)/shard_map/ppermute | solution.py:23
  64.0 4.1 %collective-permute-start.16 = (bf16[160,1024]{1,0:T(8,128)(2,1)S(1)}, bf16[160,1024]{1,0:T(8,128)(2,1)S(1)}, u32[]{:S(2)}, u32[]{:S(2)}) collective-permute-start(bf16[160,1024]{1,0:T(8,128)(2,1)S(1)} %couple.2), channel_id=1, source_target_pairs={{4,8},{8,4},{5,9},{9,5},{6,10},{10,6},{7,11},{11,7},{20,24},{24,20... | collective-permute-start | bytes 983048 | tf_op jit(solution)/shard_map/ppermute | solution.py:511
  67.4 2.1 %collective-permute-start.14 = (bf16[160,1024]{1,0:T(8,128)(2,1)S(1)}, bf16[160,1024]{1,0:T(8,128)(2,1)S(1)}, u32[]{:S(2)}, u32[]{:S(2)}) collective-permute-start(bf16[160,1024]{1,0:T(8,128)(2,1)S(1)} %couple.3), channel_id=1, source_target_pairs={{4,8},{8,4},{5,9},{9,5},{6,10},{10,6},{7,11},{11,7},{20,24},{24,20... | collective-permute-start | bytes 983048 | tf_op jit(solution)/shard_map/ppermute | solution.py:513
  68.2 24.0 %collective-permute-start.17 = (bf16[160,1024]{1,0:T(8,128)(2,1)S(1)}, bf16[160,1024]{1,0:T(8,128)(2,1)S(1)}, u32[]{:S(2)}, u32[]{:S(2)}) collective-permute-start(bf16[160,1024]{1,0:T(8,128)(2,1)S(1)} %add_convert_fusion.here_ref), channel_id=1, source_target_pairs={{4,0},{8,12},{5,1},{9,13},{6,2},{10,14},{7,3},{11,15},{20,16},{24,... | collective-permute-start | bytes 983048 | tf_op jit(solution)/shard_map/ppermute | solution.py:516
  69.6 29.6 %collective-permute-start.15 = (bf16[160,1024]{1,0:T(8,128)(2,1)S(1)}, bf16[160,1024]{1,0:T(8,128)(2,1)S(1)}, u32[]{:S(2)}, u32[]{:S(2)}) collective-permute-start(bf16[160,1024]{1,0:T(8,128)(2,1)S(1)} %add_convert_fusion.1.here_ref), channel_id=1, source_target_pairs={{4,0},{8,12},{5,1},{9,13},{6,2},{10,14},{7,3},{11,15},{20,16},{24,... | collective-permute-start | bytes 983048 | tf_op jit(solution)/shard_map/ppermute | solution.py:518

commit v7 on v6

--- a/solution.py
+++ b/solution.py
@@ -240,62 +240,79 @@
     return rate, jnp.sum(jnp.square(rate.astype(jnp.float32)), axis=1, keepdims=True)
 
 
-def planes(ref, piece):
-    starts = range(0, ref.shape[0], 2 * piece)
-    return tuple(
-        jnp.concatenate([ref[at + off : at + off + piece] for at in starts], axis=0)
-        for off in (0, piece)
-    )
-
-
 def couple_kernel(piece, row_count, col_count, *refs):
     row_refs = refs[:row_count]
     col_refs = refs[row_count : row_count + col_count]
-    weight_ref, out_ref = refs[-2:]
-    row_planes = [planes(ref, piece) for ref in row_refs]
-    row_model = jnp.concatenate([model for model, _ in row_planes], axis=0)
-    row_data = jnp.concatenate([data for _, data in row_planes], axis=0)
+    gain_ref, weight_ref, out_ref = refs[-3:]
+    sums = row_count // (gain_ref.shape[1] // piece)
+    row_models, row_datas = [], []
+    for at in range(0, row_count, sums):
+        block = row_refs[at][...]
+        if sums == 2:
+            block = (
+                block.astype(jnp.float32) + row_refs[at + 1][...].astype(jnp.float32)
+            ).astype(jnp.bfloat16)
+        row_models.append(block[:piece])
+        row_datas.append(block[piece:])
+    row_model = jnp.concatenate(row_models, axis=0)
+    row_data = jnp.concatenate(row_datas, axis=0)
     row_power = power_of(row_model)[1]
     models, datas, powers = [], [], []
     for ref in col_refs:
-        model, data = planes(ref, piece)
-        rate, power = power_of(model)
+        rate, power = power_of(ref[:piece])
         models.append(rate)
         powers.append(power)
-        wide = data.astype(jnp.float32)
+        wide = ref[piece:].astype(jnp.float32)
         datas.append(rate_of(wide[:, :NF], wide[:, NF:]))
     col_model = jnp.concatenate(models, axis=0)
     col_data = jnp.concatenate(datas, axis=0)
     powers = jnp.concatenate(powers, axis=0)
-    width = powers.shape[0]
-    diagonal = lax.broadcasted_iota(jnp.int32, (width, width), 0) == lax.broadcasted_iota(
-        jnp.int32, (width, width), 1
-    )
-    col_power = jnp.sum(jnp.where(diagonal, powers, 0.0), axis=0, keepdims=True)
+
+    def diagonal(width):
+        return lax.broadcasted_iota(jnp.int32, (width, width), 0) == lax.broadcasted_iota(
+            jnp.int32, (width, width), 1
+        )
+
+    col_power = jnp.sum(
+        jnp.where(diagonal(powers.shape[0]), powers, 0.0), axis=0, keepdims=True
+    )
+    height = gain_ref.shape[1]
+    row_gain = jnp.sum(
+        jnp.where(diagonal(height), gain_ref[...], 0.0), axis=1, keepdims=True
+    )
     cross = lax.dot_general(
         row_model, col_model, CONTRACT_LAST, preferred_element_type=jnp.float32
     ) - lax.dot_general(row_data, col_data, CONTRACT_LAST, preferred_element_type=jnp.float32)
     normalizer = 0.5 * (row_power + col_power) + epsilon
-    coupling = (weight_ref[...] * cross / normalizer).astype(jnp.bfloat16)
+    ratio = row_gain * cross / normalizer
+    coupling = jnp.concatenate(
+        [
+            (weight_ref[at : at + 1, :] * ratio[at * piece : (at + 1) * piece]).astype(
+                jnp.bfloat16
+            )
+            for at in range(height // piece)
+        ],
+        axis=0,
+    )
     out_ref[...] = jnp.dot(
         coupling, col_model, preferred_element_type=jnp.float32
     ).astype(out_ref.dtype)
 
 
-def couple(rows, cols, weights, piece):
-    args = [*rows, *cols, weights]
-    height, width = weights.shape
+def couple(rows, cols, gains, weights, piece):
+    args = [*rows, *cols, gains, weights]
+    height, width = gains.shape[1], weights.shape[1]
     return pl.pallas_call(
         functools.partial(couple_kernel, piece, len(rows), len(cols)),
         in_specs=[pl.BlockSpec(memory_space=pltpu.VMEM)] * len(args),
         out_specs=pl.BlockSpec(memory_space=pltpu.VMEM),
         out_shape=jax.ShapeDtypeStruct((height, 2 * NF), jnp.bfloat16),
+        compiler_params=pltpu.CompilerParams(vmem_limit_bytes=16 << 20),
         cost_estimate=pl.CostEstimate(
             flops=12 * height * width * NF,
             bytes_accessed=8 * (height + width) * NF,
             transcendentals=0,
         ),
-        compiler_params=pltpu.CompilerParams(vmem_limit_bytes=16 << 20),
         name="couple",
     )(*args)
 
@@ -311,7 +328,7 @@
 
 def to_time(place, is_inner, here, there, basis, span, rows, before):
     half = here.shape[0]
-    wide = math.gcd(span, 256)
+    wide = math.gcd(span, 512)
     whole = pl.BlockSpec(here.shape, lambda j, flags: (0, 0))
     specs = [whole, whole, pl.BlockSpec((wide, 2 * NF), lambda j, flags: (j, 0))]
     args = [here, there, basis]
@@ -457,7 +474,37 @@
         for block in blocks:
             arrived.append(lax.ppermute(block, "blk", inward))
 
-    here_basis, near_basis = two_bases(level * span, (level ^ 1) * span, span)
+    member = sub * pairs + pair
+    hops = [(s, q) for s in range(subs) for q in range(pairs)]
+    halves = [
+        ((sub - s) % subs * pairs + (pair - q) % pairs) * 2 * half + side * half for s, q in hops
+    ]
+    gains = station_weights.astype(jnp.float32)
+    col_gains = jnp.concatenate(
+        [lax.dynamic_slice_in_dim(gains, start, half, 0) for start in halves]
+    )[None, :]
+    firsts = [member * 2 * half + which * half for which in (side, 1 - side)]
+    own_gains, other_gains = [
+        lax.dynamic_slice_in_dim(gains, start, half, 0)[None, :] for start in firsts
+    ]
+    link = jnp.maximum(pair_mask, pair_mask.T).astype(jnp.float32)
+    link_rows = jnp.concatenate(
+        [lax.dynamic_slice_in_dim(link, start // piece, per_half, 0) for start in firsts], axis=0
+    )
+    col_pieces = jnp.concatenate(
+        [start + jnp.arange(half, dtype=jnp.int32) for start in halves]
+    ) // piece
+    chosen = jnp.arange(link.shape[0], dtype=jnp.int32)[:, None] == col_pieces[None, :]
+    active = jnp.dot(
+        link_rows, chosen.astype(jnp.float32), preferred_element_type=jnp.float32
+    )
+    weights = 4.0 / math.sqrt(stations) * col_gains * active
+    here, own_gains, other_gains, weights = lax.optimization_barrier(
+        (level, own_gains, other_gains, weights)
+    )
+    own_weights, other_weights = weights[:per_half], weights[per_half:]
+
+    here_basis, near_basis = two_bases(here * span, (here ^ 1) * span, span)
     passed_parts = own_parts(passed, here_basis)
     kept_parts = own_parts(kept, here_basis)
     to_pass, kept_rest = [], []
@@ -465,7 +512,6 @@
         (summed,) = spectra(passed_parts[place], near_passed[place], near_basis)
         to_pass.append(summed)
         kept_rest.append(lax.ppermute(summed, "blk", swapped))
-    hops = [(s, q) for s in range(subs) for q in range(pairs)]
     own, passed_rest, cols = [], [], {}
     for place in range(per_half):
         whole, summed = spectra(
@@ -478,38 +524,11 @@
             else:
                 cols[s, q, place] = shift(cols[s, 0, place], "pair", q)
         passed_rest.append(lax.ppermute(summed, "blk", swapped))
-    other = [
-        (mine.astype(jnp.float32) + theirs.astype(jnp.float32)).astype(jnp.bfloat16)
-        for mine, theirs in zip(to_pass, passed_rest)
-    ]
-
-    early = (subs - 1, 0, 0)
-    station_weights, pair_mask, cols[early] = lax.optimization_barrier(
-        (station_weights, pair_mask, cols[early])
-    )
-    member = sub * pairs + pair
-    members = jnp.stack([(sub - s) % subs * pairs + (pair - q) % pairs for s, q in hops])
-    within = jnp.arange(per_half, dtype=jnp.int32)
-    row_pieces = member * levels + jnp.concatenate(
-        [side * per_half + within, (1 - side) * per_half + within]
-    )
-    col_pieces = (members[:, None] * levels + side * per_half + within[None, :]).reshape(-1)
-    gains = station_weights.astype(jnp.float32).reshape(-1, piece)
-    link = jnp.maximum(pair_mask, pair_mask.T).astype(jnp.float32)
-    active = link[row_pieces][:, col_pieces]
-    weights = (
-        4.0
-        / math.sqrt(stations)
-        * gains[row_pieces].reshape(-1, 1)
-        * gains[col_pieces].reshape(1, -1)
-        * jnp.repeat(jnp.repeat(active, piece, axis=0), piece, axis=1)
-    )
-    own_weights, other_weights = weights[:half], weights[half:]
-
     cols = [cols[s, q, place] for s, q in hops for place in range(per_half)]
-    other_part = couple(other, cols, other_weights, piece)
+    other = [block for both in zip(to_pass, passed_rest) for block in both]
+    other_part = couple(other, cols, other_gains, other_weights, piece)
     own_rest = lax.ppermute(other_part, "blk", swapped)
-    own_part = couple(own, cols, own_weights, piece)
+    own_part = couple(own, cols, own_gains, own_weights, piece)
     other_rest = lax.ppermute(own_part, "blk", swapped)
     widen = lambda a: a.astype(jnp.float32)
     own_adjoint = (widen(own_part) + widen(own_rest)).astype(jnp.bfloat16)

time: 103 us -> 94.3 us (0.916)
  waiting for transfers between devices: 36.9 us -> 49.5 us
  local copies, waits for them, and re-layouts: 12.5 us -> 2.46 us
  Pallas kernels: 22.3 us -> 14.4 us
  other arithmetic: 6.31 us -> 1.44 us
  starting transfers between devices: 23.8 us -> 25.6 us
    ppermute x6, waiting for transfers between devices: 8.09 us -> 14.3 us  [shift(): return lax.ppermute(value, axis, pairs)]
    ppermute x4, starting transfers between devices: 11.8 us -> 16.3 us  [inner_body(): arrived.append(lax.ppermute(block, 'blk', inward))]
    unnamed x18 -> x9, local copies, waits for them, and re-layouts: 4.58 us -> 0.09 us
    pallas_call x4, Pallas kernels: 8.29 us -> 4.07 us  [spectra(): pl.pallas_call(sum_kernel, in_specs=[VMEM] * len(args), out_specs=[VMEM]...]
    ppermute x4, waiting for transfers between devices: 3.33 us -> 7.4 us  [inner_body(): arrived.append(lax.ppermute(block, 'blk', inward))]
    reshape x3 -> x0, local copies, waits for them, and re-layouts: 2.59 us -> none  [the longest x1 2.43 us: inner_body(): jnp.repeat(jnp.repeat(active, piece, axis=0), piece, axis=1)]
    pallas_call x2, Pallas kernels: 5.45 us -> 2.89 us  [couple(): pl.pallas_call(functools.partial(couple_kernel, piece, len(rows), len(col...]
    gather x5 -> x0, local copies, waits for them, and re-layouts: 2.32 us -> none  [the longest x3 1.2 us: inner_body(): active = link[row_pieces][:, col_pieces]]
  transfers between devices with their start and end apart: 18 -> 18, of which waited for: 4 -> 6; matrix products, arithmetic and copies ran while one was open for 12% -> 2% of each run, Pallas kernels for 16% -> 11%
where the time goes in v7:
time: 94.3 us; the launch traced here: 93.9 us
  waiting for transfers between devices  49.5 us (52%)
  starting transfers between devices  25.6 us (27%)
  Pallas kernels  14.4 us (15%)
  local copies, waits for them, and re-layouts  2.46 us (3%)
  other arithmetic  1.44 us (2%)
    ppermute x1, waiting for transfers between devices, inner_body(): near_own = lax.ppermute(own_adjoint, 'blk', outward)  23 us
    ppermute x4, starting transfers between devices, inner_body(): arrived.append(lax.ppermute(block, 'blk', inward))  16.3 us
    ppermute x6, waiting for transfers between devices, shift(): return lax.ppermute(value, axis, pairs)  14.3 us
    ppermute x4, waiting for transfers between devices, inner_body(): arrived.append(lax.ppermute(block, 'blk', inward))  7.4 us
    ppermute x1, waiting for transfers between devices, inner_body(): near_other = lax.ppermute(other_adjoint, 'blk', outward)  4.78 us
    pallas_call x2, Pallas kernels, to_time(): pl.pallas_call(to_time_kernel, grid_spec=pltpu.PrefetchScalarGridSpec(num...  4.49 us
    pallas_call x4, Pallas kernels, spectra(): pl.pallas_call(sum_kernel, in_specs=[VMEM] * len(args), out_specs=[VMEM]...  4.07 us
    pallas_call x2, Pallas kernels, couple(): pl.pallas_call(functools.partial(couple_kernel, piece, len(rows), len(col...  2.89 us
  transfers between devices with their start and end apart: 18, of which 6 were waited for; matrix products, arithmetic and copies ran while one was open for 2% of the time, Pallas kernels for 11%

profile of v7, /device:TPU:0, one launch (start us, length us, event | category | flops | bytes accessed | tf_op | source)
XLA Modules:
  0.0 93.9 jit_solution(17412933212299904161)
XLA Ops:
  0.0 2.2 %constant_dynamic-slice_fusion.6 = (bf16[80,1024]{1,0:T(8,128)(2,1)S(1)}, bf16[80,1024]{1,0:T(8,128)(2,1)S(1)}, bf16[80,1024]{1,0:T(8,128)(2,1)}, bf16[80,1024]{...) fusion(bf16[320,1024]{1,0:T(8,128)(2,1)} %param.5, ...), kind=kLoop, calls=%fused_computation.54 | loop fusion | bytes 2621456 | tf_op jit(solution)/shard_map/dynamic_slice | solution.py:463
  2.3 5.0 %collective-permute-start.1 = (bf16[160,1024]{1,0:T(8,128)(2,1)S(1)}, bf16[160,1024]{1,0:T(8,128)(2,1)S(1)}, u32[]{:S(2)}, u32[]{:S(2)}) collective-permute-start(bf16[160,1024]{1,0:T(8,128)(2,1)S(1)} %pad_maximum_fusion.2.refs_0_), channel_id=1, source_target_pairs={{0,4},{12,8},{1,5},{13,9},{2,6},{14,10},{3,7},{15,11},{16,20},{28,... | collective-permute-start | bytes 983048 | tf_op jit(solution)/shard_map/ppermute | solution.py:475
  7.3 2.0 %collective-permute-start = (bf16[160,1024]{1,0:T(8,128)(2,1)S(1)}, bf16[160,1024]{1,0:T(8,128)(2,1)}, u32[]{:S(2)}, u32[]{:S(2)}) collective-permute-start(bf16[160,1024]{1,0:T(8,128)(2,1)S(1)} %pad_maximum_fusion.refs_0_), channel_id=1, source_target_pairs={{0,4},{12,8},{1,5},{13,9},{2,6},{14,10},{3,7},{15,11},{16,20},{28,... | collective-permute-start | bytes 983048 | tf_op jit(solution)/shard_map/ppermute | solution.py:475
  9.3 2.0 %collective-permute-start.4 = (bf16[160,1024]{1,0:T(8,128)(2,1)S(1)}, bf16[160,1024]{1,0:T(8,128)(2,1)}, u32[]{:S(2)}, u32[]{:S(2)}) collective-permute-start(bf16[160,1024]{1,0:T(8,128)(2,1)S(1)} %pad_maximum_fusion.1.refs_1_), channel_id=1, source_target_pairs={{0,4},{12,8},{1,5},{13,9},{2,6},{14,10},{3,7},{15,11},{16,20},{28,... | collective-permute-start | bytes 983048 | tf_op jit(solution)/shard_map/ppermute | solution.py:475
  11.4 0.0 copy-done.3
  11.5 0.0 copy-done.2
  11.5 0.1 copy.6
  11.6 0.1 add_select_fusion.3
  11.7 0.1 fusion.28
  11.8 0.1 maximum_multiply_fusion
  11.8 0.1 convolution_multiply_fusion
  12.0 0.5 fusion.6
  12.5 0.3 fusion.15
  12.9 1.2 %two_bases.1 = (bf16[1024,1024]{1,0:T(8,128)(2,1)S(1)}, bf16[1024,1024]{1,0:T(8,128)(2,1)S(1)}) custom-call(f32[16,512]{1,0:T(8,128)S(1)} %get-tuple-element.57.refs_0_, f32[16,512]{1,0:T(8,128)S(1)} %get-tuple-element.58.refs_1_, f32[16,512]{1,0:T(8,128)S(1)} %get-tuple-element.52.refs_2_, f32[16,512]{1,0:T(8,128)S(1)} %get-tuple-element.51.refs_3_, ...), custom_call_target="tpu_custom_call" | custom-call | flops 8388608 | bytes 4194304 | tf_op jit(solution)/shard_map/two_bases/pallas_call | solution.py:375
  14.1 0.8 own_parts.2
  14.9 0.0 copy-start
  14.9 0.0 copy-start.1
  14.9 7.4 %collective-permute-done.near_ref = bf16[160,1024]{1,0:T(8,128)(2,1)} collective-permute-done((bf16[160,1024]{1,0:T(8,128)(2,1)S(1)}, bf16[160,1024]{1,0:T(8,128)(2,1)}, u32[]{:S(2)}, u32[]{:S(2)}) %collective-permute-start) | collective-permute-done | bytes 327712 | tf_op jit(solution)/shard_map/ppermute | solution.py:475
  22.3 1.5 %spectra.4.refs_0_ = bf16[160,1024]{1,0:T(8,128)(2,1)S(1)} custom-call(f32[160,1024]{1,0:T(8,128)S(1)} %get-tuple-element.21.part_ref, bf16[160,1024]{1,0:T(8,128)(2,1)} %collective-permute-done.near_ref, bf16[1024,1024]{1,0:T(8,128)(2,1)S(1)} %get-tuple-element.22.basis_ref), custom_call_target="tpu_custom_call" | custom-call | flops 335544320 | bytes 2097152 | tf_op jit(solution)/shard_map/spectra/pallas_call | solution.py:431
  23.8 0.7 collective-permute-start.2
  24.5 0.0 copy-done
  24.5 0.0 copy-done.1
  24.6 7.3 %collective-permute-start.5 = (bf16[160,1024]{1,0:T(8,128)(2,1)S(1)}, bf16[160,1024]{1,0:T(8,128)(2,1)S(1)}, u32[]{:S(2)}, u32[]{:S(2)}) collective-permute-start(bf16[160,1024]{1,0:T(8,128)(2,1)S(1)} %pad_maximum_fusion.3.refs_1_), channel_id=1, source_target_pairs={{0,4},{12,8},{1,5},{13,9},{2,6},{14,10},{3,7},{15,11},{16,20},{28,... | collective-permute-start | bytes 983048 | tf_op jit(solution)/shard_map/ppermute | solution.py:475
  31.9 0.0 collective-permute-done.4.near_ref
  31.9 1.5 %spectra.6.refs_2_ = bf16[160,1024]{1,0:T(8,128)(2,1)S(1)} custom-call(f32[160,1024]{1,0:T(8,128)S(1)} %get-tuple-element.25.part_ref, bf16[160,1024]{1,0:T(8,128)(2,1)} %collective-permute-done.4.near_ref, bf16[1024,1024]{1,0:T(8,128)(2,1)S(1)} %get-tuple-element.22.basis_ref), custom_call_target="tpu_custom_call" | custom-call | flops 335544320 | bytes 2097152 | tf_op jit(solution)/shard_map/spectra/pallas_call | solution.py:431
  33.4 0.7 collective-permute-start.6
  34.1 0.9 own_parts.3
  35.0 0.0 collective-permute-done.1.near_ref
  35.0 0.0 collective-permute-done.2.rest_0_
  35.0 0.5 spectra.5
  35.5 0.1 collective-permute-start.8
  35.6 1.6 %collective-permute-start.10 = (bf16[160,1024]{1,0:T(8,128)(2,1)S(1)}, bf16[160,1024]{1,0:T(8,128)(2,1)S(1)}, u32[]{:S(2)}, u32[]{:S(2)}) collective-permute-start(bf16[160,1024]{1,0:T(8,128)(2,1)S(1)} %get-tuple-element.28.refs_4_.refs_0_.refs_2_), channel_id=1, source_target_pairs={{0,2},{2,0},{1,3},{3,1},{4,6},{6,4},{5,7},{7,5},{8,10},{10,8},{9,1... | collective-permute-start | bytes 983048 | tf_op jit(solution)/shard_map/ppermute | solution.py:23
  37.2 0.0 collective-permute-done.5.near_ref
  37.2 0.0 collective-permute-done.6.rest_0_
  37.2 0.5 spectra.7
  37.7 0.9 %collective-permute-start.11 = (bf16[160,1024]{1,0:T(8,128)(2,1)S(1)}, bf16[160,1024]{1,0:T(8,128)(2,1)S(1)}, u32[]{:S(2)}, u32[]{:S(2)}) collective-permute-start(bf16[160,1024]{1,0:T(8,128)(2,1)S(1)} %get-tuple-element.29.refs_5_.refs_1_.refs_3_), channel_id=1, source_target_pairs={{0,2},{2,0},{1,3},{3,1},{4,6},{6,4},{5,7},{7,5},{8,10},{10,8},{9,1... | collective-permute-start | bytes 983048 | tf_op jit(solution)/shard_map/ppermute | solution.py:23
  38.7 0.0 collective-permute-start.9
  38.7 0.7 collective-permute-start.3
  39.4 0.0 collective-permute-done.8.refs_6_.refs_4_
  39.4 0.7 collective-permute-start.7
  40.0 6.2 %collective-permute-done.10.refs_8_.refs_6_ = bf16[160,1024]{1,0:T(8,128)(2,1)S(1)} collective-permute-done((bf16[160,1024]{1,0:T(8,128)(2,1)S(1)}, bf16[160,1024]{1,0:T(8,128)(2,1)S(1)}, u32[]{:S(2)}, u32[]{:S(2)}) %collective-permute-start.10) | collective-permute-done | bytes 327712 | tf_op jit(solution)/shard_map/ppermute | solution.py:23
  46.3 0.0 collective-permute-start.12
  46.3 6.5 %collective-permute-done.11.refs_9_.refs_7_ = bf16[160,1024]{1,0:T(8,128)(2,1)S(1)} collective-permute-done((bf16[160,1024]{1,0:T(8,128)(2,1)S(1)}, bf16[160,1024]{1,0:T(8,128)(2,1)S(1)}, u32[]{:S(2)}, u32[]{:S(2)}) %collective-permute-start.11) | collective-permute-done | bytes 327712 | tf_op jit(solution)/shard_map/ppermute | solution.py:23
  52.8 0.0 collective-permute-start.13
  52.8 0.0 collective-permute-done.9.refs_7_.refs_5_
  52.8 0.0 collective-permute-done.3.refs_1_
  52.8 0.0 collective-permute-done.7.refs_3_
  52.8 0.0 collective-permute-done.12.refs_10_.refs_8_
  52.8 1.6 %collective-permute-done.13.refs_11_.refs_9_ = bf16[160,1024]{1,0:T(8,128)(2,1)S(1)} collective-permute-done((bf16[160,1024]{1,0:T(8,128)(2,1)S(1)}, bf16[160,1024]{1,0:T(8,128)(2,1)S(1)}, u32[]{:S(2)}, u32[]{:S(2)}) %collective-permute-start.13) | collective-permute-done | bytes 327712 | tf_op jit(solution)/shard_map/ppermute | solution.py:23
  54.4 1.5 %couple.2 = bf16[160,1024]{1,0:T(8,128)(2,1)S(1)} custom-call(bf16[160,1024]{1,0:T(8,128)(2,1)S(1)} %spectra.4.refs_0_, bf16[160,1024]{1,0:T(8,128)(2,1)S(1)} %collective-permute-done.3.refs_1_, bf16[160,1024]{1,0:T(8,128)(2,1)S(1)} %spectra.6.refs_2_, bf16[160,1024]{1,0:T(8,128)(2,1)S(1)} %collective-permute-done.7.refs_3_, ...), custom_call_target="tpu_custom_call" | custom-call | flops 629145600 | bytes 3276800 | tf_op jit(solution)/shard_map/couple/pallas_call | solution.py:305
  55.9 0.7 collective-permute-start.16
  56.6 1.4 %couple.3 = bf16[160,1024]{1,0:T(8,128)(2,1)S(1)} custom-call(bf16[160,1024]{1,0:T(8,128)(2,1)S(1)} %get-tuple-element.28.refs_4_.refs_0_.refs_2_, bf16[160,1024]{1,0:T(8,128)(2,1)S(1)} %get-tuple-element.29.refs_5_.refs_1_.refs_3_, bf16[160,1024]{1,0:T(8,128)(2,1)S(1)} %get-tuple-element.28.refs_4_.refs_0_.refs_2_, ...), custom_call_target="tpu_custom_call" | custom-call | flops 629145600 | bytes 3276800 | tf_op jit(solution)/shard_map/couple/pallas_call | solution.py:305
  58.0 0.7 collective-permute-start.14
  58.7 0.0 collective-permute-done.16
  58.7 0.1 add_convert_fusion.here_ref
  58.8 1.3 %collective-permute-start.17 = (bf16[160,1024]{1,0:T(8,128)(2,1)S(1)}, bf16[160,1024]{1,0:T(8,128)(2,1)S(1)}, u32[]{:S(2)}, u32[]{:S(2)}) collective-permute-start(bf16[160,1024]{1,0:T(8,128)(2,1)S(1)} %add_convert_fusion.here_ref), channel_id=1, source_target_pairs={{4,0},{8,12},{5,1},{9,13},{6,2},{10,14},{7,3},{11,15},{20,16},{24,... | collective-permute-start | bytes 983048 | tf_op jit(solution)/shard_map/ppermute | solution.py:535
  60.1 0.0 collective-permute-done.14
  60.1 0.1 add_convert_fusion.1.here_ref
  60.2 1.3 %collective-permute-start.15 = (bf16[160,1024]{1,0:T(8,128)(2,1)S(1)}, bf16[160,1024]{1,0:T(8,128)(2,1)S(1)}, u32[]{:S(2)}, u32[]{:S(2)}) collective-permute-start(bf16[160,1024]{1,0:T(8,128)(2,1)S(1)} %add_convert_fusion.1.here_ref), channel_id=1, source_target_pairs={{4,0},{8,12},{5,1},{9,13},{6,2},{10,14},{7,3},{11,15},{20,16},{24,... | collective-permute-start | bytes 983048 | tf_op jit(solution)/shard_map/ppermute | solution.py:537
  61.5 0.1 pad_add_fusion.1
  61.6 23.0 %collective-permute-done.17.there_ref = bf16[160,1024]{1,0:T(8,128)(2,1)S(1)} collective-permute-done((bf16[160,1024]{1,0:T(8,128)(2,1)S(1)}, bf16[160,1024]{1,0:T(8,128)(2,1)S(1)}, u32[]{:S(2)}, u32[]{:S(2)}) %collective-permute-start.17) | collective-permute-done | bytes 327712 | tf_op jit(solution)/shard_map/ppermute | solution.py:535
  84.6 2.2 %to_time.2.rest_0_ = bf16[320,1024]{1,0:T(8,128)(2,1)} custom-call(s32[2]{0:T(128)S(1)} %get-tuple-element.60.flag_ref, bf16[160,1024]{1,0:T(8,128)(2,1)S(1)} %add_convert_fusion.here_ref, bf16[160,1024]{1,0:T(8,128)(2,1)S(1)} %collective-permute-done.17.there_ref, bf16[1024,1024]{1,0:T(8,128)(2,1)S(1)} %get-tuple-element.20.refs_2_.basis_ref), custom_call_target="tpu_custom_call" | custom-call | flops 335544320 | bytes 2097152 | tf_op jit(solution)/shard_map/to_time/pallas_call | solution.py:340
  86.9 4.8 %collective-permute-done.15.there_ref = bf16[160,1024]{1,0:T(8,128)(2,1)S(1)} collective-permute-done((bf16[160,1024]{1,0:T(8,128)(2,1)S(1)}, bf16[160,1024]{1,0:T(8,128)(2,1)S(1)}, u32[]{:S(2)}, u32[]{:S(2)}) %collective-permute-start.15) | collective-permute-done | bytes 327712 | tf_op jit(solution)/shard_map/ppermute | solution.py:537
  91.7 2.2 %to_time.3 = bf16[320,1024]{1,0:T(8,128)(2,1)} custom-call(s32[2]{0:T(128)S(1)} %get-tuple-element.59.flag_ref, bf16[160,1024]{1,0:T(8,128)(2,1)S(1)} %add_convert_fusion.1.here_ref, bf16[160,1024]{1,0:T(8,128)(2,1)S(1)} %collective-permute-done.15.there_ref, ...), custom_call_target="tpu_custom_call", output_to_operand_aliasing={{}: (4, {})} | custom-call | flops 335544320 | bytes 2097152 | tf_op jit(solution)/shard_map/to_time/pallas_call | solution.py:340
  (15 shorter events, 0.2 us)
Async XLA Ops:
  0.0 11.4 %copy-start.3 = (s32[1280]{0:T(1024)S(1)}, s32[1280]{0:T(1024)}, u32[]{:S(2)}) copy-start(s32[1280]{0:T(1024)} %param.6) | copy-start | bytes 15364
  0.0 11.5 %copy-start.2 = (s32[16,16]{1,0:T(8,128)S(1)}, s32[16,16]{1,0:T(8,128)}, u32[]{:S(2)}) copy-start(s32[16,16]{1,0:T(8,128)} %param.7) | copy-start | bytes 3076
  2.3 32.7 %collective-permute-start.1 = (bf16[160,1024]{1,0:T(8,128)(2,1)S(1)}, bf16[160,1024]{1,0:T(8,128)(2,1)S(1)}, u32[]{:S(2)}, u32[]{:S(2)}) collective-permute-start(bf16[160,1024]{1,0:T(8,128)(2,1)S(1)} %pad_maximum_fusion.2.refs_0_), channel_id=1, source_target_pairs={{0,4},{12,8},{1,5},{13,9},{2,6},{14,10},{3,7},{15,11},{16,20},{28,... | collective-permute-start | bytes 983048 | tf_op jit(solution)/shard_map/ppermute | solution.py:475
  7.3 15.1 %collective-permute-start = (bf16[160,1024]{1,0:T(8,128)(2,1)S(1)}, bf16[160,1024]{1,0:T(8,128)(2,1)}, u32[]{:S(2)}, u32[]{:S(2)}) collective-permute-start(bf16[160,1024]{1,0:T(8,128)(2,1)S(1)} %pad_maximum_fusion.refs_0_), channel_id=1, source_target_pairs={{0,4},{12,8},{1,5},{13,9},{2,6},{14,10},{3,7},{15,11},{16,20},{28,... | collective-permute-start | bytes 983048 | tf_op jit(solution)/shard_map/ppermute | solution.py:475
  9.3 22.6 %collective-permute-start.4 = (bf16[160,1024]{1,0:T(8,128)(2,1)S(1)}, bf16[160,1024]{1,0:T(8,128)(2,1)}, u32[]{:S(2)}, u32[]{:S(2)}) collective-permute-start(bf16[160,1024]{1,0:T(8,128)(2,1)S(1)} %pad_maximum_fusion.1.refs_1_), channel_id=1, source_target_pairs={{0,4},{12,8},{1,5},{13,9},{2,6},{14,10},{3,7},{15,11},{16,20},{28,... | collective-permute-start | bytes 983048 | tf_op jit(solution)/shard_map/ppermute | solution.py:475
  14.9 9.6 %copy-start = (bf16[80,1024]{1,0:T(8,128)(2,1)S(1)}, bf16[80,1024]{1,0:T(8,128)(2,1)}, u32[]{:S(2)}) copy-start(bf16[80,1024]{1,0:T(8,128)(2,1)} %get-tuple-element.39) | copy-start | bytes 491524
  14.9 9.6 %copy-start.1 = (bf16[80,1024]{1,0:T(8,128)(2,1)S(1)}, bf16[80,1024]{1,0:T(8,128)(2,1)}, u32[]{:S(2)}) copy-start(bf16[80,1024]{1,0:T(8,128)(2,1)} %get-tuple-element.66) | copy-start | bytes 491524
  23.8 11.1 %collective-permute-start.2 = (bf16[160,1024]{1,0:T(8,128)(2,1)S(1)}, bf16[160,1024]{1,0:T(8,128)(2,1)S(1)}, u32[]{:S(2)}, u32[]{:S(2)}) collective-permute-start(bf16[160,1024]{1,0:T(8,128)(2,1)S(1)} %spectra.4.refs_0_), channel_id=1, source_target_pairs={{4,8},{8,4},{5,9},{9,5},{6,10},{10,6},{7,11},{11,7},{20,24},{24,20... | collective-permute-start | bytes 983048 | tf_op jit(solution)/shard_map/ppermute | solution.py:514
  24.6 12.6 %collective-permute-start.5 = (bf16[160,1024]{1,0:T(8,128)(2,1)S(1)}, bf16[160,1024]{1,0:T(8,128)(2,1)S(1)}, u32[]{:S(2)}, u32[]{:S(2)}) collective-permute-start(bf16[160,1024]{1,0:T(8,128)(2,1)S(1)} %pad_maximum_fusion.3.refs_1_), channel_id=1, source_target_pairs={{0,4},{12,8},{1,5},{13,9},{2,6},{14,10},{3,7},{15,11},{16,20},{28,... | collective-permute-start | bytes 983048 | tf_op jit(solution)/shard_map/ppermute | solution.py:475
  33.4 3.8 %collective-permute-start.6 = (bf16[160,1024]{1,0:T(8,128)(2,1)S(1)}, bf16[160,1024]{1,0:T(8,128)(2,1)S(1)}, u32[]{:S(2)}, u32[]{:S(2)}) collective-permute-start(bf16[160,1024]{1,0:T(8,128)(2,1)S(1)} %spectra.6.refs_2_), channel_id=1, source_target_pairs={{4,8},{8,4},{5,9},{9,5},{6,10},{10,6},{7,11},{11,7},{20,24},{24,20... | collective-permute-start | bytes 983048 | tf_op jit(solution)/shard_map/ppermute | solution.py:514
  35.5 3.8 %collective-permute-start.8 = (bf16[160,1024]{1,0:T(8,128)(2,1)S(1)}, bf16[160,1024]{1,0:T(8,128)(2,1)S(1)}, u32[]{:S(2)}, u32[]{:S(2)}) collective-permute-start(bf16[160,1024]{1,0:T(8,128)(2,1)S(1)} %get-tuple-element.28.refs_4_.refs_0_.refs_2_), channel_id=1, source_target_pairs={{0,1},{1,0},{2,3},{3,2},{4,5},{5,4},{6,7},{7,6},{8,9},{9,8},{10,11... | collective-permute-start | bytes 983048 | tf_op jit(solution)/shard_map/ppermute | solution.py:23
  35.6 10.7 %collective-permute-start.10 = (bf16[160,1024]{1,0:T(8,128)(2,1)S(1)}, bf16[160,1024]{1,0:T(8,128)(2,1)S(1)}, u32[]{:S(2)}, u32[]{:S(2)}) collective-permute-start(bf16[160,1024]{1,0:T(8,128)(2,1)S(1)} %get-tuple-element.28.refs_4_.refs_0_.refs_2_), channel_id=1, source_target_pairs={{0,2},{2,0},{1,3},{3,1},{4,6},{6,4},{5,7},{7,5},{8,10},{10,8},{9,1... | collective-permute-start | bytes 983048 | tf_op jit(solution)/shard_map/ppermute | solution.py:23
  37.7 15.0 %collective-permute-start.11 = (bf16[160,1024]{1,0:T(8,128)(2,1)S(1)}, bf16[160,1024]{1,0:T(8,128)(2,1)S(1)}, u32[]{:S(2)}, u32[]{:S(2)}) collective-permute-start(bf16[160,1024]{1,0:T(8,128)(2,1)S(1)} %get-tuple-element.29.refs_5_.refs_1_.refs_3_), channel_id=1, source_target_pairs={{0,2},{2,0},{1,3},{3,1},{4,6},{6,4},{5,7},{7,5},{8,10},{10,8},{9,1... | collective-permute-start | bytes 983048 | tf_op jit(solution)/shard_map/ppermute | solution.py:23
  38.7 14.1 %collective-permute-start.9 = (bf16[160,1024]{1,0:T(8,128)(2,1)S(1)}, bf16[160,1024]{1,0:T(8,128)(2,1)S(1)}, u32[]{:S(2)}, u32[]{:S(2)}) collective-permute-start(bf16[160,1024]{1,0:T(8,128)(2,1)S(1)} %get-tuple-element.29.refs_5_.refs_1_.refs_3_), channel_id=1, source_target_pairs={{0,1},{1,0},{2,3},{3,2},{4,5},{5,4},{6,7},{7,6},{8,9},{9,8},{10,11... | collective-permute-start | bytes 983048 | tf_op jit(solution)/shard_map/ppermute | solution.py:23
  38.7 14.1 %collective-permute-start.3 = (bf16[160,1024]{1,0:T(8,128)(2,1)S(1)}, bf16[160,1024]{1,0:T(8,128)(2,1)S(1)}, u32[]{:S(2)}, u32[]{:S(2)}) collective-permute-start(bf16[160,1024]{1,0:T(8,128)(2,1)S(1)} %get-tuple-element.24), channel_id=1, source_target_pairs={{4,8},{8,4},{5,9},{9,5},{6,10},{10,6},{7,11},{11,7},{20,24},{24,20... | collective-permute-start | bytes 983048 | tf_op jit(solution)/shard_map/ppermute | solution.py:526
  39.4 13.4 %collective-permute-start.7 = (bf16[160,1024]{1,0:T(8,128)(2,1)S(1)}, bf16[160,1024]{1,0:T(8,128)(2,1)S(1)}, u32[]{:S(2)}, u32[]{:S(2)}) collective-permute-start(bf16[160,1024]{1,0:T(8,128)(2,1)S(1)} %get-tuple-element.27), channel_id=1, source_target_pairs={{4,8},{8,4},{5,9},{9,5},{6,10},{10,6},{7,11},{11,7},{20,24},{24,20... | collective-permute-start | bytes 983048 | tf_op jit(solution)/shard_map/ppermute | solution.py:526
  46.3 6.5 %collective-permute-start.12 = (bf16[160,1024]{1,0:T(8,128)(2,1)S(1)}, bf16[160,1024]{1,0:T(8,128)(2,1)S(1)}, u32[]{:S(2)}, u32[]{:S(2)}) collective-permute-start(bf16[160,1024]{1,0:T(8,128)(2,1)S(1)} %collective-permute-done.10.refs_8_.refs_6_), channel_id=1, source_target_pairs={{0,1},{1,0},{2,3},{3,2},{4,5},{5,4},{6,7},{7,6},{8,9},{9,8},{10,11... | collective-permute-start | bytes 983048 | tf_op jit(solution)/shard_map/ppermute | solution.py:23
  52.8 1.6 %collective-permute-start.13 = (bf16[160,1024]{1,0:T(8,128)(2,1)S(1)}, bf16[160,1024]{1,0:T(8,128)(2,1)S(1)}, u32[]{:S(2)}, u32[]{:S(2)}) collective-permute-start(bf16[160,1024]{1,0:T(8,128)(2,1)S(1)} %collective-permute-done.11.refs_9_.refs_7_), channel_id=1, source_target_pairs={{0,1},{1,0},{2,3},{3,2},{4,5},{5,4},{6,7},{7,6},{8,9},{9,8},{10,11... | collective-permute-start | bytes 983048 | tf_op jit(solution)/shard_map/ppermute | solution.py:23
  55.9 2.8 %collective-permute-start.16 = (bf16[160,1024]{1,0:T(8,128)(2,1)S(1)}, bf16[160,1024]{1,0:T(8,128)(2,1)S(1)}, u32[]{:S(2)}, u32[]{:S(2)}) collective-permute-start(bf16[160,1024]{1,0:T(8,128)(2,1)S(1)} %couple.2), channel_id=1, source_target_pairs={{4,8},{8,4},{5,9},{9,5},{6,10},{10,6},{7,11},{11,7},{20,24},{24,20... | collective-permute-start | bytes 983048 | tf_op jit(solution)/shard_map/ppermute | solution.py:530
  58.0 2.1 %collective-permute-start.14 = (bf16[160,1024]{1,0:T(8,128)(2,1)S(1)}, bf16[160,1024]{1,0:T(8,128)(2,1)S(1)}, u32[]{:S(2)}, u32[]{:S(2)}) collective-permute-start(bf16[160,1024]{1,0:T(8,128)(2,1)S(1)} %couple.3), channel_id=1, source_target_pairs={{4,8},{8,4},{5,9},{9,5},{6,10},{10,6},{7,11},{11,7},{20,24},{24,20... | collective-permute-start | bytes 983048 | tf_op jit(solution)/shard_map/ppermute | solution.py:532
  58.8 25.9 %collective-permute-start.17 = (bf16[160,1024]{1,0:T(8,128)(2,1)S(1)}, bf16[160,1024]{1,0:T(8,128)(2,1)S(1)}, u32[]{:S(2)}, u32[]{:S(2)}) collective-permute-start(bf16[160,1024]{1,0:T(8,128)(2,1)S(1)} %add_convert_fusion.here_ref), channel_id=1, source_target_pairs={{4,0},{8,12},{5,1},{9,13},{6,2},{10,14},{7,3},{11,15},{20,16},{24,... | collective-permute-start | bytes 983048 | tf_op jit(solution)/shard_map/ppermute | solution.py:535
  60.2 31.5 %collective-permute-start.15 = (bf16[160,1024]{1,0:T(8,128)(2,1)S(1)}, bf16[160,1024]{1,0:T(8,128)(2,1)S(1)}, u32[]{:S(2)}, u32[]{:S(2)}) collective-permute-start(bf16[160,1024]{1,0:T(8,128)(2,1)S(1)} %add_convert_fusion.1.here_ref), channel_id=1, source_target_pairs={{4,0},{8,12},{5,1},{9,13},{6,2},{10,14},{7,3},{11,15},{20,16},{24,... | collective-permute-start | bytes 983048 | tf_op jit(solution)/shard_map/ppermute | solution.py:537

commit v8 on v7

--- a/solution.py
+++ b/solution.py
@@ -328,7 +328,7 @@
 
 def to_time(place, is_inner, here, there, basis, span, rows, before):
     half = here.shape[0]
-    wide = math.gcd(span, 512)
+    wide = span
     whole = pl.BlockSpec(here.shape, lambda j, flags: (0, 0))
     specs = [whole, whole, pl.BlockSpec((wide, 2 * NF), lambda j, flags: (j, 0))]
     args = [here, there, basis]
@@ -456,19 +456,20 @@
     side = level // 2
     inward, swapped, outward = [(0, 1), (3, 2)], [(1, 2), (2, 1)], [(1, 0), (2, 3)]
 
-    def pieces_of(which):
-        return [
-            jnp.concatenate(
-                [
-                    lax.dynamic_slice_in_dim(source, which * half + at, piece, 0)
-                    for source in (synthetic, observed)
-                ],
-                axis=0,
-            )
-            for at in range(0, half, piece)
-        ]
-
-    passed, kept = pieces_of(1 - side), pieces_of(side)
+    def piece_of(which, at, sources):
+        return jnp.concatenate(
+            [
+                lax.dynamic_slice_in_dim(source, which * half + at, piece, 0)
+                for source in sources
+            ],
+            axis=0,
+        )
+
+    sources = (synthetic, observed)
+    front = piece_of(1 - side, 0, sources)
+    front, sources = lax.optimization_barrier((front, sources))
+    passed = [front] + [piece_of(1 - side, at, sources) for at in range(piece, half, piece)]
+    kept = [piece_of(side, at, sources) for at in range(0, half, piece)]
     near_passed, near_kept = [], []
     for blocks, arrived in ((passed, near_passed), (kept, near_kept)):
         for block in blocks:

time: 94.3 us -> 95.6 us (1.014)
  local copies, waits for them, and re-layouts: 2.46 us -> 3.8 us
    dynamic_slice x1 -> x3, local copies, waits for them, and re-layouts: 2.24 us -> 3.58 us  [piece_of(): lax.dynamic_slice_in_dim(source, which * half + at, piece, 0)]
where the time goes in v8:
time: 95.6 us; the launch traced here: 95.2 us
  waiting for transfers between devices  49.7 us (52%)
  starting transfers between devices  25.6 us (27%)
  Pallas kernels  14.1 us (15%)
  local copies, waits for them, and re-layouts  3.8 us (4%)
  other arithmetic  1.44 us (2%)
    ppermute x1, waiting for transfers between devices, inner_body(): near_own = lax.ppermute(own_adjoint, 'blk', outward)  23 us
    ppermute x4, starting transfers between devices, inner_body(): arrived.append(lax.ppermute(block, 'blk', inward))  16.4 us
    ppermute x6, waiting for transfers between devices, shift(): return lax.ppermute(value, axis, pairs)  14.3 us
    ppermute x4, waiting for transfers between devices, inner_body(): arrived.append(lax.ppermute(block, 'blk', inward))  7.42 us
    ppermute x1, waiting for transfers between devices, inner_body(): near_other = lax.ppermute(other_adjoint, 'blk', outward)  4.91 us
    pallas_call x2, Pallas kernels, to_time(): pl.pallas_call(to_time_kernel, grid_spec=pltpu.PrefetchScalarGridSpec(num...  4.21 us
    pallas_call x4, Pallas kernels, spectra(): pl.pallas_call(sum_kernel, in_specs=[VMEM] * len(args), out_specs=[VMEM]...  4.07 us
    dynamic_slice x3, local copies, waits for them, and re-layouts, piece_of(): lax.dynamic_slice_in_dim(source, which * half + at, piece, 0)  3.58 us
  transfers between devices with their start and end apart: 18, of which 6 were waited for; matrix products, arithmetic and copies ran while one was open for 2% of the time, Pallas kernels for 11%

profile of v8, /device:TPU:0, one launch (start us, length us, event | category | flops | bytes accessed | tf_op | source)
XLA Modules:
  0.0 95.2 jit_solution(7802146849967278104)
XLA Ops:
  0.0 1.1 %constant_dynamic-slice_fusion.8 = (bf16[80,1024]{1,0:T(8,128)(2,1)S(1)}, bf16[80,1024]{1,0:T(8,128)(2,1)S(1)}) fusion(bf16[320,1024]{1,0:T(8,128)(2,1)} %param.5, s32[]{:T(128)S(6)} %select_n.105, bf16[320,1024]{1,0:T(8,128)(2,1)} %param.4), kind=kLoop, calls=%fused_computation.56 | loop fusion | bytes 655364 | tf_op jit(solution)/shard_map/dynamic_slice | solution.py:462
  1.1 0.0 copy-start.4
  1.1 0.0 copy-start.3
  1.2 1.8 %constant_dynamic-slice_fusion.6 = (bf16[80,1024]{1,0:T(8,128)(2,1)S(1)}, bf16[80,1024]{1,0:T(8,128)(2,1)}, bf16[80,1024]{1,0:T(8,128)(2,1)S(1)}) fusion(bf16[320,1024]{1,0:T(8,128)(2,1)} %param.5, s32[]{:T(128)S(6)} %select_n.106, s32[]{:T(128)S(6)} %select_n.126, s32[]{:T(128)S(6)} %select_n.125), kind=kLoop, calls=%fused_computation.54 | loop fusion | bytes 983052 | tf_op jit(solution)/shard_map/dynamic_slice | solution.py:462
  3.0 0.7 constant_dynamic-slice_fusion.7
  3.7 5.0 %collective-permute-start.1 = (bf16[160,1024]{1,0:T(8,128)(2,1)S(1)}, bf16[160,1024]{1,0:T(8,128)(2,1)S(1)}, u32[]{:S(2)}, u32[]{:S(2)}) collective-permute-start(bf16[160,1024]{1,0:T(8,128)(2,1)S(1)} %pad_maximum_fusion.2.refs_0_), channel_id=1, source_target_pairs={{0,4},{12,8},{1,5},{13,9},{2,6},{14,10},{3,7},{15,11},{16,20},{28,... | collective-permute-start | bytes 983048 | tf_op jit(solution)/shard_map/ppermute | solution.py:476
  8.7 2.0 %collective-permute-start = (bf16[160,1024]{1,0:T(8,128)(2,1)S(1)}, bf16[160,1024]{1,0:T(8,128)(2,1)}, u32[]{:S(2)}, u32[]{:S(2)}) collective-permute-start(bf16[160,1024]{1,0:T(8,128)(2,1)S(1)} %pad_maximum_fusion.refs_0_), channel_id=1, source_target_pairs={{0,4},{12,8},{1,5},{13,9},{2,6},{14,10},{3,7},{15,11},{16,20},{28,... | collective-permute-start | bytes 983048 | tf_op jit(solution)/shard_map/ppermute | solution.py:476
  10.7 2.0 %collective-permute-start.4 = (bf16[160,1024]{1,0:T(8,128)(2,1)S(1)}, bf16[160,1024]{1,0:T(8,128)(2,1)}, u32[]{:S(2)}, u32[]{:S(2)}) collective-permute-start(bf16[160,1024]{1,0:T(8,128)(2,1)S(1)} %pad_maximum_fusion.1.refs_1_), channel_id=1, source_target_pairs={{0,4},{12,8},{1,5},{13,9},{2,6},{14,10},{3,7},{15,11},{16,20},{28,... | collective-permute-start | bytes 983048 | tf_op jit(solution)/shard_map/ppermute | solution.py:476
  12.8 0.0 copy-done.4
  12.9 0.1 copy.6
  13.0 0.1 add_select_fusion.3
  13.0 0.1 fusion.28
  13.2 0.1 maximum_multiply_fusion
  13.2 0.1 convolution_multiply_fusion
  13.4 0.5 fusion.6
  13.9 0.3 fusion.15
  14.3 1.2 %two_bases.1 = (bf16[1024,1024]{1,0:T(8,128)(2,1)S(1)}, bf16[1024,1024]{1,0:T(8,128)(2,1)S(1)}) custom-call(f32[16,512]{1,0:T(8,128)S(1)} %get-tuple-element.61.refs_0_, f32[16,512]{1,0:T(8,128)S(1)} %get-tuple-element.62.refs_1_, f32[16,512]{1,0:T(8,128)S(1)} %get-tuple-element.56.refs_2_, f32[16,512]{1,0:T(8,128)S(1)} %get-tuple-element.55.refs_3_, ...), custom_call_target="tpu_custom_call" | custom-call | flops 8388608 | bytes 4194304 | tf_op jit(solution)/shard_map/two_bases/pallas_call | solution.py:375
  15.5 0.8 own_parts.2
  16.3 0.0 copy-start
  16.3 7.4 %collective-permute-done.near_ref = bf16[160,1024]{1,0:T(8,128)(2,1)} collective-permute-done((bf16[160,1024]{1,0:T(8,128)(2,1)S(1)}, bf16[160,1024]{1,0:T(8,128)(2,1)}, u32[]{:S(2)}, u32[]{:S(2)}) %collective-permute-start) | collective-permute-done | bytes 327712 | tf_op jit(solution)/shard_map/ppermute | solution.py:476
  23.8 1.5 %spectra.4.refs_0_ = bf16[160,1024]{1,0:T(8,128)(2,1)S(1)} custom-call(f32[160,1024]{1,0:T(8,128)S(1)} %get-tuple-element.27.part_ref, bf16[160,1024]{1,0:T(8,128)(2,1)} %collective-permute-done.near_ref, bf16[1024,1024]{1,0:T(8,128)(2,1)S(1)} %get-tuple-element.28.basis_ref), custom_call_target="tpu_custom_call" | custom-call | flops 335544320 | bytes 2097152 | tf_op jit(solution)/shard_map/spectra/pallas_call | solution.py:431
  25.2 0.7 collective-permute-start.2
  26.0 7.3 %collective-permute-start.5 = (bf16[160,1024]{1,0:T(8,128)(2,1)S(1)}, bf16[160,1024]{1,0:T(8,128)(2,1)S(1)}, u32[]{:S(2)}, u32[]{:S(2)}) collective-permute-start(bf16[160,1024]{1,0:T(8,128)(2,1)S(1)} %pad_maximum_fusion.3.refs_1_), channel_id=1, source_target_pairs={{0,4},{12,8},{1,5},{13,9},{2,6},{14,10},{3,7},{15,11},{16,20},{28,... | collective-permute-start | bytes 983048 | tf_op jit(solution)/shard_map/ppermute | solution.py:476
  33.3 0.0 collective-permute-done.4.near_ref
  33.3 1.5 %spectra.6.refs_2_ = bf16[160,1024]{1,0:T(8,128)(2,1)S(1)} custom-call(f32[160,1024]{1,0:T(8,128)S(1)} %get-tuple-element.31.part_ref, bf16[160,1024]{1,0:T(8,128)(2,1)} %collective-permute-done.4.near_ref, bf16[1024,1024]{1,0:T(8,128)(2,1)S(1)} %get-tuple-element.28.basis_ref), custom_call_target="tpu_custom_call" | custom-call | flops 335544320 | bytes 2097152 | tf_op jit(solution)/shard_map/spectra/pallas_call | solution.py:431
  34.8 0.7 collective-permute-start.6
  35.5 0.9 own_parts.3
  36.4 0.0 collective-permute-done.1.near_ref
  36.4 0.0 collective-permute-done.2.rest_0_
  36.4 0.5 spectra.5
  37.0 0.1 collective-permute-start.8
  37.0 1.5 %collective-permute-start.10 = (bf16[160,1024]{1,0:T(8,128)(2,1)S(1)}, bf16[160,1024]{1,0:T(8,128)(2,1)S(1)}, u32[]{:S(2)}, u32[]{:S(2)}) collective-permute-start(bf16[160,1024]{1,0:T(8,128)(2,1)S(1)} %get-tuple-element.34.refs_4_.refs_0_.refs_2_), channel_id=1, source_target_pairs={{0,2},{2,0},{1,3},{3,1},{4,6},{6,4},{5,7},{7,5},{8,10},{10,8},{9,1... | collective-permute-start | bytes 983048 | tf_op jit(solution)/shard_map/ppermute | solution.py:23
  38.6 0.0 collective-permute-done.5.near_ref
  38.6 0.0 collective-permute-done.6.rest_0_
  38.6 0.5 spectra.7
  39.1 1.0 %collective-permute-start.11 = (bf16[160,1024]{1,0:T(8,128)(2,1)S(1)}, bf16[160,1024]{1,0:T(8,128)(2,1)S(1)}, u32[]{:S(2)}, u32[]{:S(2)}) collective-permute-start(bf16[160,1024]{1,0:T(8,128)(2,1)S(1)} %get-tuple-element.35.refs_5_.refs_1_.refs_3_), channel_id=1, source_target_pairs={{0,2},{2,0},{1,3},{3,1},{4,6},{6,4},{5,7},{7,5},{8,10},{10,8},{9,1... | collective-permute-start | bytes 983048 | tf_op jit(solution)/shard_map/ppermute | solution.py:23
  40.1 0.0 collective-permute-start.9
  40.1 0.7 collective-permute-start.3
  40.8 0.0 collective-permute-done.8.refs_6_.refs_4_
  40.8 0.7 collective-permute-start.7
  41.5 6.2 %collective-permute-done.10.refs_8_.refs_6_ = bf16[160,1024]{1,0:T(8,128)(2,1)S(1)} collective-permute-done((bf16[160,1024]{1,0:T(8,128)(2,1)S(1)}, bf16[160,1024]{1,0:T(8,128)(2,1)S(1)}, u32[]{:S(2)}, u32[]{:S(2)}) %collective-permute-start.10) | collective-permute-done | bytes 327712 | tf_op jit(solution)/shard_map/ppermute | solution.py:23
  47.7 0.0 collective-permute-start.12
  47.7 6.5 %collective-permute-done.11.refs_9_.refs_7_ = bf16[160,1024]{1,0:T(8,128)(2,1)S(1)} collective-permute-done((bf16[160,1024]{1,0:T(8,128)(2,1)S(1)}, bf16[160,1024]{1,0:T(8,128)(2,1)S(1)}, u32[]{:S(2)}, u32[]{:S(2)}) %collective-permute-start.11) | collective-permute-done | bytes 327712 | tf_op jit(solution)/shard_map/ppermute | solution.py:23
  54.2 0.0 collective-permute-start.13
  54.2 0.0 collective-permute-done.9.refs_7_.refs_5_
  54.2 0.0 collective-permute-done.3.refs_1_
  54.2 0.0 collective-permute-done.7.refs_3_
  54.2 0.0 collective-permute-done.12.refs_10_.refs_8_
  54.2 1.6 %collective-permute-done.13.refs_11_.refs_9_ = bf16[160,1024]{1,0:T(8,128)(2,1)S(1)} collective-permute-done((bf16[160,1024]{1,0:T(8,128)(2,1)S(1)}, bf16[160,1024]{1,0:T(8,128)(2,1)S(1)}, u32[]{:S(2)}, u32[]{:S(2)}) %collective-permute-start.13) | collective-permute-done | bytes 327712 | tf_op jit(solution)/shard_map/ppermute | solution.py:23
  55.8 1.5 %couple.2 = bf16[160,1024]{1,0:T(8,128)(2,1)S(1)} custom-call(bf16[160,1024]{1,0:T(8,128)(2,1)S(1)} %spectra.4.refs_0_, bf16[160,1024]{1,0:T(8,128)(2,1)S(1)} %collective-permute-done.3.refs_1_, bf16[160,1024]{1,0:T(8,128)(2,1)S(1)} %spectra.6.refs_2_, bf16[160,1024]{1,0:T(8,128)(2,1)S(1)} %collective-permute-done.7.refs_3_, ...), custom_call_target="tpu_custom_call" | custom-call | flops 629145600 | bytes 3276800 | tf_op jit(solution)/shard_map/couple/pallas_call | solution.py:305
  57.3 0.7 collective-permute-start.16
  58.0 1.4 %couple.3 = bf16[160,1024]{1,0:T(8,128)(2,1)S(1)} custom-call(bf16[160,1024]{1,0:T(8,128)(2,1)S(1)} %get-tuple-element.34.refs_4_.refs_0_.refs_2_, bf16[160,1024]{1,0:T(8,128)(2,1)S(1)} %get-tuple-element.35.refs_5_.refs_1_.refs_3_, bf16[160,1024]{1,0:T(8,128)(2,1)S(1)} %get-tuple-element.34.refs_4_.refs_0_.refs_2_, ...), custom_call_target="tpu_custom_call" | custom-call | flops 629145600 | bytes 3276800 | tf_op jit(solution)/shard_map/couple/pallas_call | solution.py:305
  59.4 0.7 collective-permute-start.14
  60.1 0.0 collective-permute-done.16
  60.1 0.1 add_convert_fusion.here_ref
  60.2 1.3 %collective-permute-start.17 = (bf16[160,1024]{1,0:T(8,128)(2,1)S(1)}, bf16[160,1024]{1,0:T(8,128)(2,1)S(1)}, u32[]{:S(2)}, u32[]{:S(2)}) collective-permute-start(bf16[160,1024]{1,0:T(8,128)(2,1)S(1)} %add_convert_fusion.here_ref), channel_id=1, source_target_pairs={{4,0},{8,12},{5,1},{9,13},{6,2},{10,14},{7,3},{11,15},{20,16},{24,... | collective-permute-start | bytes 983048 | tf_op jit(solution)/shard_map/ppermute | solution.py:536
  61.5 0.0 collective-permute-done.14
  61.5 0.1 add_convert_fusion.1.here_ref
  61.6 1.3 %collective-permute-start.15 = (bf16[160,1024]{1,0:T(8,128)(2,1)S(1)}, bf16[160,1024]{1,0:T(8,128)(2,1)S(1)}, u32[]{:S(2)}, u32[]{:S(2)}) collective-permute-start(bf16[160,1024]{1,0:T(8,128)(2,1)S(1)} %add_convert_fusion.1.here_ref), channel_id=1, source_target_pairs={{4,0},{8,12},{5,1},{9,13},{6,2},{10,14},{7,3},{11,15},{20,16},{24,... | collective-permute-start | bytes 983048 | tf_op jit(solution)/shard_map/ppermute | solution.py:538
  62.9 0.1 pad_add_fusion.1
  63.0 23.0 %collective-permute-done.17.there_ref = bf16[160,1024]{1,0:T(8,128)(2,1)S(1)} collective-permute-done((bf16[160,1024]{1,0:T(8,128)(2,1)S(1)}, bf16[160,1024]{1,0:T(8,128)(2,1)S(1)}, u32[]{:S(2)}, u32[]{:S(2)}) %collective-permute-start.17) | collective-permute-done | bytes 327712 | tf_op jit(solution)/shard_map/ppermute | solution.py:536
  86.1 2.1 %to_time.2.rest_0_ = bf16[320,1024]{1,0:T(8,128)(2,1)} custom-call(s32[2]{0:T(128)S(1)} %get-tuple-element.64.flag_ref, bf16[160,1024]{1,0:T(8,128)(2,1)S(1)} %add_convert_fusion.here_ref, bf16[160,1024]{1,0:T(8,128)(2,1)S(1)} %collective-permute-done.17.there_ref, bf16[1024,1024]{1,0:T(8,128)(2,1)S(1)} %get-tuple-element.26.refs_2_.basis_ref), custom_call_target="tpu_custom_call" | custom-call | flops 335544320 | bytes 2097152 | tf_op jit(solution)/shard_map/to_time/pallas_call | solution.py:340
  88.2 4.9 %collective-permute-done.15.there_ref = bf16[160,1024]{1,0:T(8,128)(2,1)S(1)} collective-permute-done((bf16[160,1024]{1,0:T(8,128)(2,1)S(1)}, bf16[160,1024]{1,0:T(8,128)(2,1)S(1)}, u32[]{:S(2)}, u32[]{:S(2)}) %collective-permute-start.15) | collective-permute-done | bytes 327712 | tf_op jit(solution)/shard_map/ppermute | solution.py:538
  93.1 2.1 %to_time.3 = bf16[320,1024]{1,0:T(8,128)(2,1)} custom-call(s32[2]{0:T(128)S(1)} %get-tuple-element.63.flag_ref, bf16[160,1024]{1,0:T(8,128)(2,1)S(1)} %add_convert_fusion.1.here_ref, bf16[160,1024]{1,0:T(8,128)(2,1)S(1)} %collective-permute-done.15.there_ref, ...), custom_call_target="tpu_custom_call", output_to_operand_aliasing={{}: (4, {})} | custom-call | flops 335544320 | bytes 2097152 | tf_op jit(solution)/shard_map/to_time/pallas_call | solution.py:340
  (19 shorter events, 0.2 us)
Async XLA Ops:
  0.0 3.0 %copy-start.2 = (bf16[320,1024]{1,0:T(8,128)(2,1)S(1)}, bf16[320,1024]{1,0:T(8,128)(2,1)}, u32[]{:S(2)}) copy-start(bf16[320,1024]{1,0:T(8,128)(2,1)} %param.4) | copy-start | bytes 1966084
  1.1 11.7 %copy-start.4 = (s32[1280]{0:T(1024)S(1)}, s32[1280]{0:T(1024)}, u32[]{:S(2)}) copy-start(s32[1280]{0:T(1024)} %param.6) | copy-start | bytes 15364
  1.1 11.7 %copy-start.3 = (s32[16,16]{1,0:T(8,128)S(1)}, s32[16,16]{1,0:T(8,128)}, u32[]{:S(2)}) copy-start(s32[16,16]{1,0:T(8,128)} %param.7) | copy-start | bytes 3076
  3.7 32.7 %collective-permute-start.1 = (bf16[160,1024]{1,0:T(8,128)(2,1)S(1)}, bf16[160,1024]{1,0:T(8,128)(2,1)S(1)}, u32[]{:S(2)}, u32[]{:S(2)}) collective-permute-start(bf16[160,1024]{1,0:T(8,128)(2,1)S(1)} %pad_maximum_fusion.2.refs_0_), channel_id=1, source_target_pairs={{0,4},{12,8},{1,5},{13,9},{2,6},{14,10},{3,7},{15,11},{16,20},{28,... | collective-permute-start | bytes 983048 | tf_op jit(solution)/shard_map/ppermute | solution.py:476
  8.7 15.1 %collective-permute-start = (bf16[160,1024]{1,0:T(8,128)(2,1)S(1)}, bf16[160,1024]{1,0:T(8,128)(2,1)}, u32[]{:S(2)}, u32[]{:S(2)}) collective-permute-start(bf16[160,1024]{1,0:T(8,128)(2,1)S(1)} %pad_maximum_fusion.refs_0_), channel_id=1, source_target_pairs={{0,4},{12,8},{1,5},{13,9},{2,6},{14,10},{3,7},{15,11},{16,20},{28,... | collective-permute-start | bytes 983048 | tf_op jit(solution)/shard_map/ppermute | solution.py:476
  10.7 22.6 %collective-permute-start.4 = (bf16[160,1024]{1,0:T(8,128)(2,1)S(1)}, bf16[160,1024]{1,0:T(8,128)(2,1)}, u32[]{:S(2)}, u32[]{:S(2)}) collective-permute-start(bf16[160,1024]{1,0:T(8,128)(2,1)S(1)} %pad_maximum_fusion.1.refs_1_), channel_id=1, source_target_pairs={{0,4},{12,8},{1,5},{13,9},{2,6},{14,10},{3,7},{15,11},{16,20},{28,... | collective-permute-start | bytes 983048 | tf_op jit(solution)/shard_map/ppermute | solution.py:476
  16.3 9.6 %copy-start = (bf16[80,1024]{1,0:T(8,128)(2,1)S(1)}, bf16[80,1024]{1,0:T(8,128)(2,1)}, u32[]{:S(2)}) copy-start(bf16[80,1024]{1,0:T(8,128)(2,1)} %get-tuple-element.43) | copy-start | bytes 491524
  16.3 9.6 %copy-start.1 = (bf16[80,1024]{1,0:T(8,128)(2,1)S(1)}, bf16[80,1024]{1,0:T(8,128)(2,1)}, u32[]{:S(2)}) copy-start(bf16[80,1024]{1,0:T(8,128)(2,1)} %get-tuple-element.40) | copy-start | bytes 491524
  25.2 11.1 %collective-permute-start.2 = (bf16[160,1024]{1,0:T(8,128)(2,1)S(1)}, bf16[160,1024]{1,0:T(8,128)(2,1)S(1)}, u32[]{:S(2)}, u32[]{:S(2)}) collective-permute-start(bf16[160,1024]{1,0:T(8,128)(2,1)S(1)} %spectra.4.refs_0_), channel_id=1, source_target_pairs={{4,8},{8,4},{5,9},{9,5},{6,10},{10,6},{7,11},{11,7},{20,24},{24,20... | collective-permute-start | bytes 983048 | tf_op jit(solution)/shard_map/ppermute | solution.py:515
  26.0 12.6 %collective-permute-start.5 = (bf16[160,1024]{1,0:T(8,128)(2,1)S(1)}, bf16[160,1024]{1,0:T(8,128)(2,1)S(1)}, u32[]{:S(2)}, u32[]{:S(2)}) collective-permute-start(bf16[160,1024]{1,0:T(8,128)(2,1)S(1)} %pad_maximum_fusion.3.refs_1_), channel_id=1, source_target_pairs={{0,4},{12,8},{1,5},{13,9},{2,6},{14,10},{3,7},{15,11},{16,20},{28,... | collective-permute-start | bytes 983048 | tf_op jit(solution)/shard_map/ppermute | solution.py:476
  34.8 3.8 %collective-permute-start.6 = (bf16[160,1024]{1,0:T(8,128)(2,1)S(1)}, bf16[160,1024]{1,0:T(8,128)(2,1)S(1)}, u32[]{:S(2)}, u32[]{:S(2)}) collective-permute-start(bf16[160,1024]{1,0:T(8,128)(2,1)S(1)} %spectra.6.refs_2_), channel_id=1, source_target_pairs={{4,8},{8,4},{5,9},{9,5},{6,10},{10,6},{7,11},{11,7},{20,24},{24,20... | collective-permute-start | bytes 983048 | tf_op jit(solution)/shard_map/ppermute | solution.py:515
  37.0 3.8 %collective-permute-start.8 = (bf16[160,1024]{1,0:T(8,128)(2,1)S(1)}, bf16[160,1024]{1,0:T(8,128)(2,1)S(1)}, u32[]{:S(2)}, u32[]{:S(2)}) collective-permute-start(bf16[160,1024]{1,0:T(8,128)(2,1)S(1)} %get-tuple-element.34.refs_4_.refs_0_.refs_2_), channel_id=1, source_target_pairs={{0,1},{1,0},{2,3},{3,2},{4,5},{5,4},{6,7},{7,6},{8,9},{9,8},{10,11... | collective-permute-start | bytes 983048 | tf_op jit(solution)/shard_map/ppermute | solution.py:23
  37.0 10.7 %collective-permute-start.10 = (bf16[160,1024]{1,0:T(8,128)(2,1)S(1)}, bf16[160,1024]{1,0:T(8,128)(2,1)S(1)}, u32[]{:S(2)}, u32[]{:S(2)}) collective-permute-start(bf16[160,1024]{1,0:T(8,128)(2,1)S(1)} %get-tuple-element.34.refs_4_.refs_0_.refs_2_), channel_id=1, source_target_pairs={{0,2},{2,0},{1,3},{3,1},{4,6},{6,4},{5,7},{7,5},{8,10},{10,8},{9,1... | collective-permute-start | bytes 983048 | tf_op jit(solution)/shard_map/ppermute | solution.py:23
  39.1 15.0 %collective-permute-start.11 = (bf16[160,1024]{1,0:T(8,128)(2,1)S(1)}, bf16[160,1024]{1,0:T(8,128)(2,1)S(1)}, u32[]{:S(2)}, u32[]{:S(2)}) collective-permute-start(bf16[160,1024]{1,0:T(8,128)(2,1)S(1)} %get-tuple-element.35.refs_5_.refs_1_.refs_3_), channel_id=1, source_target_pairs={{0,2},{2,0},{1,3},{3,1},{4,6},{6,4},{5,7},{7,5},{8,10},{10,8},{9,1... | collective-permute-start | bytes 983048 | tf_op jit(solution)/shard_map/ppermute | solution.py:23
  40.1 14.1 %collective-permute-start.9 = (bf16[160,1024]{1,0:T(8,128)(2,1)S(1)}, bf16[160,1024]{1,0:T(8,128)(2,1)S(1)}, u32[]{:S(2)}, u32[]{:S(2)}) collective-permute-start(bf16[160,1024]{1,0:T(8,128)(2,1)S(1)} %get-tuple-element.35.refs_5_.refs_1_.refs_3_), channel_id=1, source_target_pairs={{0,1},{1,0},{2,3},{3,2},{4,5},{5,4},{6,7},{7,6},{8,9},{9,8},{10,11... | collective-permute-start | bytes 983048 | tf_op jit(solution)/shard_map/ppermute | solution.py:23
  40.1 14.1 %collective-permute-start.3 = (bf16[160,1024]{1,0:T(8,128)(2,1)S(1)}, bf16[160,1024]{1,0:T(8,128)(2,1)S(1)}, u32[]{:S(2)}, u32[]{:S(2)}) collective-permute-start(bf16[160,1024]{1,0:T(8,128)(2,1)S(1)} %get-tuple-element.30), channel_id=1, source_target_pairs={{4,8},{8,4},{5,9},{9,5},{6,10},{10,6},{7,11},{11,7},{20,24},{24,20... | collective-permute-start | bytes 983048 | tf_op jit(solution)/shard_map/ppermute | solution.py:527
  40.8 13.4 %collective-permute-start.7 = (bf16[160,1024]{1,0:T(8,128)(2,1)S(1)}, bf16[160,1024]{1,0:T(8,128)(2,1)S(1)}, u32[]{:S(2)}, u32[]{:S(2)}) collective-permute-start(bf16[160,1024]{1,0:T(8,128)(2,1)S(1)} %get-tuple-element.33), channel_id=1, source_target_pairs={{4,8},{8,4},{5,9},{9,5},{6,10},{10,6},{7,11},{11,7},{20,24},{24,20... | collective-permute-start | bytes 983048 | tf_op jit(solution)/shard_map/ppermute | solution.py:527
  47.7 6.5 %collective-permute-start.12 = (bf16[160,1024]{1,0:T(8,128)(2,1)S(1)}, bf16[160,1024]{1,0:T(8,128)(2,1)S(1)}, u32[]{:S(2)}, u32[]{:S(2)}) collective-permute-start(bf16[160,1024]{1,0:T(8,128)(2,1)S(1)} %collective-permute-done.10.refs_8_.refs_6_), channel_id=1, source_target_pairs={{0,1},{1,0},{2,3},{3,2},{4,5},{5,4},{6,7},{7,6},{8,9},{9,8},{10,11... | collective-permute-start | bytes 983048 | tf_op jit(solution)/shard_map/ppermute | solution.py:23
  54.2 1.6 %collective-permute-start.13 = (bf16[160,1024]{1,0:T(8,128)(2,1)S(1)}, bf16[160,1024]{1,0:T(8,128)(2,1)S(1)}, u32[]{:S(2)}, u32[]{:S(2)}) collective-permute-start(bf16[160,1024]{1,0:T(8,128)(2,1)S(1)} %collective-permute-done.11.refs_9_.refs_7_), channel_id=1, source_target_pairs={{0,1},{1,0},{2,3},{3,2},{4,5},{5,4},{6,7},{7,6},{8,9},{9,8},{10,11... | collective-permute-start | bytes 983048 | tf_op jit(solution)/shard_map/ppermute | solution.py:23
  57.3 2.8 %collective-permute-start.16 = (bf16[160,1024]{1,0:T(8,128)(2,1)S(1)}, bf16[160,1024]{1,0:T(8,128)(2,1)S(1)}, u32[]{:S(2)}, u32[]{:S(2)}) collective-permute-start(bf16[160,1024]{1,0:T(8,128)(2,1)S(1)} %couple.2), channel_id=1, source_target_pairs={{4,8},{8,4},{5,9},{9,5},{6,10},{10,6},{7,11},{11,7},{20,24},{24,20... | collective-permute-start | bytes 983048 | tf_op jit(solution)/shard_map/ppermute | solution.py:531
  59.4 2.1 %collective-permute-start.14 = (bf16[160,1024]{1,0:T(8,128)(2,1)S(1)}, bf16[160,1024]{1,0:T(8,128)(2,1)S(1)}, u32[]{:S(2)}, u32[]{:S(2)}) collective-permute-start(bf16[160,1024]{1,0:T(8,128)(2,1)S(1)} %couple.3), channel_id=1, source_target_pairs={{4,8},{8,4},{5,9},{9,5},{6,10},{10,6},{7,11},{11,7},{20,24},{24,20... | collective-permute-start | bytes 983048 | tf_op jit(solution)/shard_map/ppermute | solution.py:533
  60.2 25.9 %collective-permute-start.17 = (bf16[160,1024]{1,0:T(8,128)(2,1)S(1)}, bf16[160,1024]{1,0:T(8,128)(2,1)S(1)}, u32[]{:S(2)}, u32[]{:S(2)}) collective-permute-start(bf16[160,1024]{1,0:T(8,128)(2,1)S(1)} %add_convert_fusion.here_ref), channel_id=1, source_target_pairs={{4,0},{8,12},{5,1},{9,13},{6,2},{10,14},{7,3},{11,15},{20,16},{24,... | collective-permute-start | bytes 983048 | tf_op jit(solution)/shard_map/ppermute | solution.py:536
  61.6 31.5 %collective-permute-start.15 = (bf16[160,1024]{1,0:T(8,128)(2,1)S(1)}, bf16[160,1024]{1,0:T(8,128)(2,1)S(1)}, u32[]{:S(2)}, u32[]{:S(2)}) collective-permute-start(bf16[160,1024]{1,0:T(8,128)(2,1)S(1)} %add_convert_fusion.1.here_ref), channel_id=1, source_target_pairs={{4,0},{8,12},{5,1},{9,13},{6,2},{10,14},{7,3},{11,15},{20,16},{24,... | collective-permute-start | bytes 983048 | tf_op jit(solution)/shard_map/ppermute | solution.py:538

commit v9 on v8

--- a/solution.py
+++ b/solution.py
@@ -15,6 +15,7 @@
 
 epsilon = 1e-06
 CONTRACT_LAST = (((1,), (1,)), ((), ()))
+VMEM = pl.BlockSpec(memory_space=pltpu.VMEM)
 
 
 def shift(value, axis, steps):
@@ -240,7 +241,7 @@
     return rate, jnp.sum(jnp.square(rate.astype(jnp.float32)), axis=1, keepdims=True)
 
 
-def couple_kernel(piece, row_count, col_count, *refs):
+def couple_kernel(piece, row_count, col_count, before, *refs):
     row_refs = refs[:row_count]
     col_refs = refs[row_count : row_count + col_count]
     gain_ref, weight_ref, out_ref = refs[-3:]
@@ -294,19 +295,20 @@
         ],
         axis=0,
     )
-    out_ref[...] = jnp.dot(
-        coupling, col_model, preferred_element_type=jnp.float32
-    ).astype(out_ref.dtype)
-
-
-def couple(rows, cols, gains, weights, piece):
-    args = [*rows, *cols, gains, weights]
+    update = jnp.dot(coupling, col_model, preferred_element_type=jnp.float32)
+    if before:
+        update = update + refs[row_count + col_count][...]
+    out_ref[...] = update.astype(out_ref.dtype)
+
+
+def couple(rows, cols, gains, weights, piece, before=None, kind=jnp.bfloat16):
+    args = [*rows, *cols] + ([] if before is None else [before]) + [gains, weights]
     height, width = gains.shape[1], weights.shape[1]
     return pl.pallas_call(
-        functools.partial(couple_kernel, piece, len(rows), len(cols)),
-        in_specs=[pl.BlockSpec(memory_space=pltpu.VMEM)] * len(args),
-        out_specs=pl.BlockSpec(memory_space=pltpu.VMEM),
-        out_shape=jax.ShapeDtypeStruct((height, 2 * NF), jnp.bfloat16),
+        functools.partial(couple_kernel, piece, len(rows), len(cols), before is not None),
+        in_specs=[VMEM] * len(args),
+        out_specs=VMEM,
+        out_shape=jax.ShapeDtypeStruct((height, 2 * NF), kind),
         compiler_params=pltpu.CompilerParams(vmem_limit_bytes=16 << 20),
         cost_estimate=pl.CostEstimate(
             flops=12 * height * width * NF,
@@ -353,9 +355,6 @@
         compiler_params=pltpu.CompilerParams(vmem_limit_bytes=12 << 20),
         name="to_time",
     )(jnp.stack([place, is_inner.astype(jnp.int32)]).astype(jnp.int32), *args)
-
-
-VMEM = pl.BlockSpec(memory_space=pltpu.VMEM)
 
 
 def two_bases_kernel(per_step, low_rows, *refs):
@@ -477,12 +476,14 @@
 
     member = sub * pairs + pair
     hops = [(s, q) for s in range(subs) for q in range(pairs)]
-    halves = [
-        ((sub - s) % subs * pairs + (pair - q) % pairs) * 2 * half + side * half for s, q in hops
+    starts = [
+        ((sub - s) % subs * pairs + (pair - q) % pairs) * 2 * half + side * half + at
+        for at in range(0, half, piece)
+        for s, q in hops
     ]
     gains = station_weights.astype(jnp.float32)
     col_gains = jnp.concatenate(
-        [lax.dynamic_slice_in_dim(gains, start, half, 0) for start in halves]
+        [lax.dynamic_slice_in_dim(gains, start, piece, 0) for start in starts]
     )[None, :]
     firsts = [member * 2 * half + which * half for which in (side, 1 - side)]
     own_gains, other_gains = [
@@ -492,18 +493,18 @@
     link_rows = jnp.concatenate(
         [lax.dynamic_slice_in_dim(link, start // piece, per_half, 0) for start in firsts], axis=0
     )
-    col_pieces = jnp.concatenate(
-        [start + jnp.arange(half, dtype=jnp.int32) for start in halves]
-    ) // piece
+    col_pieces = jnp.repeat(jnp.stack(starts) // piece, piece)
     chosen = jnp.arange(link.shape[0], dtype=jnp.int32)[:, None] == col_pieces[None, :]
     active = jnp.dot(
         link_rows, chosen.astype(jnp.float32), preferred_element_type=jnp.float32
     )
     weights = 4.0 / math.sqrt(stations) * col_gains * active
-    here, own_gains, other_gains, weights = lax.optimization_barrier(
-        (level, own_gains, other_gains, weights)
-    )
-    own_weights, other_weights = weights[:per_half], weights[per_half:]
+    late = (subs - 1) * pairs
+    early_width = (len(starts) - late) * piece
+    own_early, own_late = weights[:per_half, :early_width], weights[:per_half, early_width:]
+    here, own_gains, other_gains, own_early, own_late, other_weights = lax.optimization_barrier(
+        (level, own_gains, other_gains, own_early, own_late, weights[per_half:])
+    )
 
     here_basis, near_basis = two_bases(here * span, (here ^ 1) * span, span)
     passed_parts = own_parts(passed, here_basis)
@@ -525,21 +526,24 @@
             else:
                 cols[s, q, place] = shift(cols[s, 0, place], "pair", q)
         passed_rest.append(lax.ppermute(summed, "blk", swapped))
-    cols = [cols[s, q, place] for s, q in hops for place in range(per_half)]
+    cols = [cols[s, q, place] for place in range(per_half) for s, q in hops]
+    begun = couple(own, cols[:-late], own_gains, own_early, piece, None, jnp.float32)
+    own_part = couple(own, cols[-late:], own_gains, own_late, piece, begun)
+    other_rest = lax.ppermute(own_part, "blk", swapped)
     other = [block for both in zip(to_pass, passed_rest) for block in both]
     other_part = couple(other, cols, other_gains, other_weights, piece)
     own_rest = lax.ppermute(other_part, "blk", swapped)
-    own_part = couple(own, cols, own_gains, own_weights, piece)
-    other_rest = lax.ppermute(own_part, "blk", swapped)
     widen = lambda a: a.astype(jnp.float32)
+    other_adjoint = (widen(other_part) + widen(other_rest)).astype(jnp.bfloat16)
+    near_other = lax.ppermute(other_adjoint, "blk", outward)
     own_adjoint = (widen(own_part) + widen(own_rest)).astype(jnp.bfloat16)
     near_own = lax.ppermute(own_adjoint, "blk", outward)
-    other_adjoint = (widen(other_part) + widen(other_rest)).astype(jnp.bfloat16)
-    near_other = lax.ppermute(other_adjoint, "blk", outward)
     is_inner = (level == 1) | (level == 2)
     rows = synthetic.shape[0]
-    traces = to_time(side, is_inner, own_adjoint, near_own, here_basis, span, rows, None)
-    return to_time(1 - side, is_inner, other_adjoint, near_other, here_basis, span, rows, traces)
+    traces = to_time(
+        1 - side, is_inner, other_adjoint, near_other, here_basis, span, rows, None
+    )
+    return to_time(side, is_inner, own_adjoint, near_own, here_basis, span, rows, traces)
 
 
 def shards(*args):

time: 95.6 us -> 97 us (1.015)
  waiting for transfers between devices: 49.7 us -> 52.1 us
  starting transfers between devices: 25.6 us -> 23.8 us
    ppermute x1, waiting for transfers between devices: 4.91 us -> 30.9 us  [inner_body(): near_other = lax.ppermute(other_adjoint, 'blk', outward)]
    ppermute x1, waiting for transfers between devices: 23 us -> 4.92 us  [inner_body(): near_own = lax.ppermute(own_adjoint, 'blk', outward)]
    ppermute x6, waiting for transfers between devices: 14.3 us -> 10.6 us  [shift(): return lax.ppermute(value, axis, pairs)]
    ppermute x4, starting transfers between devices: 16.4 us -> 13.8 us  [inner_body(): arrived.append(lax.ppermute(block, 'blk', inward))]
    ppermute x4, waiting for transfers between devices: 7.42 us -> 5.58 us  [inner_body(): arrived.append(lax.ppermute(block, 'blk', inward))]
    pallas_call x2 -> x3, Pallas kernels: 2.89 us -> 3.37 us  [couple(): pl.pallas_call(functools.partial(couple_kernel, piece, len(rows), len(col...]
  transfers between devices with their start and end apart: 18 -> 18, of which waited for: 6 -> 5; matrix products, arithmetic and copies ran while one was open for 2% -> 5% of each run, Pallas kernels for 11% -> 13%
where the time goes in v9:
time: 97 us; the launch traced here: 96.6 us
  waiting for transfers between devices  52.1 us (54%)
  starting transfers between devices  23.8 us (25%)
  Pallas kernels  14.5 us (15%)
  local copies, waits for them, and re-layouts  4.27 us (4%)
  other arithmetic  1.28 us (1%)
    ppermute x1, waiting for transfers between devices, inner_body(): near_other = lax.ppermute(other_adjoint, 'blk', outward)  30.9 us
    ppermute x4, starting transfers between devices, inner_body(): arrived.append(lax.ppermute(block, 'blk', inward))  13.8 us
    ppermute x6, waiting for transfers between devices, shift(): return lax.ppermute(value, axis, pairs)  10.6 us
    ppermute x4, waiting for transfers between devices, inner_body(): arrived.append(lax.ppermute(block, 'blk', inward))  5.58 us
    ppermute x1, waiting for transfers between devices, inner_body(): near_own = lax.ppermute(own_adjoint, 'blk', outward)  4.92 us
    pallas_call x2, Pallas kernels, to_time(): pl.pallas_call(to_time_kernel, grid_spec=pltpu.PrefetchScalarGridSpec(num...  4.21 us
    pallas_call x4, Pallas kernels, spectra(): pl.pallas_call(sum_kernel, in_specs=[VMEM] * len(args), out_specs=[VMEM]...  4.06 us
    dynamic_slice x3, local copies, waits for them, and re-layouts, piece_of(): lax.dynamic_slice_in_dim(source, which * half + at, piece, 0)  3.56 us
  transfers between devices with their start and end apart: 18, of which 5 were waited for; matrix products, arithmetic and copies ran while one was open for 5% of the time, Pallas kernels for 13%

profile of v9, /device:TPU:0, one launch (start us, length us, event | category | flops | bytes accessed | tf_op | source)
XLA Modules:
  0.0 96.6 jit_solution(1037283552938194107)
XLA Ops:
  0.0 1.1 %constant_dynamic-slice_fusion.8 = (bf16[80,1024]{1,0:T(8,128)(2,1)S(1)}, bf16[80,1024]{1,0:T(8,128)(2,1)S(1)}) fusion(bf16[320,1024]{1,0:T(8,128)(2,1)} %param.5, s32[]{:T(128)S(6)} %select_n.129, bf16[320,1024]{1,0:T(8,128)(2,1)} %param.4), kind=kLoop, calls=%fused_computation.50 | loop fusion | bytes 655364 | tf_op jit(solution)/shard_map/dynamic_slice | solution.py:461
  1.1 0.0 copy-start.4
  1.1 0.0 copy-start.3
  1.1 5.0 %collective-permute-start.1 = (bf16[160,1024]{1,0:T(8,128)(2,1)S(1)}, bf16[160,1024]{1,0:T(8,128)(2,1)S(1)}, u32[]{:S(2)}, u32[]{:S(2)}) collective-permute-start(bf16[160,1024]{1,0:T(8,128)(2,1)S(1)} %pad_maximum_fusion.refs_0_), channel_id=1, source_target_pairs={{0,4},{12,8},{1,5},{13,9},{2,6},{14,10},{3,7},{15,11},{16,20},{28,... | collective-permute-start | bytes 983048 | tf_op jit(solution)/shard_map/ppermute | solution.py:475
  6.2 1.8 %constant_dynamic-slice_fusion.5 = (bf16[80,1024]{1,0:T(8,128)(2,1)}, bf16[80,1024]{1,0:T(8,128)(2,1)S(1)}, bf16[80,1024]{1,0:T(8,128)(2,1)S(1)}) fusion(bf16[320,1024]{1,0:T(8,128)(2,1)} %param.4, s32[]{:T(128)S(6)} %select_n.131, s32[]{:T(128)S(6)} %select_n.154, s32[]{:T(128)S(6)} %select_n.130), kind=kLoop, calls=%fused_computation.47 | loop fusion | bytes 983052 | tf_op jit(solution)/shard_map/dynamic_slice | solution.py:461
  7.9 0.7 constant_dynamic-slice_fusion.4
  8.7 2.0 %collective-permute-start = (bf16[160,1024]{1,0:T(8,128)(2,1)S(1)}, bf16[160,1024]{1,0:T(8,128)(2,1)}, u32[]{:S(2)}, u32[]{:S(2)}) collective-permute-start(bf16[160,1024]{1,0:T(8,128)(2,1)S(1)} %pad_maximum_fusion.1.refs_0_), channel_id=1, source_target_pairs={{0,4},{12,8},{1,5},{13,9},{2,6},{14,10},{3,7},{15,11},{16,20},{28,... | collective-permute-start | bytes 983048 | tf_op jit(solution)/shard_map/ppermute | solution.py:475
  10.7 2.0 %collective-permute-start.4 = (bf16[160,1024]{1,0:T(8,128)(2,1)S(1)}, bf16[160,1024]{1,0:T(8,128)(2,1)}, u32[]{:S(2)}, u32[]{:S(2)}) collective-permute-start(bf16[160,1024]{1,0:T(8,128)(2,1)S(1)} %pad_maximum_fusion.3.refs_1_), channel_id=1, source_target_pairs={{0,4},{12,8},{1,5},{13,9},{2,6},{14,10},{3,7},{15,11},{16,20},{28,... | collective-permute-start | bytes 983048 | tf_op jit(solution)/shard_map/ppermute | solution.py:475
  12.7 0.1 stack.58
  12.8 0.1 broadcast_in_dim.8
  12.9 0.1 eq.46
  13.0 0.1 fusion.26
  13.2 0.1 concatenate.25
  13.3 0.1 copy.6
  13.4 0.1 convolution_multiply_fusion
  13.5 0.1 slice.13.refs_6_
  13.6 0.1 fusion.27
  13.7 0.5 fusion.6
  14.2 0.3 fusion.15
  14.6 1.2 %two_bases.1 = (bf16[1024,1024]{1,0:T(8,128)(2,1)S(1)}, bf16[1024,1024]{1,0:T(8,128)(2,1)S(1)}) custom-call(f32[16,512]{1,0:T(8,128)S(1)} %get-tuple-element.67.refs_0_, f32[16,512]{1,0:T(8,128)S(1)} %get-tuple-element.68.refs_1_, f32[16,512]{1,0:T(8,128)S(1)} %get-tuple-element.62.refs_2_, f32[16,512]{1,0:T(8,128)S(1)} %get-tuple-element.61.refs_3_, ...), custom_call_target="tpu_custom_call" | custom-call | flops 8388608 | bytes 4194304 | tf_op jit(solution)/shard_map/two_bases/pallas_call | solution.py:374
  15.8 0.8 own_parts.3
  16.6 0.0 copy-start.1
  16.6 0.0 collective-permute-done.1.near_ref
  16.7 0.5 spectra.4.refs_0_
  17.2 0.7 collective-permute-start.2
  17.9 4.7 %collective-permute-start.3 = (bf16[160,1024]{1,0:T(8,128)(2,1)S(1)}, bf16[160,1024]{1,0:T(8,128)(2,1)S(1)}, u32[]{:S(2)}, u32[]{:S(2)}) collective-permute-start(bf16[160,1024]{1,0:T(8,128)(2,1)S(1)} %pad_maximum_fusion.2.refs_1_), channel_id=1, source_target_pairs={{0,4},{12,8},{1,5},{13,9},{2,6},{14,10},{3,7},{15,11},{16,20},{28,... | collective-permute-start | bytes 983048 | tf_op jit(solution)/shard_map/ppermute | solution.py:475
  22.7 5.6 %collective-permute-done.4.near_ref = bf16[160,1024]{1,0:T(8,128)(2,1)} collective-permute-done((bf16[160,1024]{1,0:T(8,128)(2,1)S(1)}, bf16[160,1024]{1,0:T(8,128)(2,1)}, u32[]{:S(2)}, u32[]{:S(2)}) %collective-permute-start.4) | collective-permute-done | bytes 327712 | tf_op jit(solution)/shard_map/ppermute | solution.py:475
  28.2 1.5 %spectra.6.refs_2_ = bf16[160,1024]{1,0:T(8,128)(2,1)S(1)} custom-call(f32[160,1024]{1,0:T(8,128)S(1)} %get-tuple-element.34.part_ref, bf16[160,1024]{1,0:T(8,128)(2,1)} %collective-permute-done.4.near_ref, bf16[1024,1024]{1,0:T(8,128)(2,1)S(1)} %get-tuple-element.29.basis_ref), custom_call_target="tpu_custom_call" | custom-call | flops 335544320 | bytes 2097152 | tf_op jit(solution)/shard_map/spectra/pallas_call | solution.py:430
  29.7 0.7 collective-permute-start.5
  30.4 0.9 own_parts.2
  31.3 0.0 collective-permute-done.near_ref
  31.3 0.0 collective-permute-done.2.rest_0_
  31.3 1.5 %spectra.5 = (bf16[160,1024]{1,0:T(8,128)(2,1)S(1)}, bf16[160,1024]{1,0:T(8,128)(2,1)S(1)}) custom-call(f32[160,1024]{1,0:T(8,128)S(1)} %get-tuple-element.28.part_ref, bf16[160,1024]{1,0:T(8,128)(2,1)} %collective-permute-done.near_ref, bf16[1024,1024]{1,0:T(8,128)(2,1)S(1)} %get-tuple-element.29.basis_ref, bf16[160,1024]{1,0:T(8,128)(2,1)S(1)} %collective-permute-done.2.rest_0_), custom_call_target="tpu_custom_call" | custom-call | flops 335544320 | bytes 2097152 | tf_op jit(solution)/shard_map/spectra/pallas_call | solution.py:430
  32.8 1.6 %collective-permute-start.9 = (bf16[160,1024]{1,0:T(8,128)(2,1)S(1)}, bf16[160,1024]{1,0:T(8,128)(2,1)S(1)}, u32[]{:S(2)}, u32[]{:S(2)}) collective-permute-start(bf16[160,1024]{1,0:T(8,128)(2,1)S(1)} %get-tuple-element.32.refs_0_.refs_2_.refs_4_), channel_id=1, source_target_pairs={{0,2},{2,0},{1,3},{3,1},{4,6},{6,4},{5,7},{7,5},{8,10},{10,8},{9,1... | collective-permute-start | bytes 983048 | tf_op jit(solution)/shard_map/ppermute | solution.py:24
  34.4 0.0 collective-permute-done.3.near_ref
  34.4 0.0 collective-permute-done.5.rest_0_
  34.4 0.5 spectra.7
  34.9 1.3 %collective-permute-start.6 = (bf16[160,1024]{1,0:T(8,128)(2,1)S(1)}, bf16[160,1024]{1,0:T(8,128)(2,1)S(1)}, u32[]{:S(2)}, u32[]{:S(2)}) collective-permute-start(bf16[160,1024]{1,0:T(8,128)(2,1)S(1)} %get-tuple-element.35.refs_1_.refs_6_.refs_8_), channel_id=1, source_target_pairs={{0,2},{2,0},{1,3},{3,1},{4,6},{6,4},{5,7},{7,5},{8,10},{10,8},{9,1... | collective-permute-start | bytes 983048 | tf_op jit(solution)/shard_map/ppermute | solution.py:24
  36.2 0.0 collective-permute-start.8
  36.2 0.5 collective-permute-start.11
  36.7 6.7 %collective-permute-done.9.refs_4_.refs_6_ = bf16[160,1024]{1,0:T(8,128)(2,1)S(1)} collective-permute-done((bf16[160,1024]{1,0:T(8,128)(2,1)S(1)}, bf16[160,1024]{1,0:T(8,128)(2,1)S(1)}, u32[]{:S(2)}, u32[]{:S(2)}) %collective-permute-start.9) | collective-permute-done | bytes 327712 | tf_op jit(solution)/shard_map/ppermute | solution.py:24
  43.5 0.0 collective-permute-start.10
  43.5 3.9 %collective-permute-done.6.refs_2_.refs_10_ = bf16[160,1024]{1,0:T(8,128)(2,1)S(1)} collective-permute-done((bf16[160,1024]{1,0:T(8,128)(2,1)S(1)}, bf16[160,1024]{1,0:T(8,128)(2,1)S(1)}, u32[]{:S(2)}, u32[]{:S(2)}) %collective-permute-start.6) | collective-permute-done | bytes 327712 | tf_op jit(solution)/shard_map/ppermute | solution.py:24
  47.4 0.0 collective-permute-start.7
  47.4 0.7 collective-permute-start.12
  48.1 0.7 collective-permute-start.13
  48.8 0.0 collective-permute-done.10.refs_5_.refs_7_
  48.8 1.2 %couple.3.refs_4_ = f32[160,1024]{1,0:T(8,128)S(1)} custom-call(bf16[160,1024]{1,0:T(8,128)(2,1)S(1)} %get-tuple-element.32.refs_0_.refs_2_.refs_4_, bf16[160,1024]{1,0:T(8,128)(2,1)S(1)} %get-tuple-element.35.refs_1_.refs_6_.refs_8_, bf16[160,1024]{1,0:T(8,128)(2,1)S(1)} %get-tuple-element.32.refs_0_.refs_2_.refs_4_, ...), custom_call_target="tpu_custom_call" | custom-call | flops 471859200 | bytes 2621440 | tf_op jit(solution)/shard_map/couple/pallas_call | solution.py:307
  50.0 0.7 couple.4
  50.7 0.7 collective-permute-start.16
  51.4 0.0 collective-permute-done.13.refs_3_
  51.4 1.5 %couple.5 = bf16[160,1024]{1,0:T(8,128)(2,1)S(1)} custom-call(bf16[160,1024]{1,0:T(8,128)(2,1)S(1)} %spectra.4.refs_0_, bf16[160,1024]{1,0:T(8,128)(2,1)S(1)} %collective-permute-done.12.refs_1_, bf16[160,1024]{1,0:T(8,128)(2,1)S(1)} %spectra.6.refs_2_, bf16[160,1024]{1,0:T(8,128)(2,1)S(1)} %collective-permute-done.13.refs_3_, ...), custom_call_target="tpu_custom_call" | custom-call | flops 629145600 | bytes 3276800 | tf_op jit(solution)/shard_map/couple/pallas_call | solution.py:307
  52.9 0.7 collective-permute-start.14
  53.6 0.0 collective-permute-done.16
  53.6 0.1 add_convert_fusion.here_ref
  53.7 1.3 %collective-permute-start.17 = (bf16[160,1024]{1,0:T(8,128)(2,1)S(1)}, bf16[160,1024]{1,0:T(8,128)(2,1)S(1)}, u32[]{:S(2)}, u32[]{:S(2)}) collective-permute-start(bf16[160,1024]{1,0:T(8,128)(2,1)S(1)} %add_convert_fusion.here_ref), channel_id=1, source_target_pairs={{4,0},{8,12},{5,1},{9,13},{6,2},{10,14},{7,3},{11,15},{20,16},{24,... | collective-permute-start | bytes 983048 | tf_op jit(solution)/shard_map/ppermute | solution.py:538
  55.0 0.0 collective-permute-done.14
  55.0 0.1 add_convert_fusion.1.here_ref
  55.1 1.3 %collective-permute-start.15 = (bf16[160,1024]{1,0:T(8,128)(2,1)S(1)}, bf16[160,1024]{1,0:T(8,128)(2,1)S(1)}, u32[]{:S(2)}, u32[]{:S(2)}) collective-permute-start(bf16[160,1024]{1,0:T(8,128)(2,1)S(1)} %add_convert_fusion.1.here_ref), channel_id=1, source_target_pairs={{4,0},{8,12},{5,1},{9,13},{6,2},{10,14},{7,3},{11,15},{20,16},{24,... | collective-permute-start | bytes 983048 | tf_op jit(solution)/shard_map/ppermute | solution.py:540
  56.4 0.1 pad_add_fusion
  56.5 30.9 %collective-permute-done.17.there_ref = bf16[160,1024]{1,0:T(8,128)(2,1)S(1)} collective-permute-done((bf16[160,1024]{1,0:T(8,128)(2,1)S(1)}, bf16[160,1024]{1,0:T(8,128)(2,1)S(1)}, u32[]{:S(2)}, u32[]{:S(2)}) %collective-permute-start.17) | collective-permute-done | bytes 327712 | tf_op jit(solution)/shard_map/ppermute | solution.py:538
  87.4 2.1 %to_time.2.rest_0_ = bf16[320,1024]{1,0:T(8,128)(2,1)} custom-call(s32[2]{0:T(128)S(1)} %get-tuple-element.70.flag_ref, bf16[160,1024]{1,0:T(8,128)(2,1)S(1)} %add_convert_fusion.here_ref, bf16[160,1024]{1,0:T(8,128)(2,1)S(1)} %collective-permute-done.17.there_ref, bf16[1024,1024]{1,0:T(8,128)(2,1)S(1)} %get-tuple-element.27.refs_2_.basis_ref), custom_call_target="tpu_custom_call" | custom-call | flops 335544320 | bytes 2097152 | tf_op jit(solution)/shard_map/to_time/pallas_call | solution.py:342
  89.5 4.9 %collective-permute-done.15.there_ref = bf16[160,1024]{1,0:T(8,128)(2,1)S(1)} collective-permute-done((bf16[160,1024]{1,0:T(8,128)(2,1)S(1)}, bf16[160,1024]{1,0:T(8,128)(2,1)S(1)}, u32[]{:S(2)}, u32[]{:S(2)}) %collective-permute-start.15) | collective-permute-done | bytes 327712 | tf_op jit(solution)/shard_map/ppermute | solution.py:540
  94.5 2.1 %to_time.3 = bf16[320,1024]{1,0:T(8,128)(2,1)} custom-call(s32[2]{0:T(128)S(1)} %get-tuple-element.69.flag_ref, bf16[160,1024]{1,0:T(8,128)(2,1)S(1)} %add_convert_fusion.1.here_ref, bf16[160,1024]{1,0:T(8,128)(2,1)S(1)} %collective-permute-done.15.there_ref, ...), custom_call_target="tpu_custom_call", output_to_operand_aliasing={{}: (4, {})} | custom-call | flops 335544320 | bytes 2097152 | tf_op jit(solution)/shard_map/to_time/pallas_call | solution.py:342
  (24 shorter events, 0.2 us)
Async XLA Ops:
  0.0 7.9 %copy-start.2 = (bf16[320,1024]{1,0:T(8,128)(2,1)S(1)}, bf16[320,1024]{1,0:T(8,128)(2,1)}, u32[]{:S(2)}) copy-start(bf16[320,1024]{1,0:T(8,128)(2,1)} %param.5) | copy-start | bytes 1966084
  1.1 11.9 %copy-start.4 = (s32[1280]{0:T(1024)S(1)}, s32[1280]{0:T(1024)}, u32[]{:S(2)}) copy-start(s32[1280]{0:T(1024)} %param.6) | copy-start | bytes 15364
  1.1 12.2 %copy-start.3 = (s32[16,16]{1,0:T(8,128)S(1)}, s32[16,16]{1,0:T(8,128)}, u32[]{:S(2)}) copy-start(s32[16,16]{1,0:T(8,128)} %param.7) | copy-start | bytes 3076
  1.1 15.5 %collective-permute-start.1 = (bf16[160,1024]{1,0:T(8,128)(2,1)S(1)}, bf16[160,1024]{1,0:T(8,128)(2,1)S(1)}, u32[]{:S(2)}, u32[]{:S(2)}) collective-permute-start(bf16[160,1024]{1,0:T(8,128)(2,1)S(1)} %pad_maximum_fusion.refs_0_), channel_id=1, source_target_pairs={{0,4},{12,8},{1,5},{13,9},{2,6},{14,10},{3,7},{15,11},{16,20},{28,... | collective-permute-start | bytes 983048 | tf_op jit(solution)/shard_map/ppermute | solution.py:475
  8.7 22.6 %collective-permute-start = (bf16[160,1024]{1,0:T(8,128)(2,1)S(1)}, bf16[160,1024]{1,0:T(8,128)(2,1)}, u32[]{:S(2)}, u32[]{:S(2)}) collective-permute-start(bf16[160,1024]{1,0:T(8,128)(2,1)S(1)} %pad_maximum_fusion.1.refs_0_), channel_id=1, source_target_pairs={{0,4},{12,8},{1,5},{13,9},{2,6},{14,10},{3,7},{15,11},{16,20},{28,... | collective-permute-start | bytes 983048 | tf_op jit(solution)/shard_map/ppermute | solution.py:475
  10.7 17.5 %collective-permute-start.4 = (bf16[160,1024]{1,0:T(8,128)(2,1)S(1)}, bf16[160,1024]{1,0:T(8,128)(2,1)}, u32[]{:S(2)}, u32[]{:S(2)}) collective-permute-start(bf16[160,1024]{1,0:T(8,128)(2,1)S(1)} %pad_maximum_fusion.3.refs_1_), channel_id=1, source_target_pairs={{0,4},{12,8},{1,5},{13,9},{2,6},{14,10},{3,7},{15,11},{16,20},{28,... | collective-permute-start | bytes 983048 | tf_op jit(solution)/shard_map/ppermute | solution.py:475
  16.6 1.2 %copy-start = (bf16[80,1024]{1,0:T(8,128)(2,1)S(1)}, bf16[80,1024]{1,0:T(8,128)(2,1)}, u32[]{:S(2)}) copy-start(bf16[80,1024]{1,0:T(8,128)(2,1)} %get-tuple-element.43) | copy-start | bytes 491524
  16.6 1.2 %copy-start.1 = (bf16[80,1024]{1,0:T(8,128)(2,1)S(1)}, bf16[80,1024]{1,0:T(8,128)(2,1)}, u32[]{:S(2)}) copy-start(bf16[80,1024]{1,0:T(8,128)(2,1)} %get-tuple-element.46) | copy-start | bytes 491524
  17.2 14.1 %collective-permute-start.2 = (bf16[160,1024]{1,0:T(8,128)(2,1)S(1)}, bf16[160,1024]{1,0:T(8,128)(2,1)S(1)}, u32[]{:S(2)}, u32[]{:S(2)}) collective-permute-start(bf16[160,1024]{1,0:T(8,128)(2,1)S(1)} %spectra.4.refs_0_), channel_id=1, source_target_pairs={{4,8},{8,4},{5,9},{9,5},{6,10},{10,6},{7,11},{11,7},{20,24},{24,20... | collective-permute-start | bytes 983048 | tf_op jit(solution)/shard_map/ppermute | solution.py:516
  17.9 16.5 %collective-permute-start.3 = (bf16[160,1024]{1,0:T(8,128)(2,1)S(1)}, bf16[160,1024]{1,0:T(8,128)(2,1)S(1)}, u32[]{:S(2)}, u32[]{:S(2)}) collective-permute-start(bf16[160,1024]{1,0:T(8,128)(2,1)S(1)} %pad_maximum_fusion.2.refs_1_), channel_id=1, source_target_pairs={{0,4},{12,8},{1,5},{13,9},{2,6},{14,10},{3,7},{15,11},{16,20},{28,... | collective-permute-start | bytes 983048 | tf_op jit(solution)/shard_map/ppermute | solution.py:475
  29.7 4.7 %collective-permute-start.5 = (bf16[160,1024]{1,0:T(8,128)(2,1)S(1)}, bf16[160,1024]{1,0:T(8,128)(2,1)S(1)}, u32[]{:S(2)}, u32[]{:S(2)}) collective-permute-start(bf16[160,1024]{1,0:T(8,128)(2,1)S(1)} %spectra.6.refs_2_), channel_id=1, source_target_pairs={{4,8},{8,4},{5,9},{9,5},{6,10},{10,6},{7,11},{11,7},{20,24},{24,20... | collective-permute-start | bytes 983048 | tf_op jit(solution)/shard_map/ppermute | solution.py:516
  32.8 10.6 %collective-permute-start.9 = (bf16[160,1024]{1,0:T(8,128)(2,1)S(1)}, bf16[160,1024]{1,0:T(8,128)(2,1)S(1)}, u32[]{:S(2)}, u32[]{:S(2)}) collective-permute-start(bf16[160,1024]{1,0:T(8,128)(2,1)S(1)} %get-tuple-element.32.refs_0_.refs_2_.refs_4_), channel_id=1, source_target_pairs={{0,2},{2,0},{1,3},{3,1},{4,6},{6,4},{5,7},{7,5},{8,10},{10,8},{9,1... | collective-permute-start | bytes 983048 | tf_op jit(solution)/shard_map/ppermute | solution.py:24
  34.9 12.4 %collective-permute-start.6 = (bf16[160,1024]{1,0:T(8,128)(2,1)S(1)}, bf16[160,1024]{1,0:T(8,128)(2,1)S(1)}, u32[]{:S(2)}, u32[]{:S(2)}) collective-permute-start(bf16[160,1024]{1,0:T(8,128)(2,1)S(1)} %get-tuple-element.35.refs_1_.refs_6_.refs_8_), channel_id=1, source_target_pairs={{0,2},{2,0},{1,3},{3,1},{4,6},{6,4},{5,7},{7,5},{8,10},{10,8},{9,1... | collective-permute-start | bytes 983048 | tf_op jit(solution)/shard_map/ppermute | solution.py:24
  36.2 11.8 %collective-permute-start.8 = (bf16[160,1024]{1,0:T(8,128)(2,1)S(1)}, bf16[160,1024]{1,0:T(8,128)(2,1)S(1)}, u32[]{:S(2)}, u32[]{:S(2)}) collective-permute-start(bf16[160,1024]{1,0:T(8,128)(2,1)S(1)} %get-tuple-element.32.refs_0_.refs_2_.refs_4_), channel_id=1, source_target_pairs={{0,1},{1,0},{2,3},{3,2},{4,5},{5,4},{6,7},{7,6},{8,9},{9,8},{10,11... | collective-permute-start | bytes 983048 | tf_op jit(solution)/shard_map/ppermute | solution.py:24
  36.2 12.5 %collective-permute-start.11 = (bf16[160,1024]{1,0:T(8,128)(2,1)S(1)}, bf16[160,1024]{1,0:T(8,128)(2,1)S(1)}, u32[]{:S(2)}, u32[]{:S(2)}) collective-permute-start(bf16[160,1024]{1,0:T(8,128)(2,1)S(1)} %get-tuple-element.35.refs_1_.refs_6_.refs_8_), channel_id=1, source_target_pairs={{0,1},{1,0},{2,3},{3,2},{4,5},{5,4},{6,7},{7,6},{8,9},{9,8},{10,11... | collective-permute-start | bytes 983048 | tf_op jit(solution)/shard_map/ppermute | solution.py:24
  43.5 5.3 %collective-permute-start.10 = (bf16[160,1024]{1,0:T(8,128)(2,1)S(1)}, bf16[160,1024]{1,0:T(8,128)(2,1)S(1)}, u32[]{:S(2)}, u32[]{:S(2)}) collective-permute-start(bf16[160,1024]{1,0:T(8,128)(2,1)S(1)} %collective-permute-done.9.refs_4_.refs_6_), channel_id=1, source_target_pairs={{0,1},{1,0},{2,3},{3,2},{4,5},{5,4},{6,7},{7,6},{8,9},{9,8},{10,11... | collective-permute-start | bytes 983048 | tf_op jit(solution)/shard_map/ppermute | solution.py:24
  47.4 2.6 %collective-permute-start.7 = (bf16[160,1024]{1,0:T(8,128)(2,1)S(1)}, bf16[160,1024]{1,0:T(8,128)(2,1)S(1)}, u32[]{:S(2)}, u32[]{:S(2)}) collective-permute-start(bf16[160,1024]{1,0:T(8,128)(2,1)S(1)} %collective-permute-done.6.refs_2_.refs_10_), channel_id=1, source_target_pairs={{0,1},{1,0},{2,3},{3,2},{4,5},{5,4},{6,7},{7,6},{8,9},{9,8},{10,11... | collective-permute-start | bytes 983048 | tf_op jit(solution)/shard_map/ppermute | solution.py:24
  47.4 4.0 %collective-permute-start.12 = (bf16[160,1024]{1,0:T(8,128)(2,1)S(1)}, bf16[160,1024]{1,0:T(8,128)(2,1)S(1)}, u32[]{:S(2)}, u32[]{:S(2)}) collective-permute-start(bf16[160,1024]{1,0:T(8,128)(2,1)S(1)} %get-tuple-element.39), channel_id=1, source_target_pairs={{4,8},{8,4},{5,9},{9,5},{6,10},{10,6},{7,11},{11,7},{20,24},{24,20... | collective-permute-start | bytes 983048 | tf_op jit(solution)/shard_map/ppermute | solution.py:528
  48.1 3.3 %collective-permute-start.13 = (bf16[160,1024]{1,0:T(8,128)(2,1)S(1)}, bf16[160,1024]{1,0:T(8,128)(2,1)S(1)}, u32[]{:S(2)}, u32[]{:S(2)}) collective-permute-start(bf16[160,1024]{1,0:T(8,128)(2,1)S(1)} %get-tuple-element.40), channel_id=1, source_target_pairs={{4,8},{8,4},{5,9},{9,5},{6,10},{10,6},{7,11},{11,7},{20,24},{24,20... | collective-permute-start | bytes 983048 | tf_op jit(solution)/shard_map/ppermute | solution.py:528
  50.7 2.9 %collective-permute-start.16 = (bf16[160,1024]{1,0:T(8,128)(2,1)S(1)}, bf16[160,1024]{1,0:T(8,128)(2,1)S(1)}, u32[]{:S(2)}, u32[]{:S(2)}) collective-permute-start(bf16[160,1024]{1,0:T(8,128)(2,1)S(1)} %couple.4), channel_id=1, source_target_pairs={{4,8},{8,4},{5,9},{9,5},{6,10},{10,6},{7,11},{11,7},{20,24},{24,20... | collective-permute-start | bytes 983048 | tf_op jit(solution)/shard_map/ppermute | solution.py:532
  52.9 2.1 %collective-permute-start.14 = (bf16[160,1024]{1,0:T(8,128)(2,1)S(1)}, bf16[160,1024]{1,0:T(8,128)(2,1)S(1)}, u32[]{:S(2)}, u32[]{:S(2)}) collective-permute-start(bf16[160,1024]{1,0:T(8,128)(2,1)S(1)} %couple.5), channel_id=1, source_target_pairs={{4,8},{8,4},{5,9},{9,5},{6,10},{10,6},{7,11},{11,7},{20,24},{24,20... | collective-permute-start | bytes 983048 | tf_op jit(solution)/shard_map/ppermute | solution.py:535
  53.7 33.8 %collective-permute-start.17 = (bf16[160,1024]{1,0:T(8,128)(2,1)S(1)}, bf16[160,1024]{1,0:T(8,128)(2,1)S(1)}, u32[]{:S(2)}, u32[]{:S(2)}) collective-permute-start(bf16[160,1024]{1,0:T(8,128)(2,1)S(1)} %add_convert_fusion.here_ref), channel_id=1, source_target_pairs={{4,0},{8,12},{5,1},{9,13},{6,2},{10,14},{7,3},{11,15},{20,16},{24,... | collective-permute-start | bytes 983048 | tf_op jit(solution)/shard_map/ppermute | solution.py:538
  55.1 39.4 %collective-permute-start.15 = (bf16[160,1024]{1,0:T(8,128)(2,1)S(1)}, bf16[160,1024]{1,0:T(8,128)(2,1)S(1)}, u32[]{:S(2)}, u32[]{:S(2)}) collective-permute-start(bf16[160,1024]{1,0:T(8,128)(2,1)S(1)} %add_convert_fusion.1.here_ref), channel_id=1, source_target_pairs={{4,0},{8,12},{5,1},{9,13},{6,2},{10,14},{7,3},{11,15},{20,16},{24,... | collective-permute-start | bytes 983048 | tf_op jit(solution)/shard_map/ppermute | solution.py:540

commit v10 on v9

--- a/solution.py
+++ b/solution.py
@@ -241,10 +241,10 @@
     return rate, jnp.sum(jnp.square(rate.astype(jnp.float32)), axis=1, keepdims=True)
 
 
-def couple_kernel(piece, row_count, col_count, before, *refs):
+def couple_kernel(piece, row_count, col_count, before, out_count, *refs):
     row_refs = refs[:row_count]
     col_refs = refs[row_count : row_count + col_count]
-    gain_ref, weight_ref, out_ref = refs[-3:]
+    gain_ref, weight_ref = refs[-out_count - 2 : -out_count]
     sums = row_count // (gain_ref.shape[1] // piece)
     row_models, row_datas = [], []
     for at in range(0, row_count, sums):
@@ -298,17 +298,21 @@
     update = jnp.dot(coupling, col_model, preferred_element_type=jnp.float32)
     if before:
         update = update + refs[row_count + col_count][...]
-    out_ref[...] = update.astype(out_ref.dtype)
-
-
-def couple(rows, cols, gains, weights, piece, before=None, kind=jnp.bfloat16):
+    for place, out_ref in enumerate(refs[-out_count:]):
+        rows = out_ref.shape[0]
+        out_ref[...] = update[place * rows : (place + 1) * rows].astype(out_ref.dtype)
+
+
+def couple(rows, cols, gains, weights, piece, outs, before=None, kind=jnp.bfloat16):
     args = [*rows, *cols] + ([] if before is None else [before]) + [gains, weights]
     height, width = gains.shape[1], weights.shape[1]
     return pl.pallas_call(
-        functools.partial(couple_kernel, piece, len(rows), len(cols), before is not None),
+        functools.partial(
+            couple_kernel, piece, len(rows), len(cols), before is not None, outs
+        ),
         in_specs=[VMEM] * len(args),
-        out_specs=VMEM,
-        out_shape=jax.ShapeDtypeStruct((height, 2 * NF), kind),
+        out_specs=[VMEM] * outs,
+        out_shape=[jax.ShapeDtypeStruct((height // outs, 2 * NF), kind)] * outs,
         compiler_params=pltpu.CompilerParams(vmem_limit_bytes=16 << 20),
         cost_estimate=pl.CostEstimate(
             flops=12 * height * width * NF,
@@ -319,40 +323,45 @@
     )(*args)
 
 
-def to_time_kernel(flag_ref, here_ref, there_ref, basis_ref, *rest):
-    out_ref = rest[-1]
-    adjoint = jnp.where(flag_ref[1] == 1, here_ref[...], there_ref[...])
+def to_time_kernel(count, flag_ref, *refs):
+    basis_ref, out_ref = refs[2 * count], refs[-1]
+    adjoint = jnp.concatenate(
+        [
+            jnp.where(flag_ref[1] == 1, here_ref[...], there_ref[...])
+            for here_ref, there_ref in zip(refs[:count], refs[count : 2 * count])
+        ],
+        axis=0,
+    )
     traces = lax.dot_general(
         adjoint, basis_ref[...], CONTRACT_LAST, preferred_element_type=jnp.float32
     )
     out_ref[...] = (traces * (1.0 / math.sqrt(NF))).astype(jnp.bfloat16)
 
 
-def to_time(place, is_inner, here, there, basis, span, rows, before):
-    half = here.shape[0]
-    wide = span
-    whole = pl.BlockSpec(here.shape, lambda j, flags: (0, 0))
-    specs = [whole, whole, pl.BlockSpec((wide, 2 * NF), lambda j, flags: (j, 0))]
-    args = [here, there, basis]
+def to_time(place, is_inner, here, there, basis, rows, before):
+    span = basis.shape[0]
+    half = sum(block.shape[0] for block in here)
+    args = [*here, *there, basis]
+    specs = [pl.BlockSpec(arg.shape, lambda j, flags: (0, 0)) for arg in args]
     aliases = {}
     if before is not None:
+        aliases = {len(args) + 1: 0}
         specs.append(pl.BlockSpec(memory_space=pl.ANY))
         args.append(before)
-        aliases = {4: 0}
-    return pl.pallas_call(
-        to_time_kernel,
+    return pl.pallas_call(
+        functools.partial(to_time_kernel, len(here)),
         grid_spec=pltpu.PrefetchScalarGridSpec(
             num_scalar_prefetch=1,
-            grid=(span // wide,),
+            grid=(1,),
             in_specs=specs,
-            out_specs=pl.BlockSpec((half, wide), lambda j, flags: (flags[0], j)),
+            out_specs=pl.BlockSpec((half, span), lambda j, flags: (flags[0], j)),
         ),
         out_shape=jax.ShapeDtypeStruct((rows, span), jnp.bfloat16),
         input_output_aliases=aliases,
+        compiler_params=pltpu.CompilerParams(vmem_limit_bytes=12 << 20),
         cost_estimate=pl.CostEstimate(
             flops=4 * half * span * NF, bytes_accessed=4 * span * NF, transcendentals=0
         ),
-        compiler_params=pltpu.CompilerParams(vmem_limit_bytes=12 << 20),
         name="to_time",
     )(jnp.stack([place, is_inner.astype(jnp.int32)]).astype(jnp.int32), *args)
 
@@ -527,23 +536,26 @@
                 cols[s, q, place] = shift(cols[s, 0, place], "pair", q)
         passed_rest.append(lax.ppermute(summed, "blk", swapped))
     cols = [cols[s, q, place] for place in range(per_half) for s, q in hops]
-    begun = couple(own, cols[:-late], own_gains, own_early, piece, None, jnp.float32)
-    own_part = couple(own, cols[-late:], own_gains, own_late, piece, begun)
-    other_rest = lax.ppermute(own_part, "blk", swapped)
+    (begun,) = couple(own, cols[:-late], own_gains, own_early, piece, 1, None, jnp.float32)
+    own_part = couple(own, cols[-late:], own_gains, own_late, piece, per_half, begun)
     other = [block for both in zip(to_pass, passed_rest) for block in both]
-    other_part = couple(other, cols, other_gains, other_weights, piece)
-    own_rest = lax.ppermute(other_part, "blk", swapped)
-    widen = lambda a: a.astype(jnp.float32)
-    other_adjoint = (widen(other_part) + widen(other_rest)).astype(jnp.bfloat16)
-    near_other = lax.ppermute(other_adjoint, "blk", outward)
-    own_adjoint = (widen(own_part) + widen(own_rest)).astype(jnp.bfloat16)
-    near_own = lax.ppermute(own_adjoint, "blk", outward)
+    other_part = couple(other, cols, other_gains, other_weights, piece, per_half)
+
+    def finish(sent, mine):
+        sums, arrived = [], []
+        for place in range(per_half):
+            rest = lax.ppermute(sent[place], "blk", swapped)
+            whole = mine[place].astype(jnp.float32) + rest.astype(jnp.float32)
+            sums.append(whole.astype(jnp.bfloat16))
+            arrived.append(lax.ppermute(sums[-1], "blk", outward))
+        return sums, arrived
+
+    first = finish(own_part, other_part)
+    second = finish(other_part, own_part)
     is_inner = (level == 1) | (level == 2)
     rows = synthetic.shape[0]
-    traces = to_time(
-        1 - side, is_inner, other_adjoint, near_other, here_basis, span, rows, None
-    )
-    return to_time(side, is_inner, own_adjoint, near_own, here_basis, span, rows, traces)
+    traces = to_time(1 - side, is_inner, *first, here_basis, rows, None)
+    return to_time(side, is_inner, *second, here_basis, rows, traces)
 
 
 def shards(*args):

time: 97 us -> 90.1 us (0.929)
  waiting for transfers between devices: 52.1 us -> 41.8 us
  starting transfers between devices: 23.8 us -> 27 us
    ppermute x4 -> x8, waiting for transfers between devices: 35.9 us -> 24 us  [the longest x4 23.9 us: finish(): arrived.append(lax.ppermute(sums[-1], 'blk', outward))]
    ppermute x4 -> x8, starting transfers between devices: 3.95 us -> 7.85 us  [the longest x4 5.17 us: finish(): arrived.append(lax.ppermute(sums[-1], 'blk', outward))]
    ppermute x6, waiting for transfers between devices: 10.6 us -> 12.2 us  [shift(): return lax.ppermute(value, axis, pairs)]
  transfers between devices with their start and end apart: 18 -> 22, of which waited for: 5 -> 6; matrix products, arithmetic and copies ran while one was open for 5% -> 5% of each run, Pallas kernels for 13% -> 12%
where the time goes in v10:
time: 90.1 us; the launch traced here: 89.5 us
  waiting for transfers between devices  41.8 us (46%)
  starting transfers between devices  27 us (30%)
  Pallas kernels  14.5 us (16%)
  local copies, waits for them, and re-layouts  4.28 us (5%)
  other arithmetic  1.26 us (1%)
    ppermute x4, waiting for transfers between devices, finish(): arrived.append(lax.ppermute(sums[-1], 'blk', outward))  23.9 us
    ppermute x4, starting transfers between devices, inner_body(): arrived.append(lax.ppermute(block, 'blk', inward))  13.8 us
    ppermute x6, waiting for transfers between devices, shift(): return lax.ppermute(value, axis, pairs)  12.2 us
    ppermute x4, waiting for transfers between devices, inner_body(): arrived.append(lax.ppermute(block, 'blk', inward))  5.58 us
    ppermute x4, starting transfers between devices, finish(): arrived.append(lax.ppermute(sums[-1], 'blk', outward))  5.17 us
    pallas_call x2, Pallas kernels, to_time(): pl.pallas_call(functools.partial(to_time_kernel, len(here)), grid_spec=pl...  4.21 us
    pallas_call x4, Pallas kernels, spectra(): pl.pallas_call(sum_kernel, in_specs=[VMEM] * len(args), out_specs=[VMEM]...  4.06 us
    dynamic_slice x3, local copies, waits for them, and re-layouts, piece_of(): lax.dynamic_slice_in_dim(source, which * half + at, piece, 0)  3.57 us
  transfers between devices with their start and end apart: 22, of which 6 were waited for; matrix products, arithmetic and copies ran while one was open for 5% of the time, Pallas kernels for 12%

profile of v10, /device:TPU:0, one launch (start us, length us, event | category | flops | bytes accessed | tf_op | source)
XLA Modules:
  0.0 89.5 jit_solution(9516989422235307923)
XLA Ops:
  0.0 1.1 %constant_dynamic-slice_fusion.8 = (bf16[80,1024]{1,0:T(8,128)(2,1)S(1)}, bf16[80,1024]{1,0:T(8,128)(2,1)S(1)}) fusion(bf16[320,1024]{1,0:T(8,128)(2,1)} %param.5, s32[]{:T(128)S(6)} %select_n.129, bf16[320,1024]{1,0:T(8,128)(2,1)} %param.4), kind=kLoop, calls=%fused_computation.52 | loop fusion | bytes 655364 | tf_op jit(solution)/shard_map/dynamic_slice | solution.py:470
  1.1 0.0 copy-start.4
  1.1 0.0 copy-start.3
  1.1 5.0 %collective-permute-start.1 = (bf16[160,1024]{1,0:T(8,128)(2,1)S(1)}, bf16[160,1024]{1,0:T(8,128)(2,1)S(1)}, u32[]{:S(2)}, u32[]{:S(2)}) collective-permute-start(bf16[160,1024]{1,0:T(8,128)(2,1)S(1)} %pad_maximum_fusion.refs_0_), channel_id=1, source_target_pairs={{0,4},{12,8},{1,5},{13,9},{2,6},{14,10},{3,7},{15,11},{16,20},{28,... | collective-permute-start | bytes 983048 | tf_op jit(solution)/shard_map/ppermute | solution.py:484
  6.2 1.8 %constant_dynamic-slice_fusion.5 = (bf16[80,1024]{1,0:T(8,128)(2,1)}, bf16[80,1024]{1,0:T(8,128)(2,1)S(1)}, bf16[80,1024]{1,0:T(8,128)(2,1)S(1)}) fusion(bf16[320,1024]{1,0:T(8,128)(2,1)} %param.4, s32[]{:T(128)S(6)} %select_n.131, s32[]{:T(128)S(6)} %select_n.154, s32[]{:T(128)S(6)} %select_n.130), kind=kLoop, calls=%fused_computation.49 | loop fusion | bytes 983052 | tf_op jit(solution)/shard_map/dynamic_slice | solution.py:470
  7.9 0.7 constant_dynamic-slice_fusion.4
  8.7 2.0 %collective-permute-start = (bf16[160,1024]{1,0:T(8,128)(2,1)S(1)}, bf16[160,1024]{1,0:T(8,128)(2,1)}, u32[]{:S(2)}, u32[]{:S(2)}) collective-permute-start(bf16[160,1024]{1,0:T(8,128)(2,1)S(1)} %pad_maximum_fusion.1.refs_0_), channel_id=1, source_target_pairs={{0,4},{12,8},{1,5},{13,9},{2,6},{14,10},{3,7},{15,11},{16,20},{28,... | collective-permute-start | bytes 983048 | tf_op jit(solution)/shard_map/ppermute | solution.py:484
  10.7 2.0 %collective-permute-start.4 = (bf16[160,1024]{1,0:T(8,128)(2,1)S(1)}, bf16[160,1024]{1,0:T(8,128)(2,1)}, u32[]{:S(2)}, u32[]{:S(2)}) collective-permute-start(bf16[160,1024]{1,0:T(8,128)(2,1)S(1)} %pad_maximum_fusion.3.refs_1_), channel_id=1, source_target_pairs={{0,4},{12,8},{1,5},{13,9},{2,6},{14,10},{3,7},{15,11},{16,20},{28,... | collective-permute-start | bytes 983048 | tf_op jit(solution)/shard_map/ppermute | solution.py:484
  12.8 0.1 stack.58
  12.9 0.1 broadcast_in_dim.8
  12.9 0.1 eq.46
  13.1 0.1 fusion.26
  13.2 0.1 concatenate.25
  13.3 0.1 copy.6
  13.4 0.1 convolution_multiply_fusion
  13.5 0.1 slice.13.refs_6_
  13.6 0.1 fusion.27
  13.7 0.5 fusion.6
  14.2 0.3 fusion.15
  14.6 1.2 %two_bases.1 = (bf16[1024,1024]{1,0:T(8,128)(2,1)S(1)}, bf16[1024,1024]{1,0:T(8,128)(2,1)S(1)}) custom-call(f32[16,512]{1,0:T(8,128)S(1)} %get-tuple-element.75.refs_0_, f32[16,512]{1,0:T(8,128)S(1)} %get-tuple-element.76.refs_1_, f32[16,512]{1,0:T(8,128)S(1)} %get-tuple-element.70.refs_2_, f32[16,512]{1,0:T(8,128)S(1)} %get-tuple-element.69.refs_3_, ...), custom_call_target="tpu_custom_call" | custom-call | flops 8388608 | bytes 4194304 | tf_op jit(solution)/shard_map/two_bases/pallas_call | solution.py:383
  15.8 0.8 own_parts.3
  16.7 0.0 copy-start.1
  16.7 0.5 spectra.4.refs_0_
  17.2 0.7 collective-permute-start.2
  17.9 4.7 %collective-permute-start.3 = (bf16[160,1024]{1,0:T(8,128)(2,1)S(1)}, bf16[160,1024]{1,0:T(8,128)(2,1)S(1)}, u32[]{:S(2)}, u32[]{:S(2)}) collective-permute-start(bf16[160,1024]{1,0:T(8,128)(2,1)S(1)} %pad_maximum_fusion.2.refs_1_), channel_id=1, source_target_pairs={{0,4},{12,8},{1,5},{13,9},{2,6},{14,10},{3,7},{15,11},{16,20},{28,... | collective-permute-start | bytes 983048 | tf_op jit(solution)/shard_map/ppermute | solution.py:484
  22.7 5.6 %collective-permute-done.4.near_ref = bf16[160,1024]{1,0:T(8,128)(2,1)} collective-permute-done((bf16[160,1024]{1,0:T(8,128)(2,1)S(1)}, bf16[160,1024]{1,0:T(8,128)(2,1)}, u32[]{:S(2)}, u32[]{:S(2)}) %collective-permute-start.4) | collective-permute-done | bytes 327712 | tf_op jit(solution)/shard_map/ppermute | solution.py:484
  28.2 1.5 %spectra.6.refs_2_ = bf16[160,1024]{1,0:T(8,128)(2,1)S(1)} custom-call(f32[160,1024]{1,0:T(8,128)S(1)} %get-tuple-element.38.part_ref, bf16[160,1024]{1,0:T(8,128)(2,1)} %collective-permute-done.4.near_ref, bf16[1024,1024]{1,0:T(8,128)(2,1)S(1)} %get-tuple-element.33.basis_ref), custom_call_target="tpu_custom_call" | custom-call | flops 335544320 | bytes 2097152 | tf_op jit(solution)/shard_map/spectra/pallas_call | solution.py:439
  29.7 0.7 collective-permute-start.5
  30.4 0.9 own_parts.2
  31.3 0.0 collective-permute-done.near_ref
  31.3 1.5 %spectra.5 = (bf16[160,1024]{1,0:T(8,128)(2,1)S(1)}, bf16[160,1024]{1,0:T(8,128)(2,1)S(1)}) custom-call(f32[160,1024]{1,0:T(8,128)S(1)} %get-tuple-element.32.part_ref, bf16[160,1024]{1,0:T(8,128)(2,1)} %collective-permute-done.near_ref, bf16[1024,1024]{1,0:T(8,128)(2,1)S(1)} %get-tuple-element.33.basis_ref, bf16[160,1024]{1,0:T(8,128)(2,1)S(1)} %collective-permute-done.2.rest_0_), custom_call_target="tpu_custom_call" | custom-call | flops 335544320 | bytes 2097152 | tf_op jit(solution)/shard_map/spectra/pallas_call | solution.py:439
  32.8 0.7 collective-permute-start.12
  33.5 1.6 %collective-permute-start.9 = (bf16[160,1024]{1,0:T(8,128)(2,1)S(1)}, bf16[160,1024]{1,0:T(8,128)(2,1)S(1)}, u32[]{:S(2)}, u32[]{:S(2)}) collective-permute-start(bf16[160,1024]{1,0:T(8,128)(2,1)S(1)} %get-tuple-element.36.refs_0_.refs_2_.refs_4_), channel_id=1, source_target_pairs={{0,2},{2,0},{1,3},{3,1},{4,6},{6,4},{5,7},{7,5},{8,10},{10,8},{9,1... | collective-permute-start | bytes 983048 | tf_op jit(solution)/shard_map/ppermute | solution.py:24
  35.1 0.0 collective-permute-done.5.rest_0_
  35.1 0.5 spectra.7
  35.6 0.6 collective-permute-start.6
  36.2 0.0 collective-permute-start.8
  36.2 0.5 collective-permute-start.11
  36.7 0.7 collective-permute-start.13
  37.4 6.7 %collective-permute-done.9.refs_4_.refs_6_ = bf16[160,1024]{1,0:T(8,128)(2,1)S(1)} collective-permute-done((bf16[160,1024]{1,0:T(8,128)(2,1)S(1)}, bf16[160,1024]{1,0:T(8,128)(2,1)S(1)}, u32[]{:S(2)}, u32[]{:S(2)}) %collective-permute-start.9) | collective-permute-done | bytes 327712 | tf_op jit(solution)/shard_map/ppermute | solution.py:24
  44.2 0.0 collective-permute-start.10
  44.2 3.9 %collective-permute-done.6.refs_2_.refs_10_ = bf16[160,1024]{1,0:T(8,128)(2,1)S(1)} collective-permute-done((bf16[160,1024]{1,0:T(8,128)(2,1)S(1)}, bf16[160,1024]{1,0:T(8,128)(2,1)S(1)}, u32[]{:S(2)}, u32[]{:S(2)}) %collective-permute-start.6) | collective-permute-done | bytes 327712 | tf_op jit(solution)/shard_map/ppermute | solution.py:24
  48.1 0.0 collective-permute-start.7
  48.1 0.0 collective-permute-done.8.refs_3_.refs_5_
  48.1 0.0 collective-permute-done.13.refs_3_
  48.1 0.0 collective-permute-done.10.refs_5_.refs_7_
  48.1 1.6 %collective-permute-done.7.refs_3_.refs_11_ = bf16[160,1024]{1,0:T(8,128)(2,1)S(1)} collective-permute-done((bf16[160,1024]{1,0:T(8,128)(2,1)S(1)}, bf16[160,1024]{1,0:T(8,128)(2,1)S(1)}, u32[]{:S(2)}, u32[]{:S(2)}) %collective-permute-start.7) | collective-permute-done | bytes 327712 | tf_op jit(solution)/shard_map/ppermute | solution.py:24
  49.7 1.5 %couple.5 = (bf16[80,1024]{1,0:T(8,128)(2,1)S(1)}, bf16[80,1024]{1,0:T(8,128)(2,1)S(1)}) custom-call(bf16[160,1024]{1,0:T(8,128)(2,1)S(1)} %spectra.4.refs_0_, bf16[160,1024]{1,0:T(8,128)(2,1)S(1)} %collective-permute-done.12.refs_1_, bf16[160,1024]{1,0:T(8,128)(2,1)S(1)} %spectra.6.refs_2_, bf16[160,1024]{1,0:T(8,128)(2,1)S(1)} %collective-permute-done.13.refs_3_, ...), custom_call_target="tpu_custom_call" | custom-call | flops 629145600 | bytes 3276800 | tf_op jit(solution)/shard_map/couple/pallas_call | solution.py:309
  51.2 0.7 collective-permute-start.14
  51.9 0.7 collective-permute-start.15
  52.6 1.2 %couple.3.refs_4_ = f32[160,1024]{1,0:T(8,128)S(1)} custom-call(bf16[160,1024]{1,0:T(8,128)(2,1)S(1)} %get-tuple-element.36.refs_0_.refs_2_.refs_4_, bf16[160,1024]{1,0:T(8,128)(2,1)S(1)} %get-tuple-element.39.refs_1_.refs_6_.refs_8_, bf16[160,1024]{1,0:T(8,128)(2,1)S(1)} %get-tuple-element.36.refs_0_.refs_2_.refs_4_, ...), custom_call_target="tpu_custom_call" | custom-call | flops 471859200 | bytes 2621440 | tf_op jit(solution)/shard_map/couple/pallas_call | solution.py:309
  53.7 0.7 couple.4
  54.4 0.7 collective-permute-start.18
  55.1 0.7 collective-permute-start.19
  55.9 1.3 %collective-permute-start.16 = (bf16[80,1024]{1,0:T(8,128)(2,1)S(1)}, bf16[80,1024]{1,0:T(8,128)(2,1)S(1)}, u32[]{:S(2)}, u32[]{:S(2)}) collective-permute-start(bf16[80,1024]{1,0:T(8,128)(2,1)S(1)} %add_convert_fusion.3.refs_0_), channel_id=1, source_target_pairs={{4,0},{8,12},{5,1},{9,13},{6,2},{10,14},{7,3},{11,15},{20,16},{24,... | collective-permute-start | bytes 491528 | tf_op jit(solution)/shard_map/ppermute | solution.py:550
  57.2 1.3 %collective-permute-start.20 = (bf16[80,1024]{1,0:T(8,128)(2,1)S(1)}, bf16[80,1024]{1,0:T(8,128)(2,1)S(1)}, u32[]{:S(2)}, u32[]{:S(2)}) collective-permute-start(bf16[80,1024]{1,0:T(8,128)(2,1)S(1)} %add_convert_fusion.1.refs_0_), channel_id=1, source_target_pairs={{4,0},{8,12},{5,1},{9,13},{6,2},{10,14},{7,3},{11,15},{20,16},{24,... | collective-permute-start | bytes 491528 | tf_op jit(solution)/shard_map/ppermute | solution.py:550
  58.6 1.3 %collective-permute-start.21 = (bf16[80,1024]{1,0:T(8,128)(2,1)S(1)}, bf16[80,1024]{1,0:T(8,128)(2,1)S(1)}, u32[]{:S(2)}, u32[]{:S(2)}) collective-permute-start(bf16[80,1024]{1,0:T(8,128)(2,1)S(1)} %add_convert_fusion.refs_1_), channel_id=1, source_target_pairs={{4,0},{8,12},{5,1},{9,13},{6,2},{10,14},{7,3},{11,15},{20,16},{24,... | collective-permute-start | bytes 491528 | tf_op jit(solution)/shard_map/ppermute | solution.py:550
  59.9 0.0 collective-permute-done.15
  59.9 1.3 %collective-permute-start.17 = (bf16[80,1024]{1,0:T(8,128)(2,1)S(1)}, bf16[80,1024]{1,0:T(8,128)(2,1)S(1)}, u32[]{:S(2)}, u32[]{:S(2)}) collective-permute-start(bf16[80,1024]{1,0:T(8,128)(2,1)S(1)} %add_convert_fusion.2.refs_1_), channel_id=1, source_target_pairs={{4,0},{8,12},{5,1},{9,13},{6,2},{10,14},{7,3},{11,15},{20,16},{24,... | collective-permute-start | bytes 491528 | tf_op jit(solution)/shard_map/ppermute | solution.py:550
  61.3 0.1 pad_add_fusion
  61.3 21.3 %collective-permute-done.20.refs_2_ = bf16[80,1024]{1,0:T(8,128)(2,1)S(1)} collective-permute-done((bf16[80,1024]{1,0:T(8,128)(2,1)S(1)}, bf16[80,1024]{1,0:T(8,128)(2,1)S(1)}, u32[]{:S(2)}, u32[]{:S(2)}) %collective-permute-start.20) | collective-permute-done | bytes 163872 | tf_op jit(solution)/shard_map/ppermute | solution.py:550
  82.6 2.6 %collective-permute-done.21.refs_3_ = bf16[80,1024]{1,0:T(8,128)(2,1)S(1)} collective-permute-done((bf16[80,1024]{1,0:T(8,128)(2,1)S(1)}, bf16[80,1024]{1,0:T(8,128)(2,1)S(1)}, u32[]{:S(2)}, u32[]{:S(2)}) %collective-permute-start.21) | collective-permute-done | bytes 163872 | tf_op jit(solution)/shard_map/ppermute | solution.py:550
  85.3 2.1 %to_time.2.refs_5_ = bf16[320,1024]{1,0:T(8,128)(2,1)} custom-call(s32[2]{0:T(128)S(1)} %get-tuple-element.78.flag_ref, bf16[80,1024]{1,0:T(8,128)(2,1)S(1)} %add_convert_fusion.1.refs_0_, bf16[80,1024]{1,0:T(8,128)(2,1)S(1)} %add_convert_fusion.refs_1_, bf16[80,1024]{1,0:T(8,128)(2,1)S(1)} %collective-permute-done.20.refs_2_, ...), custom_call_target="tpu_custom_call" | custom-call | flops 335544320 | bytes 2097152 | tf_op jit(solution)/shard_map/to_time/pallas_call | solution.py:351
  87.4 2.1 %to_time.3 = bf16[320,1024]{1,0:T(8,128)(2,1)} custom-call(s32[2]{0:T(128)S(1)} %get-tuple-element.77.flag_ref, bf16[80,1024]{1,0:T(8,128)(2,1)S(1)} %add_convert_fusion.3.refs_0_, bf16[80,1024]{1,0:T(8,128)(2,1)S(1)} %add_convert_fusion.2.refs_1_, bf16[80,1024]{1,0:T(8,128)(2,1)S(1)} %collective-permute-done.16.refs_2_, ...), custom_call_target="tpu_custom_call", output_to_operand_aliasing={{}: (6, {})} | custom-call | flops 335544320 | bytes 2097152 | tf_op jit(solution)/shard_map/to_time/pallas_call | solution.py:351
  (34 shorter events, 0.4 us)
Async XLA Ops:
  0.0 7.9 %copy-start.2 = (bf16[320,1024]{1,0:T(8,128)(2,1)S(1)}, bf16[320,1024]{1,0:T(8,128)(2,1)}, u32[]{:S(2)}) copy-start(bf16[320,1024]{1,0:T(8,128)(2,1)} %param.5) | copy-start | bytes 1966084
  1.1 11.9 %copy-start.4 = (s32[1280]{0:T(1024)S(1)}, s32[1280]{0:T(1024)}, u32[]{:S(2)}) copy-start(s32[1280]{0:T(1024)} %param.6) | copy-start | bytes 15364
  1.1 12.2 %copy-start.3 = (s32[16,16]{1,0:T(8,128)S(1)}, s32[16,16]{1,0:T(8,128)}, u32[]{:S(2)}) copy-start(s32[16,16]{1,0:T(8,128)} %param.7) | copy-start | bytes 3076
  1.1 15.5 %collective-permute-start.1 = (bf16[160,1024]{1,0:T(8,128)(2,1)S(1)}, bf16[160,1024]{1,0:T(8,128)(2,1)S(1)}, u32[]{:S(2)}, u32[]{:S(2)}) collective-permute-start(bf16[160,1024]{1,0:T(8,128)(2,1)S(1)} %pad_maximum_fusion.refs_0_), channel_id=1, source_target_pairs={{0,4},{12,8},{1,5},{13,9},{2,6},{14,10},{3,7},{15,11},{16,20},{28,... | collective-permute-start | bytes 983048 | tf_op jit(solution)/shard_map/ppermute | solution.py:484
  8.7 22.6 %collective-permute-start = (bf16[160,1024]{1,0:T(8,128)(2,1)S(1)}, bf16[160,1024]{1,0:T(8,128)(2,1)}, u32[]{:S(2)}, u32[]{:S(2)}) collective-permute-start(bf16[160,1024]{1,0:T(8,128)(2,1)S(1)} %pad_maximum_fusion.1.refs_0_), channel_id=1, source_target_pairs={{0,4},{12,8},{1,5},{13,9},{2,6},{14,10},{3,7},{15,11},{16,20},{28,... | collective-permute-start | bytes 983048 | tf_op jit(solution)/shard_map/ppermute | solution.py:484
  10.7 17.5 %collective-permute-start.4 = (bf16[160,1024]{1,0:T(8,128)(2,1)S(1)}, bf16[160,1024]{1,0:T(8,128)(2,1)}, u32[]{:S(2)}, u32[]{:S(2)}) collective-permute-start(bf16[160,1024]{1,0:T(8,128)(2,1)S(1)} %pad_maximum_fusion.3.refs_1_), channel_id=1, source_target_pairs={{0,4},{12,8},{1,5},{13,9},{2,6},{14,10},{3,7},{15,11},{16,20},{28,... | collective-permute-start | bytes 983048 | tf_op jit(solution)/shard_map/ppermute | solution.py:484
  16.7 1.2 %copy-start = (bf16[80,1024]{1,0:T(8,128)(2,1)S(1)}, bf16[80,1024]{1,0:T(8,128)(2,1)}, u32[]{:S(2)}) copy-start(bf16[80,1024]{1,0:T(8,128)(2,1)} %get-tuple-element.51) | copy-start | bytes 491524
  16.7 1.2 %copy-start.1 = (bf16[80,1024]{1,0:T(8,128)(2,1)S(1)}, bf16[80,1024]{1,0:T(8,128)(2,1)}, u32[]{:S(2)}) copy-start(bf16[80,1024]{1,0:T(8,128)(2,1)} %get-tuple-element.54) | copy-start | bytes 491524
  17.2 14.1 %collective-permute-start.2 = (bf16[160,1024]{1,0:T(8,128)(2,1)S(1)}, bf16[160,1024]{1,0:T(8,128)(2,1)S(1)}, u32[]{:S(2)}, u32[]{:S(2)}) collective-permute-start(bf16[160,1024]{1,0:T(8,128)(2,1)S(1)} %spectra.4.refs_0_), channel_id=1, source_target_pairs={{4,8},{8,4},{5,9},{9,5},{6,10},{10,6},{7,11},{11,7},{20,24},{24,20... | collective-permute-start | bytes 983048 | tf_op jit(solution)/shard_map/ppermute | solution.py:525
  17.9 17.1 %collective-permute-start.3 = (bf16[160,1024]{1,0:T(8,128)(2,1)S(1)}, bf16[160,1024]{1,0:T(8,128)(2,1)S(1)}, u32[]{:S(2)}, u32[]{:S(2)}) collective-permute-start(bf16[160,1024]{1,0:T(8,128)(2,1)S(1)} %pad_maximum_fusion.2.refs_1_), channel_id=1, source_target_pairs={{0,4},{12,8},{1,5},{13,9},{2,6},{14,10},{3,7},{15,11},{16,20},{28,... | collective-permute-start | bytes 983048 | tf_op jit(solution)/shard_map/ppermute | solution.py:484
  29.7 5.4 %collective-permute-start.5 = (bf16[160,1024]{1,0:T(8,128)(2,1)S(1)}, bf16[160,1024]{1,0:T(8,128)(2,1)S(1)}, u32[]{:S(2)}, u32[]{:S(2)}) collective-permute-start(bf16[160,1024]{1,0:T(8,128)(2,1)S(1)} %spectra.6.refs_2_), channel_id=1, source_target_pairs={{4,8},{8,4},{5,9},{9,5},{6,10},{10,6},{7,11},{11,7},{20,24},{24,20... | collective-permute-start | bytes 983048 | tf_op jit(solution)/shard_map/ppermute | solution.py:525
  32.8 3.9 %collective-permute-start.12 = (bf16[160,1024]{1,0:T(8,128)(2,1)S(1)}, bf16[160,1024]{1,0:T(8,128)(2,1)S(1)}, u32[]{:S(2)}, u32[]{:S(2)}) collective-permute-start(bf16[160,1024]{1,0:T(8,128)(2,1)S(1)} %get-tuple-element.44), channel_id=1, source_target_pairs={{4,8},{8,4},{5,9},{9,5},{6,10},{10,6},{7,11},{11,7},{20,24},{24,20... | collective-permute-start | bytes 983048 | tf_op jit(solution)/shard_map/ppermute | solution.py:537
  33.5 10.6 %collective-permute-start.9 = (bf16[160,1024]{1,0:T(8,128)(2,1)S(1)}, bf16[160,1024]{1,0:T(8,128)(2,1)S(1)}, u32[]{:S(2)}, u32[]{:S(2)}) collective-permute-start(bf16[160,1024]{1,0:T(8,128)(2,1)S(1)} %get-tuple-element.36.refs_0_.refs_2_.refs_4_), channel_id=1, source_target_pairs={{0,2},{2,0},{1,3},{3,1},{4,6},{6,4},{5,7},{7,5},{8,10},{10,8},{9,1... | collective-permute-start | bytes 983048 | tf_op jit(solution)/shard_map/ppermute | solution.py:24
  35.6 12.4 %collective-permute-start.6 = (bf16[160,1024]{1,0:T(8,128)(2,1)S(1)}, bf16[160,1024]{1,0:T(8,128)(2,1)S(1)}, u32[]{:S(2)}, u32[]{:S(2)}) collective-permute-start(bf16[160,1024]{1,0:T(8,128)(2,1)S(1)} %get-tuple-element.39.refs_1_.refs_6_.refs_8_), channel_id=1, source_target_pairs={{0,2},{2,0},{1,3},{3,1},{4,6},{6,4},{5,7},{7,5},{8,10},{10,8},{9,1... | collective-permute-start | bytes 983048 | tf_op jit(solution)/shard_map/ppermute | solution.py:24
  36.2 11.8 %collective-permute-start.8 = (bf16[160,1024]{1,0:T(8,128)(2,1)S(1)}, bf16[160,1024]{1,0:T(8,128)(2,1)S(1)}, u32[]{:S(2)}, u32[]{:S(2)}) collective-permute-start(bf16[160,1024]{1,0:T(8,128)(2,1)S(1)} %get-tuple-element.36.refs_0_.refs_2_.refs_4_), channel_id=1, source_target_pairs={{0,1},{1,0},{2,3},{3,2},{4,5},{5,4},{6,7},{7,6},{8,9},{9,8},{10,11... | collective-permute-start | bytes 983048 | tf_op jit(solution)/shard_map/ppermute | solution.py:24
  36.2 11.8 %collective-permute-start.11 = (bf16[160,1024]{1,0:T(8,128)(2,1)S(1)}, bf16[160,1024]{1,0:T(8,128)(2,1)S(1)}, u32[]{:S(2)}, u32[]{:S(2)}) collective-permute-start(bf16[160,1024]{1,0:T(8,128)(2,1)S(1)} %get-tuple-element.39.refs_1_.refs_6_.refs_8_), channel_id=1, source_target_pairs={{0,1},{1,0},{2,3},{3,2},{4,5},{5,4},{6,7},{7,6},{8,9},{9,8},{10,11... | collective-permute-start | bytes 983048 | tf_op jit(solution)/shard_map/ppermute | solution.py:24
  36.7 11.3 %collective-permute-start.13 = (bf16[160,1024]{1,0:T(8,128)(2,1)S(1)}, bf16[160,1024]{1,0:T(8,128)(2,1)S(1)}, u32[]{:S(2)}, u32[]{:S(2)}) collective-permute-start(bf16[160,1024]{1,0:T(8,128)(2,1)S(1)} %get-tuple-element.45), channel_id=1, source_target_pairs={{4,8},{8,4},{5,9},{9,5},{6,10},{10,6},{7,11},{11,7},{20,24},{24,20... | collective-permute-start | bytes 983048 | tf_op jit(solution)/shard_map/ppermute | solution.py:537
  44.2 3.9 %collective-permute-start.10 = (bf16[160,1024]{1,0:T(8,128)(2,1)S(1)}, bf16[160,1024]{1,0:T(8,128)(2,1)S(1)}, u32[]{:S(2)}, u32[]{:S(2)}) collective-permute-start(bf16[160,1024]{1,0:T(8,128)(2,1)S(1)} %collective-permute-done.9.refs_4_.refs_6_), channel_id=1, source_target_pairs={{0,1},{1,0},{2,3},{3,2},{4,5},{5,4},{6,7},{7,6},{8,9},{9,8},{10,11... | collective-permute-start | bytes 983048 | tf_op jit(solution)/shard_map/ppermute | solution.py:24
  48.1 1.6 %collective-permute-start.7 = (bf16[160,1024]{1,0:T(8,128)(2,1)S(1)}, bf16[160,1024]{1,0:T(8,128)(2,1)S(1)}, u32[]{:S(2)}, u32[]{:S(2)}) collective-permute-start(bf16[160,1024]{1,0:T(8,128)(2,1)S(1)} %collective-permute-done.6.refs_2_.refs_10_), channel_id=1, source_target_pairs={{0,1},{1,0},{2,3},{3,2},{4,5},{5,4},{6,7},{7,6},{8,9},{9,8},{10,11... | collective-permute-start | bytes 983048 | tf_op jit(solution)/shard_map/ppermute | solution.py:24
  51.2 4.6 %collective-permute-start.14 = (bf16[80,1024]{1,0:T(8,128)(2,1)S(1)}, bf16[80,1024]{1,0:T(8,128)(2,1)S(1)}, u32[]{:S(2)}, u32[]{:S(2)}) collective-permute-start(bf16[80,1024]{1,0:T(8,128)(2,1)S(1)} %get-tuple-element.48), channel_id=1, source_target_pairs={{4,8},{8,4},{5,9},{9,5},{6,10},{10,6},{7,11},{11,7},{20,24},{24,20... | collective-permute-start | bytes 491528 | tf_op jit(solution)/shard_map/ppermute | solution.py:547
  51.9 8.0 %collective-permute-start.15 = (bf16[80,1024]{1,0:T(8,128)(2,1)S(1)}, bf16[80,1024]{1,0:T(8,128)(2,1)S(1)}, u32[]{:S(2)}, u32[]{:S(2)}) collective-permute-start(bf16[80,1024]{1,0:T(8,128)(2,1)S(1)} %get-tuple-element.50), channel_id=1, source_target_pairs={{4,8},{8,4},{5,9},{9,5},{6,10},{10,6},{7,11},{11,7},{20,24},{24,20... | collective-permute-start | bytes 491528 | tf_op jit(solution)/shard_map/ppermute | solution.py:547
  54.4 2.7 %collective-permute-start.18 = (bf16[80,1024]{1,0:T(8,128)(2,1)S(1)}, bf16[80,1024]{1,0:T(8,128)(2,1)S(1)}, u32[]{:S(2)}, u32[]{:S(2)}) collective-permute-start(bf16[80,1024]{1,0:T(8,128)(2,1)S(1)} %get-tuple-element.43), channel_id=1, source_target_pairs={{4,8},{8,4},{5,9},{9,5},{6,10},{10,6},{7,11},{11,7},{20,24},{24,20... | collective-permute-start | bytes 491528 | tf_op jit(solution)/shard_map/ppermute | solution.py:547
  55.1 3.4 %collective-permute-start.19 = (bf16[80,1024]{1,0:T(8,128)(2,1)S(1)}, bf16[80,1024]{1,0:T(8,128)(2,1)S(1)}, u32[]{:S(2)}, u32[]{:S(2)}) collective-permute-start(bf16[80,1024]{1,0:T(8,128)(2,1)S(1)} %get-tuple-element.49), channel_id=1, source_target_pairs={{4,8},{8,4},{5,9},{9,5},{6,10},{10,6},{7,11},{11,7},{20,24},{24,20... | collective-permute-start | bytes 491528 | tf_op jit(solution)/shard_map/ppermute | solution.py:547
  55.9 31.5 %collective-permute-start.16 = (bf16[80,1024]{1,0:T(8,128)(2,1)S(1)}, bf16[80,1024]{1,0:T(8,128)(2,1)S(1)}, u32[]{:S(2)}, u32[]{:S(2)}) collective-permute-start(bf16[80,1024]{1,0:T(8,128)(2,1)S(1)} %add_convert_fusion.3.refs_0_), channel_id=1, source_target_pairs={{4,0},{8,12},{5,1},{9,13},{6,2},{10,14},{7,3},{11,15},{20,16},{24,... | collective-permute-start | bytes 491528 | tf_op jit(solution)/shard_map/ppermute | solution.py:550
  57.2 25.4 %collective-permute-start.20 = (bf16[80,1024]{1,0:T(8,128)(2,1)S(1)}, bf16[80,1024]{1,0:T(8,128)(2,1)S(1)}, u32[]{:S(2)}, u32[]{:S(2)}) collective-permute-start(bf16[80,1024]{1,0:T(8,128)(2,1)S(1)} %add_convert_fusion.1.refs_0_), channel_id=1, source_target_pairs={{4,0},{8,12},{5,1},{9,13},{6,2},{10,14},{7,3},{11,15},{20,16},{24,... | collective-permute-start | bytes 491528 | tf_op jit(solution)/shard_map/ppermute | solution.py:550
  58.6 26.7 %collective-permute-start.21 = (bf16[80,1024]{1,0:T(8,128)(2,1)S(1)}, bf16[80,1024]{1,0:T(8,128)(2,1)S(1)}, u32[]{:S(2)}, u32[]{:S(2)}) collective-permute-start(bf16[80,1024]{1,0:T(8,128)(2,1)S(1)} %add_convert_fusion.refs_1_), channel_id=1, source_target_pairs={{4,0},{8,12},{5,1},{9,13},{6,2},{10,14},{7,3},{11,15},{20,16},{24,... | collective-permute-start | bytes 491528 | tf_op jit(solution)/shard_map/ppermute | solution.py:550
  59.9 27.4 %collective-permute-start.17 = (bf16[80,1024]{1,0:T(8,128)(2,1)S(1)}, bf16[80,1024]{1,0:T(8,128)(2,1)S(1)}, u32[]{:S(2)}, u32[]{:S(2)}) collective-permute-start(bf16[80,1024]{1,0:T(8,128)(2,1)S(1)} %add_convert_fusion.2.refs_1_), channel_id=1, source_target_pairs={{4,0},{8,12},{5,1},{9,13},{6,2},{10,14},{7,3},{11,15},{20,16},{24,... | collective-permute-start | bytes 491528 | tf_op jit(solution)/shard_map/ppermute | solution.py:550

commit v11 on v10

--- a/solution.py
+++ b/solution.py
@@ -555,7 +555,10 @@
     is_inner = (level == 1) | (level == 2)
     rows = synthetic.shape[0]
     traces = to_time(1 - side, is_inner, *first, here_basis, rows, None)
-    return to_time(side, is_inner, *second, here_basis, rows, traces)
+    for place, (mine, arrived) in enumerate(zip(*second)):
+        block = side * per_half + place
+        traces = to_time(block, is_inner, [mine], [arrived], here_basis, rows, traces)
+    return traces
 
 
 def shards(*args):

time: 90.1 us -> 98.4 us (1.092)
  local copies, waits for them, and re-layouts: 4.28 us -> 7.6 us
  Pallas kernels: 14.5 us -> 17 us
  other arithmetic: 1.26 us -> 3.16 us
    unnamed x11 -> x31, local copies, waits for them, and re-layouts: 0.1 us -> 3.43 us
    pallas_call x2 -> x3, Pallas kernels: 4.21 us -> 6.05 us  [to_time(): pl.pallas_call(functools.partial(to_time_kernel, len(here)), grid_spec=pl...]
    convert_element_type x4, other arithmetic: 0.18 us -> 2 us  [finish(): sums.append(whole.astype(jnp.bfloat16))]
  transfers between devices with their start and end apart: 22 -> 22, of which waited for: 6 -> 6; matrix products, arithmetic and copies ran while one was open for 5% -> 7% of each run, Pallas kernels for 12% -> 13%
where the time goes in v11:
time: 98.4 us; the launch traced here: 97.7 us
  waiting for transfers between devices  41.6 us (42%)
  starting transfers between devices  27.7 us (28%)
  Pallas kernels  17 us (17%)
  local copies, waits for them, and re-layouts  7.6 us (8%)
  other arithmetic  3.16 us (3%)
    ppermute x4, waiting for transfers between devices, finish(): arrived.append(lax.ppermute(sums[-1], 'blk', outward))  23.8 us
    ppermute x4, starting transfers between devices, inner_body(): arrived.append(lax.ppermute(block, 'blk', inward))  13.8 us
    ppermute x6, waiting for transfers between devices, shift(): return lax.ppermute(value, axis, pairs)  12.2 us
    pallas_call x3, Pallas kernels, to_time(): pl.pallas_call(functools.partial(to_time_kernel, len(here)), grid_spec=pl...  6.05 us
    ppermute x4, waiting for transfers between devices, inner_body(): arrived.append(lax.ppermute(block, 'blk', inward))  5.58 us
    ppermute x4, starting transfers between devices, finish(): arrived.append(lax.ppermute(sums[-1], 'blk', outward))  5.17 us
    pallas_call x4, Pallas kernels, spectra(): pl.pallas_call(sum_kernel, in_specs=[VMEM] * len(args), out_specs=[VMEM]...  4.06 us
    pallas_call x3, Pallas kernels, couple(): pl.pallas_call(functools.partial(couple_kernel, piece, len(rows), len(col...  3.99 us
  transfers between devices with their start and end apart: 22, of which 6 were waited for; matrix products, arithmetic and copies ran while one was open for 7% of the time, Pallas kernels for 13%

profile of v11, /device:TPU:0, one launch (start us, length us, event | category | flops | bytes accessed | tf_op | source)
XLA Modules:
  0.0 97.7 jit_solution(1284332685578908547)
XLA Ops:
  0.0 1.1 %constant_dynamic-slice_fusion.8 = (bf16[80,1024]{1,0:T(8,128)(2,1)S(1)}, bf16[80,1024]{1,0:T(8,128)(2,1)S(1)}) fusion(bf16[320,1024]{1,0:T(8,128)(2,1)} %param.5, s32[]{:T(128)S(6)} %select_n.129, bf16[320,1024]{1,0:T(8,128)(2,1)} %param.4), kind=kLoop, calls=%fused_computation.52 | loop fusion | bytes 655364 | tf_op jit(solution)/shard_map/dynamic_slice | solution.py:470
  1.1 0.0 copy-start.14
  1.1 0.0 copy-start.13
  1.1 5.0 %collective-permute-start.1 = (bf16[160,1024]{1,0:T(8,128)(2,1)S(1)}, bf16[160,1024]{1,0:T(8,128)(2,1)S(1)}, u32[]{:S(2)}, u32[]{:S(2)}) collective-permute-start(bf16[160,1024]{1,0:T(8,128)(2,1)S(1)} %pad_maximum_fusion.refs_0_), channel_id=1, source_target_pairs={{0,4},{12,8},{1,5},{13,9},{2,6},{14,10},{3,7},{15,11},{16,20},{28,... | collective-permute-start | bytes 983048 | tf_op jit(solution)/shard_map/ppermute | solution.py:484
  6.2 1.8 %constant_dynamic-slice_fusion.5 = (bf16[80,1024]{1,0:T(8,128)(2,1)}, bf16[80,1024]{1,0:T(8,128)(2,1)S(1)}, bf16[80,1024]{1,0:T(8,128)(2,1)S(1)}) fusion(bf16[320,1024]{1,0:T(8,128)(2,1)} %param.4, s32[]{:T(128)S(6)} %select_n.131, s32[]{:T(128)S(6)} %select_n.154, s32[]{:T(128)S(6)} %select_n.130), kind=kLoop, calls=%fused_computation.49 | loop fusion | bytes 983052 | tf_op jit(solution)/shard_map/dynamic_slice | solution.py:470
  7.9 0.7 constant_dynamic-slice_fusion.4
  8.6 2.0 %collective-permute-start = (bf16[160,1024]{1,0:T(8,128)(2,1)S(1)}, bf16[160,1024]{1,0:T(8,128)(2,1)}, u32[]{:S(2)}, u32[]{:S(2)}) collective-permute-start(bf16[160,1024]{1,0:T(8,128)(2,1)S(1)} %pad_maximum_fusion.1.refs_0_), channel_id=1, source_target_pairs={{0,4},{12,8},{1,5},{13,9},{2,6},{14,10},{3,7},{15,11},{16,20},{28,... | collective-permute-start | bytes 983048 | tf_op jit(solution)/shard_map/ppermute | solution.py:484
  10.7 2.0 %collective-permute-start.4 = (bf16[160,1024]{1,0:T(8,128)(2,1)S(1)}, bf16[160,1024]{1,0:T(8,128)(2,1)}, u32[]{:S(2)}, u32[]{:S(2)}) collective-permute-start(bf16[160,1024]{1,0:T(8,128)(2,1)S(1)} %pad_maximum_fusion.3.refs_1_), channel_id=1, source_target_pairs={{0,4},{12,8},{1,5},{13,9},{2,6},{14,10},{3,7},{15,11},{16,20},{28,... | collective-permute-start | bytes 983048 | tf_op jit(solution)/shard_map/ppermute | solution.py:484
  12.7 0.1 stack.65
  12.8 0.1 broadcast_in_dim.8
  12.9 0.1 eq.46
  13.0 0.1 fusion.26
  13.2 0.1 concatenate.25
  13.3 0.1 copy.7
  13.4 0.1 convolution_multiply_fusion
  13.5 0.1 slice.13.refs_6_
  13.6 0.1 fusion.27
  13.7 0.5 fusion.6
  14.2 0.3 fusion.15
  14.6 1.2 %two_bases.1 = (bf16[1024,1024]{1,0:T(8,128)(2,1)S(1)}, bf16[1024,1024]{1,0:T(8,128)(2,1)S(1)}) custom-call(f32[16,512]{1,0:T(8,128)S(1)} %get-tuple-element.75.refs_0_, f32[16,512]{1,0:T(8,128)S(1)} %get-tuple-element.76.refs_1_, f32[16,512]{1,0:T(8,128)S(1)} %get-tuple-element.70.refs_2_, f32[16,512]{1,0:T(8,128)S(1)} %get-tuple-element.69.refs_3_, ...), custom_call_target="tpu_custom_call" | custom-call | flops 8388608 | bytes 4194304 | tf_op jit(solution)/shard_map/two_bases/pallas_call | solution.py:383
  15.8 0.8 own_parts.3
  16.6 0.0 copy-start.11
  16.6 0.0 collective-permute-done.1.near_ref
  16.7 0.5 spectra.4.refs_0_
  17.2 0.7 collective-permute-start.2
  17.9 4.7 %collective-permute-start.3 = (bf16[160,1024]{1,0:T(8,128)(2,1)S(1)}, bf16[160,1024]{1,0:T(8,128)(2,1)S(1)}, u32[]{:S(2)}, u32[]{:S(2)}) collective-permute-start(bf16[160,1024]{1,0:T(8,128)(2,1)S(1)} %pad_maximum_fusion.2.refs_1_), channel_id=1, source_target_pairs={{0,4},{12,8},{1,5},{13,9},{2,6},{14,10},{3,7},{15,11},{16,20},{28,... | collective-permute-start | bytes 983048 | tf_op jit(solution)/shard_map/ppermute | solution.py:484
  22.7 5.6 %collective-permute-done.4.near_ref = bf16[160,1024]{1,0:T(8,128)(2,1)} collective-permute-done((bf16[160,1024]{1,0:T(8,128)(2,1)S(1)}, bf16[160,1024]{1,0:T(8,128)(2,1)}, u32[]{:S(2)}, u32[]{:S(2)}) %collective-permute-start.4) | collective-permute-done | bytes 327712 | tf_op jit(solution)/shard_map/ppermute | solution.py:484
  28.2 1.5 %spectra.6.refs_2_ = bf16[160,1024]{1,0:T(8,128)(2,1)S(1)} custom-call(f32[160,1024]{1,0:T(8,128)S(1)} %get-tuple-element.38.part_ref, bf16[160,1024]{1,0:T(8,128)(2,1)} %collective-permute-done.4.near_ref, bf16[1024,1024]{1,0:T(8,128)(2,1)S(1)} %get-tuple-element.33.basis_ref), custom_call_target="tpu_custom_call" | custom-call | flops 335544320 | bytes 2097152 | tf_op jit(solution)/shard_map/spectra/pallas_call | solution.py:439
  29.7 0.7 collective-permute-start.5
  30.4 0.8 own_parts.2
  31.3 1.5 %spectra.5 = (bf16[160,1024]{1,0:T(8,128)(2,1)S(1)}, bf16[160,1024]{1,0:T(8,128)(2,1)S(1)}) custom-call(f32[160,1024]{1,0:T(8,128)S(1)} %get-tuple-element.32.part_ref, bf16[160,1024]{1,0:T(8,128)(2,1)} %collective-permute-done.near_ref, bf16[1024,1024]{1,0:T(8,128)(2,1)S(1)} %get-tuple-element.33.basis_ref, bf16[160,1024]{1,0:T(8,128)(2,1)S(1)} %collective-permute-done.2.rest_0_), custom_call_target="tpu_custom_call" | custom-call | flops 335544320 | bytes 2097152 | tf_op jit(solution)/shard_map/spectra/pallas_call | solution.py:439
  32.8 0.7 collective-permute-start.12
  33.5 1.6 %collective-permute-start.9 = (bf16[160,1024]{1,0:T(8,128)(2,1)S(1)}, bf16[160,1024]{1,0:T(8,128)(2,1)S(1)}, u32[]{:S(2)}, u32[]{:S(2)}) collective-permute-start(bf16[160,1024]{1,0:T(8,128)(2,1)S(1)} %get-tuple-element.36.refs_0_.refs_2_.refs_4_), channel_id=1, source_target_pairs={{0,2},{2,0},{1,3},{3,1},{4,6},{6,4},{5,7},{7,5},{8,10},{10,8},{9,1... | collective-permute-start | bytes 983048 | tf_op jit(solution)/shard_map/ppermute | solution.py:24
  35.1 0.5 spectra.7
  35.6 0.6 collective-permute-start.6
  36.2 0.5 collective-permute-start.11
  36.7 0.7 collective-permute-start.13
  37.4 6.7 %collective-permute-done.9.refs_4_.refs_6_ = bf16[160,1024]{1,0:T(8,128)(2,1)S(1)} collective-permute-done((bf16[160,1024]{1,0:T(8,128)(2,1)S(1)}, bf16[160,1024]{1,0:T(8,128)(2,1)S(1)}, u32[]{:S(2)}, u32[]{:S(2)}) %collective-permute-start.9) | collective-permute-done | bytes 327712 | tf_op jit(solution)/shard_map/ppermute | solution.py:24
  44.2 3.9 %collective-permute-done.6.refs_2_.refs_10_ = bf16[160,1024]{1,0:T(8,128)(2,1)S(1)} collective-permute-done((bf16[160,1024]{1,0:T(8,128)(2,1)S(1)}, bf16[160,1024]{1,0:T(8,128)(2,1)S(1)}, u32[]{:S(2)}, u32[]{:S(2)}) %collective-permute-start.6) | collective-permute-done | bytes 327712 | tf_op jit(solution)/shard_map/ppermute | solution.py:24
  48.1 1.6 %collective-permute-done.7.refs_3_.refs_11_ = bf16[160,1024]{1,0:T(8,128)(2,1)S(1)} collective-permute-done((bf16[160,1024]{1,0:T(8,128)(2,1)S(1)}, bf16[160,1024]{1,0:T(8,128)(2,1)S(1)}, u32[]{:S(2)}, u32[]{:S(2)}) %collective-permute-start.7) | collective-permute-done | bytes 327712 | tf_op jit(solution)/shard_map/ppermute | solution.py:24
  49.7 2.1 %couple.5 = (bf16[80,1024]{1,0:T(8,128)(2,1)S(1)}, bf16[80,1024]{1,0:T(8,128)(2,1)}) custom-call(bf16[160,1024]{1,0:T(8,128)(2,1)S(1)} %spectra.4.refs_0_, bf16[160,1024]{1,0:T(8,128)(2,1)S(1)} %collective-permute-done.12.refs_1_, bf16[160,1024]{1,0:T(8,128)(2,1)S(1)} %spectra.6.refs_2_, bf16[160,1024]{1,0:T(8,128)(2,1)S(1)} %collective-permute-done.13.refs_3_, ...), custom_call_target="tpu_custom_call" | custom-call | flops 629145600 | bytes 3276800 | tf_op jit(solution)/shard_map/couple/pallas_call | solution.py:309
  51.8 0.7 copy-done
  52.6 0.7 copy-done.8
  53.2 1.3 %collective-permute-start.14 = (bf16[80,1024]{1,0:T(8,128)(2,1)}, bf16[80,1024]{1,0:T(8,128)(2,1)}, u32[]{:S(2)}, u32[]{:S(2)}) collective-permute-start(bf16[80,1024]{1,0:T(8,128)(2,1)} %get-tuple-element.48), channel_id=1, source_target_pairs={{4,8},{8,4},{5,9},{9,5},{6,10},{10,6},{7,11},{11,7},{20,24},{24,20... | collective-permute-start | bytes 491528 | tf_op jit(solution)/shard_map/ppermute | solution.py:547
  54.5 0.7 collective-permute-start.16
  55.2 1.0 copy-done.1
  56.2 1.0 copy-done.3
  57.2 1.2 %couple.3.refs_4_ = f32[160,1024]{1,0:T(8,128)S(1)} custom-call(bf16[160,1024]{1,0:T(8,128)(2,1)S(1)} %get-tuple-element.36.refs_0_.refs_2_.refs_4_, bf16[160,1024]{1,0:T(8,128)(2,1)S(1)} %get-tuple-element.39.refs_1_.refs_6_.refs_8_, bf16[160,1024]{1,0:T(8,128)(2,1)S(1)} %get-tuple-element.36.refs_0_.refs_2_.refs_4_, ...), custom_call_target="tpu_custom_call" | custom-call | flops 471859200 | bytes 2621440 | tf_op jit(solution)/shard_map/couple/pallas_call | solution.py:309
  58.4 0.7 couple.4
  59.1 0.7 collective-permute-start.19
  59.7 0.7 collective-permute-start.18
  60.4 1.0 add_convert_fusion.3.refs_0_
  61.4 1.3 %collective-permute-start.15 = (bf16[80,1024]{1,0:T(8,128)(2,1)S(1)}, bf16[80,1024]{1,0:T(8,128)(2,1)S(1)}, u32[]{:S(2)}, u32[]{:S(2)}) collective-permute-start(bf16[80,1024]{1,0:T(8,128)(2,1)S(1)} %add_convert_fusion.3.refs_0_), channel_id=1, source_target_pairs={{4,0},{8,12},{5,1},{9,13},{6,2},{10,14},{7,3},{11,15},{20,16},{24,... | collective-permute-start | bytes 491528 | tf_op jit(solution)/shard_map/ppermute | solution.py:550
  62.7 1.3 %collective-permute-start.17 = (bf16[80,1024]{1,0:T(8,128)(2,1)S(1)}, bf16[80,1024]{1,0:T(8,128)(2,1)S(1)}, u32[]{:S(2)}, u32[]{:S(2)}) collective-permute-start(bf16[80,1024]{1,0:T(8,128)(2,1)S(1)} %add_convert_fusion.2.refs_0_), channel_id=1, source_target_pairs={{4,0},{8,12},{5,1},{9,13},{6,2},{10,14},{7,3},{11,15},{20,16},{24,... | collective-permute-start | bytes 491528 | tf_op jit(solution)/shard_map/ppermute | solution.py:550
  64.1 1.0 add_convert_fusion.refs_1_
  65.0 1.3 %collective-permute-start.21 = (bf16[80,1024]{1,0:T(8,128)(2,1)S(1)}, bf16[80,1024]{1,0:T(8,128)(2,1)S(1)}, u32[]{:S(2)}, u32[]{:S(2)}) collective-permute-start(bf16[80,1024]{1,0:T(8,128)(2,1)S(1)} %add_convert_fusion.refs_1_), channel_id=1, source_target_pairs={{4,0},{8,12},{5,1},{9,13},{6,2},{10,14},{7,3},{11,15},{20,16},{24,... | collective-permute-start | bytes 491528 | tf_op jit(solution)/shard_map/ppermute | solution.py:550
  66.4 1.3 %collective-permute-start.20 = (bf16[80,1024]{1,0:T(8,128)(2,1)S(1)}, bf16[80,1024]{1,0:T(8,128)(2,1)S(1)}, u32[]{:S(2)}, u32[]{:S(2)}) collective-permute-start(bf16[80,1024]{1,0:T(8,128)(2,1)S(1)} %add_convert_fusion.1.refs_0_), channel_id=1, source_target_pairs={{4,0},{8,12},{5,1},{9,13},{6,2},{10,14},{7,3},{11,15},{20,16},{24,... | collective-permute-start | bytes 491528 | tf_op jit(solution)/shard_map/ppermute | solution.py:550
  67.7 0.1 pad_add_fusion.2.flag_ref
  67.8 0.1 pad_add_fusion
  67.8 22.0 %collective-permute-done.21.refs_3_ = bf16[80,1024]{1,0:T(8,128)(2,1)S(1)} collective-permute-done((bf16[80,1024]{1,0:T(8,128)(2,1)S(1)}, bf16[80,1024]{1,0:T(8,128)(2,1)S(1)}, u32[]{:S(2)}, u32[]{:S(2)}) %collective-permute-start.21) | collective-permute-done | bytes 163872 | tf_op jit(solution)/shard_map/ppermute | solution.py:550
  89.9 1.8 %collective-permute-done.20.refs_2_ = bf16[80,1024]{1,0:T(8,128)(2,1)S(1)} collective-permute-done((bf16[80,1024]{1,0:T(8,128)(2,1)S(1)}, bf16[80,1024]{1,0:T(8,128)(2,1)S(1)}, u32[]{:S(2)}, u32[]{:S(2)}) %collective-permute-start.20) | collective-permute-done | bytes 163872 | tf_op jit(solution)/shard_map/ppermute | solution.py:550
  91.6 2.1 %to_time.3.refs_3_ = bf16[320,1024]{1,0:T(8,128)(2,1)} custom-call(s32[2]{0:T(128)S(1)} %pad_add_fusion.2.flag_ref, bf16[80,1024]{1,0:T(8,128)(2,1)S(1)} %add_convert_fusion.1.refs_0_, bf16[80,1024]{1,0:T(8,128)(2,1)S(1)} %add_convert_fusion.refs_1_, bf16[80,1024]{1,0:T(8,128)(2,1)S(1)} %collective-permute-done.20.refs_2_, ...), custom_call_target="tpu_custom_call" | custom-call | flops 335544320 | bytes 2097152 | tf_op jit(solution)/shard_map/to_time/pallas_call | solution.py:351
  93.7 2.0 %to_time.4.refs_3_ = bf16[320,1024]{1,0:T(8,128)(2,1)} custom-call(s32[2]{0:T(128)S(1)} %get-tuple-element.78.flag_ref, bf16[80,1024]{1,0:T(8,128)(2,1)S(1)} %add_convert_fusion.2.refs_0_, bf16[80,1024]{1,0:T(8,128)(2,1)S(1)} %collective-permute-done.17.refs_1_, ...), custom_call_target="tpu_custom_call", output_to_operand_aliasing={{}: (4, {})} | custom-call | flops 167772160 | bytes 2097152 | tf_op jit(solution)/shard_map/to_time/pallas_call | solution.py:351
  95.7 2.0 %to_time.5 = bf16[320,1024]{1,0:T(8,128)(2,1)} custom-call(s32[2]{0:T(128)S(1)} %get-tuple-element.77.flag_ref, bf16[80,1024]{1,0:T(8,128)(2,1)S(1)} %add_convert_fusion.3.refs_0_, bf16[80,1024]{1,0:T(8,128)(2,1)S(1)} %collective-permute-done.15.refs_1_, bf16[1024,1024]{1,0:T(8,128)(2,1)S(1)} %get-tuple-element.31.refs_2_.refs_4_, ...), custom_call_target="tpu_custom_call", output_to_operand_aliasing={{}: (4, {})} | custom-call | flops 167772160 | bytes 2097152 | tf_op jit(solution)/shard_map/to_time/pallas_call | solution.py:351
  (56 shorter events, 0.3 us)
Async XLA Ops:
  0.0 7.9 %copy-start.12 = (bf16[320,1024]{1,0:T(8,128)(2,1)S(1)}, bf16[320,1024]{1,0:T(8,128)(2,1)}, u32[]{:S(2)}) copy-start(bf16[320,1024]{1,0:T(8,128)(2,1)} %param.5) | copy-start | bytes 1966084
  1.1 11.9 %copy-start.14 = (s32[1280]{0:T(1024)S(1)}, s32[1280]{0:T(1024)}, u32[]{:S(2)}) copy-start(s32[1280]{0:T(1024)} %param.6) | copy-start | bytes 15364
  1.1 12.2 %copy-start.13 = (s32[16,16]{1,0:T(8,128)S(1)}, s32[16,16]{1,0:T(8,128)}, u32[]{:S(2)}) copy-start(s32[16,16]{1,0:T(8,128)} %param.7) | copy-start | bytes 3076
  1.1 15.5 %collective-permute-start.1 = (bf16[160,1024]{1,0:T(8,128)(2,1)S(1)}, bf16[160,1024]{1,0:T(8,128)(2,1)S(1)}, u32[]{:S(2)}, u32[]{:S(2)}) collective-permute-start(bf16[160,1024]{1,0:T(8,128)(2,1)S(1)} %pad_maximum_fusion.refs_0_), channel_id=1, source_target_pairs={{0,4},{12,8},{1,5},{13,9},{2,6},{14,10},{3,7},{15,11},{16,20},{28,... | collective-permute-start | bytes 983048 | tf_op jit(solution)/shard_map/ppermute | solution.py:484
  8.6 22.6 %collective-permute-start = (bf16[160,1024]{1,0:T(8,128)(2,1)S(1)}, bf16[160,1024]{1,0:T(8,128)(2,1)}, u32[]{:S(2)}, u32[]{:S(2)}) collective-permute-start(bf16[160,1024]{1,0:T(8,128)(2,1)S(1)} %pad_maximum_fusion.1.refs_0_), channel_id=1, source_target_pairs={{0,4},{12,8},{1,5},{13,9},{2,6},{14,10},{3,7},{15,11},{16,20},{28,... | collective-permute-start | bytes 983048 | tf_op jit(solution)/shard_map/ppermute | solution.py:484
  10.7 17.5 %collective-permute-start.4 = (bf16[160,1024]{1,0:T(8,128)(2,1)S(1)}, bf16[160,1024]{1,0:T(8,128)(2,1)}, u32[]{:S(2)}, u32[]{:S(2)}) collective-permute-start(bf16[160,1024]{1,0:T(8,128)(2,1)S(1)} %pad_maximum_fusion.3.refs_1_), channel_id=1, source_target_pairs={{0,4},{12,8},{1,5},{13,9},{2,6},{14,10},{3,7},{15,11},{16,20},{28,... | collective-permute-start | bytes 983048 | tf_op jit(solution)/shard_map/ppermute | solution.py:484
  16.6 1.2 %copy-start.10 = (bf16[80,1024]{1,0:T(8,128)(2,1)S(1)}, bf16[80,1024]{1,0:T(8,128)(2,1)}, u32[]{:S(2)}) copy-start(bf16[80,1024]{1,0:T(8,128)(2,1)} %get-tuple-element.51) | copy-start | bytes 491524
  16.6 1.2 %copy-start.11 = (bf16[80,1024]{1,0:T(8,128)(2,1)S(1)}, bf16[80,1024]{1,0:T(8,128)(2,1)}, u32[]{:S(2)}) copy-start(bf16[80,1024]{1,0:T(8,128)(2,1)} %get-tuple-element.54) | copy-start | bytes 491524
  17.2 14.1 %collective-permute-start.2 = (bf16[160,1024]{1,0:T(8,128)(2,1)S(1)}, bf16[160,1024]{1,0:T(8,128)(2,1)S(1)}, u32[]{:S(2)}, u32[]{:S(2)}) collective-permute-start(bf16[160,1024]{1,0:T(8,128)(2,1)S(1)} %spectra.4.refs_0_), channel_id=1, source_target_pairs={{4,8},{8,4},{5,9},{9,5},{6,10},{10,6},{7,11},{11,7},{20,24},{24,20... | collective-permute-start | bytes 983048 | tf_op jit(solution)/shard_map/ppermute | solution.py:525
  17.9 17.1 %collective-permute-start.3 = (bf16[160,1024]{1,0:T(8,128)(2,1)S(1)}, bf16[160,1024]{1,0:T(8,128)(2,1)S(1)}, u32[]{:S(2)}, u32[]{:S(2)}) collective-permute-start(bf16[160,1024]{1,0:T(8,128)(2,1)S(1)} %pad_maximum_fusion.2.refs_1_), channel_id=1, source_target_pairs={{0,4},{12,8},{1,5},{13,9},{2,6},{14,10},{3,7},{15,11},{16,20},{28,... | collective-permute-start | bytes 983048 | tf_op jit(solution)/shard_map/ppermute | solution.py:484
  29.7 5.3 %collective-permute-start.5 = (bf16[160,1024]{1,0:T(8,128)(2,1)S(1)}, bf16[160,1024]{1,0:T(8,128)(2,1)S(1)}, u32[]{:S(2)}, u32[]{:S(2)}) collective-permute-start(bf16[160,1024]{1,0:T(8,128)(2,1)S(1)} %spectra.6.refs_2_), channel_id=1, source_target_pairs={{4,8},{8,4},{5,9},{9,5},{6,10},{10,6},{7,11},{11,7},{20,24},{24,20... | collective-permute-start | bytes 983048 | tf_op jit(solution)/shard_map/ppermute | solution.py:525
  32.8 3.9 %collective-permute-start.12 = (bf16[160,1024]{1,0:T(8,128)(2,1)S(1)}, bf16[160,1024]{1,0:T(8,128)(2,1)S(1)}, u32[]{:S(2)}, u32[]{:S(2)}) collective-permute-start(bf16[160,1024]{1,0:T(8,128)(2,1)S(1)} %get-tuple-element.44), channel_id=1, source_target_pairs={{4,8},{8,4},{5,9},{9,5},{6,10},{10,6},{7,11},{11,7},{20,24},{24,20... | collective-permute-start | bytes 983048 | tf_op jit(solution)/shard_map/ppermute | solution.py:537
  33.5 10.6 %collective-permute-start.9 = (bf16[160,1024]{1,0:T(8,128)(2,1)S(1)}, bf16[160,1024]{1,0:T(8,128)(2,1)S(1)}, u32[]{:S(2)}, u32[]{:S(2)}) collective-permute-start(bf16[160,1024]{1,0:T(8,128)(2,1)S(1)} %get-tuple-element.36.refs_0_.refs_2_.refs_4_), channel_id=1, source_target_pairs={{0,2},{2,0},{1,3},{3,1},{4,6},{6,4},{5,7},{7,5},{8,10},{10,8},{9,1... | collective-permute-start | bytes 983048 | tf_op jit(solution)/shard_map/ppermute | solution.py:24
  35.6 12.4 %collective-permute-start.6 = (bf16[160,1024]{1,0:T(8,128)(2,1)S(1)}, bf16[160,1024]{1,0:T(8,128)(2,1)S(1)}, u32[]{:S(2)}, u32[]{:S(2)}) collective-permute-start(bf16[160,1024]{1,0:T(8,128)(2,1)S(1)} %get-tuple-element.39.refs_1_.refs_6_.refs_8_), channel_id=1, source_target_pairs={{0,2},{2,0},{1,3},{3,1},{4,6},{6,4},{5,7},{7,5},{8,10},{10,8},{9,1... | collective-permute-start | bytes 983048 | tf_op jit(solution)/shard_map/ppermute | solution.py:24
  36.2 11.8 %collective-permute-start.8 = (bf16[160,1024]{1,0:T(8,128)(2,1)S(1)}, bf16[160,1024]{1,0:T(8,128)(2,1)S(1)}, u32[]{:S(2)}, u32[]{:S(2)}) collective-permute-start(bf16[160,1024]{1,0:T(8,128)(2,1)S(1)} %get-tuple-element.36.refs_0_.refs_2_.refs_4_), channel_id=1, source_target_pairs={{0,1},{1,0},{2,3},{3,2},{4,5},{5,4},{6,7},{7,6},{8,9},{9,8},{10,11... | collective-permute-start | bytes 983048 | tf_op jit(solution)/shard_map/ppermute | solution.py:24
  36.2 11.8 %collective-permute-start.11 = (bf16[160,1024]{1,0:T(8,128)(2,1)S(1)}, bf16[160,1024]{1,0:T(8,128)(2,1)S(1)}, u32[]{:S(2)}, u32[]{:S(2)}) collective-permute-start(bf16[160,1024]{1,0:T(8,128)(2,1)S(1)} %get-tuple-element.39.refs_1_.refs_6_.refs_8_), channel_id=1, source_target_pairs={{0,1},{1,0},{2,3},{3,2},{4,5},{5,4},{6,7},{7,6},{8,9},{9,8},{10,11... | collective-permute-start | bytes 983048 | tf_op jit(solution)/shard_map/ppermute | solution.py:24
  36.7 11.3 %collective-permute-start.13 = (bf16[160,1024]{1,0:T(8,128)(2,1)S(1)}, bf16[160,1024]{1,0:T(8,128)(2,1)S(1)}, u32[]{:S(2)}, u32[]{:S(2)}) collective-permute-start(bf16[160,1024]{1,0:T(8,128)(2,1)S(1)} %get-tuple-element.45), channel_id=1, source_target_pairs={{4,8},{8,4},{5,9},{9,5},{6,10},{10,6},{7,11},{11,7},{20,24},{24,20... | collective-permute-start | bytes 983048 | tf_op jit(solution)/shard_map/ppermute | solution.py:537
  44.1 3.9 %collective-permute-start.10 = (bf16[160,1024]{1,0:T(8,128)(2,1)S(1)}, bf16[160,1024]{1,0:T(8,128)(2,1)S(1)}, u32[]{:S(2)}, u32[]{:S(2)}) collective-permute-start(bf16[160,1024]{1,0:T(8,128)(2,1)S(1)} %collective-permute-done.9.refs_4_.refs_6_), channel_id=1, source_target_pairs={{0,1},{1,0},{2,3},{3,2},{4,5},{5,4},{6,7},{7,6},{8,9},{9,8},{10,11... | collective-permute-start | bytes 983048 | tf_op jit(solution)/shard_map/ppermute | solution.py:24
  48.1 4.5 %copy-start.4 = (bf16[160,1024]{1,0:T(8,128)(2,1)}, bf16[160,1024]{1,0:T(8,128)(2,1)S(1)}, u32[]{:S(2)}) copy-start(bf16[160,1024]{1,0:T(8,128)(2,1)S(1)} %collective-permute-done.6.refs_2_.refs_10_) | copy-start | bytes 983044
  48.1 1.6 %collective-permute-start.7 = (bf16[160,1024]{1,0:T(8,128)(2,1)S(1)}, bf16[160,1024]{1,0:T(8,128)(2,1)S(1)}, u32[]{:S(2)}, u32[]{:S(2)}) collective-permute-start(bf16[160,1024]{1,0:T(8,128)(2,1)S(1)} %collective-permute-done.6.refs_2_.refs_10_), channel_id=1, source_target_pairs={{0,1},{1,0},{2,3},{3,2},{4,5},{5,4},{6,7},{7,6},{8,9},{9,8},{10,11... | collective-permute-start | bytes 983048 | tf_op jit(solution)/shard_map/ppermute | solution.py:24
  48.1 3.7 %copy-start.2 = (bf16[160,1024]{1,0:T(8,128)(2,1)}, bf16[160,1024]{1,0:T(8,128)(2,1)S(1)}, u32[]{:S(2)}) copy-start(bf16[160,1024]{1,0:T(8,128)(2,1)S(1)} %collective-permute-done.10.refs_5_.refs_7_) | copy-start | bytes 983044
  49.7 2.9 %copy-start.6 = (bf16[160,1024]{1,0:T(8,128)(2,1)}, bf16[160,1024]{1,0:T(8,128)(2,1)S(1)}, u32[]{:S(2)}) copy-start(bf16[160,1024]{1,0:T(8,128)(2,1)S(1)} %collective-permute-done.7.refs_3_.refs_11_) | copy-start | bytes 983044
  51.8 0.7 copy-start
  52.5 0.7 copy-start.8
  53.2 7.2 %collective-permute-start.14 = (bf16[80,1024]{1,0:T(8,128)(2,1)}, bf16[80,1024]{1,0:T(8,128)(2,1)}, u32[]{:S(2)}, u32[]{:S(2)}) collective-permute-start(bf16[80,1024]{1,0:T(8,128)(2,1)} %get-tuple-element.48), channel_id=1, source_target_pairs={{4,8},{8,4},{5,9},{9,5},{6,10},{10,6},{7,11},{11,7},{20,24},{24,20... | collective-permute-start | bytes 491528 | tf_op jit(solution)/shard_map/ppermute | solution.py:547
  54.5 8.1 %collective-permute-start.16 = (bf16[80,1024]{1,0:T(8,128)(2,1)}, bf16[80,1024]{1,0:T(8,128)(2,1)S(1)}, u32[]{:S(2)}, u32[]{:S(2)}) collective-permute-start(bf16[80,1024]{1,0:T(8,128)(2,1)} %copy-done.8), channel_id=1, source_target_pairs={{4,8},{8,4},{5,9},{9,5},{6,10},{10,6},{7,11},{11,7},{20,24},{24,20... | collective-permute-start | bytes 491528 | tf_op jit(solution)/shard_map/ppermute | solution.py:547
  55.2 1.0 copy-start.1
  56.2 1.0 copy-start.3
  57.1 1.2 %copy-start.5 = (bf16[160,1024]{1,0:T(8,128)(2,1)S(1)}, bf16[160,1024]{1,0:T(8,128)(2,1)}, u32[]{:S(2)}) copy-start(bf16[160,1024]{1,0:T(8,128)(2,1)} %copy-done.4) | copy-start | bytes 983044
  57.2 1.2 %copy-start.7 = (bf16[160,1024]{1,0:T(8,128)(2,1)S(1)}, bf16[160,1024]{1,0:T(8,128)(2,1)}, u32[]{:S(2)}) copy-start(bf16[160,1024]{1,0:T(8,128)(2,1)} %copy-done.6) | copy-start | bytes 983044
  58.3 8.0 %copy-start.9 = (bf16[80,1024]{1,0:T(8,128)(2,1)S(1)}, bf16[80,1024]{1,0:T(8,128)(2,1)}, u32[]{:S(2)}) copy-start(bf16[80,1024]{1,0:T(8,128)(2,1)} %copy-done.8) | copy-start | bytes 491524
  59.1 5.0 %collective-permute-start.19 = (bf16[80,1024]{1,0:T(8,128)(2,1)S(1)}, bf16[80,1024]{1,0:T(8,128)(2,1)S(1)}, u32[]{:S(2)}, u32[]{:S(2)}) collective-permute-start(bf16[80,1024]{1,0:T(8,128)(2,1)S(1)} %get-tuple-element.43), channel_id=1, source_target_pairs={{4,8},{8,4},{5,9},{9,5},{6,10},{10,6},{7,11},{11,7},{20,24},{24,20... | collective-permute-start | bytes 491528 | tf_op jit(solution)/shard_map/ppermute | solution.py:547
  59.7 6.6 %collective-permute-start.18 = (bf16[80,1024]{1,0:T(8,128)(2,1)S(1)}, bf16[80,1024]{1,0:T(8,128)(2,1)S(1)}, u32[]{:S(2)}, u32[]{:S(2)}) collective-permute-start(bf16[80,1024]{1,0:T(8,128)(2,1)S(1)} %get-tuple-element.49), channel_id=1, source_target_pairs={{4,8},{8,4},{5,9},{9,5},{6,10},{10,6},{7,11},{11,7},{20,24},{24,20... | collective-permute-start | bytes 491528 | tf_op jit(solution)/shard_map/ppermute | solution.py:547
  61.4 34.3 %collective-permute-start.15 = (bf16[80,1024]{1,0:T(8,128)(2,1)S(1)}, bf16[80,1024]{1,0:T(8,128)(2,1)S(1)}, u32[]{:S(2)}, u32[]{:S(2)}) collective-permute-start(bf16[80,1024]{1,0:T(8,128)(2,1)S(1)} %add_convert_fusion.3.refs_0_), channel_id=1, source_target_pairs={{4,0},{8,12},{5,1},{9,13},{6,2},{10,14},{7,3},{11,15},{20,16},{24,... | collective-permute-start | bytes 491528 | tf_op jit(solution)/shard_map/ppermute | solution.py:550
  62.7 31.0 %collective-permute-start.17 = (bf16[80,1024]{1,0:T(8,128)(2,1)S(1)}, bf16[80,1024]{1,0:T(8,128)(2,1)S(1)}, u32[]{:S(2)}, u32[]{:S(2)}) collective-permute-start(bf16[80,1024]{1,0:T(8,128)(2,1)S(1)} %add_convert_fusion.2.refs_0_), channel_id=1, source_target_pairs={{4,0},{8,12},{5,1},{9,13},{6,2},{10,14},{7,3},{11,15},{20,16},{24,... | collective-permute-start | bytes 491528 | tf_op jit(solution)/shard_map/ppermute | solution.py:550
  65.0 24.8 %collective-permute-start.21 = (bf16[80,1024]{1,0:T(8,128)(2,1)S(1)}, bf16[80,1024]{1,0:T(8,128)(2,1)S(1)}, u32[]{:S(2)}, u32[]{:S(2)}) collective-permute-start(bf16[80,1024]{1,0:T(8,128)(2,1)S(1)} %add_convert_fusion.refs_1_), channel_id=1, source_target_pairs={{4,0},{8,12},{5,1},{9,13},{6,2},{10,14},{7,3},{11,15},{20,16},{24,... | collective-permute-start | bytes 491528 | tf_op jit(solution)/shard_map/ppermute | solution.py:550
  66.4 25.2 %collective-permute-start.20 = (bf16[80,1024]{1,0:T(8,128)(2,1)S(1)}, bf16[80,1024]{1,0:T(8,128)(2,1)S(1)}, u32[]{:S(2)}, u32[]{:S(2)}) collective-permute-start(bf16[80,1024]{1,0:T(8,128)(2,1)S(1)} %add_convert_fusion.1.refs_0_), channel_id=1, source_target_pairs={{4,0},{8,12},{5,1},{9,13},{6,2},{10,14},{7,3},{11,15},{20,16},{24,... | collective-permute-start | bytes 491528 | tf_op jit(solution)/shard_map/ppermute | solution.py:550
